TPU v7x, 256 devices: a 4x2x16 block of a 4x16x16 slice. The times are simulated.
256 devices in a mesh: rep: 2 (over y), ep: 128 (over x, z, core).
Axes of the slice: x: 4, y: 2, z: 16, core: 2. Of those that a mesh axis runs over, the one named last changes fastest.
The devices are a block of a 4x16x16 slice.
Arguments:
- cache_kv: bfloat16 [512, 2048, 576], P(('rep', 'ep')), parts along dimension 0, may hold values from -6 to 6
- new_kv: bfloat16 [512, 2, 576], P(('rep', 'ep')), parts along dimension 0, may hold values from -6 to 6
- queries: bfloat16 [512, 2, 64, 576], P(('rep', 'ep')), parts along dimension 0, may hold values from -256 to 256
- lengths: int32 [512], P(('rep', 'ep')), parts along dimension 0, may hold values from 256 to 2048
- resid: bfloat16 [512, 2, 7168], P(('rep', 'ep')), parts along dimension 0, may hold values from -18 to 18
- value_up: bfloat16 [512, 8192], P(None, 'ep'), may hold values from -1.5 to 1.5
- out_proj: bfloat16 [8192, 7168], P('ep'), may hold values from -0.09375 to 0.09375
- norm_gain: bfloat16 [7168], replicated, may hold values from 0.25 to 1.75
- router: bfloat16 [7168, 16], replicated, may hold values from -0.0625 to 0.0625
- expert_ids: int32 [512, 2, 8], P(('rep', 'ep')), parts along dimension 0, may hold values from 0 to 15, as said below
- slots: int32 [512, 2, 8], P(('rep', 'ep')), parts along dimension 0, may hold values from 0 to 3, as said below
- w_gate: bfloat16 [7168, 16384], P(None, 'ep'), may hold values from -0.0625 to 0.0625
- w_up: bfloat16 [7168, 16384], P(None, 'ep'), may hold values from -0.0625 to 0.0625
- w_down: bfloat16 [16384, 7168], P('ep'), may hold values from -0.1875 to 0.1875
Outputs:
- mixed: bfloat16 [512, 2, 7168], P(('rep', 'ep')), parts along dimension 0
There are 2 independent parts, one for each index of `rep`. A program takes and returns all parts, laid end to end along the dimension named above; an argument that names none is the same for every part. Nothing has to cross between parts.
Inputs may be any that keep to these rules, and one draw needn't show every extreme that they name: `expert_ids`: each row names 8 different experts. In each aligned block of 4 rows (the rows of one device), the rows that name the same expert carry the distinct slots 0 up to their number minus one for it; in every block some expert is named by all 4 rows.
All inputs are finite; a program needn't handle non-finite values.
Results may differ from a plain program's by a relative error of at most 0.0065.
Values may be sent and summed in bfloat16 or wider, within the bound.
No kernel may reach another device: no remote copies, remote signals or barrier semaphores. Data moves between devices by JAX's collectives and lax.ppermute only.
A program may use at most 128 MiB of HBM per device.

v0:
```python
import functools
import math

import jax
import jax.numpy as jnp
from jax import lax
from jax.experimental import pallas as pl
from jax.experimental.pallas import tpu as pltpu
from jax.sharding import Mesh
from jax.sharding import PartitionSpec as P


D = 7168
LAT = 512
VH = 128
EXPERTS = 16
TOP = 8
CAP = 2
QK = 192

CORES = 2
NEAR = 4
FAR = 4
RING = NEAR * FAR
SLOTS = RING * CAP
EXTRA = 128

route_scale = 2.827
norm_eps = 1e-06


ZAX = ("zb", "j")
f32, bf16 = jnp.float32, jnp.bfloat16
NT = (((1,), (1,)), ((), ()))


def shift_x(a, step):
    n = lax.axis_size("x")
    return lax.ppermute(a, "x", [(i, (i + step) % n) for i in range(n)])


def shift_z(a, step):
    return lax.ppermute(a, ZAX, [(i, (i + step) % RING) for i in range(RING)])


def swap_core(a):
    return lax.ppermute(a, "c", [(i, (i + 1) % CORES) for i in range(CORES)])


def iota(shape, axis):
    return lax.broadcasted_iota(jnp.int32, shape, axis)


def one_hot(mask):
    return jnp.where(mask, 1.0, 0.0).astype(bf16)


def column(hop, x, nx):
    step = jnp.where(hop == 1, nx - 1, jnp.where(hop == 2, 1, jnp.where(hop == 3, 2, 0)))
    return lax.rem(x + step, nx)


def chip_at(place, j):
    group, block = place // FAR, lax.rem(place, FAR)
    step = jnp.where(group == 2, NEAR - 1, jnp.where(group == 3, 2, group))
    return NEAR * block + lax.rem(j + step, NEAR)


def smem():
    return pl.BlockSpec(memory_space=pltpu.SMEM)


def vmem():
    return pl.BlockSpec(memory_space=pltpu.VMEM)


def hbm():
    return pl.BlockSpec(memory_space=pltpu.HBM)


def params(mib):
    return pltpu.CompilerParams(vmem_limit_bytes=mib << 20)


def cost(flops, nbytes):
    return pl.CostEstimate(flops=flops, bytes_accessed=nbytes, transcendentals=0)


def context_kernel(nx, where_ref, lengths, keys, queries, new, out, held):
    seq = pl.program_id(0)
    seqs = pl.num_programs(0)
    steps, heads = queries.shape[1], queries.shape[2]
    count = steps * heads
    scale = 1.0 / math.sqrt(QK)
    query = queries[0].reshape(count, queries.shape[3])
    score = jnp.dot(query, keys[0], preferred_element_type=f32) * scale
    score = jnp.where(iota(score.shape, 1) < lengths[seq], score, -jnp.inf)
    wide = query.astype(f32)
    step_of = iota((count, 1), 0) // heads
    latest = []
    peak = jnp.max(score, axis=1, keepdims=True)
    for t in range(steps):
        key = new[0, t : t + 1, :].astype(f32)
        got = jnp.sum(wide * key, axis=1, keepdims=True) * scale
        got = jnp.where(step_of >= t, got, -jnp.inf)
        latest.append(got)
        peak = jnp.maximum(peak, got)
    probs = jnp.exp(score - peak)
    total = jnp.sum(probs, axis=1, keepdims=True)
    latest = [jnp.exp(got - peak) for got in latest]
    for got in latest:
        total = total + got
    share = 1.0 / total
    probs = (probs * share).astype(bf16)
    context = lax.dot_general(probs, keys[0, :LAT, :], NT, preferred_element_type=f32)
    for t, got in enumerate(latest):
        part = (got * share).astype(bf16).astype(f32)
        context = context + part * new[0, t : t + 1, :LAT].astype(f32)
    held[pl.ds(pl.multiple_of(seq * count, count), count), :] = context.astype(bf16)

    @pl.when(seq == seqs - 1)
    def _():
        rows = held.shape[0]
        tok = rows // heads
        shape = (rows, rows)
        to, source = iota(shape, 0), iota(shape, 1)
        hop = lax.rem(to // tok, nx)
        head = column(hop, where_ref[0], nx) * RING + to // (tok * nx)
        take = (lax.rem(to, tok) == source // heads) & (head == lax.rem(source, heads))
        out[...] = jnp.dot(one_hot(take), held[...], preferred_element_type=f32).astype(bf16)


def context_rows(where, nx, cache_kv, new_kv, queries, lengths):
    seqs, length, width = cache_kv.shape
    steps, heads = queries.shape[1:3]
    rows = seqs * steps * heads
    keys = jnp.swapaxes(cache_kv, 1, 2)
    return pl.pallas_call(
        functools.partial(context_kernel, nx),
        grid=(seqs,),
        out_shape=jax.ShapeDtypeStruct((rows, LAT), bf16),
        in_specs=[
            smem(),
            smem(),
            pl.BlockSpec((1, width, length), lambda b: (b, 0, 0)),
            pl.BlockSpec((1, steps, heads, width), lambda b: (b, 0, 0, 0)),
            pl.BlockSpec((1, steps, width), lambda b: (b, 0, 0)),
        ],
        out_specs=pl.BlockSpec((rows, LAT), lambda b: (0, 0)),
        scratch_shapes=[pltpu.VMEM((rows, LAT), bf16)],
        compiler_params=params(24),
        cost_estimate=cost(2 * rows * length * (width + LAT), 2 * cache_kv.size),
        name="context_rows",
    )(where, lengths, keys, queries, new_kv)


OUT_TILE = 512


def put_rows(got, outs, c, n, half):
    own, right, left, ahead, behind = outs
    size = own.shape[0]
    cols = pl.ds(c * half + n * OUT_TILE, OUT_TILE)
    own[:, cols] = got[:size]
    right[:, cols] = got[size : 2 * size].astype(bf16)
    left[:, cols] = got[2 * size : 3 * size].astype(bf16)
    last = ahead if c == 0 else behind
    last[:, pl.ds(n * OUT_TILE, OUT_TILE)] = got[3 * size :].astype(bf16)


def row_shapes(size, dim):
    return (
        jax.ShapeDtypeStruct((size, dim), f32),
        jax.ShapeDtypeStruct((size, dim), bf16),
        jax.ShapeDtypeStruct((size, dim), bf16),
        jax.ShapeDtypeStruct((size, dim // 2), bf16),
        jax.ShapeDtypeStruct((size, dim // 2), bf16),
    )


def attend_kernel(tok, nx, count, where_ref, arrived, *refs):
    pieces = refs[:count]
    outs = refs[count : count + 5]
    up, rows, up_sem, row_sem = refs[count + 5 :]
    half = rows.shape[1] // 2
    starts = [0]
    for piece in pieces:
        starts.append(starts[-1] + piece.shape[0])

    def up_copy(i):
        return pltpu.make_async_copy(
            pieces[i].at[:, pl.ds(0, LAT)],
            up.at[pl.ds(starts[i], pieces[i].shape[0])],
            up_sem.at[i],
        )

    def row_copy(c, i):
        return pltpu.make_async_copy(
            pieces[i].at[:, pl.ds(LAT + c * half, half)],
            rows.at[pl.ds(starts[i], pieces[i].shape[0]), pl.ds(c * half, half)],
            row_sem.at[c, i],
        )

    for i in range(count):
        up_copy(i).start()
    for c in range(2):
        for i in range(count):
            row_copy(c, i).start()
    for i in range(count):
        up_copy(i).wait()
    values = lax.dot_general(arrived[...], up[...], NT, preferred_element_type=f32)
    hop = lax.rem(iota(values.shape, 0) // tok, nx)
    values = jnp.where(hop == iota(values.shape, 1) // VH, values, 0.0).astype(bf16)
    shape = (RING * tok, arrived.shape[0])
    place, source = iota(shape, 0), iota(shape, 1)
    take = (source // (tok * nx) == chip_at(place // tok, where_ref[2])) & (
        lax.rem(source, tok) == lax.rem(place, tok)
    )
    values = jnp.dot(one_hot(take), values, preferred_element_type=f32).astype(bf16)
    for c in range(2):
        for i in range(count):
            row_copy(c, i).wait()
        for n in range(half // OUT_TILE):
            cols = pl.ds(c * half + n * OUT_TILE, OUT_TILE)
            put_rows(jnp.dot(values, rows[:, cols], preferred_element_type=f32), outs, c, n, half)


def attend_out(where, nx, arrived, pieces, tok):
    depth = sum(p.shape[0] for p in pieces)
    dim = pieces[0].shape[1] - LAT
    count = len(pieces)
    return pl.pallas_call(
        functools.partial(attend_kernel, tok, nx, count),
        out_shape=row_shapes(FAR * tok, dim),
        in_specs=[smem(), vmem()] + [hbm()] * count,
        out_specs=[vmem()] * 5,
        scratch_shapes=[
            pltpu.VMEM((depth, LAT), bf16),
            pltpu.VMEM((depth, dim), bf16),
            pltpu.SemaphoreType.DMA((count,)),
            pltpu.SemaphoreType.DMA((2, count)),
        ],
        compiler_params=params(16),
        cost_estimate=cost(8 * RING * tok * depth * dim, 2 * depth * dim),
        name="attend_out",
    )(where, arrived, *pieces)


def dispatch_kernel(tok, nx, where_ref, tokens, *refs):
    outs, spread = refs[:nx], refs[nx]
    count, width = tokens.shape
    dim = width - EXTRA
    table = tokens[:, pl.ds(dim, EXTRA)]
    shape = (nx * CAP, EXTRA)
    row, place = iota(shape, 0), iota(shape, 1)
    expert = FAR * column(row // CAP, where_ref[0], nx) + where_ref[1]
    hot = one_hot(place == lax.rem(row, CAP) * EXPERTS + expert)
    got = lax.dot_general(hot, table, NT, preferred_element_type=f32)
    shape = (SLOTS, count)
    slot, token = iota(shape, 0), iota(shape, 1)
    parts = []
    for r in range(nx):
        sel = jnp.where(lax.rem(slot, CAP) == 0, got[CAP * r : CAP * r + 1], got[CAP * r + 1 : CAP * r + 2])
        parts.append(jnp.where(slot // CAP == token // tok, sel, 0.0))
    sel = jnp.concatenate(parts, axis=0).astype(bf16)
    for n in range(pl.cdiv(width, OUT_TILE)):
        cols = pl.ds(n * OUT_TILE, min(OUT_TILE, width - n * OUT_TILE))
        rows = jnp.dot(sel, tokens[:, cols], preferred_element_type=f32).astype(bf16)
        for r in range(nx):
            outs[r][:, cols] = rows[r * SLOTS : (r + 1) * SLOTS]
    shape = (count, count)
    place, token = iota(shape, 0), iota(shape, 1)
    take = (token // tok == chip_at(place // tok, where_ref[2])) & (
        lax.rem(token, tok) == lax.rem(place, tok)
    )
    spread[...] = lax.dot_general(one_hot(take), sel, NT, preferred_element_type=f32).astype(bf16)


def dispatch(where, nx, tokens, tok):
    count, width = tokens.shape
    return pl.pallas_call(
        functools.partial(dispatch_kernel, tok, nx),
        out_shape=(jax.ShapeDtypeStruct((SLOTS, width), bf16),) * nx
        + (jax.ShapeDtypeStruct((count, nx * SLOTS), bf16),),
        in_specs=[smem(), vmem()],
        out_specs=[vmem()] * (nx + 1),
        compiler_params=params(12),
        cost_estimate=cost(2 * nx * SLOTS * count * width, 4 * count * width),
        name="dispatch",
    )(where, tokens)


CHUNKS = 7


def expert_kernel(groups, where_ref, *refs):
    tokens = refs[:groups]
    gate_a, gate_b, up_a, up_b, down_a, down_b = refs[groups : groups + 6]
    outs = refs[groups + 6 : 2 * groups + 6]
    wide, deep, held, first_sem, second_sem = refs[2 * groups + 6 :]
    dim, part = gate_a.shape
    chunk = dim // CHUNKS

    def first(k, i):
        return pltpu.make_async_copy(
            (gate_a, gate_b, up_a, up_b)[i].at[pl.ds(k * chunk, chunk)],
            wide.at[pl.ds(k * chunk, chunk), pl.ds(i * part, part)],
            first_sem.at[k, i],
        )

    def second(i):
        return pltpu.make_async_copy(
            (down_a, down_b)[i], deep.at[pl.ds(i * part, part)], second_sem.at[i]
        )

    for k in range(CHUNKS):
        for i in range(4):
            first(k, i).start()
    for i in range(2):
        second(i).start()
    rows = groups * SLOTS
    if groups > 1:
        for g, ref in enumerate(tokens):
            held[pl.ds(g * SLOTS, SLOTS)] = ref[...]
    else:
        held = tokens[0]
    total = jnp.zeros((rows, 4 * part), f32)
    for k in range(CHUNKS):
        for i in range(4):
            first(k, i).wait()
        cols = pl.ds(k * chunk, chunk)
        total = total + jnp.dot(held[:, cols], wide[cols, :], preferred_element_type=f32)
    gate, upward = total[:, : 2 * part], total[:, 2 * part :]
    act = (gate / (1.0 + jnp.exp(-gate)) * upward).astype(bf16)
    shape = (EXTRA, EXTRA)
    expert = FAR * where_ref[0] + where_ref[1]
    from_share = iota(shape, 0) - CAP * EXPERTS
    hot = (from_share >= 0) & (from_share < 3 * EXPERTS) & (lax.rem(from_share + EXTRA, EXPERTS) == expert)
    share = jnp.dot(held[:, pl.ds(dim, EXTRA)], one_hot(hot), preferred_element_type=f32)[:, :1]
    for i in range(2):
        second(i).wait()
    for k in range(CHUNKS):
        cols = pl.ds(k * chunk, chunk)
        got = jnp.dot(act, deep[:, cols], preferred_element_type=f32) * share
        for g in range(groups):
            outs[g][:, cols] = got[g * SLOTS : (g + 1) * SLOTS].astype(bf16)


def expert_part(where, tokens, weights):
    dim, part = weights[0].shape
    groups = len(tokens)
    rows = groups * SLOTS
    return pl.pallas_call(
        functools.partial(expert_kernel, groups),
        out_shape=(jax.ShapeDtypeStruct((SLOTS, dim), bf16),) * groups,
        in_specs=[smem()] + [vmem()] * groups + [hbm()] * 6,
        out_specs=[vmem()] * groups,
        scratch_shapes=[
            pltpu.VMEM((dim, 4 * part), bf16),
            pltpu.VMEM((2 * part, dim), bf16),
            pltpu.VMEM((rows if groups > 1 else 16, dim + EXTRA), bf16),
            pltpu.SemaphoreType.DMA((CHUNKS, 4)),
            pltpu.SemaphoreType.DMA((2,)),
        ],
        compiler_params=params(20),
        cost_estimate=cost(12 * rows * dim * part, 12 * dim * part),
        name="expert_part",
    )(where, *tokens, *weights)


def collect_kernel(count, spread, *refs):
    parts, outs = refs[:count], refs[count:]
    half = parts[0].shape[1] // 2
    for c in range(2):
        for n in range(half // OUT_TILE):
            cols = pl.ds(c * half + n * OUT_TILE, OUT_TILE)
            rows = jnp.concatenate([part[:, cols] for part in parts], axis=0)
            put_rows(jnp.dot(spread[...], rows, preferred_element_type=f32), outs, c, n, half)


def collect(spread, parts, tok):
    dim = parts[0].shape[1]
    count = len(parts)
    return pl.pallas_call(
        functools.partial(collect_kernel, count),
        out_shape=row_shapes(FAR * tok, dim),
        in_specs=[vmem()] * (count + 1),
        out_specs=[vmem()] * 5,
        compiler_params=params(12),
        cost_estimate=cost(2 * spread.size * dim, 8 * FAR * tok * dim),
        name="collect",
    )(spread, *parts)


def reduce_z(own, right, left, ahead, behind):
    size, dim = own.shape
    right = shift_z(right, 1)
    left = shift_z(left, -1)
    ahead = shift_z(ahead, 2)
    behind = shift_z(behind, -2)
    total = own + right.astype(f32) + left.astype(f32)
    total = total + jnp.concatenate([ahead, behind], axis=1).astype(f32)
    sent = total.astype(bf16).reshape(FAR, size // FAR, dim)
    got = lax.all_to_all(sent, "zb", split_axis=0, concat_axis=0, tiled=True)
    return jnp.sum(got.astype(f32), axis=0)


def layer(
    cache_kv,
    new_kv,
    queries,
    lengths,
    resid,
    value_up,
    out_proj,
    norm_gain,
    router,
    expert_ids,
    slots,
    w_gate,
    w_up,
    w_down,
):
    nx = lax.axis_size("x")
    seqs, steps = queries.shape[:2]
    tok = seqs * steps
    where = jnp.stack([lax.axis_index(a) for a in ("x", "zb", "j")]).astype(jnp.int32)

    mine = jnp.concatenate([value_up.T, out_proj], axis=1)
    rows = mine.shape[0]
    from_left = shift_x(mine, 1)
    from_right = shift_x(mine, -1)

    outgoing = context_rows(where, nx, cache_kv, new_kv, queries, lengths)
    from_left, from_right, _ = lax.optimization_barrier((from_left, from_right, outgoing))
    far_a = shift_x(from_left[: rows // 2], 1)
    far_b = shift_x(from_right[rows // 2 :], -1)
    pieces = [mine, swap_core(mine), from_left, swap_core(from_left), from_right, swap_core(from_right)]
    pieces += [far_a, far_b, swap_core(far_a), swap_core(far_b)]
    ffn = (w_gate, swap_core(w_gate), w_up, swap_core(w_up), w_down, swap_core(w_down))
    arrived = lax.all_to_all(
        outgoing.reshape(RING, nx * tok, LAT), ZAX, split_axis=0, concat_axis=0, tiled=True
    )
    arrived = arrived.reshape(RING * nx * tok, LAT)
    attended = reduce_z(*attend_out(where, nx, arrived, pieces, tok))

    hidden = resid.reshape(tok, D).astype(f32) + attended
    mean_square = jnp.mean(hidden * hidden, axis=-1, keepdims=True)
    normed = (hidden * lax.rsqrt(mean_square + norm_eps) * norm_gain.astype(f32)).astype(bf16)

    route_ids = expert_ids.reshape(tok, TOP)
    route_slots = slots.reshape(tok, TOP)
    logits = jnp.dot(normed, router, preferred_element_type=f32)
    is_pick = route_ids[:, :, None] == jnp.arange(EXPERTS, dtype=jnp.int32)[None, None, :]
    picked = jnp.sum(jnp.where(is_pick, logits[:, None, :], 0.0), axis=-1)
    gates = jax.nn.sigmoid(picked)
    weights = route_scale * gates / jnp.sum(gates, axis=1, keepdims=True)
    share = jnp.sum(jnp.where(is_pick, weights[:, :, None], 0.0), axis=1)
    slot = jnp.sum(jnp.where(is_pick, route_slots[:, :, None] + 1, 0), axis=1)
    places = [(slot == s + 1).astype(bf16) for s in range(CAP)]
    high = share.astype(bf16)
    rest = share - high.astype(f32)
    middle = rest.astype(bf16)
    low = (rest - middle.astype(f32)).astype(bf16)
    extra = jnp.concatenate(places + [high, middle, low], axis=1)
    extra = jnp.pad(extra, ((0, 0), (0, EXTRA - extra.shape[1])))
    payload = jnp.concatenate([normed, extra], axis=1)

    ring = lax.all_gather(payload, ZAX, axis=0, tiled=True)
    *sent, spread = dispatch(where, nx, ring, tok)
    from_right = shift_x(sent[1], -1)
    from_left = shift_x(sent[2], 1)
    from_far = shift_x(sent[3], 2)
    done = expert_part(where, (sent[0], from_right, from_left), ffn)
    back_left = shift_x(done[1], 1)
    back_right = shift_x(done[2], -1)
    (far_done,) = expert_part(where, (from_far,), ffn)
    back_far = shift_x(far_done, 2)
    expert_mix = reduce_z(*collect(spread, (done[0], back_left, back_right, back_far), tok))
    mixed = (hidden + expert_mix).astype(bf16)
    return mixed.reshape(resid.shape)


def solution(mesh):
    chips = mesh.shape["ep"] // (RING * CORES)
    grid = mesh.devices.reshape(mesh.shape["rep"], chips, FAR, NEAR, CORES)
    fine = Mesh(grid, ("rep", "x", "zb", "j", "c"))
    ep = ("x", "zb", "j", "c")
    both = ("rep",) + ep
    return jax.shard_map(
        layer,
        mesh=fine,
        in_specs=(
            P(both, None, None),
            P(both, None, None),
            P(both, None, None, None),
            P(both),
            P(both, None, None),
            P(None, ep),
            P(ep, None),
            P(),
            P(),
            P(both, None, None),
            P(both, None, None),
            P(None, ep),
            P(None, ep),
            P(ep, None),
        ),
        out_specs=P(both, None, None),
        check_vma=False,
    )
```

profile of v0, /device:TPU:40, one launch (start us, length us, event | category | flops | bytes accessed | tf_op | source)
XLA Modules:
  0.0 222.6 jit_solution(17480800196786890789)
XLA Ops:
  0.0 1.3 pad_maximum_fusion.refs_0_
  1.3 1.7 collective-permute-start.1
  3.1 1.7 collective-permute-start.2
  4.8 0.1 pad_add_fusion.where_ref
  4.8 2.3 %copy-done.4 = bf16[2,2048,576]{1,2,0:T(8,128)(2,1)S(1)} copy-done((bf16[2,2048,576]{1,2,0:T(8,128)(2,1)S(1)}, bf16[2,2048,576]{1,2,0:T(8,128)(2,1)}, u32[]{:S(2)}) %copy-start.4) | copy-done | bytes 4718616
  7.2 4.0 %context_rows.1 = bf16[256,512]{1,0:T(8,128)(2,1)S(1)} custom-call(s32[3]{0:T(128)S(1)} %pad_add_fusion.where_ref, s32[2]{0:T(128)S(1)} %copy-done.8, bf16[2,576,2048]{2,1,0:T(8,128)(2,1)S(1)} %bitcast.13, bf16[2,2,64,576]{3,2,1,0:T(8,128)(2,1)S(1)} %copy-done.6, bf16[2,2,576]{2,1,0:T(2,128)(2,1)S(1)} %copy-done.7), custom_call_target="tpu_custom_call" | custom-call | flops 1140850688 | bytes 4718592 | tf_op jit(solution)/shard_map/context_rows/pallas_call | solution.py:138
  11.2 0.7 copy-done.5
  11.9 24.0 %all-to-all-start = ((bf16[16,16,512]{2,1,0:T(8,128)(2,1)}), bf16[16,16,512]{2,1,0:T(8,128)(2,1)S(1)}, u32[]{:S(2)}, u32[]{:S(2)}) async-start(bf16[16,16,512]{2,1,0:T(8,128)(2,1)} %bitcast.15), calls=%async_computation | async-start | bytes 524288 | tf_op jit(solution)/shard_map/all_to_all | solution.py:441
  36.0 0.5 collective-permute-start.5
  36.5 3.0 %collective-permute-start.6 = (bf16[32,7680]{1,0:T(8,128)(2,1)S(1)}, bf16[32,7680]{1,0:T(8,128)(2,1)}, u32[]{:S(2)}, u32[]{:S(2)}) collective-permute-start(bf16[32,7680]{1,0:T(8,128)(2,1)S(1)} %slice.7), channel_id=1, source_target_pairs={{0,96},{32,0},{64,32},{96,64},{1,97},{33,1},{65,33},{97,65},{2,98}... | collective-permute-start | bytes 1474568 | tf_op jit(solution)/shard_map/ppermute | solution.py:39
  39.5 0.5 collective-permute-start.4
  40.0 10.8 %collective-permute-done.5.refs_6_ = bf16[32,7680]{1,0:T(8,128)(2,1)} collective-permute-done((bf16[32,7680]{1,0:T(8,128)(2,1)S(1)}, bf16[32,7680]{1,0:T(8,128)(2,1)}, u32[]{:S(2)}, u32[]{:S(2)}) %collective-permute-start.5) | collective-permute-done | bytes 491552 | tf_op jit(solution)/shard_map/ppermute | solution.py:39
  50.7 0.5 collective-permute-start.8
  51.3 3.3 %all-to-all-done = bf16[16,16,512]{2,1,0:T(8,128)(2,1)S(1)} async-done(((bf16[16,16,512]{2,1,0:T(8,128)(2,1)}), bf16[16,16,512]{2,1,0:T(8,128)(2,1)S(1)}, u32[]{:S(2)}, u32[]{:S(2)}) %all-to-all-start) | async-done | bytes 262176 | tf_op jit(solution)/shard_map/all_to_all | solution.py:441
  54.6 4.1 %attend_out.1 = (f32[16,7168]{1,0:T(8,128)S(1)}, bf16[16,7168]{1,0:T(8,128)(2,1)S(1)}, bf16[16,7168]{1,0:T(8,128)(2,1)S(1)}, bf16[16,3584]{1,0:T(8,128)(2,1)S(1)}, bf16[16,3584]{1,0:T(8,128)(2,1)S(1)}) custom-call(s32[3]{0:T(128)S(1)} %pad_add_fusion.where_ref, bf16[256,512]{1,0:T(8,128)(2,1)S(1)} %bitcast.14, bf16[64,7680]{1,0:T(8,128)(2,1)S(1)} %pad_maximum_fusion.refs_0_, ...), custom_call_target="tpu_custom_call" | custom-call | flops 1879048192 | bytes 7340032 | tf_op jit(solution)/shard_map/attend_out/pallas_call | solution.py:232
  58.7 11.1 %collective-permute-start.10 = (bf16[16,7168]{1,0:T(8,128)(2,1)S(1)}, bf16[16,7168]{1,0:T(8,128)(2,1)S(1)}, u32[]{:S(2)}, u32[]{:S(2)}) collective-permute-start(bf16[16,7168]{1,0:T(8,128)(2,1)S(1)} %get-tuple-element.29), channel_id=1, source_target_pairs={{0,30},{2,0},{4,2},{6,4},{8,6},{10,8},{12,10},{14,12},{16,14},{18,... | collective-permute-start | bytes 688136 | tf_op jit(solution)/shard_map/ppermute | solution.py:43
  69.9 4.1 %collective-permute-start.12 = (bf16[16,3584]{1,0:T(8,128)(2,1)S(1)}, bf16[16,3584]{1,0:T(8,128)(2,1)S(1)}, u32[]{:S(2)}, u32[]{:S(2)}) collective-permute-start(bf16[16,3584]{1,0:T(8,128)(2,1)S(1)} %get-tuple-element.31), channel_id=1, source_target_pairs={{0,28},{2,30},{4,0},{6,2},{8,4},{10,6},{12,8},{14,10},{16,12},{18,... | collective-permute-start | bytes 344072 | tf_op jit(solution)/shard_map/ppermute | solution.py:43
  74.0 8.1 %collective-permute-done.11 = bf16[16,3584]{1,0:T(8,128)(2,1)S(1)} collective-permute-done((bf16[16,3584]{1,0:T(8,128)(2,1)S(1)}, bf16[16,3584]{1,0:T(8,128)(2,1)S(1)}, u32[]{:S(2)}, u32[]{:S(2)}) %collective-permute-start.11) | collective-permute-done | bytes 114720 | tf_op jit(solution)/shard_map/ppermute | solution.py:43
  82.1 0.1 add_convert_fusion.1
  82.2 0.8 reshape.73
  83.0 3.5 %all-to-all-start.1 = ((bf16[4,4,7168]{2,1,0:T(4,128)(2,1)}), bf16[4,4,7168]{2,1,0:T(4,128)(2,1)S(1)}, u32[]{:S(2)}, u32[]{:S(2)}) async-start(bf16[4,4,7168]{2,1,0:T(4,128)(2,1)} %reshape.73), calls=%async_computation.1 | async-start | bytes 458752 | tf_op jit(solution)/shard_map/all_to_all | solution.py:404
  86.5 0.1 collective-permute-start.15
  86.7 0.5 collective-permute-start.16
  87.2 0.1 collective-permute-start.17
  87.4 0.1 select_reduce_fusion.2
  87.5 14.7 %all-to-all-done.1 = bf16[4,4,7168]{2,1,0:T(4,128)(2,1)S(1)} async-done(((bf16[4,4,7168]{2,1,0:T(4,128)(2,1)}), bf16[4,4,7168]{2,1,0:T(4,128)(2,1)S(1)}, u32[]{:S(2)}, u32[]{:S(2)}) %all-to-all-start.1) | async-done | bytes 229408 | tf_op jit(solution)/shard_map/all_to_all | solution.py:404
  102.2 0.1 convert_reduce_fusion.1
  102.3 0.1 reduce_sum.68
  102.4 0.2 multiply_reduce_fusion
  102.6 0.1 rsqrt.12
  102.7 0.1 multiply_convert_fusion
  102.8 0.2 fusion.5
  103.0 0.2 select_reduce_fusion.1
  103.1 0.1 fusion.4
  103.3 0.1 select_reduce_fusion
  103.4 0.1 concatenate.17
  103.6 38.7 %all-gather = bf16[16,4,7296]{2,1,0:T(4,128)(2,1)} all-gather(bf16[1,4,7296]{2,1,0:T(4,128)(2,1)S(1)} %fusion.2), channel_id=1, replica_groups=mesh['rep'=2,'x'=4,'zb'=4,'j'=4,'c'=2] {'zb','j'}, dimensions={0}, use_global_device_ids=true | all-gather | bytes 992256 | tf_op jit(solution)/shard_map/all_gather | solution.py:469
  142.3 1.7 reshape.77.tokens
  144.0 1.3 dispatch.1
  145.3 2.6 %collective-permute-start.13 = (bf16[32,7296]{1,0:T(8,128)(2,1)S(1)}, bf16[32,7296]{1,0:T(8,128)(2,1)S(1)}, u32[]{:S(2)}, u32[]{:S(2)}) collective-permute-start(bf16[32,7296]{1,0:T(8,128)(2,1)S(1)} %get-tuple-element.34), channel_id=1, source_target_pairs={{0,96},{32,0},{64,32},{96,64},{1,97},{33,1},{65,33},{97,65},{2,98}... | collective-permute-start | bytes 1400840 | tf_op jit(solution)/shard_map/ppermute | solution.py:39
  147.9 1.9 collective-permute-start.20
  149.8 11.2 %collective-permute-done.13.refs_1_ = bf16[32,7296]{1,0:T(8,128)(2,1)S(1)} collective-permute-done((bf16[32,7296]{1,0:T(8,128)(2,1)S(1)}, bf16[32,7296]{1,0:T(8,128)(2,1)S(1)}, u32[]{:S(2)}, u32[]{:S(2)}) %collective-permute-start.13) | collective-permute-done | bytes 466976 | tf_op jit(solution)/shard_map/ppermute | solution.py:39
  161.0 3.4 %collective-permute-done.14.refs_2_ = bf16[32,7296]{1,0:T(8,128)(2,1)S(1)} collective-permute-done((bf16[32,7296]{1,0:T(8,128)(2,1)S(1)}, bf16[32,7296]{1,0:T(8,128)(2,1)S(1)}, u32[]{:S(2)}, u32[]{:S(2)}) %collective-permute-start.14) | collective-permute-done | bytes 466976 | tf_op jit(solution)/shard_map/ppermute | solution.py:39
  164.4 1.5 copy-done.2
  165.9 1.5 copy-done.3
  167.4 4.4 %expert_part.2 = (bf16[32,7168]{1,0:T(8,128)(2,1)S(1)}, bf16[32,7168]{1,0:T(8,128)(2,1)S(1)}, bf16[32,7168]{1,0:T(8,128)(2,1)S(1)}) custom-call(s32[3]{0:T(128)S(1)} %pad_add_fusion.where_ref, bf16[32,7296]{1,0:T(8,128)(2,1)S(1)} %get-tuple-element.33.refs_0_, bf16[32,7296]{1,0:T(8,128)(2,1)S(1)} %collective-permute-done.13.refs_1_, ...), custom_call_target="tpu_custom_call" | custom-call | flops 1056964608 | bytes 11010048 | tf_op jit(solution)/shard_map/expert_part/pallas_call | solution.py:353
  171.8 0.1 collective-permute-start.18
  171.9 3.2 %collective-permute-start.19 = (bf16[32,7168]{1,0:T(8,128)(2,1)S(1)}, bf16[32,7168]{1,0:T(8,128)(2,1)S(1)}, u32[]{:S(2)}, u32[]{:S(2)}) collective-permute-start(bf16[32,7168]{1,0:T(8,128)(2,1)S(1)} %get-tuple-element.38), channel_id=1, source_target_pairs={{0,96},{32,0},{64,32},{96,64},{1,97},{33,1},{65,33},{97,65},{2,98}... | collective-permute-start | bytes 1376264 | tf_op jit(solution)/shard_map/ppermute | solution.py:39
  175.1 4.4 %expert_part.3 = bf16[32,7168]{1,0:T(8,128)(2,1)S(1)} custom-call(s32[3]{0:T(128)S(1)} %pad_add_fusion.where_ref, bf16[32,7296]{1,0:T(8,128)(2,1)S(1)} %collective-permute-done.20.refs_0_, bf16[7168,128]{1,0:T(8,128)(2,1)S(1)} %copy-done.1, bf16[7168,128]{1,0:T(8,128)(2,1)} %collective-permute-done.15.refs_4_.refs_2_, bf16[7168,128]{1,0:T(8,128)(2,1)S(1)} %copy-done.2, ...), custom_call_target="tpu_custom_call" | custom-call | flops 352321536 | bytes 11010048 | tf_op jit(solution)/shard_map/expert_part/pallas_call | solution.py:353
  179.5 0.8 collective-permute-start.21
  180.2 4.2 %collective-permute-done.18.refs_1_ = bf16[32,7168]{1,0:T(8,128)(2,1)S(1)} collective-permute-done((bf16[32,7168]{1,0:T(8,128)(2,1)S(1)}, bf16[32,7168]{1,0:T(8,128)(2,1)S(1)}, u32[]{:S(2)}, u32[]{:S(2)}) %collective-permute-start.18) | collective-permute-done | bytes 458784 | tf_op jit(solution)/shard_map/ppermute | solution.py:39
  184.4 5.2 %collective-permute-done.21.refs_3_ = bf16[32,7168]{1,0:T(8,128)(2,1)S(1)} collective-permute-done((bf16[32,7168]{1,0:T(8,128)(2,1)S(1)}, bf16[32,7168]{1,0:T(8,128)(2,1)S(1)}, u32[]{:S(2)}, u32[]{:S(2)}) %collective-permute-start.21) | collective-permute-done | bytes 458784 | tf_op jit(solution)/shard_map/ppermute | solution.py:39
  189.6 0.4 collect.1
  190.0 0.1 collective-permute-start.22
  190.2 3.2 %collective-permute-start.23 = (bf16[16,7168]{1,0:T(8,128)(2,1)S(1)}, bf16[16,7168]{1,0:T(8,128)(2,1)S(1)}, u32[]{:S(2)}, u32[]{:S(2)}) collective-permute-start(bf16[16,7168]{1,0:T(8,128)(2,1)S(1)} %get-tuple-element.42), channel_id=1, source_target_pairs={{0,30},{2,0},{4,2},{6,4},{8,6},{10,8},{12,10},{14,12},{16,14},{18,... | collective-permute-start | bytes 688136 | tf_op jit(solution)/shard_map/ppermute | solution.py:43
  193.4 4.1 %collective-permute-start.25 = (bf16[16,3584]{1,0:T(8,128)(2,1)S(1)}, bf16[16,3584]{1,0:T(8,128)(2,1)S(1)}, u32[]{:S(2)}, u32[]{:S(2)}) collective-permute-start(bf16[16,3584]{1,0:T(8,128)(2,1)S(1)} %get-tuple-element.44), channel_id=1, source_target_pairs={{0,28},{2,30},{4,0},{6,2},{8,4},{10,6},{12,8},{14,10},{16,12},{18,... | collective-permute-start | bytes 344072 | tf_op jit(solution)/shard_map/ppermute | solution.py:43
  197.5 2.8 %collective-permute-done.24 = bf16[16,3584]{1,0:T(8,128)(2,1)S(1)} collective-permute-done((bf16[16,3584]{1,0:T(8,128)(2,1)S(1)}, bf16[16,3584]{1,0:T(8,128)(2,1)S(1)}, u32[]{:S(2)}, u32[]{:S(2)}) %collective-permute-start.24) | collective-permute-done | bytes 114720 | tf_op jit(solution)/shard_map/ppermute | solution.py:43
  200.3 3.4 %collective-permute-done.25 = bf16[16,3584]{1,0:T(8,128)(2,1)S(1)} collective-permute-done((bf16[16,3584]{1,0:T(8,128)(2,1)S(1)}, bf16[16,3584]{1,0:T(8,128)(2,1)S(1)}, u32[]{:S(2)}, u32[]{:S(2)}) %collective-permute-start.25) | collective-permute-done | bytes 114720 | tf_op jit(solution)/shard_map/ppermute | solution.py:43
  203.7 0.1 add_convert_fusion
  203.8 0.1 reshape.74
  203.9 17.8 %all_to_all.15 = bf16[4,4,7168]{2,1,0:T(4,128)(2,1)S(1)} all-to-all(bf16[4,4,7168]{2,1,0:T(4,128)(2,1)S(1)} %reshape.74), channel_id=1, replica_groups=mesh['rep'=2,'x'=4,'zb'=4,'j'=4,'c'=2] {'zb'}, dimensions={0} | all-to-all | bytes 458752 | tf_op jit(solution)/shard_map/all_to_all | solution.py:404
  221.7 0.1 convert_reduce_fusion
  221.8 0.1 reduce_sum.75
  221.9 0.7 add_convert_fusion.2
  (57 shorter events, 0.4 us)
Async XLA Ops:
  0.0 102.8 %copy-start = (bf16[7168,16]{0,1:T(8,128)(2,1)S(1)}, bf16[7168,16]{0,1:T(8,128)(2,1)}, u32[]{:S(2)}) copy-start(bf16[7168,16]{0,1:T(8,128)(2,1)} %param.22) | copy-start | bytes 688132
  0.0 4.8 %copy-start.7 = (bf16[2,2,576]{2,1,0:T(2,128)(2,1)S(1)}, bf16[2,2,576]{2,1,0:T(2,128)(2,1)}, u32[]{:S(2)}) copy-start(bf16[2,2,576]{2,1,0:T(2,128)(2,1)} %new.1) | copy-start | bytes 13828
  0.0 4.8 %copy-start.6 = (bf16[2,2,64,576]{3,2,1,0:T(8,128)(2,1)S(1)}, bf16[2,2,64,576]{3,2,1,0:T(8,128)(2,1)}, u32[]{:S(2)}) copy-start(bf16[2,2,64,576]{3,2,1,0:T(8,128)(2,1)} %queries.1) | copy-start | bytes 884740
  0.0 4.8 %copy-start.8 = (s32[2]{0:T(128)S(1)}, s32[2]{0:T(128)}, u32[]{:S(2)}) copy-start(s32[2]{0:T(128)} %lengths.1) | copy-start | bytes 28
  1.3 34.6 %collective-permute-start.1 = (bf16[64,7680]{1,0:T(8,128)(2,1)S(1)}, bf16[64,7680]{1,0:T(8,128)(2,1)S(1)}, u32[]{:S(2)}, u32[]{:S(2)}) collective-permute-start(bf16[64,7680]{1,0:T(8,128)(2,1)S(1)} %pad_maximum_fusion.refs_0_), channel_id=1, source_target_pairs={{0,32},{32,64},{64,96},{96,0},{1,33},{33,65},{65,97},{97,1},{2,34}... | collective-permute-start | bytes 2949128 | tf_op jit(solution)/shard_map/ppermute | solution.py:39
  3.1 32.8 %collective-permute-start.2 = (bf16[64,7680]{1,0:T(8,128)(2,1)S(1)}, bf16[64,7680]{1,0:T(8,128)(2,1)S(1)}, u32[]{:S(2)}, u32[]{:S(2)}) collective-permute-start(bf16[64,7680]{1,0:T(8,128)(2,1)S(1)} %pad_maximum_fusion.refs_0_), channel_id=1, source_target_pairs={{0,96},{32,0},{64,32},{96,64},{1,97},{33,1},{65,33},{97,65},{2,98}... | collective-permute-start | bytes 2949128 | tf_op jit(solution)/shard_map/ppermute | solution.py:39
  4.7 49.8 %collective-permute-start = (bf16[64,7680]{1,0:T(8,128)(2,1)S(1)}, bf16[64,7680]{1,0:T(8,128)(2,1)}, u32[]{:S(2)}, u32[]{:S(2)}) collective-permute-start(bf16[64,7680]{1,0:T(8,128)(2,1)S(1)} %pad_maximum_fusion.refs_0_), channel_id=1, source_target_pairs={{0,1},{1,0},{2,3},{3,2},{4,5},{5,4},{6,7},{7,6},{8,9},{9,8},{10,11... | collective-permute-start | bytes 2949128 | tf_op jit(solution)/shard_map/ppermute | solution.py:47
  4.8 2.3 %copy-start.4 = (bf16[2,2048,576]{1,2,0:T(8,128)(2,1)S(1)}, bf16[2,2048,576]{1,2,0:T(8,128)(2,1)}, u32[]{:S(2)}) copy-start(bf16[2,2048,576]{1,2,0:T(8,128)(2,1)} %param.14) | copy-start | bytes 14155780
  11.2 0.7 copy-start.5
  11.9 42.6 %all-to-all-start = ((bf16[16,16,512]{2,1,0:T(8,128)(2,1)}), bf16[16,16,512]{2,1,0:T(8,128)(2,1)S(1)}, u32[]{:S(2)}, u32[]{:S(2)}) async-start(bf16[16,16,512]{2,1,0:T(8,128)(2,1)} %bitcast.15), calls=%async_computation | async-start | bytes 524288 | tf_op jit(solution)/shard_map/all_to_all | solution.py:441
  36.0 14.8 %collective-permute-start.5 = (bf16[32,7680]{1,0:T(8,128)(2,1)S(1)}, bf16[32,7680]{1,0:T(8,128)(2,1)}, u32[]{:S(2)}, u32[]{:S(2)}) collective-permute-start(bf16[32,7680]{1,0:T(8,128)(2,1)S(1)} %slice.6), channel_id=1, source_target_pairs={{0,32},{32,64},{64,96},{96,0},{1,33},{33,65},{65,97},{97,1},{2,34}... | collective-permute-start | bytes 1474568 | tf_op jit(solution)/shard_map/ppermute | solution.py:39
  36.5 14.3 %collective-permute-start.6 = (bf16[32,7680]{1,0:T(8,128)(2,1)S(1)}, bf16[32,7680]{1,0:T(8,128)(2,1)}, u32[]{:S(2)}, u32[]{:S(2)}) collective-permute-start(bf16[32,7680]{1,0:T(8,128)(2,1)S(1)} %slice.7), channel_id=1, source_target_pairs={{0,96},{32,0},{64,32},{96,64},{1,97},{33,1},{65,33},{97,65},{2,98}... | collective-permute-start | bytes 1474568 | tf_op jit(solution)/shard_map/ppermute | solution.py:39
  39.5 15.1 %collective-permute-start.3 = (bf16[64,7680]{1,0:T(8,128)(2,1)S(1)}, bf16[64,7680]{1,0:T(8,128)(2,1)}, u32[]{:S(2)}, u32[]{:S(2)}) collective-permute-start(bf16[64,7680]{1,0:T(8,128)(2,1)S(1)} %collective-permute-done.1.refs_2_), channel_id=1, source_target_pairs={{0,1},{1,0},{2,3},{3,2},{4,5},{5,4},{6,7},{7,6},{8,9},{9,8},{10,11... | collective-permute-start | bytes 2949128 | tf_op jit(solution)/shard_map/ppermute | solution.py:47
  39.5 15.1 %collective-permute-start.4 = (bf16[64,7680]{1,0:T(8,128)(2,1)S(1)}, bf16[64,7680]{1,0:T(8,128)(2,1)}, u32[]{:S(2)}, u32[]{:S(2)}) collective-permute-start(bf16[64,7680]{1,0:T(8,128)(2,1)S(1)} %collective-permute-done.2.refs_4_), channel_id=1, source_target_pairs={{0,1},{1,0},{2,3},{3,2},{4,5},{5,4},{6,7},{7,6},{8,9},{9,8},{10,11... | collective-permute-start | bytes 2949128 | tf_op jit(solution)/shard_map/ppermute | solution.py:47
  50.7 3.8 %collective-permute-start.7 = (bf16[32,7680]{1,0:T(8,128)(2,1)}, bf16[32,7680]{1,0:T(8,128)(2,1)}, u32[]{:S(2)}, u32[]{:S(2)}) collective-permute-start(bf16[32,7680]{1,0:T(8,128)(2,1)} %collective-permute-done.5.refs_6_), channel_id=1, source_target_pairs={{0,1},{1,0},{2,3},{3,2},{4,5},{5,4},{6,7},{7,6},{8,9},{9,8},{10,11... | collective-permute-start | bytes 1474568 | tf_op jit(solution)/shard_map/ppermute | solution.py:47
  50.7 3.8 %collective-permute-start.8 = (bf16[32,7680]{1,0:T(8,128)(2,1)}, bf16[32,7680]{1,0:T(8,128)(2,1)}, u32[]{:S(2)}, u32[]{:S(2)}) collective-permute-start(bf16[32,7680]{1,0:T(8,128)(2,1)} %collective-permute-done.6.refs_7_), channel_id=1, source_target_pairs={{0,1},{1,0},{2,3},{3,2},{4,5},{5,4},{6,7},{7,6},{8,9},{9,8},{10,11... | collective-permute-start | bytes 1474568 | tf_op jit(solution)/shard_map/ppermute | solution.py:47
  58.7 27.8 %copy-start.1 = (bf16[7168,128]{1,0:T(8,128)(2,1)S(1)}, bf16[7168,128]{1,0:T(8,128)(2,1)}, u32[]{:S(2)}) copy-start(bf16[7168,128]{1,0:T(8,128)(2,1)} %refs_1_.1) | copy-start | bytes 5505028
  58.7 28.6 %copy-start.9 = (bf16[2,2,7168]{2,1,0:T(2,128)(2,1)S(1)}, bf16[2,2,7168]{2,1,0:T(2,128)(2,1)}, u32[]{:S(2)}) copy-start(bf16[2,2,7168]{2,1,0:T(2,128)(2,1)} %param.18) | copy-start | bytes 172036
  58.7 28.7 %copy-start.11 = (bf16[7168]{0:T(1024)(128)(2,1)S(1)}, bf16[7168]{0:T(1024)(128)(2,1)}, u32[]{:S(2)}) copy-start(bf16[7168]{0:T(1024)(128)(2,1)} %param.21) | copy-start | bytes 43012
  58.7 28.7 %copy-start.12 = (s32[2,2,8]{2,1,0:T(2,128)S(1)}, s32[2,2,8]{2,1,0:T(2,128)}, u32[]{:S(2)}) copy-start(s32[2,2,8]{2,1,0:T(2,128)} %param.24) | copy-start | bytes 388
  58.7 28.7 %copy-start.10 = (s32[2,2,8]{2,1,0:T(2,128)S(1)}, s32[2,2,8]{2,1,0:T(2,128)}, u32[]{:S(2)}) copy-start(s32[2,2,8]{2,1,0:T(2,128)} %param.23) | copy-start | bytes 388
  58.7 23.4 %collective-permute-start.10 = (bf16[16,7168]{1,0:T(8,128)(2,1)S(1)}, bf16[16,7168]{1,0:T(8,128)(2,1)S(1)}, u32[]{:S(2)}, u32[]{:S(2)}) collective-permute-start(bf16[16,7168]{1,0:T(8,128)(2,1)S(1)} %get-tuple-element.29), channel_id=1, source_target_pairs={{0,30},{2,0},{4,2},{6,4},{8,6},{10,8},{12,10},{14,12},{16,14},{18,... | collective-permute-start | bytes 688136 | tf_op jit(solution)/shard_map/ppermute | solution.py:43
  69.9 12.2 %collective-permute-start.9 = (bf16[16,7168]{1,0:T(8,128)(2,1)S(1)}, bf16[16,7168]{1,0:T(8,128)(2,1)S(1)}, u32[]{:S(2)}, u32[]{:S(2)}) collective-permute-start(bf16[16,7168]{1,0:T(8,128)(2,1)S(1)} %get-tuple-element.28), channel_id=1, source_target_pairs={{0,2},{2,4},{4,6},{6,8},{8,10},{10,12},{12,14},{14,16},{16,18},{18... | collective-permute-start | bytes 688136 | tf_op jit(solution)/shard_map/ppermute | solution.py:43
  69.9 12.2 %collective-permute-start.11 = (bf16[16,3584]{1,0:T(8,128)(2,1)S(1)}, bf16[16,3584]{1,0:T(8,128)(2,1)S(1)}, u32[]{:S(2)}, u32[]{:S(2)}) collective-permute-start(bf16[16,3584]{1,0:T(8,128)(2,1)S(1)} %get-tuple-element.30), channel_id=1, source_target_pairs={{0,4},{2,6},{4,8},{6,10},{8,12},{10,14},{12,16},{14,18},{16,20},{1... | collective-permute-start | bytes 344072 | tf_op jit(solution)/shard_map/ppermute | solution.py:43
  69.9 12.2 %collective-permute-start.12 = (bf16[16,3584]{1,0:T(8,128)(2,1)S(1)}, bf16[16,3584]{1,0:T(8,128)(2,1)S(1)}, u32[]{:S(2)}, u32[]{:S(2)}) collective-permute-start(bf16[16,3584]{1,0:T(8,128)(2,1)S(1)} %get-tuple-element.31), channel_id=1, source_target_pairs={{0,28},{2,30},{4,0},{6,2},{8,4},{10,6},{12,8},{14,10},{16,12},{18,... | collective-permute-start | bytes 344072 | tf_op jit(solution)/shard_map/ppermute | solution.py:43
  83.0 19.2 %all-to-all-start.1 = ((bf16[4,4,7168]{2,1,0:T(4,128)(2,1)}), bf16[4,4,7168]{2,1,0:T(4,128)(2,1)S(1)}, u32[]{:S(2)}, u32[]{:S(2)}) async-start(bf16[4,4,7168]{2,1,0:T(4,128)(2,1)} %reshape.73), calls=%async_computation.1 | async-start | bytes 458752 | tf_op jit(solution)/shard_map/all_to_all | solution.py:404
  86.5 61.4 %collective-permute-start.15 = (bf16[7168,128]{1,0:T(8,128)(2,1)S(1)}, bf16[7168,128]{1,0:T(8,128)(2,1)}, u32[]{:S(2)}, u32[]{:S(2)}) collective-permute-start(bf16[7168,128]{1,0:T(8,128)(2,1)S(1)} %copy-done.1), channel_id=1, source_target_pairs={{0,1},{1,0},{2,3},{3,2},{4,5},{5,4},{6,7},{7,6},{8,9},{9,8},{10,11... | collective-permute-start | bytes 5505032 | tf_op jit(solution)/shard_map/ppermute | solution.py:47
  86.7 63.1 %collective-permute-start.16 = (bf16[7168,128]{1,0:T(8,128)(2,1)}, bf16[7168,128]{1,0:T(8,128)(2,1)}, u32[]{:S(2)}, u32[]{:S(2)}) collective-permute-start(bf16[7168,128]{1,0:T(8,128)(2,1)} %refs_3_.3), channel_id=1, source_target_pairs={{0,1},{1,0},{2,3},{3,2},{4,5},{5,4},{6,7},{7,6},{8,9},{9,8},{10,11... | collective-permute-start | bytes 5505032 | tf_op jit(solution)/shard_map/ppermute | solution.py:47
  87.2 62.7 %collective-permute-start.17 = (bf16[128,7168]{1,0:T(8,128)(2,1)}, bf16[128,7168]{1,0:T(8,128)(2,1)}, u32[]{:S(2)}, u32[]{:S(2)}) collective-permute-start(bf16[128,7168]{1,0:T(8,128)(2,1)} %refs_5_.3), channel_id=1, source_target_pairs={{0,1},{1,0},{2,3},{3,2},{4,5},{5,4},{6,7},{7,6},{8,9},{9,8},{10,11... | collective-permute-start | bytes 5505032 | tf_op jit(solution)/shard_map/ppermute | solution.py:47
  145.3 15.7 %collective-permute-start.13 = (bf16[32,7296]{1,0:T(8,128)(2,1)S(1)}, bf16[32,7296]{1,0:T(8,128)(2,1)S(1)}, u32[]{:S(2)}, u32[]{:S(2)}) collective-permute-start(bf16[32,7296]{1,0:T(8,128)(2,1)S(1)} %get-tuple-element.34), channel_id=1, source_target_pairs={{0,96},{32,0},{64,32},{96,64},{1,97},{33,1},{65,33},{97,65},{2,98}... | collective-permute-start | bytes 1400840 | tf_op jit(solution)/shard_map/ppermute | solution.py:39
  147.9 16.5 %collective-permute-start.14 = (bf16[32,7296]{1,0:T(8,128)(2,1)S(1)}, bf16[32,7296]{1,0:T(8,128)(2,1)S(1)}, u32[]{:S(2)}, u32[]{:S(2)}) collective-permute-start(bf16[32,7296]{1,0:T(8,128)(2,1)S(1)} %get-tuple-element.35), channel_id=1, source_target_pairs={{0,32},{32,64},{64,96},{96,0},{1,33},{33,65},{65,97},{97,1},{2,34}... | collective-permute-start | bytes 1400840 | tf_op jit(solution)/shard_map/ppermute | solution.py:39
  147.9 27.2 %collective-permute-start.20 = (bf16[32,7296]{1,0:T(8,128)(2,1)S(1)}, bf16[32,7296]{1,0:T(8,128)(2,1)S(1)}, u32[]{:S(2)}, u32[]{:S(2)}) collective-permute-start(bf16[32,7296]{1,0:T(8,128)(2,1)S(1)} %get-tuple-element.39), channel_id=1, source_target_pairs={{0,64},{32,96},{64,0},{96,32},{1,65},{33,97},{65,1},{97,33},{2,66}... | collective-permute-start | bytes 1400840 | tf_op jit(solution)/shard_map/ppermute | solution.py:39
  164.4 1.5 copy-start.2
  165.9 1.5 copy-start.3
  171.8 12.7 %collective-permute-start.18 = (bf16[32,7168]{1,0:T(8,128)(2,1)S(1)}, bf16[32,7168]{1,0:T(8,128)(2,1)S(1)}, u32[]{:S(2)}, u32[]{:S(2)}) collective-permute-start(bf16[32,7168]{1,0:T(8,128)(2,1)S(1)} %get-tuple-element.37), channel_id=1, source_target_pairs={{0,32},{32,64},{64,96},{96,0},{1,33},{33,65},{65,97},{97,1},{2,34}... | collective-permute-start | bytes 1376264 | tf_op jit(solution)/shard_map/ppermute | solution.py:39
  171.9 12.5 %collective-permute-start.19 = (bf16[32,7168]{1,0:T(8,128)(2,1)S(1)}, bf16[32,7168]{1,0:T(8,128)(2,1)S(1)}, u32[]{:S(2)}, u32[]{:S(2)}) collective-permute-start(bf16[32,7168]{1,0:T(8,128)(2,1)S(1)} %get-tuple-element.38), channel_id=1, source_target_pairs={{0,96},{32,0},{64,32},{96,64},{1,97},{33,1},{65,33},{97,65},{2,98}... | collective-permute-start | bytes 1376264 | tf_op jit(solution)/shard_map/ppermute | solution.py:39
  179.5 10.1 %collective-permute-start.21 = (bf16[32,7168]{1,0:T(8,128)(2,1)S(1)}, bf16[32,7168]{1,0:T(8,128)(2,1)S(1)}, u32[]{:S(2)}, u32[]{:S(2)}) collective-permute-start(bf16[32,7168]{1,0:T(8,128)(2,1)S(1)} %expert_part.3), channel_id=1, source_target_pairs={{0,64},{32,96},{64,0},{96,32},{1,65},{33,97},{65,1},{97,33},{2,66}... | collective-permute-start | bytes 1376264 | tf_op jit(solution)/shard_map/ppermute | solution.py:39
  190.0 13.7 %collective-permute-start.22 = (bf16[16,7168]{1,0:T(8,128)(2,1)S(1)}, bf16[16,7168]{1,0:T(8,128)(2,1)S(1)}, u32[]{:S(2)}, u32[]{:S(2)}) collective-permute-start(bf16[16,7168]{1,0:T(8,128)(2,1)S(1)} %get-tuple-element.41), channel_id=1, source_target_pairs={{0,2},{2,4},{4,6},{6,8},{8,10},{10,12},{12,14},{14,16},{16,18},{18... | collective-permute-start | bytes 688136 | tf_op jit(solution)/shard_map/ppermute | solution.py:43
  190.2 13.5 %collective-permute-start.23 = (bf16[16,7168]{1,0:T(8,128)(2,1)S(1)}, bf16[16,7168]{1,0:T(8,128)(2,1)S(1)}, u32[]{:S(2)}, u32[]{:S(2)}) collective-permute-start(bf16[16,7168]{1,0:T(8,128)(2,1)S(1)} %get-tuple-element.42), channel_id=1, source_target_pairs={{0,30},{2,0},{4,2},{6,4},{8,6},{10,8},{12,10},{14,12},{16,14},{18,... | collective-permute-start | bytes 688136 | tf_op jit(solution)/shard_map/ppermute | solution.py:43
  193.4 6.9 %collective-permute-start.24 = (bf16[16,3584]{1,0:T(8,128)(2,1)S(1)}, bf16[16,3584]{1,0:T(8,128)(2,1)S(1)}, u32[]{:S(2)}, u32[]{:S(2)}) collective-permute-start(bf16[16,3584]{1,0:T(8,128)(2,1)S(1)} %get-tuple-element.43), channel_id=1, source_target_pairs={{0,4},{2,6},{4,8},{6,10},{8,12},{10,14},{12,16},{14,18},{16,20},{1... | collective-permute-start | bytes 344072 | tf_op jit(solution)/shard_map/ppermute | solution.py:43
  193.4 10.3 %collective-permute-start.25 = (bf16[16,3584]{1,0:T(8,128)(2,1)S(1)}, bf16[16,3584]{1,0:T(8,128)(2,1)S(1)}, u32[]{:S(2)}, u32[]{:S(2)}) collective-permute-start(bf16[16,3584]{1,0:T(8,128)(2,1)S(1)} %get-tuple-element.44), channel_id=1, source_target_pairs={{0,28},{2,30},{4,0},{6,2},{8,4},{10,6},{12,8},{14,10},{16,12},{18,... | collective-permute-start | bytes 344072 | tf_op jit(solution)/shard_map/ppermute | solution.py:43
where the time goes:
time: 223 us
  starting transfers between devices  67.5 us (30%)
  waiting for transfers between devices  67 us (30%)
  blocking collectives  56.6 us (25%)
  Pallas kernels  18.5 us (8%)
  local copies, waits for them, and re-layouts  9.13 us (4%)
  other arithmetic  3.37 us (2%)
    all_gather x1, blocking collectives, layer(): ring = lax.all_gather(payload, ZAX, axis=0, tiled=True)  38.7 us
    ppermute x10, waiting for transfers between devices, shift_x(): return lax.ppermute(a, 'x', [(i, (i + step) % n) for i in range(n)])  34.7 us
    all_to_all x1, starting transfers between devices, layer(): lax.all_to_all(outgoing.reshape(RING, nx * tok, LAT), ZAX, split_axis=0,...  24 us
    ppermute x8, starting transfers between devices, shift_z(): return lax.ppermute(a, ZAX, [(i, (i + step) % RING) for i in range(RING)])  22.8 us
    all_to_all x1, blocking collectives, reduce_z(): got = lax.all_to_all(sent, 'zb', split_axis=0, concat_axis=0, tiled=True)  17.8 us
    ppermute x10, starting transfers between devices, shift_x(): return lax.ppermute(a, 'x', [(i, (i + step) % n) for i in range(n)])  15.5 us
    all_to_all x1, waiting for transfers between devices, reduce_z(): got = lax.all_to_all(sent, 'zb', split_axis=0, concat_axis=0, tiled=True)  14.7 us
    ppermute x8, waiting for transfers between devices, shift_z(): return lax.ppermute(a, ZAX, [(i, (i + step) % RING) for i in range(RING)])  14.3 us
  transfers between devices with their start and end apart: 28, of which 10 were waited for; matrix products, arithmetic and copies ran while one was open for 1% of the time, Pallas kernels for 6%

commit v1 on v0

--- a/solution.py
+++ b/solution.py
@@ -148,10 +148,37 @@
         ],
         out_specs=pl.BlockSpec((rows, LAT), lambda b: (0, 0)),
         scratch_shapes=[pltpu.VMEM((rows, LAT), bf16)],
-        compiler_params=params(24),
+        compiler_params=params(60),
         cost_estimate=cost(2 * rows * length * (width + LAT), 2 * cache_kv.size),
         name="context_rows",
     )(where, lengths, keys, queries, new_kv)
+
+
+def pack_kernel(up, rows, tops, lows, sem):
+    half, at = tops.shape[0], up.shape[1]
+    copies = []
+    for i, out in enumerate((tops, lows)):
+        part = pl.ds(i * half, half)
+        copies.append(pltpu.make_async_copy(rows.at[part], out.at[:, pl.ds(at, rows.shape[1])], sem.at[i, 0]))
+        copies.append(pltpu.make_async_copy(up.at[part], out.at[:, pl.ds(0, at)], sem.at[i, 1]))
+    for copy in copies:
+        copy.start()
+    for copy in copies:
+        copy.wait()
+
+
+def pack(up, rows):
+    shape = (rows.shape[0] // 2, up.shape[1] + rows.shape[1])
+    return pl.pallas_call(
+        pack_kernel,
+        out_shape=(jax.ShapeDtypeStruct(shape, bf16),) * 2,
+        in_specs=[hbm()] * 2,
+        out_specs=[vmem()] * 2,
+        scratch_shapes=[pltpu.SemaphoreType.DMA((2, 2))],
+        compiler_params=params(4),
+        cost_estimate=cost(1, 4 * rows.size),
+        name="pack",
+    )(up, rows)
 
 
 OUT_TILE = 512
@@ -178,10 +205,11 @@
     )
 
 
-def attend_kernel(tok, nx, count, where_ref, arrived, *refs):
+def attend_kernel(tok, nx, count, first, last, where_ref, arrived, *refs):
     pieces = refs[:count]
-    outs = refs[count : count + 5]
-    up, rows, up_sem, row_sem = refs[count + 5 :]
+    outs, (up, rows, up_sem, row_sem) = refs[count:-4], refs[-4:]
+    if last:
+        before, outs = outs[0], outs[1:]
     half = rows.shape[1] // 2
     starts = [0]
     for piece in pieces:
@@ -210,7 +238,7 @@
         up_copy(i).wait()
     values = lax.dot_general(arrived[...], up[...], NT, preferred_element_type=f32)
     hop = lax.rem(iota(values.shape, 0) // tok, nx)
-    values = jnp.where(hop == iota(values.shape, 1) // VH, values, 0.0).astype(bf16)
+    values = jnp.where(hop == first + iota(values.shape, 1) // VH, values, 0.0).astype(bf16)
     shape = (RING * tok, arrived.shape[0])
     place, source = iota(shape, 0), iota(shape, 1)
     take = (source // (tok * nx) == chip_at(place // tok, where_ref[2])) & (
@@ -222,28 +250,34 @@
             row_copy(c, i).wait()
         for n in range(half // OUT_TILE):
             cols = pl.ds(c * half + n * OUT_TILE, OUT_TILE)
-            put_rows(jnp.dot(values, rows[:, cols], preferred_element_type=f32), outs, c, n, half)
-
-
-def attend_out(where, nx, arrived, pieces, tok):
+            got = jnp.dot(values, rows[:, cols], preferred_element_type=f32)
+            if last:
+                put_rows(before[:, cols] + got, outs, c, n, half)
+            else:
+                outs[0][:, cols] = got
+
+
+def attend_part(where, nx, arrived, pieces, tok, first, before):
     depth = sum(p.shape[0] for p in pieces)
     dim = pieces[0].shape[1] - LAT
     count = len(pieces)
-    return pl.pallas_call(
-        functools.partial(attend_kernel, tok, nx, count),
-        out_shape=row_shapes(FAR * tok, dim),
-        in_specs=[smem(), vmem()] + [hbm()] * count,
-        out_specs=[vmem()] * 5,
+    last = before is not None
+    part = jax.ShapeDtypeStruct((RING * tok, dim), f32)
+    return pl.pallas_call(
+        functools.partial(attend_kernel, tok, nx, count, first, last),
+        out_shape=row_shapes(FAR * tok, dim) if last else part,
+        in_specs=[smem(), vmem()] + [hbm()] * count + [vmem()] * last,
+        out_specs=[vmem()] * 5 if last else vmem(),
         scratch_shapes=[
             pltpu.VMEM((depth, LAT), bf16),
             pltpu.VMEM((depth, dim), bf16),
             pltpu.SemaphoreType.DMA((count,)),
             pltpu.SemaphoreType.DMA((2, count)),
         ],
-        compiler_params=params(16),
+        compiler_params=params(12),
         cost_estimate=cost(8 * RING * tok * depth * dim, 2 * depth * dim),
-        name="attend_out",
-    )(where, arrived, *pieces)
+        name="attend_part",
+    )(where, arrived, *pieces, *([before] if last else []))
 
 
 def dispatch_kernel(tok, nx, where_ref, tokens, *refs):
@@ -293,52 +327,58 @@
 CHUNKS = 7
 
 
+def stage_kernel(gate_a, gate_b, up_a, up_b, down_a, down_b, wide, deep, sem):
+    part = gate_a.shape[1]
+    copies = [
+        pltpu.make_async_copy(ref, wide.at[:, pl.ds(i * part, part)], sem.at[i])
+        for i, ref in enumerate((gate_a, gate_b, up_a, up_b))
+    ]
+    copies += [
+        pltpu.make_async_copy(ref, deep.at[pl.ds(i * part, part)], sem.at[4 + i])
+        for i, ref in enumerate((down_a, down_b))
+    ]
+    for copy in copies:
+        copy.start()
+    for copy in copies:
+        copy.wait()
+
+
+def stage(weights):
+    dim, part = weights[0].shape
+    return pl.pallas_call(
+        stage_kernel,
+        out_shape=(
+            jax.ShapeDtypeStruct((dim, 4 * part), bf16),
+            jax.ShapeDtypeStruct((2 * part, dim), bf16),
+        ),
+        in_specs=[hbm()] * 6,
+        out_specs=[vmem()] * 2,
+        scratch_shapes=[pltpu.SemaphoreType.DMA((6,))],
+        compiler_params=params(40),
+        cost_estimate=cost(4 * 1000 * dim * part, 12 * dim * part),
+        name="stage",
+    )(*weights)
+
+
 def expert_kernel(groups, where_ref, *refs):
     tokens = refs[:groups]
-    gate_a, gate_b, up_a, up_b, down_a, down_b = refs[groups : groups + 6]
-    outs = refs[groups + 6 : 2 * groups + 6]
-    wide, deep, held, first_sem, second_sem = refs[2 * groups + 6 :]
-    dim, part = gate_a.shape
+    wide, deep = refs[groups : groups + 2]
+    outs = refs[groups + 2 : 2 * groups + 2]
+    held = refs[2 * groups + 2] if groups > 1 else tokens[0]
+    dim = wide.shape[0]
+    part = wide.shape[1] // 2
     chunk = dim // CHUNKS
-
-    def first(k, i):
-        return pltpu.make_async_copy(
-            (gate_a, gate_b, up_a, up_b)[i].at[pl.ds(k * chunk, chunk)],
-            wide.at[pl.ds(k * chunk, chunk), pl.ds(i * part, part)],
-            first_sem.at[k, i],
-        )
-
-    def second(i):
-        return pltpu.make_async_copy(
-            (down_a, down_b)[i], deep.at[pl.ds(i * part, part)], second_sem.at[i]
-        )
-
-    for k in range(CHUNKS):
-        for i in range(4):
-            first(k, i).start()
-    for i in range(2):
-        second(i).start()
-    rows = groups * SLOTS
     if groups > 1:
         for g, ref in enumerate(tokens):
             held[pl.ds(g * SLOTS, SLOTS)] = ref[...]
-    else:
-        held = tokens[0]
-    total = jnp.zeros((rows, 4 * part), f32)
-    for k in range(CHUNKS):
-        for i in range(4):
-            first(k, i).wait()
-        cols = pl.ds(k * chunk, chunk)
-        total = total + jnp.dot(held[:, cols], wide[cols, :], preferred_element_type=f32)
-    gate, upward = total[:, : 2 * part], total[:, 2 * part :]
+    total = jnp.dot(held[:, pl.ds(0, dim)], wide[...], preferred_element_type=f32)
+    gate, upward = total[:, :part], total[:, part:]
     act = (gate / (1.0 + jnp.exp(-gate)) * upward).astype(bf16)
     shape = (EXTRA, EXTRA)
     expert = FAR * where_ref[0] + where_ref[1]
     from_share = iota(shape, 0) - CAP * EXPERTS
     hot = (from_share >= 0) & (from_share < 3 * EXPERTS) & (lax.rem(from_share + EXTRA, EXPERTS) == expert)
     share = jnp.dot(held[:, pl.ds(dim, EXTRA)], one_hot(hot), preferred_element_type=f32)[:, :1]
-    for i in range(2):
-        second(i).wait()
     for k in range(CHUNKS):
         cols = pl.ds(k * chunk, chunk)
         got = jnp.dot(act, deep[:, cols], preferred_element_type=f32) * share
@@ -347,25 +387,21 @@
 
 
 def expert_part(where, tokens, weights):
-    dim, part = weights[0].shape
+    wide, deep = weights
+    dim = wide.shape[0]
     groups = len(tokens)
     rows = groups * SLOTS
+    held = [pltpu.VMEM((rows, dim + EXTRA), bf16)] if groups > 1 else []
     return pl.pallas_call(
         functools.partial(expert_kernel, groups),
         out_shape=(jax.ShapeDtypeStruct((SLOTS, dim), bf16),) * groups,
-        in_specs=[smem()] + [vmem()] * groups + [hbm()] * 6,
+        in_specs=[smem()] + [vmem()] * (groups + 2),
         out_specs=[vmem()] * groups,
-        scratch_shapes=[
-            pltpu.VMEM((dim, 4 * part), bf16),
-            pltpu.VMEM((2 * part, dim), bf16),
-            pltpu.VMEM((rows if groups > 1 else 16, dim + EXTRA), bf16),
-            pltpu.SemaphoreType.DMA((CHUNKS, 4)),
-            pltpu.SemaphoreType.DMA((2,)),
-        ],
-        compiler_params=params(20),
-        cost_estimate=cost(12 * rows * dim * part, 12 * dim * part),
+        scratch_shapes=held,
+        compiler_params=params(8),
+        cost_estimate=cost(6 * rows * wide.size, 2 * rows * dim),
         name="expert_part",
-    )(where, *tokens, *weights)
+    )(where, *tokens, wide, deep)
 
 
 def collect_kernel(count, spread, *refs):
@@ -426,23 +462,25 @@
     tok = seqs * steps
     where = jnp.stack([lax.axis_index(a) for a in ("x", "zb", "j")]).astype(jnp.int32)
 
-    mine = jnp.concatenate([value_up.T, out_proj], axis=1)
-    rows = mine.shape[0]
-    from_left = shift_x(mine, 1)
-    from_right = shift_x(mine, -1)
+    tops, lows = pack(value_up.T, out_proj)
+    top_left = shift_x(tops, 1)
+    low_right = shift_x(lows, -1)
+    low_left = shift_x(lows, 1)
+    top_right = shift_x(tops, -1)
 
     outgoing = context_rows(where, nx, cache_kv, new_kv, queries, lengths)
-    from_left, from_right, _ = lax.optimization_barrier((from_left, from_right, outgoing))
-    far_a = shift_x(from_left[: rows // 2], 1)
-    far_b = shift_x(from_right[rows // 2 :], -1)
-    pieces = [mine, swap_core(mine), from_left, swap_core(from_left), from_right, swap_core(from_right)]
-    pieces += [far_a, far_b, swap_core(far_a), swap_core(far_b)]
-    ffn = (w_gate, swap_core(w_gate), w_up, swap_core(w_up), w_down, swap_core(w_down))
     arrived = lax.all_to_all(
         outgoing.reshape(RING, nx * tok, LAT), ZAX, split_axis=0, concat_axis=0, tiled=True
     )
+    top_far = shift_x(top_left, 1)
+    low_far = shift_x(low_right, -1)
+    near = (tops, lows, top_left, low_left, top_right, low_right)
+    near = sum(([near[i], near[i + 1], swap_core(near[i]), swap_core(near[i + 1])] for i in (0, 2, 4)), [])
+    beyond = [top_far, low_far, swap_core(top_far), swap_core(low_far)]
+    weights = stage((w_gate, swap_core(w_gate), w_up, swap_core(w_up), w_down, swap_core(w_down)))
     arrived = arrived.reshape(RING * nx * tok, LAT)
-    attended = reduce_z(*attend_out(where, nx, arrived, pieces, tok))
+    most = attend_part(where, nx, arrived, near, tok, 0, None)
+    attended = reduce_z(*attend_part(where, nx, arrived, beyond, tok, nx - 1, most))
 
     hidden = resid.reshape(tok, D).astype(f32) + attended
     mean_square = jnp.mean(hidden * hidden, axis=-1, keepdims=True)
@@ -454,8 +492,8 @@
     is_pick = route_ids[:, :, None] == jnp.arange(EXPERTS, dtype=jnp.int32)[None, None, :]
     picked = jnp.sum(jnp.where(is_pick, logits[:, None, :], 0.0), axis=-1)
     gates = jax.nn.sigmoid(picked)
-    weights = route_scale * gates / jnp.sum(gates, axis=1, keepdims=True)
-    share = jnp.sum(jnp.where(is_pick, weights[:, :, None], 0.0), axis=1)
+    gates = route_scale * gates / jnp.sum(gates, axis=1, keepdims=True)
+    share = jnp.sum(jnp.where(is_pick, gates[:, :, None], 0.0), axis=1)
     slot = jnp.sum(jnp.where(is_pick, route_slots[:, :, None] + 1, 0), axis=1)
     places = [(slot == s + 1).astype(bf16) for s in range(CAP)]
     high = share.astype(bf16)
@@ -471,10 +509,10 @@
     from_right = shift_x(sent[1], -1)
     from_left = shift_x(sent[2], 1)
     from_far = shift_x(sent[3], 2)
-    done = expert_part(where, (sent[0], from_right, from_left), ffn)
+    done = expert_part(where, (sent[0], from_right, from_left), weights)
     back_left = shift_x(done[1], 1)
     back_right = shift_x(done[2], -1)
-    (far_done,) = expert_part(where, (from_far,), ffn)
+    (far_done,) = expert_part(where, (from_far,), weights)
     back_far = shift_x(far_done, 2)
     expert_mix = reduce_z(*collect(spread, (done[0], back_left, back_right, back_far), tok))
     mixed = (hidden + expert_mix).astype(bf16)

time: 223 us -> 228 us (1.022)
  waiting for transfers between devices: 67 us -> 56.3 us
  Pallas kernels: 18.5 us -> 27.3 us
  local copies, waits for them, and re-layouts: 9.13 us -> 16.8 us
    ppermute x10 -> x12, waiting for transfers between devices: 34.7 us -> 23.8 us  [shift_x(): return lax.ppermute(a, 'x', [(i, (i + step) % n) for i in range(n)])]
    pallas_call x1 -> x4, Pallas kernels: 4.1 us -> 14.5 us  [the longest x1 7.26 us: stage(): pl.pallas_call(stage_kernel, out_shape=(jax.ShapeDtypeStruct((dim, 4 * pa...]
    unnamed x27 -> x39, local copies, waits for them, and re-layouts: 7.77 us -> 15.5 us
    ppermute x8, starting transfers between devices: 22.8 us -> 18.9 us  [shift_z(): return lax.ppermute(a, ZAX, [(i, (i + step) % RING) for i in range(RING)])]
    pallas_call x2, Pallas kernels: 8.75 us -> 5.16 us  [expert_part(): pl.pallas_call(functools.partial(expert_kernel, groups), out_shape=(jax.S...]
    all_to_all x1, blocking collectives: 17.8 us -> 20.6 us  [reduce_z(): got = lax.all_to_all(sent, 'zb', split_axis=0, concat_axis=0, tiled=True)]
    all_gather x1, blocking collectives: 38.7 us -> 36.2 us  [layer(): ring = lax.all_gather(payload, ZAX, axis=0, tiled=True)]
    ppermute x10 -> x12, starting transfers between devices: 15.5 us -> 18 us  [shift_x(): return lax.ppermute(a, 'x', [(i, (i + step) % n) for i in range(n)])]
  transfers between devices with their start and end apart: 28 -> 33, of which waited for: 10 -> 11; matrix products, arithmetic and copies ran while one was open for 1% -> 2% of each run, Pallas kernels for 6% -> 10%
where the time goes in v1:
time: 228 us; the launch traced here: 227 us
  starting transfers between devices  66.8 us (29%)
  blocking collectives  56.8 us (25%)
  waiting for transfers between devices  56.3 us (25%)
  Pallas kernels  27.3 us (12%)
  local copies, waits for them, and re-layouts  16.8 us (7%)
  other arithmetic  2.66 us (1%)
    all_gather x1, blocking collectives, layer(): ring = lax.all_gather(payload, ZAX, axis=0, tiled=True)  36.2 us
    all_to_all x1, starting transfers between devices, layer(): lax.all_to_all(outgoing.reshape(RING, nx * tok, LAT), ZAX, split_axis=0,...  24 us
    ppermute x12, waiting for transfers between devices, shift_x(): return lax.ppermute(a, 'x', [(i, (i + step) % n) for i in range(n)])  23.8 us
    all_to_all x1, blocking collectives, reduce_z(): got = lax.all_to_all(sent, 'zb', split_axis=0, concat_axis=0, tiled=True)  20.6 us
    ppermute x8, starting transfers between devices, shift_z(): return lax.ppermute(a, ZAX, [(i, (i + step) % RING) for i in range(RING)])  18.9 us
    ppermute x12, starting transfers between devices, shift_x(): return lax.ppermute(a, 'x', [(i, (i + step) % n) for i in range(n)])  18 us
    all_to_all x1, waiting for transfers between devices, reduce_z(): got = lax.all_to_all(sent, 'zb', split_axis=0, concat_axis=0, tiled=True)  16.8 us
    unnamed x39, local copies, waits for them, and re-layouts  15.5 us
  transfers between devices with their start and end apart: 33, of which 11 were waited for; matrix products, arithmetic and copies ran while one was open for 2% of the time, Pallas kernels for 10%

profile of v1, /device:TPU:40, one launch (start us, length us, event | category | flops | bytes accessed | tf_op | source)
XLA Modules:
  0.0 227.2 jit_solution(15688747165363552700)
XLA Ops:
  0.0 1.2 copy-done.5
  1.2 0.8 copy-done.10
  2.1 0.2 pack.1
  2.3 3.3 %collective-permute-start.11 = (bf16[32,7680]{1,0:T(8,128)(2,1)S(1)}, bf16[32,7680]{1,0:T(8,128)(2,1)S(1)}, u32[]{:S(2)}, u32[]{:S(2)}) collective-permute-start(bf16[32,7680]{1,0:T(8,128)(2,1)S(1)} %get-tuple-element.27.refs_0_), channel_id=1, source_target_pairs={{0,96},{32,0},{64,32},{96,64},{1,97},{33,1},{65,33},{97,65},{2,98}... | collective-permute-start | bytes 1474568 | tf_op jit(solution)/shard_map/ppermute | solution.py:39
  5.6 3.2 %collective-permute-start.2 = (bf16[32,7680]{1,0:T(8,128)(2,1)S(1)}, bf16[32,7680]{1,0:T(8,128)(2,1)S(1)}, u32[]{:S(2)}, u32[]{:S(2)}) collective-permute-start(bf16[32,7680]{1,0:T(8,128)(2,1)S(1)} %get-tuple-element.28.refs_1_), channel_id=1, source_target_pairs={{0,96},{32,0},{64,32},{96,64},{1,97},{33,1},{65,33},{97,65},{2,98}... | collective-permute-start | bytes 1474568 | tf_op jit(solution)/shard_map/ppermute | solution.py:39
  8.8 0.7 pad_add_fusion.where_ref
  9.5 5.9 %context_rows.1 = bf16[256,512]{1,0:T(8,128)(2,1)} custom-call(s32[3]{0:T(128)} %pad_add_fusion.where_ref, s32[2]{0:T(128)} %lengths.1, bf16[2,576,2048]{2,1,0:T(8,128)(2,1)} %bitcast.16, bf16[2,2,64,576]{3,2,1,0:T(8,128)(2,1)} %queries.1, bf16[2,2,576]{2,1,0:T(2,128)(2,1)} %new.1), custom_call_target="tpu_custom_call" | custom-call | flops 1140850688 | bytes 4718592 | tf_op jit(solution)/shard_map/context_rows/pallas_call | solution.py:138
  15.4 24.0 %all-to-all-start = ((bf16[16,16,512]{2,1,0:T(8,128)(2,1)}), bf16[16,16,512]{2,1,0:T(8,128)(2,1)S(1)}, u32[]{:S(2)}, u32[]{:S(2)}) async-start(bf16[16,16,512]{2,1,0:T(8,128)(2,1)} %bitcast.17), calls=%async_computation | async-start | bytes 524288 | tf_op jit(solution)/shard_map/all_to_all | solution.py:472
  39.4 0.1 collective-permute-start.7
  39.6 0.5 collective-permute-start.12
  40.0 3.3 %collective-permute-start.3 = (bf16[32,7680]{1,0:T(8,128)(2,1)S(1)}, bf16[32,7680]{1,0:T(8,128)(2,1)}, u32[]{:S(2)}, u32[]{:S(2)}) collective-permute-start(bf16[32,7680]{1,0:T(8,128)(2,1)S(1)} %collective-permute-done.2.refs_9_), channel_id=1, source_target_pairs={{0,96},{32,0},{64,32},{96,64},{1,97},{33,1},{65,33},{97,65},{2,98}... | collective-permute-start | bytes 1474568 | tf_op jit(solution)/shard_map/ppermute | solution.py:39
  43.4 0.8 copy-done.6
  44.2 0.5 collective-permute-start.10
  44.7 0.8 copy-done.8
  45.5 9.4 %collective-permute-done.1.refs_0_ = bf16[32,7680]{1,0:T(8,128)(2,1)} collective-permute-done((bf16[32,7680]{1,0:T(8,128)(2,1)S(1)}, bf16[32,7680]{1,0:T(8,128)(2,1)}, u32[]{:S(2)}, u32[]{:S(2)}) %collective-permute-start.1) | collective-permute-done | bytes 491552 | tf_op jit(solution)/shard_map/ppermute | solution.py:39
  54.9 0.5 collective-permute-start.5
  55.4 2.1 all-to-all-done
  57.5 1.0 copy-done.7
  58.6 1.0 copy-done.9
  59.6 3.9 %attend_part.2.refs_4_ = f32[64,7168]{1,0:T(8,128)S(1)} custom-call(s32[3]{0:T(128)S(1)} %copy-done.11, bf16[256,512]{1,0:T(8,128)(2,1)S(1)} %bitcast.13, bf16[32,7680]{1,0:T(8,128)(2,1)S(1)} %get-tuple-element.27.refs_0_, bf16[32,7680]{1,0:T(8,128)(2,1)S(1)} %get-tuple-element.28.refs_1_, bf16[32,7680]{1,0:T(8,128)(2,1)S(1)} %collective-permute-done.6.refs_2_, ...), custom_call_target="tpu_custom_call" | custom-call | flops 1409286144 | bytes 5505024 | tf_op jit(solution)/shard_map/attend_part/pallas_call | solution.py:266
  63.5 3.1 %attend_part.3 = (f32[16,7168]{1,0:T(8,128)S(1)}, bf16[16,7168]{1,0:T(8,128)(2,1)S(1)}, bf16[16,7168]{1,0:T(8,128)(2,1)S(1)}, bf16[16,3584]{1,0:T(8,128)(2,1)S(1)}, bf16[16,3584]{1,0:T(8,128)(2,1)S(1)}) custom-call(s32[3]{0:T(128)S(1)} %copy-done.11, bf16[256,512]{1,0:T(8,128)(2,1)S(1)} %bitcast.14, bf16[32,7680]{1,0:T(8,128)(2,1)} %collective-permute-done.1.refs_0_, ...), custom_call_target="tpu_custom_call" | custom-call | flops 469762048 | bytes 1835008 | tf_op jit(solution)/shard_map/attend_part/pallas_call | solution.py:266
  66.7 1.8 collective-permute-start.14
  68.6 5.4 %collective-permute-start.15 = (bf16[16,7168]{1,0:T(8,128)(2,1)S(1)}, bf16[16,7168]{1,0:T(8,128)(2,1)S(1)}, u32[]{:S(2)}, u32[]{:S(2)}) collective-permute-start(bf16[16,7168]{1,0:T(8,128)(2,1)S(1)} %get-tuple-element.31), channel_id=1, source_target_pairs={{0,30},{2,0},{4,2},{6,4},{8,6},{10,8},{12,10},{14,12},{16,14},{18,... | collective-permute-start | bytes 688136 | tf_op jit(solution)/shard_map/ppermute | solution.py:43
  73.9 4.1 %collective-permute-start.17 = (bf16[16,3584]{1,0:T(8,128)(2,1)S(1)}, bf16[16,3584]{1,0:T(8,128)(2,1)S(1)}, u32[]{:S(2)}, u32[]{:S(2)}) collective-permute-start(bf16[16,3584]{1,0:T(8,128)(2,1)S(1)} %get-tuple-element.33), channel_id=1, source_target_pairs={{0,28},{2,30},{4,0},{6,2},{8,4},{10,6},{12,8},{14,10},{16,12},{18,... | collective-permute-start | bytes 344072 | tf_op jit(solution)/shard_map/ppermute | solution.py:43
  78.1 7.6 %collective-permute-done.16 = bf16[16,3584]{1,0:T(8,128)(2,1)S(1)} collective-permute-done((bf16[16,3584]{1,0:T(8,128)(2,1)S(1)}, bf16[16,3584]{1,0:T(8,128)(2,1)S(1)}, u32[]{:S(2)}, u32[]{:S(2)}) %collective-permute-start.16) | collective-permute-done | bytes 114720 | tf_op jit(solution)/shard_map/ppermute | solution.py:43
  85.7 0.1 add_convert_fusion.1
  85.8 0.8 reshape.73
  86.6 3.7 %all-to-all-start.1 = ((bf16[4,4,7168]{2,1,0:T(4,128)(2,1)}), bf16[4,4,7168]{2,1,0:T(4,128)(2,1)S(1)}, u32[]{:S(2)}, u32[]{:S(2)}) async-start(bf16[4,4,7168]{2,1,0:T(4,128)(2,1)} %reshape.73), calls=%async_computation.1 | async-start | bytes 458752 | tf_op jit(solution)/shard_map/all_to_all | solution.py:440
  90.3 0.5 collective-permute-start.21
  90.8 0.1 collective-permute-start.22
  91.1 16.8 %all-to-all-done.1 = bf16[4,4,7168]{2,1,0:T(4,128)(2,1)S(1)} async-done(((bf16[4,4,7168]{2,1,0:T(4,128)(2,1)}), bf16[4,4,7168]{2,1,0:T(4,128)(2,1)S(1)}, u32[]{:S(2)}, u32[]{:S(2)}) %all-to-all-start.1) | async-done | bytes 229408 | tf_op jit(solution)/shard_map/all_to_all | solution.py:440
  108.1 0.2 multiply_reduce_fusion
  108.5 0.2 fusion.5
  108.7 0.2 select_reduce_fusion.1
  108.8 0.1 fusion.4
  109.0 0.1 select_reduce_fusion
  109.3 36.2 %all-gather = bf16[16,4,7296]{2,1,0:T(4,128)(2,1)} all-gather(bf16[1,4,7296]{2,1,0:T(4,128)(2,1)S(1)} %fusion.2), channel_id=1, replica_groups=mesh['rep'=2,'x'=4,'zb'=4,'j'=4,'c'=2] {'zb','j'}, dimensions={0}, use_global_device_ids=true | all-gather | bytes 992256 | tf_op jit(solution)/shard_map/all_gather | solution.py:507
  145.5 1.7 reshape.77.tokens
  147.1 1.3 dispatch.1
  148.4 3.1 %collective-permute-start.18 = (bf16[32,7296]{1,0:T(8,128)(2,1)S(1)}, bf16[32,7296]{1,0:T(8,128)(2,1)S(1)}, u32[]{:S(2)}, u32[]{:S(2)}) collective-permute-start(bf16[32,7296]{1,0:T(8,128)(2,1)S(1)} %get-tuple-element.36), channel_id=1, source_target_pairs={{0,96},{32,0},{64,32},{96,64},{1,97},{33,1},{65,33},{97,65},{2,98}... | collective-permute-start | bytes 1400840 | tf_op jit(solution)/shard_map/ppermute | solution.py:39
  151.6 1.6 collective-permute-start.25
  153.2 1.5 copy-done.13
  154.7 1.5 copy-done.14
  156.2 7.3 %stage.1 = (bf16[7168,512]{1,0:T(8,128)(2,1)}, bf16[256,7168]{1,0:T(8,128)(2,1)}) custom-call(bf16[7168,128]{1,0:T(8,128)(2,1)S(1)} %copy-done.12, bf16[7168,128]{1,0:T(8,128)(2,1)} %collective-permute-done.20.gate_b, bf16[7168,128]{1,0:T(8,128)(2,1)S(1)} %copy-done.13, bf16[7168,128]{1,0:T(8,128)(2,1)} %collective-permute-done.21.up_b, ...), custom_call_target="tpu_custom_call" | custom-call | flops 3670016000 | bytes 11010048 | tf_op jit(solution)/shard_map/stage/pallas_call | solution.py:348
  163.4 1.0 collective-permute-done.18.refs_1_
  164.5 3.4 %collective-permute-done.19.refs_2_ = bf16[32,7296]{1,0:T(8,128)(2,1)S(1)} collective-permute-done((bf16[32,7296]{1,0:T(8,128)(2,1)S(1)}, bf16[32,7296]{1,0:T(8,128)(2,1)S(1)}, u32[]{:S(2)}, u32[]{:S(2)}) %collective-permute-start.19) | collective-permute-done | bytes 466976 | tf_op jit(solution)/shard_map/ppermute | solution.py:39
  167.9 3.1 %copy-done.1 = bf16[7168,512]{1,0:T(8,128)(2,1)S(1)} copy-done((bf16[7168,512]{1,0:T(8,128)(2,1)S(1)}, bf16[7168,512]{1,0:T(8,128)(2,1)}, u32[]{:S(2)}) %copy-start.1) | copy-done | bytes 7340056
  171.0 2.0 copy-done.3
  173.0 2.5 %expert_part.2 = (bf16[32,7168]{1,0:T(8,128)(2,1)S(1)}, bf16[32,7168]{1,0:T(8,128)(2,1)S(1)}, bf16[32,7168]{1,0:T(8,128)(2,1)S(1)}) custom-call(s32[3]{0:T(128)S(1)} %copy-done.11, bf16[32,7296]{1,0:T(8,128)(2,1)S(1)} %get-tuple-element.35.refs_0_, bf16[32,7296]{1,0:T(8,128)(2,1)S(1)} %collective-permute-done.18.refs_1_, ...), custom_call_target="tpu_custom_call" | custom-call | flops 2113929216 | bytes 1376256 | tf_op jit(solution)/shard_map/expert_part/pallas_call | solution.py:395
  175.5 0.1 collective-permute-start.23
  175.7 3.2 %collective-permute-start.24 = (bf16[32,7168]{1,0:T(8,128)(2,1)S(1)}, bf16[32,7168]{1,0:T(8,128)(2,1)S(1)}, u32[]{:S(2)}, u32[]{:S(2)}) collective-permute-start(bf16[32,7168]{1,0:T(8,128)(2,1)S(1)} %get-tuple-element.42), channel_id=1, source_target_pairs={{0,96},{32,0},{64,32},{96,64},{1,97},{33,1},{65,33},{97,65},{2,98}... | collective-permute-start | bytes 1376264 | tf_op jit(solution)/shard_map/ppermute | solution.py:39
  178.9 2.6 %expert_part.3 = bf16[32,7168]{1,0:T(8,128)(2,1)S(1)} custom-call(s32[3]{0:T(128)S(1)} %copy-done.11, bf16[32,7296]{1,0:T(8,128)(2,1)S(1)} %collective-permute-done.25.refs_0_, bf16[7168,512]{1,0:T(8,128)(2,1)S(1)} %copy-done.2, bf16[256,7168]{1,0:T(8,128)(2,1)S(1)} %copy-done.4), custom_call_target="tpu_custom_call" | custom-call | flops 704643072 | bytes 458752 | tf_op jit(solution)/shard_map/expert_part/pallas_call | solution.py:395
  181.5 0.1 collective-permute-start.26
  181.7 4.6 %collective-permute-done.23.refs_1_ = bf16[32,7168]{1,0:T(8,128)(2,1)S(1)} collective-permute-done((bf16[32,7168]{1,0:T(8,128)(2,1)S(1)}, bf16[32,7168]{1,0:T(8,128)(2,1)S(1)}, u32[]{:S(2)}, u32[]{:S(2)}) %collective-permute-start.23) | collective-permute-done | bytes 458784 | tf_op jit(solution)/shard_map/ppermute | solution.py:39
  186.3 3.5 %collective-permute-done.24.refs_2_ = bf16[32,7168]{1,0:T(8,128)(2,1)S(1)} collective-permute-done((bf16[32,7168]{1,0:T(8,128)(2,1)S(1)}, bf16[32,7168]{1,0:T(8,128)(2,1)S(1)}, u32[]{:S(2)}, u32[]{:S(2)}) %collective-permute-start.24) | collective-permute-done | bytes 458784 | tf_op jit(solution)/shard_map/ppermute | solution.py:39
  189.8 1.8 collective-permute-done.26.refs_3_
  191.6 0.4 collect.1
  192.0 0.6 collective-permute-start.27
  192.6 2.8 %collective-permute-start.28 = (bf16[16,7168]{1,0:T(8,128)(2,1)S(1)}, bf16[16,7168]{1,0:T(8,128)(2,1)S(1)}, u32[]{:S(2)}, u32[]{:S(2)}) collective-permute-start(bf16[16,7168]{1,0:T(8,128)(2,1)S(1)} %get-tuple-element.46), channel_id=1, source_target_pairs={{0,30},{2,0},{4,2},{6,4},{8,6},{10,8},{12,10},{14,12},{16,14},{18,... | collective-permute-start | bytes 688136 | tf_op jit(solution)/shard_map/ppermute | solution.py:43
  195.4 4.1 %collective-permute-start.30 = (bf16[16,3584]{1,0:T(8,128)(2,1)S(1)}, bf16[16,3584]{1,0:T(8,128)(2,1)S(1)}, u32[]{:S(2)}, u32[]{:S(2)}) collective-permute-start(bf16[16,3584]{1,0:T(8,128)(2,1)S(1)} %get-tuple-element.48), channel_id=1, source_target_pairs={{0,28},{2,30},{4,0},{6,2},{8,4},{10,6},{12,8},{14,10},{16,12},{18,... | collective-permute-start | bytes 344072 | tf_op jit(solution)/shard_map/ppermute | solution.py:43
  199.5 2.9 %collective-permute-done.29 = bf16[16,3584]{1,0:T(8,128)(2,1)S(1)} collective-permute-done((bf16[16,3584]{1,0:T(8,128)(2,1)S(1)}, bf16[16,3584]{1,0:T(8,128)(2,1)S(1)}, u32[]{:S(2)}, u32[]{:S(2)}) %collective-permute-start.29) | collective-permute-done | bytes 114720 | tf_op jit(solution)/shard_map/ppermute | solution.py:43
  202.4 3.1 %collective-permute-done.30 = bf16[16,3584]{1,0:T(8,128)(2,1)S(1)} collective-permute-done((bf16[16,3584]{1,0:T(8,128)(2,1)S(1)}, bf16[16,3584]{1,0:T(8,128)(2,1)S(1)}, u32[]{:S(2)}, u32[]{:S(2)}) %collective-permute-start.30) | collective-permute-done | bytes 114720 | tf_op jit(solution)/shard_map/ppermute | solution.py:43
  205.7 20.6 %all_to_all.15 = bf16[4,4,7168]{2,1,0:T(4,128)(2,1)S(1)} all-to-all(bf16[4,4,7168]{2,1,0:T(4,128)(2,1)S(1)} %reshape.74), channel_id=1, replica_groups=mesh['rep'=2,'x'=4,'zb'=4,'j'=4,'c'=2] {'zb'}, dimensions={0} | all-to-all | bytes 458752 | tf_op jit(solution)/shard_map/all_to_all | solution.py:440
  226.5 0.7 add_convert_fusion.2
  (79 shorter events, 1.3 us)
Async XLA Ops:
  0.0 108.5 %copy-start = (bf16[7168,16]{0,1:T(8,128)(2,1)S(1)}, bf16[7168,16]{0,1:T(8,128)(2,1)}, u32[]{:S(2)}) copy-start(bf16[7168,16]{0,1:T(8,128)(2,1)} %param.22) | copy-start | bytes 688132
  0.0 1.2 copy-start.5
  1.2 0.8 copy-start.10
  2.3 37.1 %collective-permute-start.11 = (bf16[32,7680]{1,0:T(8,128)(2,1)S(1)}, bf16[32,7680]{1,0:T(8,128)(2,1)S(1)}, u32[]{:S(2)}, u32[]{:S(2)}) collective-permute-start(bf16[32,7680]{1,0:T(8,128)(2,1)S(1)} %get-tuple-element.27.refs_0_), channel_id=1, source_target_pairs={{0,96},{32,0},{64,32},{96,64},{1,97},{33,1},{65,33},{97,65},{2,98}... | collective-permute-start | bytes 1474568 | tf_op jit(solution)/shard_map/ppermute | solution.py:39
  5.6 34.0 %collective-permute-start.6 = (bf16[32,7680]{1,0:T(8,128)(2,1)S(1)}, bf16[32,7680]{1,0:T(8,128)(2,1)S(1)}, u32[]{:S(2)}, u32[]{:S(2)}) collective-permute-start(bf16[32,7680]{1,0:T(8,128)(2,1)S(1)} %get-tuple-element.27.refs_0_), channel_id=1, source_target_pairs={{0,1},{1,0},{2,3},{3,2},{4,5},{5,4},{6,7},{7,6},{8,9},{9,8},{10,11... | collective-permute-start | bytes 1474568 | tf_op jit(solution)/shard_map/ppermute | solution.py:47
  5.6 34.5 %collective-permute-start = (bf16[32,7680]{1,0:T(8,128)(2,1)S(1)}, bf16[32,7680]{1,0:T(8,128)(2,1)S(1)}, u32[]{:S(2)}, u32[]{:S(2)}) collective-permute-start(bf16[32,7680]{1,0:T(8,128)(2,1)S(1)} %get-tuple-element.27.refs_0_), channel_id=1, source_target_pairs={{0,32},{32,64},{64,96},{96,0},{1,33},{33,65},{65,97},{97,1},{2,34}... | collective-permute-start | bytes 1474568 | tf_op jit(solution)/shard_map/ppermute | solution.py:39
  5.6 34.5 %collective-permute-start.2 = (bf16[32,7680]{1,0:T(8,128)(2,1)S(1)}, bf16[32,7680]{1,0:T(8,128)(2,1)S(1)}, u32[]{:S(2)}, u32[]{:S(2)}) collective-permute-start(bf16[32,7680]{1,0:T(8,128)(2,1)S(1)} %get-tuple-element.28.refs_1_), channel_id=1, source_target_pairs={{0,96},{32,0},{64,32},{96,64},{1,97},{33,1},{65,33},{97,65},{2,98}... | collective-permute-start | bytes 1474568 | tf_op jit(solution)/shard_map/ppermute | solution.py:39
  8.8 34.6 %collective-permute-start.8 = (bf16[32,7680]{1,0:T(8,128)(2,1)S(1)}, bf16[32,7680]{1,0:T(8,128)(2,1)}, u32[]{:S(2)}, u32[]{:S(2)}) collective-permute-start(bf16[32,7680]{1,0:T(8,128)(2,1)S(1)} %get-tuple-element.28.refs_1_), channel_id=1, source_target_pairs={{0,32},{32,64},{64,96},{96,0},{1,33},{33,65},{65,97},{97,1},{2,34}... | collective-permute-start | bytes 1474568 | tf_op jit(solution)/shard_map/ppermute | solution.py:39
  9.5 48.0 %copy-start.11 = (s32[3]{0:T(128)S(1)}, s32[3]{0:T(128)}, u32[]{:S(2)}) copy-start(s32[3]{0:T(128)} %pad_add_fusion.where_ref) | copy-start | bytes 40
  15.4 42.1 %all-to-all-start = ((bf16[16,16,512]{2,1,0:T(8,128)(2,1)}), bf16[16,16,512]{2,1,0:T(8,128)(2,1)S(1)}, u32[]{:S(2)}, u32[]{:S(2)}) async-start(bf16[16,16,512]{2,1,0:T(8,128)(2,1)} %bitcast.17), calls=%async_computation | async-start | bytes 524288 | tf_op jit(solution)/shard_map/all_to_all | solution.py:472
  39.4 4.0 %collective-permute-start.7 = (bf16[32,7680]{1,0:T(8,128)(2,1)S(1)}, bf16[32,7680]{1,0:T(8,128)(2,1)S(1)}, u32[]{:S(2)}, u32[]{:S(2)}) collective-permute-start(bf16[32,7680]{1,0:T(8,128)(2,1)S(1)} %get-tuple-element.28.refs_1_), channel_id=1, source_target_pairs={{0,1},{1,0},{2,3},{3,2},{4,5},{5,4},{6,7},{7,6},{8,9},{9,8},{10,11... | collective-permute-start | bytes 1474568 | tf_op jit(solution)/shard_map/ppermute | solution.py:47
  39.6 5.2 %collective-permute-start.12 = (bf16[32,7680]{1,0:T(8,128)(2,1)S(1)}, bf16[32,7680]{1,0:T(8,128)(2,1)S(1)}, u32[]{:S(2)}, u32[]{:S(2)}) collective-permute-start(bf16[32,7680]{1,0:T(8,128)(2,1)S(1)} %collective-permute-done.11.refs_8_), channel_id=1, source_target_pairs={{0,1},{1,0},{2,3},{3,2},{4,5},{5,4},{6,7},{7,6},{8,9},{9,8},{10,11... | collective-permute-start | bytes 1474568 | tf_op jit(solution)/shard_map/ppermute | solution.py:47
  40.0 14.9 %collective-permute-start.1 = (bf16[32,7680]{1,0:T(8,128)(2,1)S(1)}, bf16[32,7680]{1,0:T(8,128)(2,1)}, u32[]{:S(2)}, u32[]{:S(2)}) collective-permute-start(bf16[32,7680]{1,0:T(8,128)(2,1)S(1)} %collective-permute-done.refs_4_), channel_id=1, source_target_pairs={{0,32},{32,64},{64,96},{96,0},{1,33},{33,65},{65,97},{97,1},{2,34}... | collective-permute-start | bytes 1474568 | tf_op jit(solution)/shard_map/ppermute | solution.py:39
  40.0 14.9 %collective-permute-start.3 = (bf16[32,7680]{1,0:T(8,128)(2,1)S(1)}, bf16[32,7680]{1,0:T(8,128)(2,1)}, u32[]{:S(2)}, u32[]{:S(2)}) collective-permute-start(bf16[32,7680]{1,0:T(8,128)(2,1)S(1)} %collective-permute-done.2.refs_9_), channel_id=1, source_target_pairs={{0,96},{32,0},{64,32},{96,64},{1,97},{33,1},{65,33},{97,65},{2,98}... | collective-permute-start | bytes 1474568 | tf_op jit(solution)/shard_map/ppermute | solution.py:39
  43.4 14.1 %collective-permute-start.9 = (bf16[32,7680]{1,0:T(8,128)(2,1)S(1)}, bf16[32,7680]{1,0:T(8,128)(2,1)}, u32[]{:S(2)}, u32[]{:S(2)}) collective-permute-start(bf16[32,7680]{1,0:T(8,128)(2,1)S(1)} %collective-permute-done.refs_4_), channel_id=1, source_target_pairs={{0,1},{1,0},{2,3},{3,2},{4,5},{5,4},{6,7},{7,6},{8,9},{9,8},{10,11... | collective-permute-start | bytes 1474568 | tf_op jit(solution)/shard_map/ppermute | solution.py:47
  43.4 0.8 copy-start.6
  44.2 13.3 %collective-permute-start.10 = (bf16[32,7680]{1,0:T(8,128)(2,1)}, bf16[32,7680]{1,0:T(8,128)(2,1)}, u32[]{:S(2)}, u32[]{:S(2)}) collective-permute-start(bf16[32,7680]{1,0:T(8,128)(2,1)} %collective-permute-done.8.refs_5_), channel_id=1, source_target_pairs={{0,1},{1,0},{2,3},{3,2},{4,5},{5,4},{6,7},{7,6},{8,9},{9,8},{10,11... | collective-permute-start | bytes 1474568 | tf_op jit(solution)/shard_map/ppermute | solution.py:47
  44.7 0.8 copy-start.8
  45.5 12.0 %collective-permute-start.13 = (bf16[32,7680]{1,0:T(8,128)(2,1)S(1)}, bf16[32,7680]{1,0:T(8,128)(2,1)}, u32[]{:S(2)}, u32[]{:S(2)}) collective-permute-start(bf16[32,7680]{1,0:T(8,128)(2,1)S(1)} %collective-permute-done.2.refs_9_), channel_id=1, source_target_pairs={{0,1},{1,0},{2,3},{3,2},{4,5},{5,4},{6,7},{7,6},{8,9},{9,8},{10,11... | collective-permute-start | bytes 1474568 | tf_op jit(solution)/shard_map/ppermute | solution.py:47
  54.9 8.6 %collective-permute-start.4 = (bf16[32,7680]{1,0:T(8,128)(2,1)}, bf16[32,7680]{1,0:T(8,128)(2,1)}, u32[]{:S(2)}, u32[]{:S(2)}) collective-permute-start(bf16[32,7680]{1,0:T(8,128)(2,1)} %collective-permute-done.1.refs_0_), channel_id=1, source_target_pairs={{0,1},{1,0},{2,3},{3,2},{4,5},{5,4},{6,7},{7,6},{8,9},{9,8},{10,11... | collective-permute-start | bytes 1474568 | tf_op jit(solution)/shard_map/ppermute | solution.py:47
  54.9 8.6 %collective-permute-start.5 = (bf16[32,7680]{1,0:T(8,128)(2,1)}, bf16[32,7680]{1,0:T(8,128)(2,1)}, u32[]{:S(2)}, u32[]{:S(2)}) collective-permute-start(bf16[32,7680]{1,0:T(8,128)(2,1)} %collective-permute-done.3.refs_1_), channel_id=1, source_target_pairs={{0,1},{1,0},{2,3},{3,2},{4,5},{5,4},{6,7},{7,6},{8,9},{9,8},{10,11... | collective-permute-start | bytes 1474568 | tf_op jit(solution)/shard_map/ppermute | solution.py:47
  57.5 1.0 copy-start.7
  58.6 1.0 copy-start.9
  66.6 23.6 %copy-start.12 = (bf16[7168,128]{1,0:T(8,128)(2,1)S(1)}, bf16[7168,128]{1,0:T(8,128)(2,1)}, u32[]{:S(2)}) copy-start(bf16[7168,128]{1,0:T(8,128)(2,1)} %gate_a.1) | copy-start | bytes 5505028
  66.7 24.3 %copy-start.17 = (bf16[7168]{0:T(1024)(128)(2,1)S(1)}, bf16[7168]{0:T(1024)(128)(2,1)}, u32[]{:S(2)}) copy-start(bf16[7168]{0:T(1024)(128)(2,1)} %param.21) | copy-start | bytes 43012
  66.7 24.3 %copy-start.15 = (bf16[2,2,7168]{2,1,0:T(2,128)(2,1)S(1)}, bf16[2,2,7168]{2,1,0:T(2,128)(2,1)}, u32[]{:S(2)}) copy-start(bf16[2,2,7168]{2,1,0:T(2,128)(2,1)} %param.18) | copy-start | bytes 172036
  66.7 24.3 %copy-start.18 = (s32[2,2,8]{2,1,0:T(2,128)S(1)}, s32[2,2,8]{2,1,0:T(2,128)}, u32[]{:S(2)}) copy-start(s32[2,2,8]{2,1,0:T(2,128)} %param.24) | copy-start | bytes 388
  66.7 24.3 %copy-start.16 = (s32[2,2,8]{2,1,0:T(2,128)S(1)}, s32[2,2,8]{2,1,0:T(2,128)}, u32[]{:S(2)}) copy-start(s32[2,2,8]{2,1,0:T(2,128)} %param.23) | copy-start | bytes 388
  66.7 19.0 %collective-permute-start.14 = (bf16[16,7168]{1,0:T(8,128)(2,1)S(1)}, bf16[16,7168]{1,0:T(8,128)(2,1)S(1)}, u32[]{:S(2)}, u32[]{:S(2)}) collective-permute-start(bf16[16,7168]{1,0:T(8,128)(2,1)S(1)} %get-tuple-element.30), channel_id=1, source_target_pairs={{0,2},{2,4},{4,6},{6,8},{8,10},{10,12},{12,14},{14,16},{16,18},{18... | collective-permute-start | bytes 688136 | tf_op jit(solution)/shard_map/ppermute | solution.py:43
  68.6 17.1 %collective-permute-start.15 = (bf16[16,7168]{1,0:T(8,128)(2,1)S(1)}, bf16[16,7168]{1,0:T(8,128)(2,1)S(1)}, u32[]{:S(2)}, u32[]{:S(2)}) collective-permute-start(bf16[16,7168]{1,0:T(8,128)(2,1)S(1)} %get-tuple-element.31), channel_id=1, source_target_pairs={{0,30},{2,0},{4,2},{6,4},{8,6},{10,8},{12,10},{14,12},{16,14},{18,... | collective-permute-start | bytes 688136 | tf_op jit(solution)/shard_map/ppermute | solution.py:43
  73.9 11.7 %collective-permute-start.16 = (bf16[16,3584]{1,0:T(8,128)(2,1)S(1)}, bf16[16,3584]{1,0:T(8,128)(2,1)S(1)}, u32[]{:S(2)}, u32[]{:S(2)}) collective-permute-start(bf16[16,3584]{1,0:T(8,128)(2,1)S(1)} %get-tuple-element.32), channel_id=1, source_target_pairs={{0,4},{2,6},{4,8},{6,10},{8,12},{10,14},{12,16},{14,18},{16,20},{1... | collective-permute-start | bytes 344072 | tf_op jit(solution)/shard_map/ppermute | solution.py:43
  73.9 11.7 %collective-permute-start.17 = (bf16[16,3584]{1,0:T(8,128)(2,1)S(1)}, bf16[16,3584]{1,0:T(8,128)(2,1)S(1)}, u32[]{:S(2)}, u32[]{:S(2)}) collective-permute-start(bf16[16,3584]{1,0:T(8,128)(2,1)S(1)} %get-tuple-element.33), channel_id=1, source_target_pairs={{0,28},{2,30},{4,0},{6,2},{8,4},{10,6},{12,8},{14,10},{16,12},{18,... | collective-permute-start | bytes 344072 | tf_op jit(solution)/shard_map/ppermute | solution.py:43
  86.6 21.3 %all-to-all-start.1 = ((bf16[4,4,7168]{2,1,0:T(4,128)(2,1)}), bf16[4,4,7168]{2,1,0:T(4,128)(2,1)S(1)}, u32[]{:S(2)}, u32[]{:S(2)}) async-start(bf16[4,4,7168]{2,1,0:T(4,128)(2,1)} %reshape.73), calls=%async_computation.1 | async-start | bytes 458752 | tf_op jit(solution)/shard_map/all_to_all | solution.py:440
  90.3 61.3 %collective-permute-start.20 = (bf16[7168,128]{1,0:T(8,128)(2,1)S(1)}, bf16[7168,128]{1,0:T(8,128)(2,1)}, u32[]{:S(2)}, u32[]{:S(2)}) collective-permute-start(bf16[7168,128]{1,0:T(8,128)(2,1)S(1)} %copy-done.12), channel_id=1, source_target_pairs={{0,1},{1,0},{2,3},{3,2},{4,5},{5,4},{6,7},{7,6},{8,9},{9,8},{10,11... | collective-permute-start | bytes 5505032 | tf_op jit(solution)/shard_map/ppermute | solution.py:47
  90.3 62.9 %collective-permute-start.21 = (bf16[7168,128]{1,0:T(8,128)(2,1)}, bf16[7168,128]{1,0:T(8,128)(2,1)}, u32[]{:S(2)}, u32[]{:S(2)}) collective-permute-start(bf16[7168,128]{1,0:T(8,128)(2,1)} %up_a.1), channel_id=1, source_target_pairs={{0,1},{1,0},{2,3},{3,2},{4,5},{5,4},{6,7},{7,6},{8,9},{9,8},{10,11... | collective-permute-start | bytes 5505032 | tf_op jit(solution)/shard_map/ppermute | solution.py:47
  90.8 62.4 %collective-permute-start.22 = (bf16[128,7168]{1,0:T(8,128)(2,1)}, bf16[128,7168]{1,0:T(8,128)(2,1)}, u32[]{:S(2)}, u32[]{:S(2)}) collective-permute-start(bf16[128,7168]{1,0:T(8,128)(2,1)} %down_a.1), channel_id=1, source_target_pairs={{0,1},{1,0},{2,3},{3,2},{4,5},{5,4},{6,7},{7,6},{8,9},{9,8},{10,11... | collective-permute-start | bytes 5505032 | tf_op jit(solution)/shard_map/ppermute | solution.py:47
  148.4 16.0 %collective-permute-start.18 = (bf16[32,7296]{1,0:T(8,128)(2,1)S(1)}, bf16[32,7296]{1,0:T(8,128)(2,1)S(1)}, u32[]{:S(2)}, u32[]{:S(2)}) collective-permute-start(bf16[32,7296]{1,0:T(8,128)(2,1)S(1)} %get-tuple-element.36), channel_id=1, source_target_pairs={{0,96},{32,0},{64,32},{96,64},{1,97},{33,1},{65,33},{97,65},{2,98}... | collective-permute-start | bytes 1400840 | tf_op jit(solution)/shard_map/ppermute | solution.py:39
  151.6 16.3 %collective-permute-start.19 = (bf16[32,7296]{1,0:T(8,128)(2,1)S(1)}, bf16[32,7296]{1,0:T(8,128)(2,1)S(1)}, u32[]{:S(2)}, u32[]{:S(2)}) collective-permute-start(bf16[32,7296]{1,0:T(8,128)(2,1)S(1)} %get-tuple-element.37), channel_id=1, source_target_pairs={{0,32},{32,64},{64,96},{96,0},{1,33},{33,65},{65,97},{97,1},{2,34}... | collective-permute-start | bytes 1400840 | tf_op jit(solution)/shard_map/ppermute | solution.py:39
  151.6 27.3 %collective-permute-start.25 = (bf16[32,7296]{1,0:T(8,128)(2,1)S(1)}, bf16[32,7296]{1,0:T(8,128)(2,1)S(1)}, u32[]{:S(2)}, u32[]{:S(2)}) collective-permute-start(bf16[32,7296]{1,0:T(8,128)(2,1)S(1)} %get-tuple-element.43), channel_id=1, source_target_pairs={{0,64},{32,96},{64,0},{96,32},{1,65},{33,97},{65,1},{97,33},{2,66}... | collective-permute-start | bytes 1400840 | tf_op jit(solution)/shard_map/ppermute | solution.py:39
  153.2 1.5 copy-start.13
  154.7 1.5 copy-start.14
  167.9 3.1 %copy-start.1 = (bf16[7168,512]{1,0:T(8,128)(2,1)S(1)}, bf16[7168,512]{1,0:T(8,128)(2,1)}, u32[]{:S(2)}) copy-start(bf16[7168,512]{1,0:T(8,128)(2,1)} %get-tuple-element.38.refs_3_.refs_1_) | copy-start | bytes 22020100
  171.0 2.0 copy-start.3
  173.0 5.9 %copy-start.2 = (bf16[7168,512]{1,0:T(8,128)(2,1)S(1)}, bf16[7168,512]{1,0:T(8,128)(2,1)}, u32[]{:S(2)}) copy-start(bf16[7168,512]{1,0:T(8,128)(2,1)} %get-tuple-element.38.refs_3_.refs_1_) | copy-start | bytes 22020100
  173.0 5.9 %copy-start.4 = (bf16[256,7168]{1,0:T(8,128)(2,1)S(1)}, bf16[256,7168]{1,0:T(8,128)(2,1)}, u32[]{:S(2)}) copy-start(bf16[256,7168]{1,0:T(8,128)(2,1)} %get-tuple-element.39.refs_4_.refs_2_) | copy-start | bytes 11010052
  175.5 10.7 %collective-permute-start.23 = (bf16[32,7168]{1,0:T(8,128)(2,1)S(1)}, bf16[32,7168]{1,0:T(8,128)(2,1)S(1)}, u32[]{:S(2)}, u32[]{:S(2)}) collective-permute-start(bf16[32,7168]{1,0:T(8,128)(2,1)S(1)} %get-tuple-element.41), channel_id=1, source_target_pairs={{0,32},{32,64},{64,96},{96,0},{1,33},{33,65},{65,97},{97,1},{2,34}... | collective-permute-start | bytes 1376264 | tf_op jit(solution)/shard_map/ppermute | solution.py:39
  175.7 14.1 %collective-permute-start.24 = (bf16[32,7168]{1,0:T(8,128)(2,1)S(1)}, bf16[32,7168]{1,0:T(8,128)(2,1)S(1)}, u32[]{:S(2)}, u32[]{:S(2)}) collective-permute-start(bf16[32,7168]{1,0:T(8,128)(2,1)S(1)} %get-tuple-element.42), channel_id=1, source_target_pairs={{0,96},{32,0},{64,32},{96,64},{1,97},{33,1},{65,33},{97,65},{2,98}... | collective-permute-start | bytes 1376264 | tf_op jit(solution)/shard_map/ppermute | solution.py:39
  181.5 10.1 %collective-permute-start.26 = (bf16[32,7168]{1,0:T(8,128)(2,1)S(1)}, bf16[32,7168]{1,0:T(8,128)(2,1)S(1)}, u32[]{:S(2)}, u32[]{:S(2)}) collective-permute-start(bf16[32,7168]{1,0:T(8,128)(2,1)S(1)} %expert_part.3), channel_id=1, source_target_pairs={{0,64},{32,96},{64,0},{96,32},{1,65},{33,97},{65,1},{97,33},{2,66}... | collective-permute-start | bytes 1376264 | tf_op jit(solution)/shard_map/ppermute | solution.py:39
  192.0 13.4 %collective-permute-start.27 = (bf16[16,7168]{1,0:T(8,128)(2,1)S(1)}, bf16[16,7168]{1,0:T(8,128)(2,1)S(1)}, u32[]{:S(2)}, u32[]{:S(2)}) collective-permute-start(bf16[16,7168]{1,0:T(8,128)(2,1)S(1)} %get-tuple-element.45), channel_id=1, source_target_pairs={{0,2},{2,4},{4,6},{6,8},{8,10},{10,12},{12,14},{14,16},{16,18},{18... | collective-permute-start | bytes 688136 | tf_op jit(solution)/shard_map/ppermute | solution.py:43
  192.6 12.9 %collective-permute-start.28 = (bf16[16,7168]{1,0:T(8,128)(2,1)S(1)}, bf16[16,7168]{1,0:T(8,128)(2,1)S(1)}, u32[]{:S(2)}, u32[]{:S(2)}) collective-permute-start(bf16[16,7168]{1,0:T(8,128)(2,1)S(1)} %get-tuple-element.46), channel_id=1, source_target_pairs={{0,30},{2,0},{4,2},{6,4},{8,6},{10,8},{12,10},{14,12},{16,14},{18,... | collective-permute-start | bytes 688136 | tf_op jit(solution)/shard_map/ppermute | solution.py:43
  195.4 7.0 %collective-permute-start.29 = (bf16[16,3584]{1,0:T(8,128)(2,1)S(1)}, bf16[16,3584]{1,0:T(8,128)(2,1)S(1)}, u32[]{:S(2)}, u32[]{:S(2)}) collective-permute-start(bf16[16,3584]{1,0:T(8,128)(2,1)S(1)} %get-tuple-element.47), channel_id=1, source_target_pairs={{0,4},{2,6},{4,8},{6,10},{8,12},{10,14},{12,16},{14,18},{16,20},{1... | collective-permute-start | bytes 344072 | tf_op jit(solution)/shard_map/ppermute | solution.py:43
  195.4 10.1 %collective-permute-start.30 = (bf16[16,3584]{1,0:T(8,128)(2,1)S(1)}, bf16[16,3584]{1,0:T(8,128)(2,1)S(1)}, u32[]{:S(2)}, u32[]{:S(2)}) collective-permute-start(bf16[16,3584]{1,0:T(8,128)(2,1)S(1)} %get-tuple-element.48), channel_id=1, source_target_pairs={{0,28},{2,30},{4,0},{6,2},{8,4},{10,6},{12,8},{14,10},{16,12},{18,... | collective-permute-start | bytes 344072 | tf_op jit(solution)/shard_map/ppermute | solution.py:43

commit v2 on v1

--- a/solution.py
+++ b/solution.py
@@ -76,6 +76,14 @@
 
 def hbm():
     return pl.BlockSpec(memory_space=pltpu.HBM)
+
+
+def held_in_hbm(a):
+    return pltpu.with_memory_space_constraint(a, pltpu.HBM)
+
+
+def held_in_vmem(a):
+    return pltpu.with_memory_space_constraint(a, pltpu.VMEM)
 
 
 def params(mib):
@@ -148,10 +156,10 @@
         ],
         out_specs=pl.BlockSpec((rows, LAT), lambda b: (0, 0)),
         scratch_shapes=[pltpu.VMEM((rows, LAT), bf16)],
-        compiler_params=params(60),
+        compiler_params=params(24),
         cost_estimate=cost(2 * rows * length * (width + LAT), 2 * cache_kv.size),
         name="context_rows",
-    )(where, lengths, keys, queries, new_kv)
+    )(where, lengths, held_in_hbm(keys), held_in_hbm(queries), new_kv)
 
 
 def pack_kernel(up, rows, tops, lows, sem):
@@ -175,10 +183,10 @@
         in_specs=[hbm()] * 2,
         out_specs=[vmem()] * 2,
         scratch_shapes=[pltpu.SemaphoreType.DMA((2, 2))],
-        compiler_params=params(4),
+        compiler_params=params(12),
         cost_estimate=cost(1, 4 * rows.size),
         name="pack",
-    )(up, rows)
+    )(held_in_hbm(up), held_in_hbm(rows))
 
 
 OUT_TILE = 512
@@ -277,7 +285,7 @@
         compiler_params=params(12),
         cost_estimate=cost(8 * RING * tok * depth * dim, 2 * depth * dim),
         name="attend_part",
-    )(where, arrived, *pieces, *([before] if last else []))
+    )(where, arrived, *[held_in_hbm(p) for p in pieces], *([before] if last else []))
 
 
 def dispatch_kernel(tok, nx, where_ref, tokens, *refs):
@@ -354,10 +362,10 @@
         in_specs=[hbm()] * 6,
         out_specs=[vmem()] * 2,
         scratch_shapes=[pltpu.SemaphoreType.DMA((6,))],
-        compiler_params=params(40),
+        compiler_params=params(4),
         cost_estimate=cost(4 * 1000 * dim * part, 12 * dim * part),
         name="stage",
-    )(*weights)
+    )(*[held_in_hbm(w) for w in weights])
 
 
 def expert_kernel(groups, where_ref, *refs):
@@ -401,7 +409,7 @@
         compiler_params=params(8),
         cost_estimate=cost(6 * rows * wide.size, 2 * rows * dim),
         name="expert_part",
-    )(where, *tokens, wide, deep)
+    )(where, *tokens, held_in_vmem(wide), held_in_vmem(deep))
 
 
 def collect_kernel(count, spread, *refs):

time: 228 us -> 222 us (0.974)
  the two profiles are of different devices: /device:TPU:40 before, /device:TPU:34 now
where the time goes in v2:
time: 222 us
  starting transfers between devices  68.6 us (31%)
  waiting for transfers between devices  63.9 us (29%)
  blocking collectives  56.6 us (25%)
  Pallas kernels  26.5 us (12%)
  local copies, waits for them, and re-layouts  3.67 us (2%)
    ppermute x12, starting transfers between devices, shift_x(): return lax.ppermute(a, 'x', [(i, (i + step) % n) for i in range(n)])  36.6 us
    ppermute x12, waiting for transfers between devices, shift_x(): return lax.ppermute(a, 'x', [(i, (i + step) % n) for i in range(n)])  33.9 us
    all_gather x1, blocking collectives, layer(): ring = lax.all_gather(payload, ZAX, axis=0, tiled=True)  33.8 us
    all_to_all x1, blocking collectives, reduce_z(): got = lax.all_to_all(sent, 'zb', split_axis=0, concat_axis=0, tiled=True)  22.8 us
    ppermute x8, starting transfers between devices, shift_z(): return lax.ppermute(a, ZAX, [(i, (i + step) % RING) for i in range(RING)])  16.7 us
    all_to_all x1, waiting for transfers between devices, reduce_z(): got = lax.all_to_all(sent, 'zb', split_axis=0, concat_axis=0, tiled=True)  16.1 us
    ppermute x8, waiting for transfers between devices, shift_z(): return lax.ppermute(a, ZAX, [(i, (i + step) % RING) for i in range(RING)])  13.8 us
    pallas_call x2, Pallas kernels, attend_part(): pl.pallas_call(functools.partial(attend_kernel, tok, nx, count, first, la...  8.28 us
  transfers between devices with their start and end apart: 33, of which 9 were waited for; matrix products, arithmetic and copies ran while one was open for 1% of the time, Pallas kernels for 10%

profile of v2, /device:TPU:34, one launch (start us, length us, event | category | flops | bytes accessed | tf_op | source)
XLA Modules:
  0.0 221.9 jit_solution(3576989594277949299)
XLA Ops:
  0.0 1.2 pack.1
  1.3 19.5 %collective-permute-start.11 = (bf16[32,7680]{1,0:T(8,128)(2,1)S(1)}, bf16[32,7680]{1,0:T(8,128)(2,1)S(1)}, u32[]{:S(2)}, u32[]{:S(2)}) collective-permute-start(bf16[32,7680]{1,0:T(8,128)(2,1)S(1)} %get-tuple-element.27.refs_0_), channel_id=1, source_target_pairs={{0,96},{32,0},{64,32},{96,64},{1,97},{33,1},{65,33},{97,65},{2,98}... | collective-permute-start | bytes 1474568 | tf_op jit(solution)/shard_map/ppermute | solution.py:39
  20.8 2.0 collective-permute-start.2
  22.9 0.7 copy-done.3
  23.6 0.7 copy-done.4
  24.2 5.8 %context_rows.1 = bf16[256,512]{1,0:T(8,128)(2,1)} custom-call(s32[3]{0:T(128)S(1)} %pad_add_fusion.where_ref, s32[2]{0:T(128)S(1)} %copy-done.4, bf16[2,576,2048]{2,1,0:T(8,128)(2,1)} %bitcast.15, bf16[2,2,64,576]{3,2,1,0:T(8,128)(2,1)} %queries.1, bf16[2,2,576]{2,1,0:T(2,128)(2,1)S(1)} %copy-done.3), custom_call_target="tpu_custom_call" | custom-call | flops 1140850688 | bytes 4718592 | tf_op jit(solution)/shard_map/context_rows/pallas_call | solution.py:146
  30.0 6.6 %all-to-all-start = ((bf16[16,16,512]{2,1,0:T(8,128)(2,1)}), bf16[16,16,512]{2,1,0:T(8,128)(2,1)S(1)}, u32[]{:S(2)}, u32[]{:S(2)}) async-start(bf16[16,16,512]{2,1,0:T(8,128)(2,1)} %bitcast.4), calls=%async_computation | async-start | bytes 524288 | tf_op jit(solution)/shard_map/all_to_all | solution.py:480
  36.7 0.1 collective-permute-start.7
  36.9 0.5 collective-permute-start.12
  37.3 2.1 collective-permute-start.1
  39.5 0.7 collective-permute-start.3
  40.2 5.3 %collective-permute-done.8.refs_5_ = bf16[32,7680]{1,0:T(8,128)(2,1)} collective-permute-done((bf16[32,7680]{1,0:T(8,128)(2,1)S(1)}, bf16[32,7680]{1,0:T(8,128)(2,1)}, u32[]{:S(2)}, u32[]{:S(2)}) %collective-permute-start.8) | collective-permute-done | bytes 491552 | tf_op jit(solution)/shard_map/ppermute | solution.py:39
  45.5 0.5 collective-permute-start.10
  46.0 0.1 collective-permute-start.13
  46.2 9.3 %collective-permute-done.1.refs_0_ = bf16[32,7680]{1,0:T(8,128)(2,1)S(1)} collective-permute-done((bf16[32,7680]{1,0:T(8,128)(2,1)S(1)}, bf16[32,7680]{1,0:T(8,128)(2,1)S(1)}, u32[]{:S(2)}, u32[]{:S(2)}) %collective-permute-start.1) | collective-permute-done | bytes 491552 | tf_op jit(solution)/shard_map/ppermute | solution.py:39
  55.5 0.8 collective-permute-start.5
  56.4 5.2 %attend_part.2.refs_4_ = f32[64,7168]{1,0:T(8,128)S(1)} custom-call(s32[3]{0:T(128)S(1)} %pad_add_fusion.where_ref, bf16[256,512]{1,0:T(8,128)(2,1)S(1)} %bitcast.13, bf16[32,7680]{1,0:T(8,128)(2,1)} %copy-done.1, bf16[32,7680]{1,0:T(8,128)(2,1)} %copy-done.2, bf16[32,7680]{1,0:T(8,128)(2,1)} %copy-done.7, bf16[32,7680]{1,0:T(8,128)(2,1)} %copy-done.11, ...), custom_call_target="tpu_custom_call" | custom-call | flops 1409286144 | bytes 5505024 | tf_op jit(solution)/shard_map/attend_part/pallas_call | solution.py:274
  61.6 0.8 copy-done.13
  62.4 3.1 %attend_part.3 = (f32[16,7168]{1,0:T(8,128)S(1)}, bf16[16,7168]{1,0:T(8,128)(2,1)S(1)}, bf16[16,7168]{1,0:T(8,128)(2,1)S(1)}, bf16[16,3584]{1,0:T(8,128)(2,1)S(1)}, bf16[16,3584]{1,0:T(8,128)(2,1)S(1)}) custom-call(s32[3]{0:T(128)S(1)} %pad_add_fusion.where_ref, bf16[256,512]{1,0:T(8,128)(2,1)S(1)} %bitcast.14, bf16[32,7680]{1,0:T(8,128)(2,1)} %copy-done.10, ...), custom_call_target="tpu_custom_call" | custom-call | flops 469762048 | bytes 1835008 | tf_op jit(solution)/shard_map/attend_part/pallas_call | solution.py:274
  65.5 0.1 collective-permute-start.14
  65.7 4.9 %collective-permute-start.15 = (bf16[16,7168]{1,0:T(8,128)(2,1)S(1)}, bf16[16,7168]{1,0:T(8,128)(2,1)S(1)}, u32[]{:S(2)}, u32[]{:S(2)}) collective-permute-start(bf16[16,7168]{1,0:T(8,128)(2,1)S(1)} %get-tuple-element.31), channel_id=1, source_target_pairs={{0,30},{2,0},{4,2},{6,4},{8,6},{10,8},{12,10},{14,12},{16,14},{18,... | collective-permute-start | bytes 688136 | tf_op jit(solution)/shard_map/ppermute | solution.py:43
  70.6 4.1 %collective-permute-start.17 = (bf16[16,3584]{1,0:T(8,128)(2,1)S(1)}, bf16[16,3584]{1,0:T(8,128)(2,1)S(1)}, u32[]{:S(2)}, u32[]{:S(2)}) collective-permute-start(bf16[16,3584]{1,0:T(8,128)(2,1)S(1)} %get-tuple-element.33), channel_id=1, source_target_pairs={{0,28},{2,30},{4,0},{6,2},{8,4},{10,6},{12,8},{14,10},{16,12},{18,... | collective-permute-start | bytes 344072 | tf_op jit(solution)/shard_map/ppermute | solution.py:43
  74.7 7.6 %collective-permute-done.16 = bf16[16,3584]{1,0:T(8,128)(2,1)S(1)} collective-permute-done((bf16[16,3584]{1,0:T(8,128)(2,1)S(1)}, bf16[16,3584]{1,0:T(8,128)(2,1)S(1)}, u32[]{:S(2)}, u32[]{:S(2)}) %collective-permute-start.16) | collective-permute-done | bytes 114720 | tf_op jit(solution)/shard_map/ppermute | solution.py:43
  82.4 0.1 add_convert_fusion.1
  82.5 0.8 reshape.73
  83.3 6.2 %all-to-all-start.1 = ((bf16[4,4,7168]{2,1,0:T(4,128)(2,1)}), bf16[4,4,7168]{2,1,0:T(4,128)(2,1)S(1)}, u32[]{:S(2)}, u32[]{:S(2)}) async-start(bf16[4,4,7168]{2,1,0:T(4,128)(2,1)} %reshape.73), calls=%async_computation.1 | async-start | bytes 458752 | tf_op jit(solution)/shard_map/all_to_all | solution.py:448
  89.5 0.5 collective-permute-start.21
  90.1 0.1 select_reduce_fusion.2
  90.2 16.1 %all-to-all-done.1 = bf16[4,4,7168]{2,1,0:T(4,128)(2,1)S(1)} async-done(((bf16[4,4,7168]{2,1,0:T(4,128)(2,1)}), bf16[4,4,7168]{2,1,0:T(4,128)(2,1)S(1)}, u32[]{:S(2)}, u32[]{:S(2)}) %all-to-all-start.1) | async-done | bytes 229408 | tf_op jit(solution)/shard_map/all_to_all | solution.py:448
  106.3 0.1 convert_reduce_fusion.1
  106.4 0.1 reduce_sum.68
  106.5 0.2 multiply_reduce_fusion
  106.7 0.1 multiply_convert_fusion
  106.9 0.2 fusion.5
  107.0 0.2 select_reduce_fusion.1
  107.2 0.1 fusion.4
  107.4 0.1 select_reduce_fusion
  107.5 0.1 concatenate.13
  107.7 33.8 %all-gather = bf16[16,4,7296]{2,1,0:T(4,128)(2,1)S(1)} all-gather(bf16[1,4,7296]{2,1,0:T(4,128)(2,1)S(1)} %fusion.2), channel_id=1, replica_groups=mesh['rep'=2,'x'=4,'zb'=4,'j'=4,'c'=2] {'zb','j'}, dimensions={0}, use_global_device_ids=true | all-gather | bytes 992256 | tf_op jit(solution)/shard_map/all_gather | solution.py:515
  141.5 0.2 reshape.77.tokens
  141.7 1.3 dispatch.1
  143.0 1.4 collective-permute-start.18
  144.4 0.7 collective-permute-start.19
  145.1 5.7 %collective-permute-start.25 = (bf16[32,7296]{1,0:T(8,128)(2,1)S(1)}, bf16[32,7296]{1,0:T(8,128)(2,1)S(1)}, u32[]{:S(2)}, u32[]{:S(2)}) collective-permute-start(bf16[32,7296]{1,0:T(8,128)(2,1)S(1)} %get-tuple-element.43), channel_id=1, source_target_pairs={{0,64},{32,96},{64,0},{96,32},{1,65},{33,97},{65,1},{97,33},{2,66}... | collective-permute-start | bytes 1400840 | tf_op jit(solution)/shard_map/ppermute | solution.py:39
  150.9 4.3 %stage.1 = (bf16[7168,512]{1,0:T(8,128)(2,1)S(1)}, bf16[256,7168]{1,0:T(8,128)(2,1)S(1)}) custom-call(bf16[7168,128]{1,0:T(8,128)(2,1)} %gate_a.1, bf16[7168,128]{1,0:T(8,128)(2,1)} %collective-permute-done.20.gate_b, bf16[7168,128]{1,0:T(8,128)(2,1)} %up_a.1, bf16[7168,128]{1,0:T(8,128)(2,1)} %collective-permute-done.21.up_b, bf16[128,7168]{1,0:T(8,128)(2,1)} %down_a.1, ...), custom_call_target="tpu_custom_call" | custom-call | flops 3670016000 | bytes 11010048 | tf_op jit(solution)/shard_map/stage/pallas_call | solution.py:356
  155.2 0.8 collective-permute-done.18.refs_1_
  156.0 9.5 %collective-permute-done.19.refs_2_ = bf16[32,7296]{1,0:T(8,128)(2,1)S(1)} collective-permute-done((bf16[32,7296]{1,0:T(8,128)(2,1)S(1)}, bf16[32,7296]{1,0:T(8,128)(2,1)S(1)}, u32[]{:S(2)}, u32[]{:S(2)}) %collective-permute-start.19) | collective-permute-done | bytes 466976 | tf_op jit(solution)/shard_map/ppermute | solution.py:39
  165.5 2.5 %expert_part.2 = (bf16[32,7168]{1,0:T(8,128)(2,1)S(1)}, bf16[32,7168]{1,0:T(8,128)(2,1)S(1)}, bf16[32,7168]{1,0:T(8,128)(2,1)S(1)}) custom-call(s32[3]{0:T(128)S(1)} %pad_add_fusion.where_ref, bf16[32,7296]{1,0:T(8,128)(2,1)S(1)} %get-tuple-element.35.refs_0_, bf16[32,7296]{1,0:T(8,128)(2,1)S(1)} %collective-permute-done.18.refs_1_, ...), custom_call_target="tpu_custom_call" | custom-call | flops 2113929216 | bytes 1376256 | tf_op jit(solution)/shard_map/expert_part/pallas_call | solution.py:403
  168.0 2.6 %collective-permute-start.23 = (bf16[32,7168]{1,0:T(8,128)(2,1)S(1)}, bf16[32,7168]{1,0:T(8,128)(2,1)S(1)}, u32[]{:S(2)}, u32[]{:S(2)}) collective-permute-start(bf16[32,7168]{1,0:T(8,128)(2,1)S(1)} %get-tuple-element.41), channel_id=1, source_target_pairs={{0,32},{32,64},{64,96},{96,0},{1,33},{33,65},{65,97},{97,1},{2,34}... | collective-permute-start | bytes 1376264 | tf_op jit(solution)/shard_map/ppermute | solution.py:39
  170.6 2.6 %expert_part.3 = bf16[32,7168]{1,0:T(8,128)(2,1)S(1)} custom-call(s32[3]{0:T(128)S(1)} %pad_add_fusion.where_ref, bf16[32,7296]{1,0:T(8,128)(2,1)S(1)} %collective-permute-done.25.refs_0_, bf16[7168,512]{1,0:T(8,128)(2,1)S(1)} %get-tuple-element.38.refs_3_.refs_1_, bf16[256,7168]{1,0:T(8,128)(2,1)S(1)} %get-tuple-element.39.refs_4_.refs_2_), custom_call_target="tpu_custom_call" | custom-call | flops 704643072 | bytes 458752 | tf_op jit(solution)/shard_map/expert_part/pallas_call | solution.py:403
  173.2 1.7 collective-permute-start.26
  174.9 1.8 collective-permute-done.23.refs_1_
  176.7 7.3 %collective-permute-done.24.refs_2_ = bf16[32,7168]{1,0:T(8,128)(2,1)S(1)} collective-permute-done((bf16[32,7168]{1,0:T(8,128)(2,1)S(1)}, bf16[32,7168]{1,0:T(8,128)(2,1)S(1)}, u32[]{:S(2)}, u32[]{:S(2)}) %collective-permute-start.24) | collective-permute-done | bytes 458784 | tf_op jit(solution)/shard_map/ppermute | solution.py:39
  184.0 0.4 collect.1
  184.4 0.1 collective-permute-start.27
  184.5 3.2 %collective-permute-start.28 = (bf16[16,7168]{1,0:T(8,128)(2,1)S(1)}, bf16[16,7168]{1,0:T(8,128)(2,1)S(1)}, u32[]{:S(2)}, u32[]{:S(2)}) collective-permute-start(bf16[16,7168]{1,0:T(8,128)(2,1)S(1)} %get-tuple-element.46), channel_id=1, source_target_pairs={{0,30},{2,0},{4,2},{6,4},{8,6},{10,8},{12,10},{14,12},{16,14},{18,... | collective-permute-start | bytes 688136 | tf_op jit(solution)/shard_map/ppermute | solution.py:43
  187.7 4.1 %collective-permute-start.30 = (bf16[16,3584]{1,0:T(8,128)(2,1)S(1)}, bf16[16,3584]{1,0:T(8,128)(2,1)S(1)}, u32[]{:S(2)}, u32[]{:S(2)}) collective-permute-start(bf16[16,3584]{1,0:T(8,128)(2,1)S(1)} %get-tuple-element.48), channel_id=1, source_target_pairs={{0,28},{2,30},{4,0},{6,2},{8,4},{10,6},{12,8},{14,10},{16,12},{18,... | collective-permute-start | bytes 344072 | tf_op jit(solution)/shard_map/ppermute | solution.py:43
  191.9 6.2 %collective-permute-done.29 = bf16[16,3584]{1,0:T(8,128)(2,1)S(1)} collective-permute-done((bf16[16,3584]{1,0:T(8,128)(2,1)S(1)}, bf16[16,3584]{1,0:T(8,128)(2,1)S(1)}, u32[]{:S(2)}, u32[]{:S(2)}) %collective-permute-start.29) | collective-permute-done | bytes 114720 | tf_op jit(solution)/shard_map/ppermute | solution.py:43
  198.0 0.1 add_convert_fusion
  198.2 0.1 reshape.74
  198.3 22.8 %all_to_all.15 = bf16[4,4,7168]{2,1,0:T(4,128)(2,1)S(1)} all-to-all(bf16[4,4,7168]{2,1,0:T(4,128)(2,1)S(1)} %reshape.74), channel_id=1, replica_groups=mesh['rep'=2,'x'=4,'zb'=4,'j'=4,'c'=2] {'zb'}, dimensions={0} | all-to-all | bytes 458752 | tf_op jit(solution)/shard_map/all_to_all | solution.py:448
  221.0 0.1 convert_reduce_fusion
  221.1 0.1 reduce_sum.75
  221.2 0.7 add_convert_fusion.2
  (75 shorter events, 0.5 us)
Async XLA Ops:
  0.0 106.9 %copy-start = (bf16[7168,16]{0,1:T(8,128)(2,1)S(1)}, bf16[7168,16]{0,1:T(8,128)(2,1)}, u32[]{:S(2)}) copy-start(bf16[7168,16]{0,1:T(8,128)(2,1)} %param.22) | copy-start | bytes 688132
  1.3 28.8 %copy-start.1 = (bf16[32,7680]{1,0:T(8,128)(2,1)}, bf16[32,7680]{1,0:T(8,128)(2,1)S(1)}, u32[]{:S(2)}) copy-start(bf16[32,7680]{1,0:T(8,128)(2,1)S(1)} %get-tuple-element.27.refs_0_) | copy-start | bytes 1474564
  1.3 35.4 %copy-start.2 = (bf16[32,7680]{1,0:T(8,128)(2,1)}, bf16[32,7680]{1,0:T(8,128)(2,1)S(1)}, u32[]{:S(2)}) copy-start(bf16[32,7680]{1,0:T(8,128)(2,1)S(1)} %get-tuple-element.28.refs_1_) | copy-start | bytes 1474564
  1.3 35.4 %collective-permute-start.11 = (bf16[32,7680]{1,0:T(8,128)(2,1)S(1)}, bf16[32,7680]{1,0:T(8,128)(2,1)S(1)}, u32[]{:S(2)}, u32[]{:S(2)}) collective-permute-start(bf16[32,7680]{1,0:T(8,128)(2,1)S(1)} %get-tuple-element.27.refs_0_), channel_id=1, source_target_pairs={{0,96},{32,0},{64,32},{96,64},{1,97},{33,1},{65,33},{97,65},{2,98}... | collective-permute-start | bytes 1474568 | tf_op jit(solution)/shard_map/ppermute | solution.py:39
  20.8 16.1 %collective-permute-start.6 = (bf16[32,7680]{1,0:T(8,128)(2,1)S(1)}, bf16[32,7680]{1,0:T(8,128)(2,1)S(1)}, u32[]{:S(2)}, u32[]{:S(2)}) collective-permute-start(bf16[32,7680]{1,0:T(8,128)(2,1)S(1)} %get-tuple-element.27.refs_0_), channel_id=1, source_target_pairs={{0,1},{1,0},{2,3},{3,2},{4,5},{5,4},{6,7},{7,6},{8,9},{9,8},{10,11... | collective-permute-start | bytes 1474568 | tf_op jit(solution)/shard_map/ppermute | solution.py:47
  20.8 16.6 %collective-permute-start = (bf16[32,7680]{1,0:T(8,128)(2,1)S(1)}, bf16[32,7680]{1,0:T(8,128)(2,1)S(1)}, u32[]{:S(2)}, u32[]{:S(2)}) collective-permute-start(bf16[32,7680]{1,0:T(8,128)(2,1)S(1)} %get-tuple-element.27.refs_0_), channel_id=1, source_target_pairs={{0,32},{32,64},{64,96},{96,0},{1,33},{33,65},{65,97},{97,1},{2,34}... | collective-permute-start | bytes 1474568 | tf_op jit(solution)/shard_map/ppermute | solution.py:39
  20.8 18.7 %collective-permute-start.2 = (bf16[32,7680]{1,0:T(8,128)(2,1)S(1)}, bf16[32,7680]{1,0:T(8,128)(2,1)S(1)}, u32[]{:S(2)}, u32[]{:S(2)}) collective-permute-start(bf16[32,7680]{1,0:T(8,128)(2,1)S(1)} %get-tuple-element.28.refs_1_), channel_id=1, source_target_pairs={{0,96},{32,0},{64,32},{96,64},{1,97},{33,1},{65,33},{97,65},{2,98}... | collective-permute-start | bytes 1474568 | tf_op jit(solution)/shard_map/ppermute | solution.py:39
  22.8 22.7 %collective-permute-start.8 = (bf16[32,7680]{1,0:T(8,128)(2,1)S(1)}, bf16[32,7680]{1,0:T(8,128)(2,1)}, u32[]{:S(2)}, u32[]{:S(2)}) collective-permute-start(bf16[32,7680]{1,0:T(8,128)(2,1)S(1)} %get-tuple-element.28.refs_1_), channel_id=1, source_target_pairs={{0,32},{32,64},{64,96},{96,0},{1,33},{33,65},{65,97},{97,1},{2,34}... | collective-permute-start | bytes 1474568 | tf_op jit(solution)/shard_map/ppermute | solution.py:39
  22.9 0.7 copy-start.3
  23.6 0.7 copy-start.4
  30.0 26.3 %all-to-all-start = ((bf16[16,16,512]{2,1,0:T(8,128)(2,1)}), bf16[16,16,512]{2,1,0:T(8,128)(2,1)S(1)}, u32[]{:S(2)}, u32[]{:S(2)}) async-start(bf16[16,16,512]{2,1,0:T(8,128)(2,1)} %bitcast.4), calls=%async_computation | async-start | bytes 524288 | tf_op jit(solution)/shard_map/all_to_all | solution.py:480
  36.7 19.6 %copy-start.6 = (bf16[32,7680]{1,0:T(8,128)(2,1)}, bf16[32,7680]{1,0:T(8,128)(2,1)S(1)}, u32[]{:S(2)}) copy-start(bf16[32,7680]{1,0:T(8,128)(2,1)S(1)} %collective-permute-done.11.refs_8_) | copy-start | bytes 1474564
  36.7 8.8 %collective-permute-start.7 = (bf16[32,7680]{1,0:T(8,128)(2,1)S(1)}, bf16[32,7680]{1,0:T(8,128)(2,1)S(1)}, u32[]{:S(2)}, u32[]{:S(2)}) collective-permute-start(bf16[32,7680]{1,0:T(8,128)(2,1)S(1)} %get-tuple-element.28.refs_1_), channel_id=1, source_target_pairs={{0,1},{1,0},{2,3},{3,2},{4,5},{5,4},{6,7},{7,6},{8,9},{9,8},{10,11... | collective-permute-start | bytes 1474568 | tf_op jit(solution)/shard_map/ppermute | solution.py:47
  36.9 19.5 %copy-start.7 = (bf16[32,7680]{1,0:T(8,128)(2,1)}, bf16[32,7680]{1,0:T(8,128)(2,1)S(1)}, u32[]{:S(2)}) copy-start(bf16[32,7680]{1,0:T(8,128)(2,1)S(1)} %collective-permute-done.6.refs_2_) | copy-start | bytes 1474564
  36.9 9.2 %collective-permute-start.12 = (bf16[32,7680]{1,0:T(8,128)(2,1)S(1)}, bf16[32,7680]{1,0:T(8,128)(2,1)S(1)}, u32[]{:S(2)}, u32[]{:S(2)}) collective-permute-start(bf16[32,7680]{1,0:T(8,128)(2,1)S(1)} %collective-permute-done.11.refs_8_), channel_id=1, source_target_pairs={{0,1},{1,0},{2,3},{3,2},{4,5},{5,4},{6,7},{7,6},{8,9},{9,8},{10,11... | collective-permute-start | bytes 1474568 | tf_op jit(solution)/shard_map/ppermute | solution.py:47
  37.3 19.0 %copy-start.8 = (bf16[32,7680]{1,0:T(8,128)(2,1)}, bf16[32,7680]{1,0:T(8,128)(2,1)S(1)}, u32[]{:S(2)}) copy-start(bf16[32,7680]{1,0:T(8,128)(2,1)S(1)} %collective-permute-done.refs_4_) | copy-start | bytes 1474564
  37.3 18.1 %collective-permute-start.1 = (bf16[32,7680]{1,0:T(8,128)(2,1)S(1)}, bf16[32,7680]{1,0:T(8,128)(2,1)S(1)}, u32[]{:S(2)}, u32[]{:S(2)}) collective-permute-start(bf16[32,7680]{1,0:T(8,128)(2,1)S(1)} %collective-permute-done.refs_4_), channel_id=1, source_target_pairs={{0,32},{32,64},{64,96},{96,0},{1,33},{33,65},{65,97},{97,1},{2,34}... | collective-permute-start | bytes 1474568 | tf_op jit(solution)/shard_map/ppermute | solution.py:39
  39.5 16.9 %copy-start.9 = (bf16[32,7680]{1,0:T(8,128)(2,1)}, bf16[32,7680]{1,0:T(8,128)(2,1)S(1)}, u32[]{:S(2)}) copy-start(bf16[32,7680]{1,0:T(8,128)(2,1)S(1)} %collective-permute-done.2.refs_9_) | copy-start | bytes 1474564
  39.5 16.0 %collective-permute-start.3 = (bf16[32,7680]{1,0:T(8,128)(2,1)S(1)}, bf16[32,7680]{1,0:T(8,128)(2,1)}, u32[]{:S(2)}, u32[]{:S(2)}) collective-permute-start(bf16[32,7680]{1,0:T(8,128)(2,1)S(1)} %collective-permute-done.2.refs_9_), channel_id=1, source_target_pairs={{0,96},{32,0},{64,32},{96,64},{1,97},{33,1},{65,33},{97,65},{2,98}... | collective-permute-start | bytes 1474568 | tf_op jit(solution)/shard_map/ppermute | solution.py:39
  45.5 10.8 %collective-permute-start.9 = (bf16[32,7680]{1,0:T(8,128)(2,1)S(1)}, bf16[32,7680]{1,0:T(8,128)(2,1)}, u32[]{:S(2)}, u32[]{:S(2)}) collective-permute-start(bf16[32,7680]{1,0:T(8,128)(2,1)S(1)} %collective-permute-done.refs_4_), channel_id=1, source_target_pairs={{0,1},{1,0},{2,3},{3,2},{4,5},{5,4},{6,7},{7,6},{8,9},{9,8},{10,11... | collective-permute-start | bytes 1474568 | tf_op jit(solution)/shard_map/ppermute | solution.py:47
  45.5 10.0 %copy-start.11 = (bf16[32,7680]{1,0:T(8,128)(2,1)}, bf16[32,7680]{1,0:T(8,128)(2,1)S(1)}, u32[]{:S(2)}) copy-start(bf16[32,7680]{1,0:T(8,128)(2,1)S(1)} %collective-permute-done.7.refs_3_) | copy-start | bytes 1474564
  45.5 10.8 %collective-permute-start.10 = (bf16[32,7680]{1,0:T(8,128)(2,1)}, bf16[32,7680]{1,0:T(8,128)(2,1)}, u32[]{:S(2)}, u32[]{:S(2)}) collective-permute-start(bf16[32,7680]{1,0:T(8,128)(2,1)} %collective-permute-done.8.refs_5_), channel_id=1, source_target_pairs={{0,1},{1,0},{2,3},{3,2},{4,5},{5,4},{6,7},{7,6},{8,9},{9,8},{10,11... | collective-permute-start | bytes 1474568 | tf_op jit(solution)/shard_map/ppermute | solution.py:47
  46.0 9.5 %copy-start.12 = (bf16[32,7680]{1,0:T(8,128)(2,1)}, bf16[32,7680]{1,0:T(8,128)(2,1)S(1)}, u32[]{:S(2)}) copy-start(bf16[32,7680]{1,0:T(8,128)(2,1)S(1)} %collective-permute-done.12.refs_10_) | copy-start | bytes 1474564
  46.0 10.3 %collective-permute-start.13 = (bf16[32,7680]{1,0:T(8,128)(2,1)S(1)}, bf16[32,7680]{1,0:T(8,128)(2,1)}, u32[]{:S(2)}, u32[]{:S(2)}) collective-permute-start(bf16[32,7680]{1,0:T(8,128)(2,1)S(1)} %collective-permute-done.2.refs_9_), channel_id=1, source_target_pairs={{0,1},{1,0},{2,3},{3,2},{4,5},{5,4},{6,7},{7,6},{8,9},{9,8},{10,11... | collective-permute-start | bytes 1474568 | tf_op jit(solution)/shard_map/ppermute | solution.py:47
  55.5 6.1 %copy-start.10 = (bf16[32,7680]{1,0:T(8,128)(2,1)}, bf16[32,7680]{1,0:T(8,128)(2,1)S(1)}, u32[]{:S(2)}) copy-start(bf16[32,7680]{1,0:T(8,128)(2,1)S(1)} %collective-permute-done.1.refs_0_) | copy-start | bytes 1474564
  55.5 6.1 %collective-permute-start.4 = (bf16[32,7680]{1,0:T(8,128)(2,1)S(1)}, bf16[32,7680]{1,0:T(8,128)(2,1)S(1)}, u32[]{:S(2)}, u32[]{:S(2)}) collective-permute-start(bf16[32,7680]{1,0:T(8,128)(2,1)S(1)} %collective-permute-done.1.refs_0_), channel_id=1, source_target_pairs={{0,1},{1,0},{2,3},{3,2},{4,5},{5,4},{6,7},{7,6},{8,9},{9,8},{10,11... | collective-permute-start | bytes 1474568 | tf_op jit(solution)/shard_map/ppermute | solution.py:47
  55.5 6.1 %collective-permute-start.5 = (bf16[32,7680]{1,0:T(8,128)(2,1)}, bf16[32,7680]{1,0:T(8,128)(2,1)}, u32[]{:S(2)}, u32[]{:S(2)}) collective-permute-start(bf16[32,7680]{1,0:T(8,128)(2,1)} %collective-permute-done.3.refs_1_), channel_id=1, source_target_pairs={{0,1},{1,0},{2,3},{3,2},{4,5},{5,4},{6,7},{7,6},{8,9},{9,8},{10,11... | collective-permute-start | bytes 1474568 | tf_op jit(solution)/shard_map/ppermute | solution.py:47
  61.6 0.8 copy-start.13
  65.5 24.5 %copy-start.15 = (bf16[7168]{0:T(1024)(128)(2,1)S(1)}, bf16[7168]{0:T(1024)(128)(2,1)}, u32[]{:S(2)}) copy-start(bf16[7168]{0:T(1024)(128)(2,1)} %param.21) | copy-start | bytes 43012
  65.5 24.5 %copy-start.5 = (bf16[2,2,7168]{2,1,0:T(2,128)(2,1)S(1)}, bf16[2,2,7168]{2,1,0:T(2,128)(2,1)}, u32[]{:S(2)}) copy-start(bf16[2,2,7168]{2,1,0:T(2,128)(2,1)} %param.18) | copy-start | bytes 172036
  65.5 24.5 %copy-start.16 = (s32[2,2,8]{2,1,0:T(2,128)S(1)}, s32[2,2,8]{2,1,0:T(2,128)}, u32[]{:S(2)}) copy-start(s32[2,2,8]{2,1,0:T(2,128)} %param.24) | copy-start | bytes 388
  65.5 24.5 %copy-start.14 = (s32[2,2,8]{2,1,0:T(2,128)S(1)}, s32[2,2,8]{2,1,0:T(2,128)}, u32[]{:S(2)}) copy-start(s32[2,2,8]{2,1,0:T(2,128)} %param.23) | copy-start | bytes 388
  65.5 16.8 %collective-permute-start.14 = (bf16[16,7168]{1,0:T(8,128)(2,1)S(1)}, bf16[16,7168]{1,0:T(8,128)(2,1)S(1)}, u32[]{:S(2)}, u32[]{:S(2)}) collective-permute-start(bf16[16,7168]{1,0:T(8,128)(2,1)S(1)} %get-tuple-element.30), channel_id=1, source_target_pairs={{0,2},{2,4},{4,6},{6,8},{8,10},{10,12},{12,14},{14,16},{16,18},{18... | collective-permute-start | bytes 688136 | tf_op jit(solution)/shard_map/ppermute | solution.py:43
  65.7 16.7 %collective-permute-start.15 = (bf16[16,7168]{1,0:T(8,128)(2,1)S(1)}, bf16[16,7168]{1,0:T(8,128)(2,1)S(1)}, u32[]{:S(2)}, u32[]{:S(2)}) collective-permute-start(bf16[16,7168]{1,0:T(8,128)(2,1)S(1)} %get-tuple-element.31), channel_id=1, source_target_pairs={{0,30},{2,0},{4,2},{6,4},{8,6},{10,8},{12,10},{14,12},{16,14},{18,... | collective-permute-start | bytes 688136 | tf_op jit(solution)/shard_map/ppermute | solution.py:43
  70.6 11.8 %collective-permute-start.16 = (bf16[16,3584]{1,0:T(8,128)(2,1)S(1)}, bf16[16,3584]{1,0:T(8,128)(2,1)S(1)}, u32[]{:S(2)}, u32[]{:S(2)}) collective-permute-start(bf16[16,3584]{1,0:T(8,128)(2,1)S(1)} %get-tuple-element.32), channel_id=1, source_target_pairs={{0,4},{2,6},{4,8},{6,10},{8,12},{10,14},{12,16},{14,18},{16,20},{1... | collective-permute-start | bytes 344072 | tf_op jit(solution)/shard_map/ppermute | solution.py:43
  70.6 11.8 %collective-permute-start.17 = (bf16[16,3584]{1,0:T(8,128)(2,1)S(1)}, bf16[16,3584]{1,0:T(8,128)(2,1)S(1)}, u32[]{:S(2)}, u32[]{:S(2)}) collective-permute-start(bf16[16,3584]{1,0:T(8,128)(2,1)S(1)} %get-tuple-element.33), channel_id=1, source_target_pairs={{0,28},{2,30},{4,0},{6,2},{8,4},{10,6},{12,8},{14,10},{16,12},{18,... | collective-permute-start | bytes 344072 | tf_op jit(solution)/shard_map/ppermute | solution.py:43
  83.3 23.0 %all-to-all-start.1 = ((bf16[4,4,7168]{2,1,0:T(4,128)(2,1)}), bf16[4,4,7168]{2,1,0:T(4,128)(2,1)S(1)}, u32[]{:S(2)}, u32[]{:S(2)}) async-start(bf16[4,4,7168]{2,1,0:T(4,128)(2,1)} %reshape.73), calls=%async_computation.1 | async-start | bytes 458752 | tf_op jit(solution)/shard_map/all_to_all | solution.py:448
  89.5 55.7 %collective-permute-start.20 = (bf16[7168,128]{1,0:T(8,128)(2,1)}, bf16[7168,128]{1,0:T(8,128)(2,1)}, u32[]{:S(2)}, u32[]{:S(2)}) collective-permute-start(bf16[7168,128]{1,0:T(8,128)(2,1)} %gate_a.1), channel_id=1, source_target_pairs={{0,1},{1,0},{2,3},{3,2},{4,5},{5,4},{6,7},{7,6},{8,9},{9,8},{10,11... | collective-permute-start | bytes 5505032 | tf_op jit(solution)/shard_map/ppermute | solution.py:47
  89.5 61.4 %collective-permute-start.21 = (bf16[7168,128]{1,0:T(8,128)(2,1)}, bf16[7168,128]{1,0:T(8,128)(2,1)}, u32[]{:S(2)}, u32[]{:S(2)}) collective-permute-start(bf16[7168,128]{1,0:T(8,128)(2,1)} %up_a.1), channel_id=1, source_target_pairs={{0,1},{1,0},{2,3},{3,2},{4,5},{5,4},{6,7},{7,6},{8,9},{9,8},{10,11... | collective-permute-start | bytes 5505032 | tf_op jit(solution)/shard_map/ppermute | solution.py:47
  90.0 60.9 %collective-permute-start.22 = (bf16[128,7168]{1,0:T(8,128)(2,1)}, bf16[128,7168]{1,0:T(8,128)(2,1)}, u32[]{:S(2)}, u32[]{:S(2)}) collective-permute-start(bf16[128,7168]{1,0:T(8,128)(2,1)} %down_a.1), channel_id=1, source_target_pairs={{0,1},{1,0},{2,3},{3,2},{4,5},{5,4},{6,7},{7,6},{8,9},{9,8},{10,11... | collective-permute-start | bytes 5505032 | tf_op jit(solution)/shard_map/ppermute | solution.py:47
  143.0 13.0 %collective-permute-start.18 = (bf16[32,7296]{1,0:T(8,128)(2,1)S(1)}, bf16[32,7296]{1,0:T(8,128)(2,1)S(1)}, u32[]{:S(2)}, u32[]{:S(2)}) collective-permute-start(bf16[32,7296]{1,0:T(8,128)(2,1)S(1)} %get-tuple-element.36), channel_id=1, source_target_pairs={{0,96},{32,0},{64,32},{96,64},{1,97},{33,1},{65,33},{97,65},{2,98}... | collective-permute-start | bytes 1400840 | tf_op jit(solution)/shard_map/ppermute | solution.py:39
  144.4 21.1 %collective-permute-start.19 = (bf16[32,7296]{1,0:T(8,128)(2,1)S(1)}, bf16[32,7296]{1,0:T(8,128)(2,1)S(1)}, u32[]{:S(2)}, u32[]{:S(2)}) collective-permute-start(bf16[32,7296]{1,0:T(8,128)(2,1)S(1)} %get-tuple-element.37), channel_id=1, source_target_pairs={{0,32},{32,64},{64,96},{96,0},{1,33},{33,65},{65,97},{97,1},{2,34}... | collective-permute-start | bytes 1400840 | tf_op jit(solution)/shard_map/ppermute | solution.py:39
  145.1 25.5 %collective-permute-start.25 = (bf16[32,7296]{1,0:T(8,128)(2,1)S(1)}, bf16[32,7296]{1,0:T(8,128)(2,1)S(1)}, u32[]{:S(2)}, u32[]{:S(2)}) collective-permute-start(bf16[32,7296]{1,0:T(8,128)(2,1)S(1)} %get-tuple-element.43), channel_id=1, source_target_pairs={{0,64},{32,96},{64,0},{96,32},{1,65},{33,97},{65,1},{97,33},{2,66}... | collective-permute-start | bytes 1400840 | tf_op jit(solution)/shard_map/ppermute | solution.py:39
  168.0 8.7 %collective-permute-start.23 = (bf16[32,7168]{1,0:T(8,128)(2,1)S(1)}, bf16[32,7168]{1,0:T(8,128)(2,1)S(1)}, u32[]{:S(2)}, u32[]{:S(2)}) collective-permute-start(bf16[32,7168]{1,0:T(8,128)(2,1)S(1)} %get-tuple-element.41), channel_id=1, source_target_pairs={{0,32},{32,64},{64,96},{96,0},{1,33},{33,65},{65,97},{97,1},{2,34}... | collective-permute-start | bytes 1376264 | tf_op jit(solution)/shard_map/ppermute | solution.py:39
  170.6 13.4 %collective-permute-start.24 = (bf16[32,7168]{1,0:T(8,128)(2,1)S(1)}, bf16[32,7168]{1,0:T(8,128)(2,1)S(1)}, u32[]{:S(2)}, u32[]{:S(2)}) collective-permute-start(bf16[32,7168]{1,0:T(8,128)(2,1)S(1)} %get-tuple-element.42), channel_id=1, source_target_pairs={{0,96},{32,0},{64,32},{96,64},{1,97},{33,1},{65,33},{97,65},{2,98}... | collective-permute-start | bytes 1376264 | tf_op jit(solution)/shard_map/ppermute | solution.py:39
  173.2 10.8 %collective-permute-start.26 = (bf16[32,7168]{1,0:T(8,128)(2,1)S(1)}, bf16[32,7168]{1,0:T(8,128)(2,1)S(1)}, u32[]{:S(2)}, u32[]{:S(2)}) collective-permute-start(bf16[32,7168]{1,0:T(8,128)(2,1)S(1)} %expert_part.3), channel_id=1, source_target_pairs={{0,64},{32,96},{64,0},{96,32},{1,65},{33,97},{65,1},{97,33},{2,66}... | collective-permute-start | bytes 1376264 | tf_op jit(solution)/shard_map/ppermute | solution.py:39
  184.4 13.6 %collective-permute-start.27 = (bf16[16,7168]{1,0:T(8,128)(2,1)S(1)}, bf16[16,7168]{1,0:T(8,128)(2,1)S(1)}, u32[]{:S(2)}, u32[]{:S(2)}) collective-permute-start(bf16[16,7168]{1,0:T(8,128)(2,1)S(1)} %get-tuple-element.45), channel_id=1, source_target_pairs={{0,2},{2,4},{4,6},{6,8},{8,10},{10,12},{12,14},{14,16},{16,18},{18... | collective-permute-start | bytes 688136 | tf_op jit(solution)/shard_map/ppermute | solution.py:43
  184.5 13.5 %collective-permute-start.28 = (bf16[16,7168]{1,0:T(8,128)(2,1)S(1)}, bf16[16,7168]{1,0:T(8,128)(2,1)S(1)}, u32[]{:S(2)}, u32[]{:S(2)}) collective-permute-start(bf16[16,7168]{1,0:T(8,128)(2,1)S(1)} %get-tuple-element.46), channel_id=1, source_target_pairs={{0,30},{2,0},{4,2},{6,4},{8,6},{10,8},{12,10},{14,12},{16,14},{18,... | collective-permute-start | bytes 688136 | tf_op jit(solution)/shard_map/ppermute | solution.py:43
  187.7 10.3 %collective-permute-start.29 = (bf16[16,3584]{1,0:T(8,128)(2,1)S(1)}, bf16[16,3584]{1,0:T(8,128)(2,1)S(1)}, u32[]{:S(2)}, u32[]{:S(2)}) collective-permute-start(bf16[16,3584]{1,0:T(8,128)(2,1)S(1)} %get-tuple-element.47), channel_id=1, source_target_pairs={{0,4},{2,6},{4,8},{6,10},{8,12},{10,14},{12,16},{14,18},{16,20},{1... | collective-permute-start | bytes 344072 | tf_op jit(solution)/shard_map/ppermute | solution.py:43
  187.7 10.3 %collective-permute-start.30 = (bf16[16,3584]{1,0:T(8,128)(2,1)S(1)}, bf16[16,3584]{1,0:T(8,128)(2,1)S(1)}, u32[]{:S(2)}, u32[]{:S(2)}) collective-permute-start(bf16[16,3584]{1,0:T(8,128)(2,1)S(1)} %get-tuple-element.48), channel_id=1, source_target_pairs={{0,28},{2,30},{4,0},{6,2},{8,4},{10,6},{12,8},{14,10},{16,12},{18,... | collective-permute-start | bytes 344072 | tf_op jit(solution)/shard_map/ppermute | solution.py:43

commit v3 on v2

--- a/solution.py
+++ b/solution.py
@@ -189,110 +189,89 @@
     )(held_in_hbm(up), held_in_hbm(rows))
 
 
-OUT_TILE = 512
-
-
-def put_rows(got, outs, c, n, half):
+HALVES = 2
+TILE = 256
+
+
+def put_rows(got, outs, n):
     own, right, left, ahead, behind = outs
-    size = own.shape[0]
-    cols = pl.ds(c * half + n * OUT_TILE, OUT_TILE)
+    size, width = own.shape[0], ahead.shape[1]
+    cols = pl.ds(n * TILE, TILE)
     own[:, cols] = got[:size]
     right[:, cols] = got[size : 2 * size].astype(bf16)
     left[:, cols] = got[2 * size : 3 * size].astype(bf16)
-    last = ahead if c == 0 else behind
-    last[:, pl.ds(n * OUT_TILE, OUT_TILE)] = got[3 * size :].astype(bf16)
-
-
-def row_shapes(size, dim):
+    last, at = (ahead, n * TILE) if n * TILE < width else (behind, n * TILE - width)
+    last[:, pl.ds(at, TILE)] = got[3 * size :].astype(bf16)
+
+
+def row_shapes(size, width):
     return (
-        jax.ShapeDtypeStruct((size, dim), f32),
-        jax.ShapeDtypeStruct((size, dim), bf16),
-        jax.ShapeDtypeStruct((size, dim), bf16),
-        jax.ShapeDtypeStruct((size, dim // 2), bf16),
-        jax.ShapeDtypeStruct((size, dim // 2), bf16),
+        jax.ShapeDtypeStruct((size, width), f32),
+        jax.ShapeDtypeStruct((size, width), bf16),
+        jax.ShapeDtypeStruct((size, width), bf16),
+        jax.ShapeDtypeStruct((size, width // 2), bf16),
+        jax.ShapeDtypeStruct((size, width // 2), bf16),
     )
 
 
+def tiles_of(parts, at, n):
+    half = (parts[0].shape[1] - at) // HALVES
+    got = [p[:, pl.ds(at + c * half + n * TILE, TILE)] for c in range(HALVES) for p in parts]
+    return jnp.concatenate(got, axis=0)
+
+
 def attend_kernel(tok, nx, count, first, last, where_ref, arrived, *refs):
-    pieces = refs[:count]
-    outs, (up, rows, up_sem, row_sem) = refs[count:-4], refs[-4:]
+    pieces, outs = refs[:count], refs[count:]
     if last:
         before, outs = outs[0], outs[1:]
-    half = rows.shape[1] // 2
-    starts = [0]
-    for piece in pieces:
-        starts.append(starts[-1] + piece.shape[0])
-
-    def up_copy(i):
-        return pltpu.make_async_copy(
-            pieces[i].at[:, pl.ds(0, LAT)],
-            up.at[pl.ds(starts[i], pieces[i].shape[0])],
-            up_sem.at[i],
-        )
-
-    def row_copy(c, i):
-        return pltpu.make_async_copy(
-            pieces[i].at[:, pl.ds(LAT + c * half, half)],
-            rows.at[pl.ds(starts[i], pieces[i].shape[0]), pl.ds(c * half, half)],
-            row_sem.at[c, i],
-        )
-
-    for i in range(count):
-        up_copy(i).start()
-    for c in range(2):
-        for i in range(count):
-            row_copy(c, i).start()
-    for i in range(count):
-        up_copy(i).wait()
-    values = lax.dot_general(arrived[...], up[...], NT, preferred_element_type=f32)
+    up = jnp.concatenate([piece[:, pl.ds(0, LAT)] for piece in pieces], axis=0)
+    values = lax.dot_general(arrived[...], up, NT, preferred_element_type=f32)
     hop = lax.rem(iota(values.shape, 0) // tok, nx)
     values = jnp.where(hop == first + iota(values.shape, 1) // VH, values, 0.0).astype(bf16)
-    shape = (RING * tok, arrived.shape[0])
-    place, source = iota(shape, 0), iota(shape, 1)
-    take = (source // (tok * nx) == chip_at(place // tok, where_ref[2])) & (
-        lax.rem(source, tok) == lax.rem(place, tok)
-    )
-    values = jnp.dot(one_hot(take), values, preferred_element_type=f32).astype(bf16)
-    for c in range(2):
-        for i in range(count):
-            row_copy(c, i).wait()
-        for n in range(half // OUT_TILE):
-            cols = pl.ds(c * half + n * OUT_TILE, OUT_TILE)
-            got = jnp.dot(values, rows[:, cols], preferred_element_type=f32)
-            if last:
-                put_rows(before[:, cols] + got, outs, c, n, half)
-            else:
-                outs[0][:, cols] = got
+    shape = (RING * HALVES * tok, arrived.shape[0])
+    row, source = iota(shape, 0), iota(shape, 1)
+    chip = chip_at(row // (HALVES * tok), where_ref[2])
+    take = (source // (tok * nx) == chip) & (lax.rem(source, tok) == lax.rem(row, tok))
+    half = lax.rem(row // tok, HALVES)
+    taken = [
+        jnp.dot(one_hot(take & (half == c)), values, preferred_element_type=f32).astype(bf16)
+        for c in range(HALVES)
+    ]
+    values = jnp.concatenate(taken, axis=1)
+    for n in range(outs[0].shape[1] // TILE):
+        got = jnp.dot(values, tiles_of(pieces, LAT, n), preferred_element_type=f32)
+        cols = pl.ds(n * TILE, TILE)
+        if last:
+            put_rows(before[:, cols] + got, outs, n)
+        else:
+            outs[0][:, cols] = got
 
 
 def attend_part(where, nx, arrived, pieces, tok, first, before):
     depth = sum(p.shape[0] for p in pieces)
-    dim = pieces[0].shape[1] - LAT
+    width = (pieces[0].shape[1] - LAT) // HALVES
     count = len(pieces)
     last = before is not None
-    part = jax.ShapeDtypeStruct((RING * tok, dim), f32)
+    part = jax.ShapeDtypeStruct((RING * HALVES * tok, width), f32)
     return pl.pallas_call(
         functools.partial(attend_kernel, tok, nx, count, first, last),
-        out_shape=row_shapes(FAR * tok, dim) if last else part,
-        in_specs=[smem(), vmem()] + [hbm()] * count + [vmem()] * last,
+        out_shape=row_shapes(FAR * HALVES * tok, width) if last else part,
+        in_specs=[smem(), vmem()] + [vmem()] * count + [vmem()] * last,
         out_specs=[vmem()] * 5 if last else vmem(),
-        scratch_shapes=[
-            pltpu.VMEM((depth, LAT), bf16),
-            pltpu.VMEM((depth, dim), bf16),
-            pltpu.SemaphoreType.DMA((count,)),
-            pltpu.SemaphoreType.DMA((2, count)),
-        ],
-        compiler_params=params(12),
-        cost_estimate=cost(8 * RING * tok * depth * dim, 2 * depth * dim),
+        compiler_params=params(6),
+        cost_estimate=cost(8 * RING * tok * depth * width * HALVES, 4 * depth * width),
         name="attend_part",
-    )(where, arrived, *[held_in_hbm(p) for p in pieces], *([before] if last else []))
+    )(where, arrived, *[held_in_vmem(p) for p in pieces], *([before] if last else []))
+
+
+SEND_TILE = 512
 
 
 def dispatch_kernel(tok, nx, where_ref, tokens, *refs):
     outs, spread = refs[:nx], refs[nx]
     count, width = tokens.shape
-    dim = width - EXTRA
-    table = tokens[:, pl.ds(dim, EXTRA)]
+    half = width - EXTRA
+    table = tokens[:, pl.ds(half, EXTRA)]
     shape = (nx * CAP, EXTRA)
     row, place = iota(shape, 0), iota(shape, 1)
     expert = FAR * column(row // CAP, where_ref[0], nx) + where_ref[1]
@@ -303,31 +282,41 @@
     parts = []
     for r in range(nx):
         sel = jnp.where(lax.rem(slot, CAP) == 0, got[CAP * r : CAP * r + 1], got[CAP * r + 1 : CAP * r + 2])
-        parts.append(jnp.where(slot // CAP == token // tok, sel, 0.0))
-    sel = jnp.concatenate(parts, axis=0).astype(bf16)
-    for n in range(pl.cdiv(width, OUT_TILE)):
-        cols = pl.ds(n * OUT_TILE, min(OUT_TILE, width - n * OUT_TILE))
-        rows = jnp.dot(sel, tokens[:, cols], preferred_element_type=f32).astype(bf16)
-        for r in range(nx):
-            outs[r][:, cols] = rows[r * SLOTS : (r + 1) * SLOTS]
+        parts.append(jnp.where(slot // CAP == token // (HALVES * tok), sel, 0.0))
+    sel = jnp.concatenate(parts, axis=0)
+    of_half = lax.rem(iota(sel.shape, 1) // tok, HALVES)
+    sels = [jnp.where(of_half == c, sel, 0.0).astype(bf16) for c in range(HALVES)]
+    both = jnp.concatenate(sels, axis=0)
+    rows = nx * SLOTS
+    for n in range(half // SEND_TILE):
+        got = jnp.dot(both, tokens[:, pl.ds(n * SEND_TILE, SEND_TILE)], preferred_element_type=f32).astype(bf16)
+        for c in range(HALVES):
+            for r in range(nx):
+                at = c * rows + r * SLOTS
+                outs[r][:, pl.ds(c * half + n * SEND_TILE, SEND_TILE)] = got[at : at + SLOTS]
+    got = jnp.dot(sels[0], table, preferred_element_type=f32).astype(bf16)
+    for r in range(nx):
+        outs[r][:, pl.ds(HALVES * half, EXTRA)] = got[r * SLOTS : (r + 1) * SLOTS]
     shape = (count, count)
-    place, token = iota(shape, 0), iota(shape, 1)
-    take = (token // tok == chip_at(place // tok, where_ref[2])) & (
-        lax.rem(token, tok) == lax.rem(place, tok)
-    )
-    spread[...] = lax.dot_general(one_hot(take), sel, NT, preferred_element_type=f32).astype(bf16)
+    row, token = iota(shape, 0), iota(shape, 1)
+    chip = chip_at(row // (HALVES * tok), where_ref[2])
+    take = (token // (HALVES * tok) == chip) & (lax.rem(token, HALVES * tok) == lax.rem(row, HALVES * tok))
+    for c in range(HALVES):
+        got = lax.dot_general(one_hot(take), sels[c], NT, preferred_element_type=f32)
+        spread[:, pl.ds(c * rows, rows)] = got.astype(bf16)
 
 
 def dispatch(where, nx, tokens, tok):
     count, width = tokens.shape
+    full = HALVES * (width - EXTRA) + EXTRA
     return pl.pallas_call(
         functools.partial(dispatch_kernel, tok, nx),
-        out_shape=(jax.ShapeDtypeStruct((SLOTS, width), bf16),) * nx
-        + (jax.ShapeDtypeStruct((count, nx * SLOTS), bf16),),
+        out_shape=(jax.ShapeDtypeStruct((SLOTS, full), bf16),) * nx
+        + (jax.ShapeDtypeStruct((count, HALVES * nx * SLOTS), bf16),),
         in_specs=[smem(), vmem()],
         out_specs=[vmem()] * (nx + 1),
         compiler_params=params(12),
-        cost_estimate=cost(2 * nx * SLOTS * count * width, 4 * count * width),
+        cost_estimate=cost(2 * nx * SLOTS * count * full, 4 * count * width),
         name="dispatch",
     )(where, tokens)
 
@@ -414,37 +403,33 @@
 
 def collect_kernel(count, spread, *refs):
     parts, outs = refs[:count], refs[count:]
-    half = parts[0].shape[1] // 2
-    for c in range(2):
-        for n in range(half // OUT_TILE):
-            cols = pl.ds(c * half + n * OUT_TILE, OUT_TILE)
-            rows = jnp.concatenate([part[:, cols] for part in parts], axis=0)
-            put_rows(jnp.dot(spread[...], rows, preferred_element_type=f32), outs, c, n, half)
-
-
-def collect(spread, parts, tok):
-    dim = parts[0].shape[1]
+    for n in range(outs[0].shape[1] // TILE):
+        put_rows(jnp.dot(spread[...], tiles_of(parts, 0, n), preferred_element_type=f32), outs, n)
+
+
+def collect(spread, parts):
+    width = parts[0].shape[1] // HALVES
     count = len(parts)
     return pl.pallas_call(
         functools.partial(collect_kernel, count),
-        out_shape=row_shapes(FAR * tok, dim),
+        out_shape=row_shapes(spread.shape[0] // NEAR, width),
         in_specs=[vmem()] * (count + 1),
         out_specs=[vmem()] * 5,
         compiler_params=params(12),
-        cost_estimate=cost(2 * spread.size * dim, 8 * FAR * tok * dim),
+        cost_estimate=cost(2 * spread.size * width, 4 * spread.shape[0] * width),
         name="collect",
     )(spread, *parts)
 
 
 def reduce_z(own, right, left, ahead, behind):
-    size, dim = own.shape
+    size, width = own.shape
+    ahead = shift_z(ahead, 2)
+    behind = shift_z(behind, -2)
     right = shift_z(right, 1)
     left = shift_z(left, -1)
-    ahead = shift_z(ahead, 2)
-    behind = shift_z(behind, -2)
     total = own + right.astype(f32) + left.astype(f32)
     total = total + jnp.concatenate([ahead, behind], axis=1).astype(f32)
-    sent = total.astype(bf16).reshape(FAR, size // FAR, dim)
+    sent = total.astype(bf16).reshape(FAR, size // FAR, width)
     got = lax.all_to_all(sent, "zb", split_axis=0, concat_axis=0, tiled=True)
     return jnp.sum(got.astype(f32), axis=0)
 
@@ -490,13 +475,19 @@
     most = attend_part(where, nx, arrived, near, tok, 0, None)
     attended = reduce_z(*attend_part(where, nx, arrived, beyond, tok, nx - 1, most))
 
-    hidden = resid.reshape(tok, D).astype(f32) + attended
-    mean_square = jnp.mean(hidden * hidden, axis=-1, keepdims=True)
-    normed = (hidden * lax.rsqrt(mean_square + norm_eps) * norm_gain.astype(f32)).astype(bf16)
+    half = D // HALVES
+    rows = resid.reshape(tok, HALVES, half).swapaxes(0, 1).reshape(HALVES * tok, half)
+    hidden = rows.astype(f32) + attended
+    square = jnp.sum(hidden * hidden, axis=-1).reshape(HALVES, tok)
+    scale = lax.rsqrt(jnp.sum(square, axis=0) / D + norm_eps)
+    gain = jnp.repeat(norm_gain.astype(f32).reshape(HALVES, half), tok, axis=0)
+    normed = (hidden * jnp.tile(scale, HALVES)[:, None] * gain).astype(bf16)
 
     route_ids = expert_ids.reshape(tok, TOP)
     route_slots = slots.reshape(tok, TOP)
-    logits = jnp.dot(normed, router, preferred_element_type=f32)
+    wide_router = router.reshape(HALVES, half, EXPERTS).swapaxes(0, 1).reshape(half, HALVES * EXPERTS)
+    logits = jnp.dot(normed, wide_router, preferred_element_type=f32).reshape(HALVES, tok, HALVES, EXPERTS)
+    logits = sum(logits[c, :, c] for c in range(HALVES))
     is_pick = route_ids[:, :, None] == jnp.arange(EXPERTS, dtype=jnp.int32)[None, None, :]
     picked = jnp.sum(jnp.where(is_pick, logits[:, None, :], 0.0), axis=-1)
     gates = jax.nn.sigmoid(picked)
@@ -510,7 +501,7 @@
     low = (rest - middle.astype(f32)).astype(bf16)
     extra = jnp.concatenate(places + [high, middle, low], axis=1)
     extra = jnp.pad(extra, ((0, 0), (0, EXTRA - extra.shape[1])))
-    payload = jnp.concatenate([normed, extra], axis=1)
+    payload = jnp.concatenate([normed, jnp.tile(extra, (HALVES, 1))], axis=1)
 
     ring = lax.all_gather(payload, ZAX, axis=0, tiled=True)
     *sent, spread = dispatch(where, nx, ring, tok)
@@ -522,9 +513,9 @@
     back_right = shift_x(done[2], -1)
     (far_done,) = expert_part(where, (from_far,), weights)
     back_far = shift_x(far_done, 2)
-    expert_mix = reduce_z(*collect(spread, (done[0], back_left, back_right, back_far), tok))
-    mixed = (hidden + expert_mix).astype(bf16)
-    return mixed.reshape(resid.shape)
+    expert_mix = reduce_z(*collect(spread, (done[0], back_left, back_right, back_far)))
+    mixed = (hidden + expert_mix).astype(bf16).reshape(HALVES, tok, half)
+    return mixed.swapaxes(0, 1).reshape(resid.shape)
 
 
 def solution(mesh):

time: 222 us -> 220 us (level)
  the two profiles are of different devices: /device:TPU:34 before, /device:TPU:42 now
where the time goes in v3:
time: 220 us
  starting transfers between devices  69 us (31%)
  waiting for transfers between devices  61.3 us (28%)
  blocking collectives  56.8 us (26%)
  Pallas kernels  23.5 us (11%)
  local copies, waits for them, and re-layouts  6.35 us (3%)
    all_gather x1, blocking collectives, layer(): ring = lax.all_gather(payload, ZAX, axis=0, tiled=True)  33.9 us
    ppermute x12, waiting for transfers between devices, shift_x(): return lax.ppermute(a, 'x', [(i, (i + step) % n) for i in range(n)])  31.2 us
    all_to_all x1, starting transfers between devices, layer(): lax.all_to_all(outgoing.reshape(RING, nx * tok, LAT), ZAX, split_axis=0,...  24 us
    all_to_all x1, blocking collectives, reduce_z(): got = lax.all_to_all(sent, 'zb', split_axis=0, concat_axis=0, tiled=True)  22.9 us
    ppermute x12, starting transfers between devices, shift_x(): return lax.ppermute(a, 'x', [(i, (i + step) % n) for i in range(n)])  19.1 us
    ppermute x8, starting transfers between devices, shift_z(): return lax.ppermute(a, ZAX, [(i, (i + step) % RING) for i in range(RING)])  17.8 us
    all_to_all x1, waiting for transfers between devices, reduce_z(): got = lax.all_to_all(sent, 'zb', split_axis=0, concat_axis=0, tiled=True)  15.7 us
    ppermute x8, waiting for transfers between devices, shift_z(): return lax.ppermute(a, ZAX, [(i, (i + step) % RING) for i in range(RING)])  13.5 us
  transfers between devices with their start and end apart: 33, of which 10 were waited for; matrix products, arithmetic and copies ran while one was open for 1% of the time, Pallas kernels for 9%

profile of v3, /device:TPU:42, one launch (start us, length us, event | category | flops | bytes accessed | tf_op | source)
XLA Modules:
  0.0 219.7 jit_solution(11370883255798577542)
XLA Ops:
  0.0 1.2 pack.1
  1.2 0.5 collective-permute-start.11
  1.7 1.6 collective-permute-start
  3.4 1.5 collective-permute-start.2
  4.9 0.5 collective-permute-start.8
  5.4 0.1 pad_add_fusion.where_ref
  5.5 0.7 copy-done.4
  6.2 0.7 copy-done.5
  6.8 5.8 %context_rows.1 = bf16[256,512]{1,0:T(8,128)(2,1)} custom-call(s32[3]{0:T(128)S(1)} %pad_add_fusion.where_ref, s32[2]{0:T(128)S(1)} %copy-done.5, bf16[2,576,2048]{2,1,0:T(8,128)(2,1)} %bitcast.49, bf16[2,2,64,576]{3,2,1,0:T(8,128)(2,1)} %queries.1, bf16[2,2,576]{2,1,0:T(2,128)(2,1)S(1)} %copy-done.4), custom_call_target="tpu_custom_call" | custom-call | flops 1140850688 | bytes 4718592 | tf_op jit(solution)/shard_map/context_rows/pallas_call | solution.py:146
  12.6 24.0 %all-to-all-start = ((bf16[16,16,512]{2,1,0:T(8,128)(2,1)}), bf16[16,16,512]{2,1,0:T(8,128)(2,1)S(1)}, u32[]{:S(2)}, u32[]{:S(2)}) async-start(bf16[16,16,512]{2,1,0:T(8,128)(2,1)} %bitcast.5), calls=%async_computation | async-start | bytes 524288 | tf_op jit(solution)/shard_map/all_to_all | solution.py:465
  36.6 0.1 collective-permute-start.7
  36.8 0.5 collective-permute-start.12
  37.3 2.1 collective-permute-start.1
  39.4 0.7 collective-permute-start.3
  40.2 0.8 copy-done
  41.0 0.5 collective-permute-start.10
  41.5 0.8 copy-done.2
  42.3 9.4 %collective-permute-done.1.refs_0_ = bf16[32,7680]{1,0:T(8,128)(2,1)} collective-permute-done((bf16[32,7680]{1,0:T(8,128)(2,1)S(1)}, bf16[32,7680]{1,0:T(8,128)(2,1)}, u32[]{:S(2)}, u32[]{:S(2)}) %collective-permute-start.1) | collective-permute-done | bytes 491552 | tf_op jit(solution)/shard_map/ppermute | solution.py:39
  51.7 2.4 %collective-permute-done.3.refs_1_ = bf16[32,7680]{1,0:T(8,128)(2,1)} collective-permute-done((bf16[32,7680]{1,0:T(8,128)(2,1)S(1)}, bf16[32,7680]{1,0:T(8,128)(2,1)}, u32[]{:S(2)}, u32[]{:S(2)}) %collective-permute-start.3) | collective-permute-done | bytes 491552 | tf_op jit(solution)/shard_map/ppermute | solution.py:39
  54.0 0.9 all-to-all-done
  55.0 1.0 copy-done.1
  56.0 1.0 copy-done.3
  57.0 2.8 %attend_part.2.refs_4_ = f32[128,3584]{1,0:T(8,128)S(1)} custom-call(s32[3]{0:T(128)S(1)} %pad_add_fusion.where_ref, bf16[256,512]{1,0:T(8,128)(2,1)S(1)} %bitcast.47, bf16[32,7680]{1,0:T(8,128)(2,1)S(1)} %get-tuple-element.27.refs_0_, bf16[32,7680]{1,0:T(8,128)(2,1)S(1)} %get-tuple-element.28.refs_1_, bf16[32,7680]{1,0:T(8,128)(2,1)S(1)} %collective-permute-done.6.refs_2_, ...), custom_call_target="tpu_custom_call" | custom-call | flops 1409286144 | bytes 5505024 | tf_op jit(solution)/shard_map/attend_part/pallas_call | solution.py:256
  59.9 2.4 %attend_part.3 = (f32[32,3584]{1,0:T(8,128)S(1)}, bf16[32,3584]{1,0:T(8,128)(2,1)S(1)}, bf16[32,3584]{1,0:T(8,128)(2,1)S(1)}, bf16[32,1792]{1,0:T(8,128)(2,1)S(1)}, bf16[32,1792]{1,0:T(8,128)(2,1)S(1)}) custom-call(s32[3]{0:T(128)S(1)} %pad_add_fusion.where_ref, bf16[256,512]{1,0:T(8,128)(2,1)S(1)} %bitcast.48, ...), custom_call_target="tpu_custom_call" | custom-call | flops 469762048 | bytes 1835008 | tf_op jit(solution)/shard_map/attend_part/pallas_call | solution.py:256
  62.3 1.1 collective-permute-start.14
  63.4 5.1 %collective-permute-start.15 = (bf16[32,3584]{1,0:T(8,128)(2,1)S(1)}, bf16[32,3584]{1,0:T(8,128)(2,1)S(1)}, u32[]{:S(2)}, u32[]{:S(2)}) collective-permute-start(bf16[32,3584]{1,0:T(8,128)(2,1)S(1)} %get-tuple-element.31), channel_id=1, source_target_pairs={{0,30},{2,0},{4,2},{6,4},{8,6},{10,8},{12,10},{14,12},{16,14},{18,... | collective-permute-start | bytes 688136 | tf_op jit(solution)/shard_map/ppermute | solution.py:43
  68.5 4.1 %collective-permute-start.17 = (bf16[32,1792]{1,0:T(8,128)(2,1)S(1)}, bf16[32,1792]{1,0:T(8,128)(2,1)S(1)}, u32[]{:S(2)}, u32[]{:S(2)}) collective-permute-start(bf16[32,1792]{1,0:T(8,128)(2,1)S(1)} %get-tuple-element.33), channel_id=1, source_target_pairs={{0,28},{2,30},{4,0},{6,2},{8,4},{10,6},{12,8},{14,10},{16,12},{18,... | collective-permute-start | bytes 344072 | tf_op jit(solution)/shard_map/ppermute | solution.py:43
  72.7 7.6 %collective-permute-done.16 = bf16[32,1792]{1,0:T(8,128)(2,1)S(1)} collective-permute-done((bf16[32,1792]{1,0:T(8,128)(2,1)S(1)}, bf16[32,1792]{1,0:T(8,128)(2,1)S(1)}, u32[]{:S(2)}, u32[]{:S(2)}) %collective-permute-start.16) | collective-permute-done | bytes 114720 | tf_op jit(solution)/shard_map/ppermute | solution.py:43
  80.3 0.8 fusion
  81.1 6.4 %all-to-all-start.1 = ((bf16[4,8,3584]{2,1,0:T(8,128)(2,1)}), bf16[4,8,3584]{2,1,0:T(8,128)(2,1)S(1)}, u32[]{:S(2)}, u32[]{:S(2)}) async-start(bf16[4,8,3584]{2,1,0:T(8,128)(2,1)} %fusion), calls=%async_computation.1 | async-start | bytes 458752 | tf_op jit(solution)/shard_map/all_to_all | solution.py:433
  87.5 0.5 collective-permute-start.21
  88.3 0.2 reshape.113
  88.5 0.1 select_reduce_fusion.2
  88.6 15.7 %all-to-all-done.1 = bf16[4,8,3584]{2,1,0:T(8,128)(2,1)S(1)} async-done(((bf16[4,8,3584]{2,1,0:T(8,128)(2,1)}), bf16[4,8,3584]{2,1,0:T(8,128)(2,1)S(1)}, u32[]{:S(2)}, u32[]{:S(2)}) %all-to-all-start.1) | async-done | bytes 229408 | tf_op jit(solution)/shard_map/all_to_all | solution.py:433
  104.4 0.2 multiply_reduce_fusion
  104.6 0.4 fusion.2
  105.0 0.2 select_reduce_fusion.1
  105.2 0.1 fusion.12
  105.4 0.1 select_reduce_fusion
  105.5 0.1 mul.36
  105.6 0.1 concatenate.13
  105.7 0.1 multiply_convert_fusion.1
  105.8 33.9 %all_gather.3.tokens = bf16[128,3712]{1,0:T(8,128)(2,1)S(1)} all-gather(bf16[8,3712]{1,0:T(8,128)(2,1)S(1)} %pad_maximum_fusion), channel_id=1, replica_groups=mesh['rep'=2,'x'=4,'zb'=4,'j'=4,'c'=2] {'zb','j'}, dimensions={0}, use_global_device_ids=true | all-gather | bytes 1009664 | tf_op jit(solution)/shard_map/all_gather | solution.py:506
  139.7 1.3 dispatch.1
  141.1 1.2 collective-permute-start.18
  142.3 1.0 collective-permute-start.19
  143.2 5.7 %collective-permute-start.25 = (bf16[32,7296]{1,0:T(8,128)(2,1)S(1)}, bf16[32,7296]{1,0:T(8,128)(2,1)S(1)}, u32[]{:S(2)}, u32[]{:S(2)}) collective-permute-start(bf16[32,7296]{1,0:T(8,128)(2,1)S(1)} %get-tuple-element.43), channel_id=1, source_target_pairs={{0,64},{32,96},{64,0},{96,32},{1,65},{33,97},{65,1},{97,33},{2,66}... | collective-permute-start | bytes 1400840 | tf_op jit(solution)/shard_map/ppermute | solution.py:39
  148.9 4.3 %stage.1 = (bf16[7168,512]{1,0:T(8,128)(2,1)S(1)}, bf16[256,7168]{1,0:T(8,128)(2,1)S(1)}) custom-call(bf16[7168,128]{1,0:T(8,128)(2,1)} %gate_a.1, bf16[7168,128]{1,0:T(8,128)(2,1)} %copy-done.11, bf16[7168,128]{1,0:T(8,128)(2,1)} %up_a.1, bf16[7168,128]{1,0:T(8,128)(2,1)} %collective-permute-done.21.up_b, bf16[128,7168]{1,0:T(8,128)(2,1)} %down_a.1, ...), custom_call_target="tpu_custom_call" | custom-call | flops 3670016000 | bytes 11010048 | tf_op jit(solution)/shard_map/stage/pallas_call | solution.py:345
  153.2 0.9 collective-permute-done.18.refs_1_
  154.1 9.4 %collective-permute-done.19.refs_2_ = bf16[32,7296]{1,0:T(8,128)(2,1)S(1)} collective-permute-done((bf16[32,7296]{1,0:T(8,128)(2,1)S(1)}, bf16[32,7296]{1,0:T(8,128)(2,1)S(1)}, u32[]{:S(2)}, u32[]{:S(2)}) %collective-permute-start.19) | collective-permute-done | bytes 466976 | tf_op jit(solution)/shard_map/ppermute | solution.py:39
  163.5 2.5 %expert_part.2 = (bf16[32,7168]{1,0:T(8,128)(2,1)S(1)}, bf16[32,7168]{1,0:T(8,128)(2,1)S(1)}, bf16[32,7168]{1,0:T(8,128)(2,1)S(1)}) custom-call(s32[3]{0:T(128)S(1)} %pad_add_fusion.where_ref, bf16[32,7296]{1,0:T(8,128)(2,1)S(1)} %get-tuple-element.35.refs_0_, bf16[32,7296]{1,0:T(8,128)(2,1)S(1)} %collective-permute-done.18.refs_1_, ...), custom_call_target="tpu_custom_call" | custom-call | flops 2113929216 | bytes 1376256 | tf_op jit(solution)/shard_map/expert_part/pallas_call | solution.py:392
  166.0 2.6 %collective-permute-start.23 = (bf16[32,7168]{1,0:T(8,128)(2,1)S(1)}, bf16[32,7168]{1,0:T(8,128)(2,1)S(1)}, u32[]{:S(2)}, u32[]{:S(2)}) collective-permute-start(bf16[32,7168]{1,0:T(8,128)(2,1)S(1)} %get-tuple-element.41), channel_id=1, source_target_pairs={{0,32},{32,64},{64,96},{96,0},{1,33},{33,65},{65,97},{97,1},{2,34}... | collective-permute-start | bytes 1376264 | tf_op jit(solution)/shard_map/ppermute | solution.py:39
  168.6 2.6 %expert_part.3 = bf16[32,7168]{1,0:T(8,128)(2,1)S(1)} custom-call(s32[3]{0:T(128)S(1)} %pad_add_fusion.where_ref, bf16[32,7296]{1,0:T(8,128)(2,1)S(1)} %collective-permute-done.25.refs_0_, bf16[7168,512]{1,0:T(8,128)(2,1)S(1)} %get-tuple-element.38.refs_3_.refs_1_, bf16[256,7168]{1,0:T(8,128)(2,1)S(1)} %get-tuple-element.39.refs_4_.refs_2_), custom_call_target="tpu_custom_call" | custom-call | flops 704643072 | bytes 458752 | tf_op jit(solution)/shard_map/expert_part/pallas_call | solution.py:392
  171.2 1.7 collective-permute-start.26
  172.9 1.8 collective-permute-done.23.refs_1_
  174.8 7.2 %collective-permute-done.24.refs_2_ = bf16[32,7168]{1,0:T(8,128)(2,1)S(1)} collective-permute-done((bf16[32,7168]{1,0:T(8,128)(2,1)S(1)}, bf16[32,7168]{1,0:T(8,128)(2,1)S(1)}, u32[]{:S(2)}, u32[]{:S(2)}) %collective-permute-start.24) | collective-permute-done | bytes 458784 | tf_op jit(solution)/shard_map/ppermute | solution.py:39
  182.0 0.4 collect.1
  182.4 0.4 collective-permute-start.27
  182.9 2.9 %collective-permute-start.28 = (bf16[32,3584]{1,0:T(8,128)(2,1)S(1)}, bf16[32,3584]{1,0:T(8,128)(2,1)S(1)}, u32[]{:S(2)}, u32[]{:S(2)}) collective-permute-start(bf16[32,3584]{1,0:T(8,128)(2,1)S(1)} %get-tuple-element.46), channel_id=1, source_target_pairs={{0,30},{2,0},{4,2},{6,4},{8,6},{10,8},{12,10},{14,12},{16,14},{18,... | collective-permute-start | bytes 688136 | tf_op jit(solution)/shard_map/ppermute | solution.py:43
  185.8 4.1 %collective-permute-start.30 = (bf16[32,1792]{1,0:T(8,128)(2,1)S(1)}, bf16[32,1792]{1,0:T(8,128)(2,1)S(1)}, u32[]{:S(2)}, u32[]{:S(2)}) collective-permute-start(bf16[32,1792]{1,0:T(8,128)(2,1)S(1)} %get-tuple-element.48), channel_id=1, source_target_pairs={{0,28},{2,30},{4,0},{6,2},{8,4},{10,6},{12,8},{14,10},{16,12},{18,... | collective-permute-start | bytes 344072 | tf_op jit(solution)/shard_map/ppermute | solution.py:43
  189.9 5.8 %collective-permute-done.29 = bf16[32,1792]{1,0:T(8,128)(2,1)S(1)} collective-permute-done((bf16[32,1792]{1,0:T(8,128)(2,1)S(1)}, bf16[32,1792]{1,0:T(8,128)(2,1)S(1)}, u32[]{:S(2)}, u32[]{:S(2)}) %collective-permute-start.29) | collective-permute-done | bytes 114720 | tf_op jit(solution)/shard_map/ppermute | solution.py:43
  195.8 0.1 fusion.1
  195.9 22.9 %all_to_all.15 = bf16[4,8,3584]{2,1,0:T(8,128)(2,1)S(1)} all-to-all(bf16[4,8,3584]{2,1,0:T(8,128)(2,1)S(1)} %fusion.1), channel_id=1, replica_groups=mesh['rep'=2,'x'=4,'zb'=4,'j'=4,'c'=2] {'zb'}, dimensions={0} | all-to-all | bytes 458752 | tf_op jit(solution)/shard_map/all_to_all | solution.py:433
  219.0 0.7 reshape.116
  (73 shorter events, 0.7 us)
Async XLA Ops:
  1.2 35.4 %collective-permute-start.11 = (bf16[32,7680]{1,0:T(8,128)(2,1)S(1)}, bf16[32,7680]{1,0:T(8,128)(2,1)S(1)}, u32[]{:S(2)}, u32[]{:S(2)}) collective-permute-start(bf16[32,7680]{1,0:T(8,128)(2,1)S(1)} %get-tuple-element.27.refs_0_), channel_id=1, source_target_pairs={{0,96},{32,0},{64,32},{96,64},{1,97},{33,1},{65,33},{97,65},{2,98}... | collective-permute-start | bytes 1474568 | tf_op jit(solution)/shard_map/ppermute | solution.py:39
  1.7 35.1 %collective-permute-start.6 = (bf16[32,7680]{1,0:T(8,128)(2,1)S(1)}, bf16[32,7680]{1,0:T(8,128)(2,1)S(1)}, u32[]{:S(2)}, u32[]{:S(2)}) collective-permute-start(bf16[32,7680]{1,0:T(8,128)(2,1)S(1)} %get-tuple-element.27.refs_0_), channel_id=1, source_target_pairs={{0,1},{1,0},{2,3},{3,2},{4,5},{5,4},{6,7},{7,6},{8,9},{9,8},{10,11... | collective-permute-start | bytes 1474568 | tf_op jit(solution)/shard_map/ppermute | solution.py:47
  1.7 35.6 %collective-permute-start = (bf16[32,7680]{1,0:T(8,128)(2,1)S(1)}, bf16[32,7680]{1,0:T(8,128)(2,1)S(1)}, u32[]{:S(2)}, u32[]{:S(2)}) collective-permute-start(bf16[32,7680]{1,0:T(8,128)(2,1)S(1)} %get-tuple-element.27.refs_0_), channel_id=1, source_target_pairs={{0,32},{32,64},{64,96},{96,0},{1,33},{33,65},{65,97},{97,1},{2,34}... | collective-permute-start | bytes 1474568 | tf_op jit(solution)/shard_map/ppermute | solution.py:39
  3.4 36.1 %collective-permute-start.2 = (bf16[32,7680]{1,0:T(8,128)(2,1)S(1)}, bf16[32,7680]{1,0:T(8,128)(2,1)S(1)}, u32[]{:S(2)}, u32[]{:S(2)}) collective-permute-start(bf16[32,7680]{1,0:T(8,128)(2,1)S(1)} %get-tuple-element.28.refs_1_), channel_id=1, source_target_pairs={{0,96},{32,0},{64,32},{96,64},{1,97},{33,1},{65,33},{97,65},{2,98}... | collective-permute-start | bytes 1474568 | tf_op jit(solution)/shard_map/ppermute | solution.py:39
  4.9 35.3 %collective-permute-start.8 = (bf16[32,7680]{1,0:T(8,128)(2,1)S(1)}, bf16[32,7680]{1,0:T(8,128)(2,1)}, u32[]{:S(2)}, u32[]{:S(2)}) collective-permute-start(bf16[32,7680]{1,0:T(8,128)(2,1)S(1)} %get-tuple-element.28.refs_1_), channel_id=1, source_target_pairs={{0,32},{32,64},{64,96},{96,0},{1,33},{33,65},{65,97},{97,1},{2,34}... | collective-permute-start | bytes 1474568 | tf_op jit(solution)/shard_map/ppermute | solution.py:39
  5.5 0.7 copy-start.4
  6.2 0.7 copy-start.5
  12.6 42.3 %all-to-all-start = ((bf16[16,16,512]{2,1,0:T(8,128)(2,1)}), bf16[16,16,512]{2,1,0:T(8,128)(2,1)S(1)}, u32[]{:S(2)}, u32[]{:S(2)}) async-start(bf16[16,16,512]{2,1,0:T(8,128)(2,1)} %bitcast.5), calls=%async_computation | async-start | bytes 524288 | tf_op jit(solution)/shard_map/all_to_all | solution.py:465
  36.6 3.5 %collective-permute-start.7 = (bf16[32,7680]{1,0:T(8,128)(2,1)S(1)}, bf16[32,7680]{1,0:T(8,128)(2,1)S(1)}, u32[]{:S(2)}, u32[]{:S(2)}) collective-permute-start(bf16[32,7680]{1,0:T(8,128)(2,1)S(1)} %get-tuple-element.28.refs_1_), channel_id=1, source_target_pairs={{0,1},{1,0},{2,3},{3,2},{4,5},{5,4},{6,7},{7,6},{8,9},{9,8},{10,11... | collective-permute-start | bytes 1474568 | tf_op jit(solution)/shard_map/ppermute | solution.py:47
  36.8 4.7 %collective-permute-start.12 = (bf16[32,7680]{1,0:T(8,128)(2,1)S(1)}, bf16[32,7680]{1,0:T(8,128)(2,1)S(1)}, u32[]{:S(2)}, u32[]{:S(2)}) collective-permute-start(bf16[32,7680]{1,0:T(8,128)(2,1)S(1)} %collective-permute-done.11.refs_8_), channel_id=1, source_target_pairs={{0,1},{1,0},{2,3},{3,2},{4,5},{5,4},{6,7},{7,6},{8,9},{9,8},{10,11... | collective-permute-start | bytes 1474568 | tf_op jit(solution)/shard_map/ppermute | solution.py:47
  37.3 14.4 %collective-permute-start.1 = (bf16[32,7680]{1,0:T(8,128)(2,1)S(1)}, bf16[32,7680]{1,0:T(8,128)(2,1)}, u32[]{:S(2)}, u32[]{:S(2)}) collective-permute-start(bf16[32,7680]{1,0:T(8,128)(2,1)S(1)} %collective-permute-done.refs_4_), channel_id=1, source_target_pairs={{0,32},{32,64},{64,96},{96,0},{1,33},{33,65},{65,97},{97,1},{2,34}... | collective-permute-start | bytes 1474568 | tf_op jit(solution)/shard_map/ppermute | solution.py:39
  39.4 14.6 %collective-permute-start.3 = (bf16[32,7680]{1,0:T(8,128)(2,1)S(1)}, bf16[32,7680]{1,0:T(8,128)(2,1)}, u32[]{:S(2)}, u32[]{:S(2)}) collective-permute-start(bf16[32,7680]{1,0:T(8,128)(2,1)S(1)} %collective-permute-done.2.refs_9_), channel_id=1, source_target_pairs={{0,96},{32,0},{64,32},{96,64},{1,97},{33,1},{65,33},{97,65},{2,98}... | collective-permute-start | bytes 1474568 | tf_op jit(solution)/shard_map/ppermute | solution.py:39
  40.2 14.8 %collective-permute-start.9 = (bf16[32,7680]{1,0:T(8,128)(2,1)S(1)}, bf16[32,7680]{1,0:T(8,128)(2,1)}, u32[]{:S(2)}, u32[]{:S(2)}) collective-permute-start(bf16[32,7680]{1,0:T(8,128)(2,1)S(1)} %collective-permute-done.refs_4_), channel_id=1, source_target_pairs={{0,1},{1,0},{2,3},{3,2},{4,5},{5,4},{6,7},{7,6},{8,9},{9,8},{10,11... | collective-permute-start | bytes 1474568 | tf_op jit(solution)/shard_map/ppermute | solution.py:47
  40.2 0.8 copy-start
  41.0 14.0 %collective-permute-start.10 = (bf16[32,7680]{1,0:T(8,128)(2,1)}, bf16[32,7680]{1,0:T(8,128)(2,1)}, u32[]{:S(2)}, u32[]{:S(2)}) collective-permute-start(bf16[32,7680]{1,0:T(8,128)(2,1)} %collective-permute-done.8.refs_5_), channel_id=1, source_target_pairs={{0,1},{1,0},{2,3},{3,2},{4,5},{5,4},{6,7},{7,6},{8,9},{9,8},{10,11... | collective-permute-start | bytes 1474568 | tf_op jit(solution)/shard_map/ppermute | solution.py:47
  41.5 0.8 copy-start.2
  42.2 12.7 %collective-permute-start.13 = (bf16[32,7680]{1,0:T(8,128)(2,1)S(1)}, bf16[32,7680]{1,0:T(8,128)(2,1)}, u32[]{:S(2)}, u32[]{:S(2)}) collective-permute-start(bf16[32,7680]{1,0:T(8,128)(2,1)S(1)} %collective-permute-done.2.refs_9_), channel_id=1, source_target_pairs={{0,1},{1,0},{2,3},{3,2},{4,5},{5,4},{6,7},{7,6},{8,9},{9,8},{10,11... | collective-permute-start | bytes 1474568 | tf_op jit(solution)/shard_map/ppermute | solution.py:47
  51.7 8.2 %collective-permute-start.4 = (bf16[32,7680]{1,0:T(8,128)(2,1)}, bf16[32,7680]{1,0:T(8,128)(2,1)}, u32[]{:S(2)}, u32[]{:S(2)}) collective-permute-start(bf16[32,7680]{1,0:T(8,128)(2,1)} %collective-permute-done.1.refs_0_), channel_id=1, source_target_pairs={{0,1},{1,0},{2,3},{3,2},{4,5},{5,4},{6,7},{7,6},{8,9},{9,8},{10,11... | collective-permute-start | bytes 1474568 | tf_op jit(solution)/shard_map/ppermute | solution.py:47
  54.0 5.8 %collective-permute-start.5 = (bf16[32,7680]{1,0:T(8,128)(2,1)}, bf16[32,7680]{1,0:T(8,128)(2,1)}, u32[]{:S(2)}, u32[]{:S(2)}) collective-permute-start(bf16[32,7680]{1,0:T(8,128)(2,1)} %collective-permute-done.3.refs_1_), channel_id=1, source_target_pairs={{0,1},{1,0},{2,3},{3,2},{4,5},{5,4},{6,7},{7,6},{8,9},{9,8},{10,11... | collective-permute-start | bytes 1474568 | tf_op jit(solution)/shard_map/ppermute | solution.py:47
  54.9 1.0 copy-start.1
  56.0 1.0 copy-start.3
  62.3 25.7 %copy-start.9 = (bf16[7168]{0:T(1024)(128)(2,1)S(1)}, bf16[7168]{0:T(1024)(128)(2,1)}, u32[]{:S(2)}) copy-start(bf16[7168]{0:T(1024)(128)(2,1)} %param.21) | copy-start | bytes 43012
  62.3 25.7 %copy-start.7 = (bf16[2,2,7168]{2,1,0:T(2,128)(2,1)S(1)}, bf16[2,2,7168]{2,1,0:T(2,128)(2,1)}, u32[]{:S(2)}) copy-start(bf16[2,2,7168]{2,1,0:T(2,128)(2,1)} %param.18) | copy-start | bytes 172036
  62.3 26.0 %copy-start.6 = (bf16[7168,16]{0,1:T(8,128)(2,1)S(1)}, bf16[7168,16]{0,1:T(8,128)(2,1)}, u32[]{:S(2)}) copy-start(bf16[7168,16]{0,1:T(8,128)(2,1)} %param.22) | copy-start | bytes 688132
  62.3 26.2 %copy-start.10 = (s32[2,2,8]{2,1,0:T(2,128)S(1)}, s32[2,2,8]{2,1,0:T(2,128)}, u32[]{:S(2)}) copy-start(s32[2,2,8]{2,1,0:T(2,128)} %param.24) | copy-start | bytes 388
  62.3 26.2 %copy-start.8 = (s32[2,2,8]{2,1,0:T(2,128)S(1)}, s32[2,2,8]{2,1,0:T(2,128)}, u32[]{:S(2)}) copy-start(s32[2,2,8]{2,1,0:T(2,128)} %param.23) | copy-start | bytes 388
  62.3 17.9 %collective-permute-start.14 = (bf16[32,3584]{1,0:T(8,128)(2,1)S(1)}, bf16[32,3584]{1,0:T(8,128)(2,1)S(1)}, u32[]{:S(2)}, u32[]{:S(2)}) collective-permute-start(bf16[32,3584]{1,0:T(8,128)(2,1)S(1)} %get-tuple-element.30), channel_id=1, source_target_pairs={{0,2},{2,4},{4,6},{6,8},{8,10},{10,12},{12,14},{14,16},{16,18},{18... | collective-permute-start | bytes 688136 | tf_op jit(solution)/shard_map/ppermute | solution.py:43
  63.4 16.9 %collective-permute-start.15 = (bf16[32,3584]{1,0:T(8,128)(2,1)S(1)}, bf16[32,3584]{1,0:T(8,128)(2,1)S(1)}, u32[]{:S(2)}, u32[]{:S(2)}) collective-permute-start(bf16[32,3584]{1,0:T(8,128)(2,1)S(1)} %get-tuple-element.31), channel_id=1, source_target_pairs={{0,30},{2,0},{4,2},{6,4},{8,6},{10,8},{12,10},{14,12},{16,14},{18,... | collective-permute-start | bytes 688136 | tf_op jit(solution)/shard_map/ppermute | solution.py:43
  68.5 11.7 %collective-permute-start.16 = (bf16[32,1792]{1,0:T(8,128)(2,1)S(1)}, bf16[32,1792]{1,0:T(8,128)(2,1)S(1)}, u32[]{:S(2)}, u32[]{:S(2)}) collective-permute-start(bf16[32,1792]{1,0:T(8,128)(2,1)S(1)} %get-tuple-element.32), channel_id=1, source_target_pairs={{0,4},{2,6},{4,8},{6,10},{8,12},{10,14},{12,16},{14,18},{16,20},{1... | collective-permute-start | bytes 344072 | tf_op jit(solution)/shard_map/ppermute | solution.py:43
  68.5 11.7 %collective-permute-start.17 = (bf16[32,1792]{1,0:T(8,128)(2,1)S(1)}, bf16[32,1792]{1,0:T(8,128)(2,1)S(1)}, u32[]{:S(2)}, u32[]{:S(2)}) collective-permute-start(bf16[32,1792]{1,0:T(8,128)(2,1)S(1)} %get-tuple-element.33), channel_id=1, source_target_pairs={{0,28},{2,30},{4,0},{6,2},{8,4},{10,6},{12,8},{14,10},{16,12},{18,... | collective-permute-start | bytes 344072 | tf_op jit(solution)/shard_map/ppermute | solution.py:43
  81.1 23.3 %all-to-all-start.1 = ((bf16[4,8,3584]{2,1,0:T(8,128)(2,1)}), bf16[4,8,3584]{2,1,0:T(8,128)(2,1)S(1)}, u32[]{:S(2)}, u32[]{:S(2)}) async-start(bf16[4,8,3584]{2,1,0:T(8,128)(2,1)} %fusion), calls=%async_computation.1 | async-start | bytes 458752 | tf_op jit(solution)/shard_map/all_to_all | solution.py:433
  87.5 55.7 %collective-permute-start.20 = (bf16[7168,128]{1,0:T(8,128)(2,1)}, bf16[7168,128]{1,0:T(8,128)(2,1)S(1)}, u32[]{:S(2)}, u32[]{:S(2)}) collective-permute-start(bf16[7168,128]{1,0:T(8,128)(2,1)} %gate_a.1), channel_id=1, source_target_pairs={{0,1},{1,0},{2,3},{3,2},{4,5},{5,4},{6,7},{7,6},{8,9},{9,8},{10,11... | collective-permute-start | bytes 5505032 | tf_op jit(solution)/shard_map/ppermute | solution.py:47
  87.5 61.4 %collective-permute-start.21 = (bf16[7168,128]{1,0:T(8,128)(2,1)}, bf16[7168,128]{1,0:T(8,128)(2,1)}, u32[]{:S(2)}, u32[]{:S(2)}) collective-permute-start(bf16[7168,128]{1,0:T(8,128)(2,1)} %up_a.1), channel_id=1, source_target_pairs={{0,1},{1,0},{2,3},{3,2},{4,5},{5,4},{6,7},{7,6},{8,9},{9,8},{10,11... | collective-permute-start | bytes 5505032 | tf_op jit(solution)/shard_map/ppermute | solution.py:47
  88.0 60.9 %collective-permute-start.22 = (bf16[128,7168]{1,0:T(8,128)(2,1)}, bf16[128,7168]{1,0:T(8,128)(2,1)}, u32[]{:S(2)}, u32[]{:S(2)}) collective-permute-start(bf16[128,7168]{1,0:T(8,128)(2,1)} %down_a.1), channel_id=1, source_target_pairs={{0,1},{1,0},{2,3},{3,2},{4,5},{5,4},{6,7},{7,6},{8,9},{9,8},{10,11... | collective-permute-start | bytes 5505032 | tf_op jit(solution)/shard_map/ppermute | solution.py:47
  141.1 13.0 %collective-permute-start.18 = (bf16[32,7296]{1,0:T(8,128)(2,1)S(1)}, bf16[32,7296]{1,0:T(8,128)(2,1)S(1)}, u32[]{:S(2)}, u32[]{:S(2)}) collective-permute-start(bf16[32,7296]{1,0:T(8,128)(2,1)S(1)} %get-tuple-element.36), channel_id=1, source_target_pairs={{0,96},{32,0},{64,32},{96,64},{1,97},{33,1},{65,33},{97,65},{2,98}... | collective-permute-start | bytes 1400840 | tf_op jit(solution)/shard_map/ppermute | solution.py:39
  142.3 21.2 %collective-permute-start.19 = (bf16[32,7296]{1,0:T(8,128)(2,1)S(1)}, bf16[32,7296]{1,0:T(8,128)(2,1)S(1)}, u32[]{:S(2)}, u32[]{:S(2)}) collective-permute-start(bf16[32,7296]{1,0:T(8,128)(2,1)S(1)} %get-tuple-element.37), channel_id=1, source_target_pairs={{0,32},{32,64},{64,96},{96,0},{1,33},{33,65},{65,97},{97,1},{2,34}... | collective-permute-start | bytes 1400840 | tf_op jit(solution)/shard_map/ppermute | solution.py:39
  143.2 5.7 %copy-start.11 = (bf16[7168,128]{1,0:T(8,128)(2,1)}, bf16[7168,128]{1,0:T(8,128)(2,1)S(1)}, u32[]{:S(2)}) copy-start(bf16[7168,128]{1,0:T(8,128)(2,1)S(1)} %collective-permute-done.20.gate_b) | copy-start | bytes 5505028
  143.2 25.4 %collective-permute-start.25 = (bf16[32,7296]{1,0:T(8,128)(2,1)S(1)}, bf16[32,7296]{1,0:T(8,128)(2,1)S(1)}, u32[]{:S(2)}, u32[]{:S(2)}) collective-permute-start(bf16[32,7296]{1,0:T(8,128)(2,1)S(1)} %get-tuple-element.43), channel_id=1, source_target_pairs={{0,64},{32,96},{64,0},{96,32},{1,65},{33,97},{65,1},{97,33},{2,66}... | collective-permute-start | bytes 1400840 | tf_op jit(solution)/shard_map/ppermute | solution.py:39
  166.0 8.7 %collective-permute-start.23 = (bf16[32,7168]{1,0:T(8,128)(2,1)S(1)}, bf16[32,7168]{1,0:T(8,128)(2,1)S(1)}, u32[]{:S(2)}, u32[]{:S(2)}) collective-permute-start(bf16[32,7168]{1,0:T(8,128)(2,1)S(1)} %get-tuple-element.41), channel_id=1, source_target_pairs={{0,32},{32,64},{64,96},{96,0},{1,33},{33,65},{65,97},{97,1},{2,34}... | collective-permute-start | bytes 1376264 | tf_op jit(solution)/shard_map/ppermute | solution.py:39
  168.6 13.4 %collective-permute-start.24 = (bf16[32,7168]{1,0:T(8,128)(2,1)S(1)}, bf16[32,7168]{1,0:T(8,128)(2,1)S(1)}, u32[]{:S(2)}, u32[]{:S(2)}) collective-permute-start(bf16[32,7168]{1,0:T(8,128)(2,1)S(1)} %get-tuple-element.42), channel_id=1, source_target_pairs={{0,96},{32,0},{64,32},{96,64},{1,97},{33,1},{65,33},{97,65},{2,98}... | collective-permute-start | bytes 1376264 | tf_op jit(solution)/shard_map/ppermute | solution.py:39
  171.2 10.8 %collective-permute-start.26 = (bf16[32,7168]{1,0:T(8,128)(2,1)S(1)}, bf16[32,7168]{1,0:T(8,128)(2,1)S(1)}, u32[]{:S(2)}, u32[]{:S(2)}) collective-permute-start(bf16[32,7168]{1,0:T(8,128)(2,1)S(1)} %expert_part.3), channel_id=1, source_target_pairs={{0,64},{32,96},{64,0},{96,32},{1,65},{33,97},{65,1},{97,33},{2,66}... | collective-permute-start | bytes 1376264 | tf_op jit(solution)/shard_map/ppermute | solution.py:39
  182.4 13.3 %collective-permute-start.27 = (bf16[32,3584]{1,0:T(8,128)(2,1)S(1)}, bf16[32,3584]{1,0:T(8,128)(2,1)S(1)}, u32[]{:S(2)}, u32[]{:S(2)}) collective-permute-start(bf16[32,3584]{1,0:T(8,128)(2,1)S(1)} %get-tuple-element.45), channel_id=1, source_target_pairs={{0,2},{2,4},{4,6},{6,8},{8,10},{10,12},{12,14},{14,16},{16,18},{18... | collective-permute-start | bytes 688136 | tf_op jit(solution)/shard_map/ppermute | solution.py:43
  182.9 12.9 %collective-permute-start.28 = (bf16[32,3584]{1,0:T(8,128)(2,1)S(1)}, bf16[32,3584]{1,0:T(8,128)(2,1)S(1)}, u32[]{:S(2)}, u32[]{:S(2)}) collective-permute-start(bf16[32,3584]{1,0:T(8,128)(2,1)S(1)} %get-tuple-element.46), channel_id=1, source_target_pairs={{0,30},{2,0},{4,2},{6,4},{8,6},{10,8},{12,10},{14,12},{16,14},{18,... | collective-permute-start | bytes 688136 | tf_op jit(solution)/shard_map/ppermute | solution.py:43
  185.8 10.0 %collective-permute-start.29 = (bf16[32,1792]{1,0:T(8,128)(2,1)S(1)}, bf16[32,1792]{1,0:T(8,128)(2,1)S(1)}, u32[]{:S(2)}, u32[]{:S(2)}) collective-permute-start(bf16[32,1792]{1,0:T(8,128)(2,1)S(1)} %get-tuple-element.47), channel_id=1, source_target_pairs={{0,4},{2,6},{4,8},{6,10},{8,12},{10,14},{12,16},{14,18},{16,20},{1... | collective-permute-start | bytes 344072 | tf_op jit(solution)/shard_map/ppermute | solution.py:43
  185.8 10.0 %collective-permute-start.30 = (bf16[32,1792]{1,0:T(8,128)(2,1)S(1)}, bf16[32,1792]{1,0:T(8,128)(2,1)S(1)}, u32[]{:S(2)}, u32[]{:S(2)}) collective-permute-start(bf16[32,1792]{1,0:T(8,128)(2,1)S(1)} %get-tuple-element.48), channel_id=1, source_target_pairs={{0,28},{2,30},{4,0},{6,2},{8,4},{10,6},{12,8},{14,10},{16,12},{18,... | collective-permute-start | bytes 344072 | tf_op jit(solution)/shard_map/ppermute | solution.py:43

commit v4 on v3

--- a/solution.py
+++ b/solution.py
@@ -60,10 +60,10 @@
     return lax.rem(x + step, nx)
 
 
-def chip_at(place, j):
+def chip_at(place, where_ref):
     group, block = place // FAR, lax.rem(place, FAR)
-    step = jnp.where(group == 2, NEAR - 1, jnp.where(group == 3, 2, group))
-    return NEAR * block + lax.rem(j + step, NEAR)
+    step = jnp.where(group == 2, RING - 1, jnp.where(group == 3, 2, group))
+    return lax.rem(NEAR * where_ref[1] + where_ref[2] + step + NEAR * block, RING)
 
 
 def smem():
@@ -94,7 +94,7 @@
     return pl.CostEstimate(flops=flops, bytes_accessed=nbytes, transcendentals=0)
 
 
-def context_kernel(nx, where_ref, lengths, keys, queries, new, out, held):
+def context_kernel(nx, where_ref, keys, queries, new, out, held):
     seq = pl.program_id(0)
     seqs = pl.num_programs(0)
     steps, heads = queries.shape[1], queries.shape[2]
@@ -102,7 +102,7 @@
     scale = 1.0 / math.sqrt(QK)
     query = queries[0].reshape(count, queries.shape[3])
     score = jnp.dot(query, keys[0], preferred_element_type=f32) * scale
-    score = jnp.where(iota(score.shape, 1) < lengths[seq], score, -jnp.inf)
+    score = jnp.where(iota(score.shape, 1) < where_ref[3 + seq], score, -jnp.inf)
     wide = query.astype(f32)
     step_of = iota((count, 1), 0) // heads
     latest = []
@@ -138,7 +138,7 @@
         out[...] = jnp.dot(one_hot(take), held[...], preferred_element_type=f32).astype(bf16)
 
 
-def context_rows(where, nx, cache_kv, new_kv, queries, lengths):
+def context_rows(where, nx, cache_kv, new_kv, queries):
     seqs, length, width = cache_kv.shape
     steps, heads = queries.shape[1:3]
     rows = seqs * steps * heads
@@ -148,7 +148,6 @@
         grid=(seqs,),
         out_shape=jax.ShapeDtypeStruct((rows, LAT), bf16),
         in_specs=[
-            smem(),
             smem(),
             pl.BlockSpec((1, width, length), lambda b: (b, 0, 0)),
             pl.BlockSpec((1, steps, heads, width), lambda b: (b, 0, 0, 0)),
@@ -159,7 +158,7 @@
         compiler_params=params(24),
         cost_estimate=cost(2 * rows * length * (width + LAT), 2 * cache_kv.size),
         name="context_rows",
-    )(where, lengths, held_in_hbm(keys), held_in_hbm(queries), new_kv)
+    )(where, held_in_hbm(keys), held_in_hbm(queries), held_in_hbm(new_kv))
 
 
 def pack_kernel(up, rows, tops, lows, sem):
@@ -200,8 +199,13 @@
     own[:, cols] = got[:size]
     right[:, cols] = got[size : 2 * size].astype(bf16)
     left[:, cols] = got[2 * size : 3 * size].astype(bf16)
-    last, at = (ahead, n * TILE) if n * TILE < width else (behind, n * TILE - width)
-    last[:, pl.ds(at, TILE)] = got[3 * size :].astype(bf16)
+    rows = got[3 * size :].astype(bf16)
+    if n * TILE < width:
+        ahead[:, cols] = rows
+    else:
+        block, cols = size // FAR, pl.ds(n * TILE - width, TILE)
+        behind[pl.ds(block, size - block), cols] = rows[: size - block]
+        behind[pl.ds(0, block), cols] = rows[size - block :]
 
 
 def row_shapes(size, width):
@@ -230,7 +234,7 @@
     values = jnp.where(hop == first + iota(values.shape, 1) // VH, values, 0.0).astype(bf16)
     shape = (RING * HALVES * tok, arrived.shape[0])
     row, source = iota(shape, 0), iota(shape, 1)
-    chip = chip_at(row // (HALVES * tok), where_ref[2])
+    chip = chip_at(row // (HALVES * tok), where_ref)
     take = (source // (tok * nx) == chip) & (lax.rem(source, tok) == lax.rem(row, tok))
     half = lax.rem(row // tok, HALVES)
     taken = [
@@ -261,7 +265,7 @@
         compiler_params=params(6),
         cost_estimate=cost(8 * RING * tok * depth * width * HALVES, 4 * depth * width),
         name="attend_part",
-    )(where, arrived, *[held_in_vmem(p) for p in pieces], *([before] if last else []))
+    )(where, arrived, *pieces, *([before] if last else []))
 
 
 SEND_TILE = 512
@@ -299,7 +303,7 @@
         outs[r][:, pl.ds(HALVES * half, EXTRA)] = got[r * SLOTS : (r + 1) * SLOTS]
     shape = (count, count)
     row, token = iota(shape, 0), iota(shape, 1)
-    chip = chip_at(row // (HALVES * tok), where_ref[2])
+    chip = chip_at(row // (HALVES * tok), where_ref)
     take = (token // (HALVES * tok) == chip) & (lax.rem(token, HALVES * tok) == lax.rem(row, HALVES * tok))
     for c in range(HALVES):
         got = lax.dot_general(one_hot(take), sels[c], NT, preferred_element_type=f32)
@@ -421,17 +425,42 @@
     )(spread, *parts)
 
 
+def merge_kernel(own, right, left, ahead, behind, first, *rest):
+    block = first.shape[0]
+    width = ahead.shape[1]
+    for c, last in enumerate((ahead, behind)):
+        cols = pl.ds(c * width, width)
+        total = own[:, cols] + right[:, cols].astype(f32) + left[:, cols].astype(f32)
+        total = total + last[...].astype(f32)
+        first[:, cols] = total[:block]
+        for k, out in enumerate(rest):
+            out[:, cols] = total[(k + 1) * block : (k + 2) * block].astype(bf16)
+
+
+def merge(own, *others):
+    size, width = own.shape
+    block = (size // FAR, width)
+    return pl.pallas_call(
+        merge_kernel,
+        out_shape=(jax.ShapeDtypeStruct(block, f32),) + (jax.ShapeDtypeStruct(block, bf16),) * (FAR - 1),
+        in_specs=[vmem()] * 5,
+        out_specs=[vmem()] * FAR,
+        compiler_params=params(4),
+        cost_estimate=cost(4 * size * width, 12 * size * width),
+        name="merge",
+    )(own, *others)
+
+
 def reduce_z(own, right, left, ahead, behind):
-    size, width = own.shape
+    right = shift_z(right, 1)
+    left = shift_z(left, -1)
     ahead = shift_z(ahead, 2)
     behind = shift_z(behind, -2)
-    right = shift_z(right, 1)
-    left = shift_z(left, -1)
-    total = own + right.astype(f32) + left.astype(f32)
-    total = total + jnp.concatenate([ahead, behind], axis=1).astype(f32)
-    sent = total.astype(bf16).reshape(FAR, size // FAR, width)
-    got = lax.all_to_all(sent, "zb", split_axis=0, concat_axis=0, tiled=True)
-    return jnp.sum(got.astype(f32), axis=0)
+    out, *sent = merge(own, right, left, ahead, behind)
+    for k, rows in enumerate(sent):
+        step = NEAR * (k + 1)
+        out = out + shift_z(rows, step if step <= RING // 2 else step - RING).astype(f32)
+    return out
 
 
 def layer(
@@ -454,6 +483,7 @@
     seqs, steps = queries.shape[:2]
     tok = seqs * steps
     where = jnp.stack([lax.axis_index(a) for a in ("x", "zb", "j")]).astype(jnp.int32)
+    where = jnp.concatenate([where, lengths.astype(jnp.int32)])
 
     tops, lows = pack(value_up.T, out_proj)
     top_left = shift_x(tops, 1)
@@ -461,14 +491,15 @@
     low_left = shift_x(lows, 1)
     top_right = shift_x(tops, -1)
 
-    outgoing = context_rows(where, nx, cache_kv, new_kv, queries, lengths)
+    outgoing = context_rows(where, nx, cache_kv, new_kv, queries)
     arrived = lax.all_to_all(
         outgoing.reshape(RING, nx * tok, LAT), ZAX, split_axis=0, concat_axis=0, tiled=True
     )
     top_far = shift_x(top_left, 1)
     low_far = shift_x(low_right, -1)
-    near = (tops, lows, top_left, low_left, top_right, low_right)
-    near = sum(([near[i], near[i + 1], swap_core(near[i]), swap_core(near[i + 1])] for i in (0, 2, 4)), [])
+    near = [tops, lows, swap_core(tops), swap_core(lows)]
+    for pair in ((top_left, low_left), (top_right, low_right)):
+        near += [*pair, *map(swap_core, pair)]
     beyond = [top_far, low_far, swap_core(top_far), swap_core(low_far)]
     weights = stage((w_gate, swap_core(w_gate), w_up, swap_core(w_up), w_down, swap_core(w_down)))
     arrived = arrived.reshape(RING * nx * tok, LAT)

time: 220 us -> 212 us (0.964)
  the two profiles are of different devices: /device:TPU:42 before, /device:TPU:164 now
where the time goes in v4:
time: 212 us; the launch traced here: 208 us
  starting transfers between devices  80.7 us (38%)
  waiting for transfers between devices  60 us (28%)
  blocking collectives  34.6 us (16%)
  Pallas kernels  23.7 us (11%)
  local copies, waits for them, and re-layouts  6.91 us (3%)
    ppermute x14, starting transfers between devices, shift_z(): return lax.ppermute(a, ZAX, [(i, (i + step) % RING) for i in range(RING)])  40.8 us
    ppermute x12, waiting for transfers between devices, shift_x(): return lax.ppermute(a, 'x', [(i, (i + step) % n) for i in range(n)])  34.7 us
    all_gather x1, blocking collectives, layer(): ring = lax.all_gather(payload, ZAX, axis=0, tiled=True)  34.6 us
    ppermute x14, waiting for transfers between devices, shift_z(): return lax.ppermute(a, ZAX, [(i, (i + step) % RING) for i in range(RING)])  25.3 us
    all_to_all x1, starting transfers between devices, layer(): lax.all_to_all(outgoing.reshape(RING, nx * tok, LAT), ZAX, split_axis=0,...  22.9 us
    ppermute x12, starting transfers between devices, shift_x(): return lax.ppermute(a, 'x', [(i, (i + step) % n) for i in range(n)])  15 us
    pallas_call x1, Pallas kernels, context_rows(): pl.pallas_call(functools.partial(context_kernel, nx), grid=(seqs,), out_s...  5.91 us
    unnamed x24, local copies, waits for them, and re-layouts  5.49 us
  transfers between devices with their start and end apart: 38, of which 14 were waited for; matrix products, arithmetic and copies ran while one was open for 1% of the time, Pallas kernels for 11%

profile of v4, /device:TPU:164, one launch (start us, length us, event | category | flops | bytes accessed | tf_op | source)
XLA Modules:
  0.0 208.2 jit_solution(2279546108298563887)
XLA Ops:
  0.0 1.2 pack.1
  1.2 0.5 collective-permute-start.11
  1.7 1.6 collective-permute-start
  3.4 0.4 collective-permute-start.2
  3.8 2.1 %collective-permute-start.8 = (bf16[32,7680]{1,0:T(8,128)(2,1)S(1)}, bf16[32,7680]{1,0:T(8,128)(2,1)}, u32[]{:S(2)}, u32[]{:S(2)}) collective-permute-start(bf16[32,7680]{1,0:T(8,128)(2,1)S(1)} %get-tuple-element.36.refs_1_), channel_id=1, source_target_pairs={{0,32},{32,64},{64,96},{96,0},{1,33},{33,65},{65,97},{97,1},{2,34}... | collective-permute-start | bytes 1474568 | tf_op jit(solution)/shard_map/ppermute | solution.py:39
  5.9 0.7 pad_add_fusion.where_ref
  6.6 5.9 %context_rows.1 = bf16[256,512]{1,0:T(8,128)(2,1)} custom-call(s32[5]{0:T(128)S(1)} %pad_add_fusion.where_ref, bf16[2,576,2048]{2,1,0:T(8,128)(2,1)} %bitcast.33, bf16[2,2,64,576]{3,2,1,0:T(8,128)(2,1)} %queries.1, bf16[2,2,576]{2,1,0:T(2,128)(2,1)} %new.1), custom_call_target="tpu_custom_call" | custom-call | flops 1140850688 | bytes 4718592 | tf_op jit(solution)/shard_map/context_rows/pallas_call | solution.py:146
  12.6 22.9 %all-to-all-start = ((bf16[16,16,512]{2,1,0:T(8,128)(2,1)}), bf16[16,16,512]{2,1,0:T(8,128)(2,1)S(1)}, u32[]{:S(2)}, u32[]{:S(2)}) async-start(bf16[16,16,512]{2,1,0:T(8,128)(2,1)} %bitcast.5), calls=%async_computation | async-start | bytes 524288 | tf_op jit(solution)/shard_map/all_to_all | solution.py:495
  35.5 0.1 collective-permute-start.7
  35.6 0.5 collective-permute-start.12
  36.1 3.2 %collective-permute-start.1 = (bf16[32,7680]{1,0:T(8,128)(2,1)S(1)}, bf16[32,7680]{1,0:T(8,128)(2,1)}, u32[]{:S(2)}, u32[]{:S(2)}) collective-permute-start(bf16[32,7680]{1,0:T(8,128)(2,1)S(1)} %collective-permute-done.refs_4_), channel_id=1, source_target_pairs={{0,32},{32,64},{64,96},{96,0},{1,33},{33,65},{65,97},{97,1},{2,34}... | collective-permute-start | bytes 1474568 | tf_op jit(solution)/shard_map/ppermute | solution.py:39
  39.5 0.8 copy-done
  40.3 0.5 collective-permute-start.10
  40.8 0.8 copy-done.2
  41.6 8.5 %collective-permute-done.1.refs_0_ = bf16[32,7680]{1,0:T(8,128)(2,1)} collective-permute-done((bf16[32,7680]{1,0:T(8,128)(2,1)S(1)}, bf16[32,7680]{1,0:T(8,128)(2,1)}, u32[]{:S(2)}, u32[]{:S(2)}) %collective-permute-start.1) | collective-permute-done | bytes 491552 | tf_op jit(solution)/shard_map/ppermute | solution.py:39
  50.2 2.3 %collective-permute-done.3.refs_1_ = bf16[32,7680]{1,0:T(8,128)(2,1)} collective-permute-done((bf16[32,7680]{1,0:T(8,128)(2,1)S(1)}, bf16[32,7680]{1,0:T(8,128)(2,1)}, u32[]{:S(2)}, u32[]{:S(2)}) %collective-permute-start.3) | collective-permute-done | bytes 491552 | tf_op jit(solution)/shard_map/ppermute | solution.py:39
  52.5 0.8 copy-done.4
  53.3 0.5 collective-permute-start.23
  53.8 1.0 copy-done.1
  54.8 1.0 copy-done.3
  55.9 1.0 copy-done.5
  56.9 2.7 %attend_part.2.refs_4_ = f32[128,3584]{1,0:T(8,128)S(1)} custom-call(s32[5]{0:T(128)S(1)} %pad_add_fusion.where_ref, bf16[256,512]{1,0:T(8,128)(2,1)S(1)} %bitcast.31, bf16[32,7680]{1,0:T(8,128)(2,1)S(1)} %get-tuple-element.35.refs_0_, bf16[32,7680]{1,0:T(8,128)(2,1)S(1)} %get-tuple-element.36.refs_1_, bf16[32,7680]{1,0:T(8,128)(2,1)S(1)} %collective-permute-done.6.refs_2_, ...), custom_call_target="tpu_custom_call" | custom-call | flops 1409286144 | bytes 5505024 | tf_op jit(solution)/shard_map/attend_part/pallas_call | solution.py:260
  59.7 2.4 %attend_part.3 = (f32[32,3584]{1,0:T(8,128)S(1)}, bf16[32,3584]{1,0:T(8,128)(2,1)S(1)}, bf16[32,3584]{1,0:T(8,128)(2,1)S(1)}, bf16[32,1792]{1,0:T(8,128)(2,1)S(1)}, bf16[32,1792]{1,0:T(8,128)(2,1)S(1)}) custom-call(s32[5]{0:T(128)S(1)} %pad_add_fusion.where_ref, bf16[256,512]{1,0:T(8,128)(2,1)S(1)} %bitcast.32, ...), custom_call_target="tpu_custom_call" | custom-call | flops 469762048 | bytes 1835008 | tf_op jit(solution)/shard_map/attend_part/pallas_call | solution.py:260
  62.1 1.6 collective-permute-start.14
  63.7 0.6 collective-permute-start.15
  64.2 3.1 %collective-permute-start.16 = (bf16[32,1792]{1,0:T(8,128)(2,1)S(1)}, bf16[32,1792]{1,0:T(8,128)(2,1)S(1)}, u32[]{:S(2)}, u32[]{:S(2)}) collective-permute-start(bf16[32,1792]{1,0:T(8,128)(2,1)S(1)} %get-tuple-element.40), channel_id=1, source_target_pairs={{0,4},{2,6},{4,8},{6,10},{8,12},{10,14},{12,16},{14,18},{16,20},{1... | collective-permute-start | bytes 344072 | tf_op jit(solution)/shard_map/ppermute | solution.py:43
  67.4 3.6 %collective-permute-start.17 = (bf16[32,1792]{1,0:T(8,128)(2,1)S(1)}, bf16[32,1792]{1,0:T(8,128)(2,1)S(1)}, u32[]{:S(2)}, u32[]{:S(2)}) collective-permute-start(bf16[32,1792]{1,0:T(8,128)(2,1)S(1)} %get-tuple-element.41), channel_id=1, source_target_pairs={{0,28},{2,30},{4,0},{6,2},{8,4},{10,6},{12,8},{14,10},{16,12},{18,... | collective-permute-start | bytes 344072 | tf_op jit(solution)/shard_map/ppermute | solution.py:43
  71.0 7.9 %collective-permute-done.16.ahead = bf16[32,1792]{1,0:T(8,128)(2,1)S(1)} collective-permute-done((bf16[32,1792]{1,0:T(8,128)(2,1)S(1)}, bf16[32,1792]{1,0:T(8,128)(2,1)S(1)}, u32[]{:S(2)}, u32[]{:S(2)}) %collective-permute-start.16) | collective-permute-done | bytes 114720 | tf_op jit(solution)/shard_map/ppermute | solution.py:43
  79.0 2.4 %collective-permute-start.18 = (bf16[8,3584]{1,0:T(8,128)(2,1)S(1)}, bf16[8,3584]{1,0:T(8,128)(2,1)S(1)}, u32[]{:S(2)}, u32[]{:S(2)}) collective-permute-start(bf16[8,3584]{1,0:T(8,128)(2,1)S(1)} %get-tuple-element.43), channel_id=1, source_target_pairs={{0,8},{2,10},{4,12},{6,14},{8,16},{10,18},{12,20},{14,22},{16,24},... | collective-permute-start | bytes 172040 | tf_op jit(solution)/shard_map/ppermute | solution.py:43
  81.5 5.4 %collective-permute-start.19 = (bf16[8,3584]{1,0:T(8,128)(2,1)S(1)}, bf16[8,3584]{1,0:T(8,128)(2,1)S(1)}, u32[]{:S(2)}, u32[]{:S(2)}) collective-permute-start(bf16[8,3584]{1,0:T(8,128)(2,1)S(1)} %get-tuple-element.44), channel_id=1, source_target_pairs={{0,16},{2,18},{4,20},{6,22},{8,24},{10,26},{12,28},{14,30},{16,0},... | collective-permute-start | bytes 172040 | tf_op jit(solution)/shard_map/ppermute | solution.py:43
  86.9 5.4 %collective-permute-start.20 = (bf16[8,3584]{1,0:T(8,128)(2,1)S(1)}, bf16[8,3584]{1,0:T(8,128)(2,1)S(1)}, u32[]{:S(2)}, u32[]{:S(2)}) collective-permute-start(bf16[8,3584]{1,0:T(8,128)(2,1)S(1)} %get-tuple-element.45), channel_id=1, source_target_pairs={{0,24},{2,26},{4,28},{6,30},{8,0},{10,2},{12,4},{14,6},{16,8},{18,... | collective-permute-start | bytes 172040 | tf_op jit(solution)/shard_map/ppermute | solution.py:43
  92.5 0.2 reshape.98
  92.7 0.1 collective-permute-start.25
  92.9 3.7 %collective-permute-done.19 = bf16[8,3584]{1,0:T(8,128)(2,1)S(1)} collective-permute-done((bf16[8,3584]{1,0:T(8,128)(2,1)S(1)}, bf16[8,3584]{1,0:T(8,128)(2,1)S(1)}, u32[]{:S(2)}, u32[]{:S(2)}) %collective-permute-start.19) | collective-permute-done | bytes 57376 | tf_op jit(solution)/shard_map/ppermute | solution.py:43
  96.5 2.5 %collective-permute-done.20 = bf16[8,3584]{1,0:T(8,128)(2,1)S(1)} collective-permute-done((bf16[8,3584]{1,0:T(8,128)(2,1)S(1)}, bf16[8,3584]{1,0:T(8,128)(2,1)S(1)}, u32[]{:S(2)}, u32[]{:S(2)}) %collective-permute-start.20) | collective-permute-done | bytes 57376 | tf_op jit(solution)/shard_map/ppermute | solution.py:43
  99.0 0.2 multiply_reduce_fusion
  99.5 0.4 fusion
  99.9 0.2 select_reduce_fusion.1
  100.5 34.6 %all_gather.3.tokens = bf16[128,3712]{1,0:T(8,128)(2,1)S(1)} all-gather(bf16[8,3712]{1,0:T(8,128)(2,1)S(1)} %pad_maximum_fusion), channel_id=1, replica_groups=mesh['rep'=2,'x'=4,'zb'=4,'j'=4,'c'=2] {'zb','j'}, dimensions={0}, use_global_device_ids=true | all-gather | bytes 1009664 | tf_op jit(solution)/shard_map/all_gather | solution.py:537
  135.0 1.3 dispatch.1
  136.4 1.0 collective-permute-start.21
  137.4 1.7 collective-permute-start.22
  139.2 2.0 collective-permute-start.28
  141.2 4.3 %stage.1 = (bf16[7168,512]{1,0:T(8,128)(2,1)S(1)}, bf16[256,7168]{1,0:T(8,128)(2,1)S(1)}) custom-call(bf16[7168,128]{1,0:T(8,128)(2,1)} %gate_a.1, bf16[7168,128]{1,0:T(8,128)(2,1)} %collective-permute-done.23.gate_b, bf16[7168,128]{1,0:T(8,128)(2,1)} %up_a.1, bf16[7168,128]{1,0:T(8,128)(2,1)} %collective-permute-done.24.up_b, bf16[128,7168]{1,0:T(8,128)(2,1)} %down_a.1, ...), custom_call_target="tpu_custom_call" | custom-call | flops 3670016000 | bytes 11010048 | tf_op jit(solution)/shard_map/stage/pallas_call | solution.py:349
  145.5 2.5 %collective-permute-done.21.refs_1_ = bf16[32,7296]{1,0:T(8,128)(2,1)S(1)} collective-permute-done((bf16[32,7296]{1,0:T(8,128)(2,1)S(1)}, bf16[32,7296]{1,0:T(8,128)(2,1)S(1)}, u32[]{:S(2)}, u32[]{:S(2)}) %collective-permute-start.21) | collective-permute-done | bytes 466976 | tf_op jit(solution)/shard_map/ppermute | solution.py:39
  148.0 11.4 %collective-permute-done.22.refs_2_ = bf16[32,7296]{1,0:T(8,128)(2,1)S(1)} collective-permute-done((bf16[32,7296]{1,0:T(8,128)(2,1)S(1)}, bf16[32,7296]{1,0:T(8,128)(2,1)S(1)}, u32[]{:S(2)}, u32[]{:S(2)}) %collective-permute-start.22) | collective-permute-done | bytes 466976 | tf_op jit(solution)/shard_map/ppermute | solution.py:39
  159.4 2.5 %expert_part.2 = (bf16[32,7168]{1,0:T(8,128)(2,1)S(1)}, bf16[32,7168]{1,0:T(8,128)(2,1)S(1)}, bf16[32,7168]{1,0:T(8,128)(2,1)S(1)}) custom-call(s32[5]{0:T(128)S(1)} %pad_add_fusion.where_ref, bf16[32,7296]{1,0:T(8,128)(2,1)S(1)} %get-tuple-element.47.refs_0_, bf16[32,7296]{1,0:T(8,128)(2,1)S(1)} %collective-permute-done.21.refs_1_, ...), custom_call_target="tpu_custom_call" | custom-call | flops 2113929216 | bytes 1376256 | tf_op jit(solution)/shard_map/expert_part/pallas_call | solution.py:396
  162.1 2.0 collective-permute-start.27
  164.1 2.6 %expert_part.3 = bf16[32,7168]{1,0:T(8,128)(2,1)S(1)} custom-call(s32[5]{0:T(128)S(1)} %pad_add_fusion.where_ref, bf16[32,7296]{1,0:T(8,128)(2,1)S(1)} %collective-permute-done.28.refs_0_, bf16[7168,512]{1,0:T(8,128)(2,1)S(1)} %get-tuple-element.50.refs_3_.refs_1_, bf16[256,7168]{1,0:T(8,128)(2,1)S(1)} %get-tuple-element.51.refs_4_.refs_2_), custom_call_target="tpu_custom_call" | custom-call | flops 704643072 | bytes 458752 | tf_op jit(solution)/shard_map/expert_part/pallas_call | solution.py:396
  166.9 3.7 %collective-permute-done.26.refs_1_ = bf16[32,7168]{1,0:T(8,128)(2,1)S(1)} collective-permute-done((bf16[32,7168]{1,0:T(8,128)(2,1)S(1)}, bf16[32,7168]{1,0:T(8,128)(2,1)S(1)}, u32[]{:S(2)}, u32[]{:S(2)}) %collective-permute-start.26) | collective-permute-done | bytes 458784 | tf_op jit(solution)/shard_map/ppermute | solution.py:39
  170.6 4.5 %collective-permute-done.27.refs_2_ = bf16[32,7168]{1,0:T(8,128)(2,1)S(1)} collective-permute-done((bf16[32,7168]{1,0:T(8,128)(2,1)S(1)}, bf16[32,7168]{1,0:T(8,128)(2,1)S(1)}, u32[]{:S(2)}, u32[]{:S(2)}) %collective-permute-start.27) | collective-permute-done | bytes 458784 | tf_op jit(solution)/shard_map/ppermute | solution.py:39
  175.1 1.8 collective-permute-done.29.refs_3_
  176.8 0.4 collect.1
  177.4 2.0 collective-permute-start.31
  179.4 1.0 collective-permute-start.32
  180.4 3.1 %collective-permute-start.33 = (bf16[32,1792]{1,0:T(8,128)(2,1)S(1)}, bf16[32,1792]{1,0:T(8,128)(2,1)S(1)}, u32[]{:S(2)}, u32[]{:S(2)}) collective-permute-start(bf16[32,1792]{1,0:T(8,128)(2,1)S(1)} %get-tuple-element.60), channel_id=1, source_target_pairs={{0,28},{2,30},{4,0},{6,2},{8,4},{10,6},{12,8},{14,10},{16,12},{18,... | collective-permute-start | bytes 344072 | tf_op jit(solution)/shard_map/ppermute | solution.py:43
  183.5 3.3 %collective-permute-done.32.ahead = bf16[32,1792]{1,0:T(8,128)(2,1)S(1)} collective-permute-done((bf16[32,1792]{1,0:T(8,128)(2,1)S(1)}, bf16[32,1792]{1,0:T(8,128)(2,1)S(1)}, u32[]{:S(2)}, u32[]{:S(2)}) %collective-permute-start.32) | collective-permute-done | bytes 114720 | tf_op jit(solution)/shard_map/ppermute | solution.py:43
  186.8 2.3 %collective-permute-done.33.behind = bf16[32,1792]{1,0:T(8,128)(2,1)S(1)} collective-permute-done((bf16[32,1792]{1,0:T(8,128)(2,1)S(1)}, bf16[32,1792]{1,0:T(8,128)(2,1)S(1)}, u32[]{:S(2)}, u32[]{:S(2)}) %collective-permute-start.33) | collective-permute-done | bytes 114720 | tf_op jit(solution)/shard_map/ppermute | solution.py:43
  189.3 4.7 %collective-permute-start.34 = (bf16[8,3584]{1,0:T(8,128)(2,1)S(1)}, bf16[8,3584]{1,0:T(8,128)(2,1)S(1)}, u32[]{:S(2)}, u32[]{:S(2)}) collective-permute-start(bf16[8,3584]{1,0:T(8,128)(2,1)S(1)} %get-tuple-element.62), channel_id=1, source_target_pairs={{0,8},{2,10},{4,12},{6,14},{8,16},{10,18},{12,20},{14,22},{16,24},... | collective-permute-start | bytes 172040 | tf_op jit(solution)/shard_map/ppermute | solution.py:43
  193.9 5.4 %collective-permute-start.35 = (bf16[8,3584]{1,0:T(8,128)(2,1)S(1)}, bf16[8,3584]{1,0:T(8,128)(2,1)S(1)}, u32[]{:S(2)}, u32[]{:S(2)}) collective-permute-start(bf16[8,3584]{1,0:T(8,128)(2,1)S(1)} %get-tuple-element.63), channel_id=1, source_target_pairs={{0,16},{2,18},{4,20},{6,22},{8,24},{10,26},{12,28},{14,30},{16,0},... | collective-permute-start | bytes 172040 | tf_op jit(solution)/shard_map/ppermute | solution.py:43
  199.3 2.5 %collective-permute-start.36 = (bf16[8,3584]{1,0:T(8,128)(2,1)S(1)}, bf16[8,3584]{1,0:T(8,128)(2,1)S(1)}, u32[]{:S(2)}, u32[]{:S(2)}) collective-permute-start(bf16[8,3584]{1,0:T(8,128)(2,1)S(1)} %get-tuple-element.64), channel_id=1, source_target_pairs={{0,24},{2,26},{4,28},{6,30},{8,0},{10,2},{12,4},{14,6},{16,8},{18,... | collective-permute-start | bytes 172040 | tf_op jit(solution)/shard_map/ppermute | solution.py:43
  201.8 5.0 %collective-permute-done.35 = bf16[8,3584]{1,0:T(8,128)(2,1)S(1)} collective-permute-done((bf16[8,3584]{1,0:T(8,128)(2,1)S(1)}, bf16[8,3584]{1,0:T(8,128)(2,1)S(1)}, u32[]{:S(2)}, u32[]{:S(2)}) %collective-permute-start.35) | collective-permute-done | bytes 57376 | tf_op jit(solution)/shard_map/ppermute | solution.py:43
  206.8 0.6 collective-permute-done.36
  207.6 0.7 reshape.101
  (82 shorter events, 2.1 us)
Async XLA Ops:
  1.2 34.3 %collective-permute-start.11 = (bf16[32,7680]{1,0:T(8,128)(2,1)S(1)}, bf16[32,7680]{1,0:T(8,128)(2,1)S(1)}, u32[]{:S(2)}, u32[]{:S(2)}) collective-permute-start(bf16[32,7680]{1,0:T(8,128)(2,1)S(1)} %get-tuple-element.35.refs_0_), channel_id=1, source_target_pairs={{0,96},{32,0},{64,32},{96,64},{1,97},{33,1},{65,33},{97,65},{2,98}... | collective-permute-start | bytes 1474568 | tf_op jit(solution)/shard_map/ppermute | solution.py:39
  1.7 33.9 %collective-permute-start.6 = (bf16[32,7680]{1,0:T(8,128)(2,1)S(1)}, bf16[32,7680]{1,0:T(8,128)(2,1)S(1)}, u32[]{:S(2)}, u32[]{:S(2)}) collective-permute-start(bf16[32,7680]{1,0:T(8,128)(2,1)S(1)} %get-tuple-element.35.refs_0_), channel_id=1, source_target_pairs={{0,1},{1,0},{2,3},{3,2},{4,5},{5,4},{6,7},{7,6},{8,9},{9,8},{10,11... | collective-permute-start | bytes 1474568 | tf_op jit(solution)/shard_map/ppermute | solution.py:47
  1.7 34.4 %collective-permute-start = (bf16[32,7680]{1,0:T(8,128)(2,1)S(1)}, bf16[32,7680]{1,0:T(8,128)(2,1)S(1)}, u32[]{:S(2)}, u32[]{:S(2)}) collective-permute-start(bf16[32,7680]{1,0:T(8,128)(2,1)S(1)} %get-tuple-element.35.refs_0_), channel_id=1, source_target_pairs={{0,32},{32,64},{64,96},{96,0},{1,33},{33,65},{65,97},{97,1},{2,34}... | collective-permute-start | bytes 1474568 | tf_op jit(solution)/shard_map/ppermute | solution.py:39
  3.4 36.0 %collective-permute-start.2 = (bf16[32,7680]{1,0:T(8,128)(2,1)S(1)}, bf16[32,7680]{1,0:T(8,128)(2,1)S(1)}, u32[]{:S(2)}, u32[]{:S(2)}) collective-permute-start(bf16[32,7680]{1,0:T(8,128)(2,1)S(1)} %get-tuple-element.36.refs_1_), channel_id=1, source_target_pairs={{0,96},{32,0},{64,32},{96,64},{1,97},{33,1},{65,33},{97,65},{2,98}... | collective-permute-start | bytes 1474568 | tf_op jit(solution)/shard_map/ppermute | solution.py:39
  3.8 35.6 %collective-permute-start.8 = (bf16[32,7680]{1,0:T(8,128)(2,1)S(1)}, bf16[32,7680]{1,0:T(8,128)(2,1)}, u32[]{:S(2)}, u32[]{:S(2)}) collective-permute-start(bf16[32,7680]{1,0:T(8,128)(2,1)S(1)} %get-tuple-element.36.refs_1_), channel_id=1, source_target_pairs={{0,32},{32,64},{64,96},{96,0},{1,33},{33,65},{65,97},{97,1},{2,34}... | collective-permute-start | bytes 1474568 | tf_op jit(solution)/shard_map/ppermute | solution.py:39
  12.6 41.2 %all-to-all-start = ((bf16[16,16,512]{2,1,0:T(8,128)(2,1)}), bf16[16,16,512]{2,1,0:T(8,128)(2,1)S(1)}, u32[]{:S(2)}, u32[]{:S(2)}) async-start(bf16[16,16,512]{2,1,0:T(8,128)(2,1)} %bitcast.5), calls=%async_computation | async-start | bytes 524288 | tf_op jit(solution)/shard_map/all_to_all | solution.py:495
  35.5 4.1 %collective-permute-start.7 = (bf16[32,7680]{1,0:T(8,128)(2,1)S(1)}, bf16[32,7680]{1,0:T(8,128)(2,1)S(1)}, u32[]{:S(2)}, u32[]{:S(2)}) collective-permute-start(bf16[32,7680]{1,0:T(8,128)(2,1)S(1)} %get-tuple-element.36.refs_1_), channel_id=1, source_target_pairs={{0,1},{1,0},{2,3},{3,2},{4,5},{5,4},{6,7},{7,6},{8,9},{9,8},{10,11... | collective-permute-start | bytes 1474568 | tf_op jit(solution)/shard_map/ppermute | solution.py:47
  35.6 5.2 %collective-permute-start.12 = (bf16[32,7680]{1,0:T(8,128)(2,1)S(1)}, bf16[32,7680]{1,0:T(8,128)(2,1)S(1)}, u32[]{:S(2)}, u32[]{:S(2)}) collective-permute-start(bf16[32,7680]{1,0:T(8,128)(2,1)S(1)} %collective-permute-done.11.refs_8_), channel_id=1, source_target_pairs={{0,1},{1,0},{2,3},{3,2},{4,5},{5,4},{6,7},{7,6},{8,9},{9,8},{10,11... | collective-permute-start | bytes 1474568 | tf_op jit(solution)/shard_map/ppermute | solution.py:47
  36.1 14.0 %collective-permute-start.1 = (bf16[32,7680]{1,0:T(8,128)(2,1)S(1)}, bf16[32,7680]{1,0:T(8,128)(2,1)}, u32[]{:S(2)}, u32[]{:S(2)}) collective-permute-start(bf16[32,7680]{1,0:T(8,128)(2,1)S(1)} %collective-permute-done.refs_4_), channel_id=1, source_target_pairs={{0,32},{32,64},{64,96},{96,0},{1,33},{33,65},{65,97},{97,1},{2,34}... | collective-permute-start | bytes 1474568 | tf_op jit(solution)/shard_map/ppermute | solution.py:39
  39.4 13.1 %collective-permute-start.3 = (bf16[32,7680]{1,0:T(8,128)(2,1)S(1)}, bf16[32,7680]{1,0:T(8,128)(2,1)}, u32[]{:S(2)}, u32[]{:S(2)}) collective-permute-start(bf16[32,7680]{1,0:T(8,128)(2,1)S(1)} %collective-permute-done.2.refs_9_), channel_id=1, source_target_pairs={{0,96},{32,0},{64,32},{96,64},{1,97},{33,1},{65,33},{97,65},{2,98}... | collective-permute-start | bytes 1474568 | tf_op jit(solution)/shard_map/ppermute | solution.py:39
  39.4 13.1 %collective-permute-start.9 = (bf16[32,7680]{1,0:T(8,128)(2,1)S(1)}, bf16[32,7680]{1,0:T(8,128)(2,1)S(1)}, u32[]{:S(2)}, u32[]{:S(2)}) collective-permute-start(bf16[32,7680]{1,0:T(8,128)(2,1)S(1)} %collective-permute-done.refs_4_), channel_id=1, source_target_pairs={{0,1},{1,0},{2,3},{3,2},{4,5},{5,4},{6,7},{7,6},{8,9},{9,8},{10,11... | collective-permute-start | bytes 1474568 | tf_op jit(solution)/shard_map/ppermute | solution.py:47
  39.5 0.8 copy-start
  40.3 13.5 %collective-permute-start.10 = (bf16[32,7680]{1,0:T(8,128)(2,1)}, bf16[32,7680]{1,0:T(8,128)(2,1)}, u32[]{:S(2)}, u32[]{:S(2)}) collective-permute-start(bf16[32,7680]{1,0:T(8,128)(2,1)} %collective-permute-done.8.refs_5_), channel_id=1, source_target_pairs={{0,1},{1,0},{2,3},{3,2},{4,5},{5,4},{6,7},{7,6},{8,9},{9,8},{10,11... | collective-permute-start | bytes 1474568 | tf_op jit(solution)/shard_map/ppermute | solution.py:47
  40.8 0.8 copy-start.2
  41.6 12.2 %collective-permute-start.13 = (bf16[32,7680]{1,0:T(8,128)(2,1)S(1)}, bf16[32,7680]{1,0:T(8,128)(2,1)}, u32[]{:S(2)}, u32[]{:S(2)}) collective-permute-start(bf16[32,7680]{1,0:T(8,128)(2,1)S(1)} %collective-permute-done.2.refs_9_), channel_id=1, source_target_pairs={{0,1},{1,0},{2,3},{3,2},{4,5},{5,4},{6,7},{7,6},{8,9},{9,8},{10,11... | collective-permute-start | bytes 1474568 | tf_op jit(solution)/shard_map/ppermute | solution.py:47
  50.2 9.5 %collective-permute-start.4 = (bf16[32,7680]{1,0:T(8,128)(2,1)}, bf16[32,7680]{1,0:T(8,128)(2,1)}, u32[]{:S(2)}, u32[]{:S(2)}) collective-permute-start(bf16[32,7680]{1,0:T(8,128)(2,1)} %collective-permute-done.1.refs_0_), channel_id=1, source_target_pairs={{0,1},{1,0},{2,3},{3,2},{4,5},{5,4},{6,7},{7,6},{8,9},{9,8},{10,11... | collective-permute-start | bytes 1474568 | tf_op jit(solution)/shard_map/ppermute | solution.py:47
  52.5 7.2 %collective-permute-start.5 = (bf16[32,7680]{1,0:T(8,128)(2,1)}, bf16[32,7680]{1,0:T(8,128)(2,1)}, u32[]{:S(2)}, u32[]{:S(2)}) collective-permute-start(bf16[32,7680]{1,0:T(8,128)(2,1)} %collective-permute-done.3.refs_1_), channel_id=1, source_target_pairs={{0,1},{1,0},{2,3},{3,2},{4,5},{5,4},{6,7},{7,6},{8,9},{9,8},{10,11... | collective-permute-start | bytes 1474568 | tf_op jit(solution)/shard_map/ppermute | solution.py:47
  52.5 0.8 copy-start.4
  53.3 85.9 %collective-permute-start.23 = (bf16[7168,128]{1,0:T(8,128)(2,1)}, bf16[7168,128]{1,0:T(8,128)(2,1)}, u32[]{:S(2)}, u32[]{:S(2)}) collective-permute-start(bf16[7168,128]{1,0:T(8,128)(2,1)} %gate_a.1), channel_id=1, source_target_pairs={{0,1},{1,0},{2,3},{3,2},{4,5},{5,4},{6,7},{7,6},{8,9},{9,8},{10,11... | collective-permute-start | bytes 5505032 | tf_op jit(solution)/shard_map/ppermute | solution.py:47
  53.8 1.0 copy-start.1
  54.8 1.0 copy-start.3
  55.9 1.0 copy-start.5
  59.6 4.7 %copy-start.10 = (s32[2,2,8]{2,1,0:T(2,128)S(1)}, s32[2,2,8]{2,1,0:T(2,128)}, u32[]{:S(2)}) copy-start(s32[2,2,8]{2,1,0:T(2,128)} %param.24) | copy-start | bytes 388
  59.6 11.3 %copy-start.8 = (s32[2,2,8]{2,1,0:T(2,128)S(1)}, s32[2,2,8]{2,1,0:T(2,128)}, u32[]{:S(2)}) copy-start(s32[2,2,8]{2,1,0:T(2,128)} %param.23) | copy-start | bytes 388
  59.6 32.6 %copy-start.9 = (bf16[7168]{0:T(1024)(128)(2,1)S(1)}, bf16[7168]{0:T(1024)(128)(2,1)}, u32[]{:S(2)}) copy-start(bf16[7168]{0:T(1024)(128)(2,1)} %param.21) | copy-start | bytes 43012
  59.6 32.7 %copy-start.7 = (bf16[2,2,7168]{2,1,0:T(2,128)(2,1)S(1)}, bf16[2,2,7168]{2,1,0:T(2,128)(2,1)}, u32[]{:S(2)}) copy-start(bf16[2,2,7168]{2,1,0:T(2,128)(2,1)} %param.18) | copy-start | bytes 172036
  62.1 30.4 %copy-start.6 = (bf16[7168,16]{0,1:T(8,128)(2,1)S(1)}, bf16[7168,16]{0,1:T(8,128)(2,1)}, u32[]{:S(2)}) copy-start(bf16[7168,16]{0,1:T(8,128)(2,1)} %param.22) | copy-start | bytes 688132
  62.1 30.6 %copy-start.11 = (bf16[128,7168]{1,0:T(8,128)(2,1)S(1)}, bf16[128,7168]{1,0:T(8,128)(2,1)}, u32[]{:S(2)}) copy-start(bf16[128,7168]{1,0:T(8,128)(2,1)} %down_a.1) | copy-start | bytes 5505028
  62.1 16.8 %collective-permute-start.14 = (bf16[32,3584]{1,0:T(8,128)(2,1)S(1)}, bf16[32,3584]{1,0:T(8,128)(2,1)S(1)}, u32[]{:S(2)}, u32[]{:S(2)}) collective-permute-start(bf16[32,3584]{1,0:T(8,128)(2,1)S(1)} %get-tuple-element.38), channel_id=1, source_target_pairs={{0,2},{2,4},{4,6},{6,8},{8,10},{10,12},{12,14},{14,16},{16,18},{18... | collective-permute-start | bytes 688136 | tf_op jit(solution)/shard_map/ppermute | solution.py:43
  63.7 15.2 %collective-permute-start.15 = (bf16[32,3584]{1,0:T(8,128)(2,1)S(1)}, bf16[32,3584]{1,0:T(8,128)(2,1)S(1)}, u32[]{:S(2)}, u32[]{:S(2)}) collective-permute-start(bf16[32,3584]{1,0:T(8,128)(2,1)S(1)} %get-tuple-element.39), channel_id=1, source_target_pairs={{0,30},{2,0},{4,2},{6,4},{8,6},{10,8},{12,10},{14,12},{16,14},{18,... | collective-permute-start | bytes 688136 | tf_op jit(solution)/shard_map/ppermute | solution.py:43
  64.2 14.7 %collective-permute-start.16 = (bf16[32,1792]{1,0:T(8,128)(2,1)S(1)}, bf16[32,1792]{1,0:T(8,128)(2,1)S(1)}, u32[]{:S(2)}, u32[]{:S(2)}) collective-permute-start(bf16[32,1792]{1,0:T(8,128)(2,1)S(1)} %get-tuple-element.40), channel_id=1, source_target_pairs={{0,4},{2,6},{4,8},{6,10},{8,12},{10,14},{12,16},{14,18},{16,20},{1... | collective-permute-start | bytes 344072 | tf_op jit(solution)/shard_map/ppermute | solution.py:43
  67.4 11.5 %collective-permute-start.17 = (bf16[32,1792]{1,0:T(8,128)(2,1)S(1)}, bf16[32,1792]{1,0:T(8,128)(2,1)S(1)}, u32[]{:S(2)}, u32[]{:S(2)}) collective-permute-start(bf16[32,1792]{1,0:T(8,128)(2,1)S(1)} %get-tuple-element.41), channel_id=1, source_target_pairs={{0,28},{2,30},{4,0},{6,2},{8,4},{10,6},{12,8},{14,10},{16,12},{18,... | collective-permute-start | bytes 344072 | tf_op jit(solution)/shard_map/ppermute | solution.py:43
  78.9 62.3 %collective-permute-start.24 = (bf16[7168,128]{1,0:T(8,128)(2,1)}, bf16[7168,128]{1,0:T(8,128)(2,1)}, u32[]{:S(2)}, u32[]{:S(2)}) collective-permute-start(bf16[7168,128]{1,0:T(8,128)(2,1)} %up_a.1), channel_id=1, source_target_pairs={{0,1},{1,0},{2,3},{3,2},{4,5},{5,4},{6,7},{7,6},{8,9},{9,8},{10,11... | collective-permute-start | bytes 5505032 | tf_op jit(solution)/shard_map/ppermute | solution.py:47
  79.0 13.6 %collective-permute-start.18 = (bf16[8,3584]{1,0:T(8,128)(2,1)S(1)}, bf16[8,3584]{1,0:T(8,128)(2,1)S(1)}, u32[]{:S(2)}, u32[]{:S(2)}) collective-permute-start(bf16[8,3584]{1,0:T(8,128)(2,1)S(1)} %get-tuple-element.43), channel_id=1, source_target_pairs={{0,8},{2,10},{4,12},{6,14},{8,16},{10,18},{12,20},{14,22},{16,24},... | collective-permute-start | bytes 172040 | tf_op jit(solution)/shard_map/ppermute | solution.py:43
  81.5 15.0 %collective-permute-start.19 = (bf16[8,3584]{1,0:T(8,128)(2,1)S(1)}, bf16[8,3584]{1,0:T(8,128)(2,1)S(1)}, u32[]{:S(2)}, u32[]{:S(2)}) collective-permute-start(bf16[8,3584]{1,0:T(8,128)(2,1)S(1)} %get-tuple-element.44), channel_id=1, source_target_pairs={{0,16},{2,18},{4,20},{6,22},{8,24},{10,26},{12,28},{14,30},{16,0},... | collective-permute-start | bytes 172040 | tf_op jit(solution)/shard_map/ppermute | solution.py:43
  86.9 12.1 %collective-permute-start.20 = (bf16[8,3584]{1,0:T(8,128)(2,1)S(1)}, bf16[8,3584]{1,0:T(8,128)(2,1)S(1)}, u32[]{:S(2)}, u32[]{:S(2)}) collective-permute-start(bf16[8,3584]{1,0:T(8,128)(2,1)S(1)} %get-tuple-element.45), channel_id=1, source_target_pairs={{0,24},{2,26},{4,28},{6,30},{8,0},{10,2},{12,4},{14,6},{16,8},{18,... | collective-permute-start | bytes 172040 | tf_op jit(solution)/shard_map/ppermute | solution.py:43
  92.7 48.5 %collective-permute-start.25 = (bf16[128,7168]{1,0:T(8,128)(2,1)S(1)}, bf16[128,7168]{1,0:T(8,128)(2,1)}, u32[]{:S(2)}, u32[]{:S(2)}) collective-permute-start(bf16[128,7168]{1,0:T(8,128)(2,1)S(1)} %copy-done.11), channel_id=1, source_target_pairs={{0,1},{1,0},{2,3},{3,2},{4,5},{5,4},{6,7},{7,6},{8,9},{9,8},{10,11... | collective-permute-start | bytes 5505032 | tf_op jit(solution)/shard_map/ppermute | solution.py:47
  136.4 11.6 %collective-permute-start.21 = (bf16[32,7296]{1,0:T(8,128)(2,1)S(1)}, bf16[32,7296]{1,0:T(8,128)(2,1)S(1)}, u32[]{:S(2)}, u32[]{:S(2)}) collective-permute-start(bf16[32,7296]{1,0:T(8,128)(2,1)S(1)} %get-tuple-element.48), channel_id=1, source_target_pairs={{0,96},{32,0},{64,32},{96,64},{1,97},{33,1},{65,33},{97,65},{2,98}... | collective-permute-start | bytes 1400840 | tf_op jit(solution)/shard_map/ppermute | solution.py:39
  137.4 22.0 %collective-permute-start.22 = (bf16[32,7296]{1,0:T(8,128)(2,1)S(1)}, bf16[32,7296]{1,0:T(8,128)(2,1)S(1)}, u32[]{:S(2)}, u32[]{:S(2)}) collective-permute-start(bf16[32,7296]{1,0:T(8,128)(2,1)S(1)} %get-tuple-element.49), channel_id=1, source_target_pairs={{0,32},{32,64},{64,96},{96,0},{1,33},{33,65},{65,97},{97,1},{2,34}... | collective-permute-start | bytes 1400840 | tf_op jit(solution)/shard_map/ppermute | solution.py:39
  139.2 24.9 %collective-permute-start.28 = (bf16[32,7296]{1,0:T(8,128)(2,1)S(1)}, bf16[32,7296]{1,0:T(8,128)(2,1)S(1)}, u32[]{:S(2)}, u32[]{:S(2)}) collective-permute-start(bf16[32,7296]{1,0:T(8,128)(2,1)S(1)} %get-tuple-element.55), channel_id=1, source_target_pairs={{0,64},{32,96},{64,0},{96,32},{1,65},{33,97},{65,1},{97,33},{2,66}... | collective-permute-start | bytes 1400840 | tf_op jit(solution)/shard_map/ppermute | solution.py:39
  162.0 8.6 %collective-permute-start.26 = (bf16[32,7168]{1,0:T(8,128)(2,1)S(1)}, bf16[32,7168]{1,0:T(8,128)(2,1)S(1)}, u32[]{:S(2)}, u32[]{:S(2)}) collective-permute-start(bf16[32,7168]{1,0:T(8,128)(2,1)S(1)} %get-tuple-element.53), channel_id=1, source_target_pairs={{0,32},{32,64},{64,96},{96,0},{1,33},{33,65},{65,97},{97,1},{2,34}... | collective-permute-start | bytes 1376264 | tf_op jit(solution)/shard_map/ppermute | solution.py:39
  162.1 12.9 %collective-permute-start.27 = (bf16[32,7168]{1,0:T(8,128)(2,1)S(1)}, bf16[32,7168]{1,0:T(8,128)(2,1)S(1)}, u32[]{:S(2)}, u32[]{:S(2)}) collective-permute-start(bf16[32,7168]{1,0:T(8,128)(2,1)S(1)} %get-tuple-element.54), channel_id=1, source_target_pairs={{0,96},{32,0},{64,32},{96,64},{1,97},{33,1},{65,33},{97,65},{2,98}... | collective-permute-start | bytes 1376264 | tf_op jit(solution)/shard_map/ppermute | solution.py:39
  166.7 10.1 %collective-permute-start.29 = (bf16[32,7168]{1,0:T(8,128)(2,1)S(1)}, bf16[32,7168]{1,0:T(8,128)(2,1)S(1)}, u32[]{:S(2)}, u32[]{:S(2)}) collective-permute-start(bf16[32,7168]{1,0:T(8,128)(2,1)S(1)} %expert_part.3), channel_id=1, source_target_pairs={{0,64},{32,96},{64,0},{96,32},{1,65},{33,97},{65,1},{97,33},{2,66}... | collective-permute-start | bytes 1376264 | tf_op jit(solution)/shard_map/ppermute | solution.py:39
  177.2 11.9 %collective-permute-start.30 = (bf16[32,3584]{1,0:T(8,128)(2,1)S(1)}, bf16[32,3584]{1,0:T(8,128)(2,1)S(1)}, u32[]{:S(2)}, u32[]{:S(2)}) collective-permute-start(bf16[32,3584]{1,0:T(8,128)(2,1)S(1)} %get-tuple-element.57), channel_id=1, source_target_pairs={{0,2},{2,4},{4,6},{6,8},{8,10},{10,12},{12,14},{14,16},{16,18},{18... | collective-permute-start | bytes 688136 | tf_op jit(solution)/shard_map/ppermute | solution.py:43
  177.4 11.8 %collective-permute-start.31 = (bf16[32,3584]{1,0:T(8,128)(2,1)S(1)}, bf16[32,3584]{1,0:T(8,128)(2,1)S(1)}, u32[]{:S(2)}, u32[]{:S(2)}) collective-permute-start(bf16[32,3584]{1,0:T(8,128)(2,1)S(1)} %get-tuple-element.58), channel_id=1, source_target_pairs={{0,30},{2,0},{4,2},{6,4},{8,6},{10,8},{12,10},{14,12},{16,14},{18,... | collective-permute-start | bytes 688136 | tf_op jit(solution)/shard_map/ppermute | solution.py:43
  179.4 7.5 %collective-permute-start.32 = (bf16[32,1792]{1,0:T(8,128)(2,1)S(1)}, bf16[32,1792]{1,0:T(8,128)(2,1)S(1)}, u32[]{:S(2)}, u32[]{:S(2)}) collective-permute-start(bf16[32,1792]{1,0:T(8,128)(2,1)S(1)} %get-tuple-element.59), channel_id=1, source_target_pairs={{0,4},{2,6},{4,8},{6,10},{8,12},{10,14},{12,16},{14,18},{16,20},{1... | collective-permute-start | bytes 344072 | tf_op jit(solution)/shard_map/ppermute | solution.py:43
  180.4 8.7 %collective-permute-start.33 = (bf16[32,1792]{1,0:T(8,128)(2,1)S(1)}, bf16[32,1792]{1,0:T(8,128)(2,1)S(1)}, u32[]{:S(2)}, u32[]{:S(2)}) collective-permute-start(bf16[32,1792]{1,0:T(8,128)(2,1)S(1)} %get-tuple-element.60), channel_id=1, source_target_pairs={{0,28},{2,30},{4,0},{6,2},{8,4},{10,6},{12,8},{14,10},{16,12},{18,... | collective-permute-start | bytes 344072 | tf_op jit(solution)/shard_map/ppermute | solution.py:43
  189.3 12.6 %collective-permute-start.34 = (bf16[8,3584]{1,0:T(8,128)(2,1)S(1)}, bf16[8,3584]{1,0:T(8,128)(2,1)S(1)}, u32[]{:S(2)}, u32[]{:S(2)}) collective-permute-start(bf16[8,3584]{1,0:T(8,128)(2,1)S(1)} %get-tuple-element.62), channel_id=1, source_target_pairs={{0,8},{2,10},{4,12},{6,14},{8,16},{10,18},{12,20},{14,22},{16,24},... | collective-permute-start | bytes 172040 | tf_op jit(solution)/shard_map/ppermute | solution.py:43
  193.9 12.9 %collective-permute-start.35 = (bf16[8,3584]{1,0:T(8,128)(2,1)S(1)}, bf16[8,3584]{1,0:T(8,128)(2,1)S(1)}, u32[]{:S(2)}, u32[]{:S(2)}) collective-permute-start(bf16[8,3584]{1,0:T(8,128)(2,1)S(1)} %get-tuple-element.63), channel_id=1, source_target_pairs={{0,16},{2,18},{4,20},{6,22},{8,24},{10,26},{12,28},{14,30},{16,0},... | collective-permute-start | bytes 172040 | tf_op jit(solution)/shard_map/ppermute | solution.py:43
  199.3 8.1 %collective-permute-start.36 = (bf16[8,3584]{1,0:T(8,128)(2,1)S(1)}, bf16[8,3584]{1,0:T(8,128)(2,1)S(1)}, u32[]{:S(2)}, u32[]{:S(2)}) collective-permute-start(bf16[8,3584]{1,0:T(8,128)(2,1)S(1)} %get-tuple-element.64), channel_id=1, source_target_pairs={{0,24},{2,26},{4,28},{6,30},{8,0},{10,2},{12,4},{14,6},{16,8},{18,... | collective-permute-start | bytes 172040 | tf_op jit(solution)/shard_map/ppermute | solution.py:43

commit v5 on v4

--- a/solution.py
+++ b/solution.py
@@ -452,15 +452,14 @@
 
 
 def reduce_z(own, right, left, ahead, behind):
+    ahead = shift_z(ahead, 2)
+    behind = shift_z(behind, -2)
     right = shift_z(right, 1)
     left = shift_z(left, -1)
-    ahead = shift_z(ahead, 2)
-    behind = shift_z(behind, -2)
-    out, *sent = merge(own, right, left, ahead, behind)
-    for k, rows in enumerate(sent):
-        step = NEAR * (k + 1)
-        out = out + shift_z(rows, step if step <= RING // 2 else step - RING).astype(f32)
-    return out
+    first, *sent = merge(own, right, left, ahead, behind)
+    middle = shift_z(sent[1], 2 * NEAR)
+    others = [middle, shift_z(sent[0], NEAR), shift_z(sent[2], -NEAR)]
+    return first + sum(rows.astype(f32) for rows in others)
 
 
 def layer(
@@ -497,11 +496,12 @@
     )
     top_far = shift_x(top_left, 1)
     low_far = shift_x(low_right, -1)
-    near = [tops, lows, swap_core(tops), swap_core(lows)]
-    for pair in ((top_left, low_left), (top_right, low_right)):
+    near = []
+    for pair in ((tops, lows), (top_left, low_left), (top_right, low_right)):
         near += [*pair, *map(swap_core, pair)]
     beyond = [top_far, low_far, swap_core(top_far), swap_core(low_far)]
-    weights = stage((w_gate, swap_core(w_gate), w_up, swap_core(w_up), w_down, swap_core(w_down)))
+    others = [swap_core(w) for w in (w_gate, w_up, w_down)]
+    weights = stage((w_gate, others[0], w_up, others[1], w_down, others[2]))
     arrived = arrived.reshape(RING * nx * tok, LAT)
     most = attend_part(where, nx, arrived, near, tok, 0, None)
     attended = reduce_z(*attend_part(where, nx, arrived, beyond, tok, nx - 1, most))

time: 212 us -> 211 us (level)
  waiting for transfers between devices: 60 us -> 63.8 us
  starting transfers between devices: 80.7 us -> 77.6 us
    ppermute x14, starting transfers between devices: 40.8 us -> 36.7 us  [shift_z(): return lax.ppermute(a, ZAX, [(i, (i + step) % RING) for i in range(RING)])]
    ppermute x14, waiting for transfers between devices: 25.3 us -> 29.1 us  [shift_z(): return lax.ppermute(a, ZAX, [(i, (i + step) % RING) for i in range(RING)])]
  transfers between devices with their start and end apart: 38 -> 38, of which waited for: 14 -> 13; matrix products, arithmetic and copies ran while one was open for 1% -> 1% of each run, Pallas kernels for 11% -> 11%
where the time goes in v5:
time: 211 us; the launch traced here: 208 us
  starting transfers between devices  77.6 us (37%)
  waiting for transfers between devices  63.8 us (30%)
  blocking collectives  34.1 us (16%)
  Pallas kernels  23.7 us (11%)
  local copies, waits for them, and re-layouts  6.91 us (3%)
    ppermute x14, starting transfers between devices, shift_z(): return lax.ppermute(a, ZAX, [(i, (i + step) % RING) for i in range(RING)])  36.7 us
    ppermute x12, waiting for transfers between devices, shift_x(): return lax.ppermute(a, 'x', [(i, (i + step) % n) for i in range(n)])  34.6 us
    all_gather x1, blocking collectives, layer(): ring = lax.all_gather(payload, ZAX, axis=0, tiled=True)  34.1 us
    ppermute x14, waiting for transfers between devices, shift_z(): return lax.ppermute(a, ZAX, [(i, (i + step) % RING) for i in range(RING)])  29.1 us
    all_to_all x1, starting transfers between devices, layer(): lax.all_to_all(outgoing.reshape(RING, nx * tok, LAT), ZAX, split_axis=0,...  22.9 us
    ppermute x12, starting transfers between devices, shift_x(): return lax.ppermute(a, 'x', [(i, (i + step) % n) for i in range(n)])  16.2 us
    pallas_call x1, Pallas kernels, context_rows(): pl.pallas_call(functools.partial(context_kernel, nx), grid=(seqs,), out_s...  5.91 us
    unnamed x24, local copies, waits for them, and re-layouts  5.49 us
  transfers between devices with their start and end apart: 38, of which 13 were waited for; matrix products, arithmetic and copies ran while one was open for 1% of the time, Pallas kernels for 11%

profile of v5, /device:TPU:164, one launch (start us, length us, event | category | flops | bytes accessed | tf_op | source)
XLA Modules:
  0.0 208.4 jit_solution(49066805021059963)
XLA Ops:
  0.0 1.2 pack.1
  1.2 0.5 collective-permute-start.11
  1.7 1.6 collective-permute-start
  3.4 0.4 collective-permute-start.2
  3.8 2.1 %collective-permute-start.8 = (bf16[32,7680]{1,0:T(8,128)(2,1)S(1)}, bf16[32,7680]{1,0:T(8,128)(2,1)}, u32[]{:S(2)}, u32[]{:S(2)}) collective-permute-start(bf16[32,7680]{1,0:T(8,128)(2,1)S(1)} %get-tuple-element.36.refs_1_), channel_id=1, source_target_pairs={{0,32},{32,64},{64,96},{96,0},{1,33},{33,65},{65,97},{97,1},{2,34}... | collective-permute-start | bytes 1474568 | tf_op jit(solution)/shard_map/ppermute | solution.py:39
  5.9 0.7 pad_add_fusion.where_ref
  6.6 5.9 %context_rows.1 = bf16[256,512]{1,0:T(8,128)(2,1)} custom-call(s32[5]{0:T(128)S(1)} %pad_add_fusion.where_ref, bf16[2,576,2048]{2,1,0:T(8,128)(2,1)} %bitcast.33, bf16[2,2,64,576]{3,2,1,0:T(8,128)(2,1)} %queries.1, bf16[2,2,576]{2,1,0:T(2,128)(2,1)} %new.1), custom_call_target="tpu_custom_call" | custom-call | flops 1140850688 | bytes 4718592 | tf_op jit(solution)/shard_map/context_rows/pallas_call | solution.py:146
  12.6 22.9 %all-to-all-start = ((bf16[16,16,512]{2,1,0:T(8,128)(2,1)}), bf16[16,16,512]{2,1,0:T(8,128)(2,1)S(1)}, u32[]{:S(2)}, u32[]{:S(2)}) async-start(bf16[16,16,512]{2,1,0:T(8,128)(2,1)} %bitcast.5), calls=%async_computation | async-start | bytes 524288 | tf_op jit(solution)/shard_map/all_to_all | solution.py:494
  35.5 0.1 collective-permute-start.7
  35.6 0.5 collective-permute-start.12
  36.1 3.2 %collective-permute-start.1 = (bf16[32,7680]{1,0:T(8,128)(2,1)S(1)}, bf16[32,7680]{1,0:T(8,128)(2,1)}, u32[]{:S(2)}, u32[]{:S(2)}) collective-permute-start(bf16[32,7680]{1,0:T(8,128)(2,1)S(1)} %collective-permute-done.refs_4_), channel_id=1, source_target_pairs={{0,32},{32,64},{64,96},{96,0},{1,33},{33,65},{65,97},{97,1},{2,34}... | collective-permute-start | bytes 1474568 | tf_op jit(solution)/shard_map/ppermute | solution.py:39
  39.4 0.1 collective-permute-start.9
  39.5 0.8 copy-done
  40.3 0.5 collective-permute-start.10
  40.8 0.8 copy-done.2
  41.6 8.5 %collective-permute-done.1.refs_0_ = bf16[32,7680]{1,0:T(8,128)(2,1)} collective-permute-done((bf16[32,7680]{1,0:T(8,128)(2,1)S(1)}, bf16[32,7680]{1,0:T(8,128)(2,1)}, u32[]{:S(2)}, u32[]{:S(2)}) %collective-permute-start.1) | collective-permute-done | bytes 491552 | tf_op jit(solution)/shard_map/ppermute | solution.py:39
  50.2 2.3 %collective-permute-done.3.refs_1_ = bf16[32,7680]{1,0:T(8,128)(2,1)} collective-permute-done((bf16[32,7680]{1,0:T(8,128)(2,1)S(1)}, bf16[32,7680]{1,0:T(8,128)(2,1)}, u32[]{:S(2)}, u32[]{:S(2)}) %collective-permute-start.3) | collective-permute-done | bytes 491552 | tf_op jit(solution)/shard_map/ppermute | solution.py:39
  52.5 0.8 copy-done.4
  53.3 0.5 collective-permute-start.23
  53.8 1.0 copy-done.1
  54.8 1.0 copy-done.3
  55.9 1.0 copy-done.5
  56.9 2.7 %attend_part.2.refs_4_ = f32[128,3584]{1,0:T(8,128)S(1)} custom-call(s32[5]{0:T(128)S(1)} %pad_add_fusion.where_ref, bf16[256,512]{1,0:T(8,128)(2,1)S(1)} %bitcast.31, bf16[32,7680]{1,0:T(8,128)(2,1)S(1)} %get-tuple-element.35.refs_0_, bf16[32,7680]{1,0:T(8,128)(2,1)S(1)} %get-tuple-element.36.refs_1_, bf16[32,7680]{1,0:T(8,128)(2,1)S(1)} %collective-permute-done.6.refs_2_, ...), custom_call_target="tpu_custom_call" | custom-call | flops 1409286144 | bytes 5505024 | tf_op jit(solution)/shard_map/attend_part/pallas_call | solution.py:260
  59.7 2.4 %attend_part.3 = (f32[32,3584]{1,0:T(8,128)S(1)}, bf16[32,3584]{1,0:T(8,128)(2,1)S(1)}, bf16[32,3584]{1,0:T(8,128)(2,1)S(1)}, bf16[32,1792]{1,0:T(8,128)(2,1)S(1)}, bf16[32,1792]{1,0:T(8,128)(2,1)S(1)}) custom-call(s32[5]{0:T(128)S(1)} %pad_add_fusion.where_ref, bf16[256,512]{1,0:T(8,128)(2,1)S(1)} %bitcast.32, ...), custom_call_target="tpu_custom_call" | custom-call | flops 469762048 | bytes 1835008 | tf_op jit(solution)/shard_map/attend_part/pallas_call | solution.py:260
  62.1 1.6 collective-permute-start.14
  63.7 0.6 collective-permute-start.15
  64.2 3.1 %collective-permute-start.16 = (bf16[32,1792]{1,0:T(8,128)(2,1)S(1)}, bf16[32,1792]{1,0:T(8,128)(2,1)S(1)}, u32[]{:S(2)}, u32[]{:S(2)}) collective-permute-start(bf16[32,1792]{1,0:T(8,128)(2,1)S(1)} %get-tuple-element.40), channel_id=1, source_target_pairs={{0,4},{2,6},{4,8},{6,10},{8,12},{10,14},{12,16},{14,18},{16,20},{1... | collective-permute-start | bytes 344072 | tf_op jit(solution)/shard_map/ppermute | solution.py:43
  67.4 3.6 %collective-permute-start.17 = (bf16[32,1792]{1,0:T(8,128)(2,1)S(1)}, bf16[32,1792]{1,0:T(8,128)(2,1)S(1)}, u32[]{:S(2)}, u32[]{:S(2)}) collective-permute-start(bf16[32,1792]{1,0:T(8,128)(2,1)S(1)} %get-tuple-element.41), channel_id=1, source_target_pairs={{0,28},{2,30},{4,0},{6,2},{8,4},{10,6},{12,8},{14,10},{16,12},{18,... | collective-permute-start | bytes 344072 | tf_op jit(solution)/shard_map/ppermute | solution.py:43
  71.0 7.9 %collective-permute-done.16.ahead = bf16[32,1792]{1,0:T(8,128)(2,1)S(1)} collective-permute-done((bf16[32,1792]{1,0:T(8,128)(2,1)S(1)}, bf16[32,1792]{1,0:T(8,128)(2,1)S(1)}, u32[]{:S(2)}, u32[]{:S(2)}) %collective-permute-start.16) | collective-permute-done | bytes 114720 | tf_op jit(solution)/shard_map/ppermute | solution.py:43
  79.0 7.3 %collective-permute-start.18 = (bf16[8,3584]{1,0:T(8,128)(2,1)S(1)}, bf16[8,3584]{1,0:T(8,128)(2,1)S(1)}, u32[]{:S(2)}, u32[]{:S(2)}) collective-permute-start(bf16[8,3584]{1,0:T(8,128)(2,1)S(1)} %get-tuple-element.43), channel_id=1, source_target_pairs={{0,16},{2,18},{4,20},{6,22},{8,24},{10,26},{12,28},{14,30},{16,0},... | collective-permute-start | bytes 172040 | tf_op jit(solution)/shard_map/ppermute | solution.py:43
  86.3 0.6 collective-permute-start.19
  86.9 5.4 %collective-permute-start.20 = (bf16[8,3584]{1,0:T(8,128)(2,1)S(1)}, bf16[8,3584]{1,0:T(8,128)(2,1)S(1)}, u32[]{:S(2)}, u32[]{:S(2)}) collective-permute-start(bf16[8,3584]{1,0:T(8,128)(2,1)S(1)} %get-tuple-element.45), channel_id=1, source_target_pairs={{0,24},{2,26},{4,28},{6,30},{8,0},{10,2},{12,4},{14,6},{16,8},{18,... | collective-permute-start | bytes 172040 | tf_op jit(solution)/shard_map/ppermute | solution.py:43
  92.5 0.2 reshape.98
  92.7 2.8 %collective-permute-done.18 = bf16[8,3584]{1,0:T(8,128)(2,1)S(1)} collective-permute-done((bf16[8,3584]{1,0:T(8,128)(2,1)S(1)}, bf16[8,3584]{1,0:T(8,128)(2,1)S(1)}, u32[]{:S(2)}, u32[]{:S(2)}) %collective-permute-start.18) | collective-permute-done | bytes 57376 | tf_op jit(solution)/shard_map/ppermute | solution.py:43
  95.5 1.9 collective-permute-done.19
  97.4 0.2 multiply_reduce_fusion
  97.9 0.4 fusion
  98.3 0.2 select_reduce_fusion.1
  98.4 0.1 fusion.6
  98.9 34.1 %all_gather.3.tokens = bf16[128,3712]{1,0:T(8,128)(2,1)S(1)} all-gather(bf16[8,3712]{1,0:T(8,128)(2,1)S(1)} %pad_maximum_fusion), channel_id=1, replica_groups=mesh['rep'=2,'x'=4,'zb'=4,'j'=4,'c'=2] {'zb','j'}, dimensions={0}, use_global_device_ids=true | all-gather | bytes 1009664 | tf_op jit(solution)/shard_map/all_gather | solution.py:537
  133.0 1.3 dispatch.1
  134.3 0.9 collective-permute-start.21
  135.2 1.7 collective-permute-start.22
  136.9 3.5 %collective-permute-start.28 = (bf16[32,7296]{1,0:T(8,128)(2,1)S(1)}, bf16[32,7296]{1,0:T(8,128)(2,1)S(1)}, u32[]{:S(2)}, u32[]{:S(2)}) collective-permute-start(bf16[32,7296]{1,0:T(8,128)(2,1)S(1)} %get-tuple-element.55), channel_id=1, source_target_pairs={{0,64},{32,96},{64,0},{96,32},{1,65},{33,97},{65,1},{97,33},{2,66}... | collective-permute-start | bytes 1400840 | tf_op jit(solution)/shard_map/ppermute | solution.py:39
  140.3 4.3 %stage.1 = (bf16[7168,512]{1,0:T(8,128)(2,1)S(1)}, bf16[256,7168]{1,0:T(8,128)(2,1)S(1)}) custom-call(bf16[7168,128]{1,0:T(8,128)(2,1)} %gate_a.1, bf16[7168,128]{1,0:T(8,128)(2,1)} %collective-permute-done.23.gate_b, bf16[7168,128]{1,0:T(8,128)(2,1)} %up_a.1, bf16[7168,128]{1,0:T(8,128)(2,1)} %collective-permute-done.24.up_b, bf16[128,7168]{1,0:T(8,128)(2,1)} %down_a.1, ...), custom_call_target="tpu_custom_call" | custom-call | flops 3670016000 | bytes 11010048 | tf_op jit(solution)/shard_map/stage/pallas_call | solution.py:349
  144.6 1.2 collective-permute-done.21.refs_1_
  145.8 12.6 %collective-permute-done.22.refs_2_ = bf16[32,7296]{1,0:T(8,128)(2,1)S(1)} collective-permute-done((bf16[32,7296]{1,0:T(8,128)(2,1)S(1)}, bf16[32,7296]{1,0:T(8,128)(2,1)S(1)}, u32[]{:S(2)}, u32[]{:S(2)}) %collective-permute-start.22) | collective-permute-done | bytes 466976 | tf_op jit(solution)/shard_map/ppermute | solution.py:39
  158.4 2.5 %expert_part.2 = (bf16[32,7168]{1,0:T(8,128)(2,1)S(1)}, bf16[32,7168]{1,0:T(8,128)(2,1)S(1)}, bf16[32,7168]{1,0:T(8,128)(2,1)S(1)}) custom-call(s32[5]{0:T(128)S(1)} %pad_add_fusion.where_ref, bf16[32,7296]{1,0:T(8,128)(2,1)S(1)} %get-tuple-element.47.refs_0_, bf16[32,7296]{1,0:T(8,128)(2,1)S(1)} %collective-permute-done.21.refs_1_, ...), custom_call_target="tpu_custom_call" | custom-call | flops 2113929216 | bytes 1376256 | tf_op jit(solution)/shard_map/expert_part/pallas_call | solution.py:396
  161.1 2.0 collective-permute-start.27
  163.1 2.6 %expert_part.3 = bf16[32,7168]{1,0:T(8,128)(2,1)S(1)} custom-call(s32[5]{0:T(128)S(1)} %pad_add_fusion.where_ref, bf16[32,7296]{1,0:T(8,128)(2,1)S(1)} %collective-permute-done.28.refs_0_, bf16[7168,512]{1,0:T(8,128)(2,1)S(1)} %get-tuple-element.50.refs_3_.refs_1_, bf16[256,7168]{1,0:T(8,128)(2,1)S(1)} %get-tuple-element.51.refs_4_.refs_2_), custom_call_target="tpu_custom_call" | custom-call | flops 704643072 | bytes 458752 | tf_op jit(solution)/shard_map/expert_part/pallas_call | solution.py:396
  165.9 3.7 %collective-permute-done.26.refs_1_ = bf16[32,7168]{1,0:T(8,128)(2,1)S(1)} collective-permute-done((bf16[32,7168]{1,0:T(8,128)(2,1)S(1)}, bf16[32,7168]{1,0:T(8,128)(2,1)S(1)}, u32[]{:S(2)}, u32[]{:S(2)}) %collective-permute-start.26) | collective-permute-done | bytes 458784 | tf_op jit(solution)/shard_map/ppermute | solution.py:39
  169.6 4.5 %collective-permute-done.27.refs_2_ = bf16[32,7168]{1,0:T(8,128)(2,1)S(1)} collective-permute-done((bf16[32,7168]{1,0:T(8,128)(2,1)S(1)}, bf16[32,7168]{1,0:T(8,128)(2,1)S(1)}, u32[]{:S(2)}, u32[]{:S(2)}) %collective-permute-start.27) | collective-permute-done | bytes 458784 | tf_op jit(solution)/shard_map/ppermute | solution.py:39
  174.0 1.8 collective-permute-done.29.refs_3_
  175.8 0.4 collect.1
  176.2 0.1 collective-permute-start.30
  176.4 2.0 collective-permute-start.31
  178.4 0.4 collective-permute-start.32
  178.8 3.7 %collective-permute-start.33 = (bf16[32,1792]{1,0:T(8,128)(2,1)S(1)}, bf16[32,1792]{1,0:T(8,128)(2,1)S(1)}, u32[]{:S(2)}, u32[]{:S(2)}) collective-permute-start(bf16[32,1792]{1,0:T(8,128)(2,1)S(1)} %get-tuple-element.60), channel_id=1, source_target_pairs={{0,28},{2,30},{4,0},{6,2},{8,4},{10,6},{12,8},{14,10},{16,12},{18,... | collective-permute-start | bytes 344072 | tf_op jit(solution)/shard_map/ppermute | solution.py:43
  182.5 8.5 %collective-permute-done.32.ahead = bf16[32,1792]{1,0:T(8,128)(2,1)S(1)} collective-permute-done((bf16[32,1792]{1,0:T(8,128)(2,1)S(1)}, bf16[32,1792]{1,0:T(8,128)(2,1)S(1)}, u32[]{:S(2)}, u32[]{:S(2)}) %collective-permute-start.32) | collective-permute-done | bytes 114720 | tf_op jit(solution)/shard_map/ppermute | solution.py:43
  191.1 1.2 collective-permute-start.34
  192.3 7.2 %collective-permute-start.35 = (bf16[8,3584]{1,0:T(8,128)(2,1)S(1)}, bf16[8,3584]{1,0:T(8,128)(2,1)S(1)}, u32[]{:S(2)}, u32[]{:S(2)}) collective-permute-start(bf16[8,3584]{1,0:T(8,128)(2,1)S(1)} %get-tuple-element.63), channel_id=1, source_target_pairs={{0,8},{2,10},{4,12},{6,14},{8,16},{10,18},{12,20},{14,22},{16,24},... | collective-permute-start | bytes 172040 | tf_op jit(solution)/shard_map/ppermute | solution.py:43
  199.5 4.7 %collective-permute-done.34 = bf16[8,3584]{1,0:T(8,128)(2,1)S(1)} collective-permute-done((bf16[8,3584]{1,0:T(8,128)(2,1)S(1)}, bf16[8,3584]{1,0:T(8,128)(2,1)S(1)}, u32[]{:S(2)}, u32[]{:S(2)}) %collective-permute-start.34) | collective-permute-done | bytes 57376 | tf_op jit(solution)/shard_map/ppermute | solution.py:43
  204.2 3.4 %collective-permute-done.36 = bf16[8,3584]{1,0:T(8,128)(2,1)S(1)} collective-permute-done((bf16[8,3584]{1,0:T(8,128)(2,1)S(1)}, bf16[8,3584]{1,0:T(8,128)(2,1)S(1)}, u32[]{:S(2)}, u32[]{:S(2)}) %collective-permute-start.36) | collective-permute-done | bytes 57376 | tf_op jit(solution)/shard_map/ppermute | solution.py:43
  207.7 0.7 reshape.101
  (82 shorter events, 1.7 us)
Async XLA Ops:
  1.2 34.3 %collective-permute-start.11 = (bf16[32,7680]{1,0:T(8,128)(2,1)S(1)}, bf16[32,7680]{1,0:T(8,128)(2,1)S(1)}, u32[]{:S(2)}, u32[]{:S(2)}) collective-permute-start(bf16[32,7680]{1,0:T(8,128)(2,1)S(1)} %get-tuple-element.35.refs_0_), channel_id=1, source_target_pairs={{0,96},{32,0},{64,32},{96,64},{1,97},{33,1},{65,33},{97,65},{2,98}... | collective-permute-start | bytes 1474568 | tf_op jit(solution)/shard_map/ppermute | solution.py:39
  1.7 33.9 %collective-permute-start.6 = (bf16[32,7680]{1,0:T(8,128)(2,1)S(1)}, bf16[32,7680]{1,0:T(8,128)(2,1)S(1)}, u32[]{:S(2)}, u32[]{:S(2)}) collective-permute-start(bf16[32,7680]{1,0:T(8,128)(2,1)S(1)} %get-tuple-element.35.refs_0_), channel_id=1, source_target_pairs={{0,1},{1,0},{2,3},{3,2},{4,5},{5,4},{6,7},{7,6},{8,9},{9,8},{10,11... | collective-permute-start | bytes 1474568 | tf_op jit(solution)/shard_map/ppermute | solution.py:47
  1.7 34.4 %collective-permute-start = (bf16[32,7680]{1,0:T(8,128)(2,1)S(1)}, bf16[32,7680]{1,0:T(8,128)(2,1)S(1)}, u32[]{:S(2)}, u32[]{:S(2)}) collective-permute-start(bf16[32,7680]{1,0:T(8,128)(2,1)S(1)} %get-tuple-element.35.refs_0_), channel_id=1, source_target_pairs={{0,32},{32,64},{64,96},{96,0},{1,33},{33,65},{65,97},{97,1},{2,34}... | collective-permute-start | bytes 1474568 | tf_op jit(solution)/shard_map/ppermute | solution.py:39
  3.4 36.0 %collective-permute-start.2 = (bf16[32,7680]{1,0:T(8,128)(2,1)S(1)}, bf16[32,7680]{1,0:T(8,128)(2,1)S(1)}, u32[]{:S(2)}, u32[]{:S(2)}) collective-permute-start(bf16[32,7680]{1,0:T(8,128)(2,1)S(1)} %get-tuple-element.36.refs_1_), channel_id=1, source_target_pairs={{0,96},{32,0},{64,32},{96,64},{1,97},{33,1},{65,33},{97,65},{2,98}... | collective-permute-start | bytes 1474568 | tf_op jit(solution)/shard_map/ppermute | solution.py:39
  3.8 35.6 %collective-permute-start.8 = (bf16[32,7680]{1,0:T(8,128)(2,1)S(1)}, bf16[32,7680]{1,0:T(8,128)(2,1)}, u32[]{:S(2)}, u32[]{:S(2)}) collective-permute-start(bf16[32,7680]{1,0:T(8,128)(2,1)S(1)} %get-tuple-element.36.refs_1_), channel_id=1, source_target_pairs={{0,32},{32,64},{64,96},{96,0},{1,33},{33,65},{65,97},{97,1},{2,34}... | collective-permute-start | bytes 1474568 | tf_op jit(solution)/shard_map/ppermute | solution.py:39
  12.6 41.2 %all-to-all-start = ((bf16[16,16,512]{2,1,0:T(8,128)(2,1)}), bf16[16,16,512]{2,1,0:T(8,128)(2,1)S(1)}, u32[]{:S(2)}, u32[]{:S(2)}) async-start(bf16[16,16,512]{2,1,0:T(8,128)(2,1)} %bitcast.5), calls=%async_computation | async-start | bytes 524288 | tf_op jit(solution)/shard_map/all_to_all | solution.py:494
  35.5 4.1 %collective-permute-start.7 = (bf16[32,7680]{1,0:T(8,128)(2,1)S(1)}, bf16[32,7680]{1,0:T(8,128)(2,1)S(1)}, u32[]{:S(2)}, u32[]{:S(2)}) collective-permute-start(bf16[32,7680]{1,0:T(8,128)(2,1)S(1)} %get-tuple-element.36.refs_1_), channel_id=1, source_target_pairs={{0,1},{1,0},{2,3},{3,2},{4,5},{5,4},{6,7},{7,6},{8,9},{9,8},{10,11... | collective-permute-start | bytes 1474568 | tf_op jit(solution)/shard_map/ppermute | solution.py:47
  35.6 5.2 %collective-permute-start.12 = (bf16[32,7680]{1,0:T(8,128)(2,1)S(1)}, bf16[32,7680]{1,0:T(8,128)(2,1)S(1)}, u32[]{:S(2)}, u32[]{:S(2)}) collective-permute-start(bf16[32,7680]{1,0:T(8,128)(2,1)S(1)} %collective-permute-done.11.refs_8_), channel_id=1, source_target_pairs={{0,1},{1,0},{2,3},{3,2},{4,5},{5,4},{6,7},{7,6},{8,9},{9,8},{10,11... | collective-permute-start | bytes 1474568 | tf_op jit(solution)/shard_map/ppermute | solution.py:47
  36.1 14.0 %collective-permute-start.1 = (bf16[32,7680]{1,0:T(8,128)(2,1)S(1)}, bf16[32,7680]{1,0:T(8,128)(2,1)}, u32[]{:S(2)}, u32[]{:S(2)}) collective-permute-start(bf16[32,7680]{1,0:T(8,128)(2,1)S(1)} %collective-permute-done.refs_4_), channel_id=1, source_target_pairs={{0,32},{32,64},{64,96},{96,0},{1,33},{33,65},{65,97},{97,1},{2,34}... | collective-permute-start | bytes 1474568 | tf_op jit(solution)/shard_map/ppermute | solution.py:39
  39.4 13.1 %collective-permute-start.3 = (bf16[32,7680]{1,0:T(8,128)(2,1)S(1)}, bf16[32,7680]{1,0:T(8,128)(2,1)}, u32[]{:S(2)}, u32[]{:S(2)}) collective-permute-start(bf16[32,7680]{1,0:T(8,128)(2,1)S(1)} %collective-permute-done.2.refs_9_), channel_id=1, source_target_pairs={{0,96},{32,0},{64,32},{96,64},{1,97},{33,1},{65,33},{97,65},{2,98}... | collective-permute-start | bytes 1474568 | tf_op jit(solution)/shard_map/ppermute | solution.py:39
  39.4 13.1 %collective-permute-start.9 = (bf16[32,7680]{1,0:T(8,128)(2,1)S(1)}, bf16[32,7680]{1,0:T(8,128)(2,1)S(1)}, u32[]{:S(2)}, u32[]{:S(2)}) collective-permute-start(bf16[32,7680]{1,0:T(8,128)(2,1)S(1)} %collective-permute-done.refs_4_), channel_id=1, source_target_pairs={{0,1},{1,0},{2,3},{3,2},{4,5},{5,4},{6,7},{7,6},{8,9},{9,8},{10,11... | collective-permute-start | bytes 1474568 | tf_op jit(solution)/shard_map/ppermute | solution.py:47
  39.5 0.8 copy-start
  40.3 13.5 %collective-permute-start.10 = (bf16[32,7680]{1,0:T(8,128)(2,1)}, bf16[32,7680]{1,0:T(8,128)(2,1)}, u32[]{:S(2)}, u32[]{:S(2)}) collective-permute-start(bf16[32,7680]{1,0:T(8,128)(2,1)} %collective-permute-done.8.refs_5_), channel_id=1, source_target_pairs={{0,1},{1,0},{2,3},{3,2},{4,5},{5,4},{6,7},{7,6},{8,9},{9,8},{10,11... | collective-permute-start | bytes 1474568 | tf_op jit(solution)/shard_map/ppermute | solution.py:47
  40.8 0.8 copy-start.2
  41.6 12.2 %collective-permute-start.13 = (bf16[32,7680]{1,0:T(8,128)(2,1)S(1)}, bf16[32,7680]{1,0:T(8,128)(2,1)}, u32[]{:S(2)}, u32[]{:S(2)}) collective-permute-start(bf16[32,7680]{1,0:T(8,128)(2,1)S(1)} %collective-permute-done.2.refs_9_), channel_id=1, source_target_pairs={{0,1},{1,0},{2,3},{3,2},{4,5},{5,4},{6,7},{7,6},{8,9},{9,8},{10,11... | collective-permute-start | bytes 1474568 | tf_op jit(solution)/shard_map/ppermute | solution.py:47
  50.2 9.5 %collective-permute-start.4 = (bf16[32,7680]{1,0:T(8,128)(2,1)}, bf16[32,7680]{1,0:T(8,128)(2,1)}, u32[]{:S(2)}, u32[]{:S(2)}) collective-permute-start(bf16[32,7680]{1,0:T(8,128)(2,1)} %collective-permute-done.1.refs_0_), channel_id=1, source_target_pairs={{0,1},{1,0},{2,3},{3,2},{4,5},{5,4},{6,7},{7,6},{8,9},{9,8},{10,11... | collective-permute-start | bytes 1474568 | tf_op jit(solution)/shard_map/ppermute | solution.py:47
  52.5 7.2 %collective-permute-start.5 = (bf16[32,7680]{1,0:T(8,128)(2,1)}, bf16[32,7680]{1,0:T(8,128)(2,1)}, u32[]{:S(2)}, u32[]{:S(2)}) collective-permute-start(bf16[32,7680]{1,0:T(8,128)(2,1)} %collective-permute-done.3.refs_1_), channel_id=1, source_target_pairs={{0,1},{1,0},{2,3},{3,2},{4,5},{5,4},{6,7},{7,6},{8,9},{9,8},{10,11... | collective-permute-start | bytes 1474568 | tf_op jit(solution)/shard_map/ppermute | solution.py:47
  52.5 0.8 copy-start.4
  53.3 83.6 %collective-permute-start.23 = (bf16[7168,128]{1,0:T(8,128)(2,1)}, bf16[7168,128]{1,0:T(8,128)(2,1)}, u32[]{:S(2)}, u32[]{:S(2)}) collective-permute-start(bf16[7168,128]{1,0:T(8,128)(2,1)} %gate_a.1), channel_id=1, source_target_pairs={{0,1},{1,0},{2,3},{3,2},{4,5},{5,4},{6,7},{7,6},{8,9},{9,8},{10,11... | collective-permute-start | bytes 5505032 | tf_op jit(solution)/shard_map/ppermute | solution.py:47
  53.8 1.0 copy-start.1
  54.8 1.0 copy-start.3
  55.9 1.0 copy-start.5
  59.6 4.7 %copy-start.10 = (s32[2,2,8]{2,1,0:T(2,128)S(1)}, s32[2,2,8]{2,1,0:T(2,128)}, u32[]{:S(2)}) copy-start(s32[2,2,8]{2,1,0:T(2,128)} %param.24) | copy-start | bytes 388
  59.6 11.3 %copy-start.8 = (s32[2,2,8]{2,1,0:T(2,128)S(1)}, s32[2,2,8]{2,1,0:T(2,128)}, u32[]{:S(2)}) copy-start(s32[2,2,8]{2,1,0:T(2,128)} %param.23) | copy-start | bytes 388
  59.6 32.6 %copy-start.9 = (bf16[7168]{0:T(1024)(128)(2,1)S(1)}, bf16[7168]{0:T(1024)(128)(2,1)}, u32[]{:S(2)}) copy-start(bf16[7168]{0:T(1024)(128)(2,1)} %param.21) | copy-start | bytes 43012
  59.6 32.7 %copy-start.7 = (bf16[2,2,7168]{2,1,0:T(2,128)(2,1)S(1)}, bf16[2,2,7168]{2,1,0:T(2,128)(2,1)}, u32[]{:S(2)}) copy-start(bf16[2,2,7168]{2,1,0:T(2,128)(2,1)} %param.18) | copy-start | bytes 172036
  62.1 30.5 %copy-start.6 = (bf16[7168,16]{0,1:T(8,128)(2,1)S(1)}, bf16[7168,16]{0,1:T(8,128)(2,1)}, u32[]{:S(2)}) copy-start(bf16[7168,16]{0,1:T(8,128)(2,1)} %param.22) | copy-start | bytes 688132
  62.1 33.4 %copy-start.11 = (bf16[128,7168]{1,0:T(8,128)(2,1)S(1)}, bf16[128,7168]{1,0:T(8,128)(2,1)}, u32[]{:S(2)}) copy-start(bf16[128,7168]{1,0:T(8,128)(2,1)} %down_a.1) | copy-start | bytes 5505028
  62.1 16.8 %collective-permute-start.14 = (bf16[32,3584]{1,0:T(8,128)(2,1)S(1)}, bf16[32,3584]{1,0:T(8,128)(2,1)S(1)}, u32[]{:S(2)}, u32[]{:S(2)}) collective-permute-start(bf16[32,3584]{1,0:T(8,128)(2,1)S(1)} %get-tuple-element.38), channel_id=1, source_target_pairs={{0,2},{2,4},{4,6},{6,8},{8,10},{10,12},{12,14},{14,16},{16,18},{18... | collective-permute-start | bytes 688136 | tf_op jit(solution)/shard_map/ppermute | solution.py:43
  63.7 15.2 %collective-permute-start.15 = (bf16[32,3584]{1,0:T(8,128)(2,1)S(1)}, bf16[32,3584]{1,0:T(8,128)(2,1)S(1)}, u32[]{:S(2)}, u32[]{:S(2)}) collective-permute-start(bf16[32,3584]{1,0:T(8,128)(2,1)S(1)} %get-tuple-element.39), channel_id=1, source_target_pairs={{0,30},{2,0},{4,2},{6,4},{8,6},{10,8},{12,10},{14,12},{16,14},{18,... | collective-permute-start | bytes 688136 | tf_op jit(solution)/shard_map/ppermute | solution.py:43
  64.2 14.7 %collective-permute-start.16 = (bf16[32,1792]{1,0:T(8,128)(2,1)S(1)}, bf16[32,1792]{1,0:T(8,128)(2,1)S(1)}, u32[]{:S(2)}, u32[]{:S(2)}) collective-permute-start(bf16[32,1792]{1,0:T(8,128)(2,1)S(1)} %get-tuple-element.40), channel_id=1, source_target_pairs={{0,4},{2,6},{4,8},{6,10},{8,12},{10,14},{12,16},{14,18},{16,20},{1... | collective-permute-start | bytes 344072 | tf_op jit(solution)/shard_map/ppermute | solution.py:43
  67.4 11.5 %collective-permute-start.17 = (bf16[32,1792]{1,0:T(8,128)(2,1)S(1)}, bf16[32,1792]{1,0:T(8,128)(2,1)S(1)}, u32[]{:S(2)}, u32[]{:S(2)}) collective-permute-start(bf16[32,1792]{1,0:T(8,128)(2,1)S(1)} %get-tuple-element.41), channel_id=1, source_target_pairs={{0,28},{2,30},{4,0},{6,2},{8,4},{10,6},{12,8},{14,10},{16,12},{18,... | collective-permute-start | bytes 344072 | tf_op jit(solution)/shard_map/ppermute | solution.py:43
  78.9 61.4 %collective-permute-start.24 = (bf16[7168,128]{1,0:T(8,128)(2,1)}, bf16[7168,128]{1,0:T(8,128)(2,1)}, u32[]{:S(2)}, u32[]{:S(2)}) collective-permute-start(bf16[7168,128]{1,0:T(8,128)(2,1)} %up_a.1), channel_id=1, source_target_pairs={{0,1},{1,0},{2,3},{3,2},{4,5},{5,4},{6,7},{7,6},{8,9},{9,8},{10,11... | collective-permute-start | bytes 5505032 | tf_op jit(solution)/shard_map/ppermute | solution.py:47
  79.0 16.4 %collective-permute-start.18 = (bf16[8,3584]{1,0:T(8,128)(2,1)S(1)}, bf16[8,3584]{1,0:T(8,128)(2,1)S(1)}, u32[]{:S(2)}, u32[]{:S(2)}) collective-permute-start(bf16[8,3584]{1,0:T(8,128)(2,1)S(1)} %get-tuple-element.43), channel_id=1, source_target_pairs={{0,16},{2,18},{4,20},{6,22},{8,24},{10,26},{12,28},{14,30},{16,0},... | collective-permute-start | bytes 172040 | tf_op jit(solution)/shard_map/ppermute | solution.py:43
  86.3 11.1 %collective-permute-start.19 = (bf16[8,3584]{1,0:T(8,128)(2,1)S(1)}, bf16[8,3584]{1,0:T(8,128)(2,1)S(1)}, u32[]{:S(2)}, u32[]{:S(2)}) collective-permute-start(bf16[8,3584]{1,0:T(8,128)(2,1)S(1)} %get-tuple-element.44), channel_id=1, source_target_pairs={{0,8},{2,10},{4,12},{6,14},{8,16},{10,18},{12,20},{14,22},{16,24},... | collective-permute-start | bytes 172040 | tf_op jit(solution)/shard_map/ppermute | solution.py:43
  86.9 10.5 %collective-permute-start.20 = (bf16[8,3584]{1,0:T(8,128)(2,1)S(1)}, bf16[8,3584]{1,0:T(8,128)(2,1)S(1)}, u32[]{:S(2)}, u32[]{:S(2)}) collective-permute-start(bf16[8,3584]{1,0:T(8,128)(2,1)S(1)} %get-tuple-element.45), channel_id=1, source_target_pairs={{0,24},{2,26},{4,28},{6,30},{8,0},{10,2},{12,4},{14,6},{16,8},{18,... | collective-permute-start | bytes 172040 | tf_op jit(solution)/shard_map/ppermute | solution.py:43
  95.5 44.8 %collective-permute-start.25 = (bf16[128,7168]{1,0:T(8,128)(2,1)S(1)}, bf16[128,7168]{1,0:T(8,128)(2,1)}, u32[]{:S(2)}, u32[]{:S(2)}) collective-permute-start(bf16[128,7168]{1,0:T(8,128)(2,1)S(1)} %copy-done.11), channel_id=1, source_target_pairs={{0,1},{1,0},{2,3},{3,2},{4,5},{5,4},{6,7},{7,6},{8,9},{9,8},{10,11... | collective-permute-start | bytes 5505032 | tf_op jit(solution)/shard_map/ppermute | solution.py:47
  134.3 11.5 %collective-permute-start.21 = (bf16[32,7296]{1,0:T(8,128)(2,1)S(1)}, bf16[32,7296]{1,0:T(8,128)(2,1)S(1)}, u32[]{:S(2)}, u32[]{:S(2)}) collective-permute-start(bf16[32,7296]{1,0:T(8,128)(2,1)S(1)} %get-tuple-element.48), channel_id=1, source_target_pairs={{0,96},{32,0},{64,32},{96,64},{1,97},{33,1},{65,33},{97,65},{2,98}... | collective-permute-start | bytes 1400840 | tf_op jit(solution)/shard_map/ppermute | solution.py:39
  135.2 23.2 %collective-permute-start.22 = (bf16[32,7296]{1,0:T(8,128)(2,1)S(1)}, bf16[32,7296]{1,0:T(8,128)(2,1)S(1)}, u32[]{:S(2)}, u32[]{:S(2)}) collective-permute-start(bf16[32,7296]{1,0:T(8,128)(2,1)S(1)} %get-tuple-element.49), channel_id=1, source_target_pairs={{0,32},{32,64},{64,96},{96,0},{1,33},{33,65},{65,97},{97,1},{2,34}... | collective-permute-start | bytes 1400840 | tf_op jit(solution)/shard_map/ppermute | solution.py:39
  136.9 26.2 %collective-permute-start.28 = (bf16[32,7296]{1,0:T(8,128)(2,1)S(1)}, bf16[32,7296]{1,0:T(8,128)(2,1)S(1)}, u32[]{:S(2)}, u32[]{:S(2)}) collective-permute-start(bf16[32,7296]{1,0:T(8,128)(2,1)S(1)} %get-tuple-element.55), channel_id=1, source_target_pairs={{0,64},{32,96},{64,0},{96,32},{1,65},{33,97},{65,1},{97,33},{2,66}... | collective-permute-start | bytes 1400840 | tf_op jit(solution)/shard_map/ppermute | solution.py:39
  161.0 8.6 %collective-permute-start.26 = (bf16[32,7168]{1,0:T(8,128)(2,1)S(1)}, bf16[32,7168]{1,0:T(8,128)(2,1)S(1)}, u32[]{:S(2)}, u32[]{:S(2)}) collective-permute-start(bf16[32,7168]{1,0:T(8,128)(2,1)S(1)} %get-tuple-element.53), channel_id=1, source_target_pairs={{0,32},{32,64},{64,96},{96,0},{1,33},{33,65},{65,97},{97,1},{2,34}... | collective-permute-start | bytes 1376264 | tf_op jit(solution)/shard_map/ppermute | solution.py:39
  161.1 12.9 %collective-permute-start.27 = (bf16[32,7168]{1,0:T(8,128)(2,1)S(1)}, bf16[32,7168]{1,0:T(8,128)(2,1)S(1)}, u32[]{:S(2)}, u32[]{:S(2)}) collective-permute-start(bf16[32,7168]{1,0:T(8,128)(2,1)S(1)} %get-tuple-element.54), channel_id=1, source_target_pairs={{0,96},{32,0},{64,32},{96,64},{1,97},{33,1},{65,33},{97,65},{2,98}... | collective-permute-start | bytes 1376264 | tf_op jit(solution)/shard_map/ppermute | solution.py:39
  165.7 10.1 %collective-permute-start.29 = (bf16[32,7168]{1,0:T(8,128)(2,1)S(1)}, bf16[32,7168]{1,0:T(8,128)(2,1)S(1)}, u32[]{:S(2)}, u32[]{:S(2)}) collective-permute-start(bf16[32,7168]{1,0:T(8,128)(2,1)S(1)} %expert_part.3), channel_id=1, source_target_pairs={{0,64},{32,96},{64,0},{96,32},{1,65},{33,97},{65,1},{97,33},{2,66}... | collective-permute-start | bytes 1376264 | tf_op jit(solution)/shard_map/ppermute | solution.py:39
  176.2 14.7 %collective-permute-start.30 = (bf16[32,3584]{1,0:T(8,128)(2,1)S(1)}, bf16[32,3584]{1,0:T(8,128)(2,1)S(1)}, u32[]{:S(2)}, u32[]{:S(2)}) collective-permute-start(bf16[32,3584]{1,0:T(8,128)(2,1)S(1)} %get-tuple-element.57), channel_id=1, source_target_pairs={{0,2},{2,4},{4,6},{6,8},{8,10},{10,12},{12,14},{14,16},{16,18},{18... | collective-permute-start | bytes 688136 | tf_op jit(solution)/shard_map/ppermute | solution.py:43
  176.4 14.6 %collective-permute-start.31 = (bf16[32,3584]{1,0:T(8,128)(2,1)S(1)}, bf16[32,3584]{1,0:T(8,128)(2,1)S(1)}, u32[]{:S(2)}, u32[]{:S(2)}) collective-permute-start(bf16[32,3584]{1,0:T(8,128)(2,1)S(1)} %get-tuple-element.58), channel_id=1, source_target_pairs={{0,30},{2,0},{4,2},{6,4},{8,6},{10,8},{12,10},{14,12},{16,14},{18,... | collective-permute-start | bytes 688136 | tf_op jit(solution)/shard_map/ppermute | solution.py:43
  178.4 12.6 %collective-permute-start.32 = (bf16[32,1792]{1,0:T(8,128)(2,1)S(1)}, bf16[32,1792]{1,0:T(8,128)(2,1)S(1)}, u32[]{:S(2)}, u32[]{:S(2)}) collective-permute-start(bf16[32,1792]{1,0:T(8,128)(2,1)S(1)} %get-tuple-element.59), channel_id=1, source_target_pairs={{0,4},{2,6},{4,8},{6,10},{8,12},{10,14},{12,16},{14,18},{16,20},{1... | collective-permute-start | bytes 344072 | tf_op jit(solution)/shard_map/ppermute | solution.py:43
  178.8 12.2 %collective-permute-start.33 = (bf16[32,1792]{1,0:T(8,128)(2,1)S(1)}, bf16[32,1792]{1,0:T(8,128)(2,1)S(1)}, u32[]{:S(2)}, u32[]{:S(2)}) collective-permute-start(bf16[32,1792]{1,0:T(8,128)(2,1)S(1)} %get-tuple-element.60), channel_id=1, source_target_pairs={{0,28},{2,30},{4,0},{6,2},{8,4},{10,6},{12,8},{14,10},{16,12},{18,... | collective-permute-start | bytes 344072 | tf_op jit(solution)/shard_map/ppermute | solution.py:43
  191.1 13.2 %collective-permute-start.34 = (bf16[8,3584]{1,0:T(8,128)(2,1)S(1)}, bf16[8,3584]{1,0:T(8,128)(2,1)S(1)}, u32[]{:S(2)}, u32[]{:S(2)}) collective-permute-start(bf16[8,3584]{1,0:T(8,128)(2,1)S(1)} %get-tuple-element.62), channel_id=1, source_target_pairs={{0,16},{2,18},{4,20},{6,22},{8,24},{10,26},{12,28},{14,30},{16,0},... | collective-permute-start | bytes 172040 | tf_op jit(solution)/shard_map/ppermute | solution.py:43
  192.3 12.0 %collective-permute-start.35 = (bf16[8,3584]{1,0:T(8,128)(2,1)S(1)}, bf16[8,3584]{1,0:T(8,128)(2,1)S(1)}, u32[]{:S(2)}, u32[]{:S(2)}) collective-permute-start(bf16[8,3584]{1,0:T(8,128)(2,1)S(1)} %get-tuple-element.63), channel_id=1, source_target_pairs={{0,8},{2,10},{4,12},{6,14},{8,16},{10,18},{12,20},{14,22},{16,24},... | collective-permute-start | bytes 172040 | tf_op jit(solution)/shard_map/ppermute | solution.py:43
  199.5 8.1 %collective-permute-start.36 = (bf16[8,3584]{1,0:T(8,128)(2,1)S(1)}, bf16[8,3584]{1,0:T(8,128)(2,1)S(1)}, u32[]{:S(2)}, u32[]{:S(2)}) collective-permute-start(bf16[8,3584]{1,0:T(8,128)(2,1)S(1)} %get-tuple-element.64), channel_id=1, source_target_pairs={{0,24},{2,26},{4,28},{6,30},{8,0},{10,2},{12,4},{14,6},{16,8},{18,... | collective-permute-start | bytes 172040 | tf_op jit(solution)/shard_map/ppermute | solution.py:43

commit v6 on v4

--- a/solution.py
+++ b/solution.py
@@ -451,16 +451,92 @@
     )(own, *others)
 
 
+def half_swap(a):
+    middle = a.shape[0] // 2
+    return jnp.concatenate([a[middle:], a[:middle]], axis=0)
+
+
+def route_kernel(first, one, two, three, rows, gain, router, ids, slots, hidden, payload):
+    count, half = rows.shape
+    total = first[...] + one[...].astype(f32) + two[...].astype(f32) + three[...].astype(f32)
+    total = rows[...].astype(f32) + total
+    hidden[...] = total
+    square = jnp.sum(total * total, axis=1, keepdims=True)
+    scale = lax.rsqrt((square + half_swap(square)) / D + norm_eps)
+    normed = (total * scale * gain[...]).astype(bf16)
+    payload[:, pl.ds(0, half)] = normed
+    parts = [
+        lax.dot_general(normed, router[:, pl.ds(c * half, half)], NT, preferred_element_type=f32)
+        for c in range(HALVES)
+    ]
+    logits = jnp.where(iota(parts[0].shape, 0) < count // 2, parts[0], parts[1])
+    logits = logits + half_swap(logits)
+    logits = jnp.concatenate([logits] * (EXTRA // EXPERTS), axis=1)
+    lane = iota(logits.shape, 1)
+    place = jnp.zeros(logits.shape, jnp.int32)
+    for k in range(TOP):
+        place = jnp.where(lax.rem(lane, EXPERTS) == ids[:, k : k + 1], slots[:, k : k + 1] + 1, place)
+    gates = jnp.where(place > 0, 1.0 / (1.0 + jnp.exp(-logits)), 0.0)
+    share = route_scale * gates / jnp.sum(jnp.where(lane < EXPERTS, gates, 0.0), axis=1, keepdims=True)
+    kind = lane // EXPERTS
+    table = jnp.zeros(logits.shape, f32)
+    for n in range(CAP):
+        table = jnp.where((kind == n) & (place == n + 1), 1.0, table)
+    rest = share
+    for n in range(3):
+        piece = rest.astype(bf16).astype(f32)
+        table = jnp.where(kind == CAP + n, piece, table)
+        rest = rest - piece
+    payload[:, pl.ds(half, EXTRA)] = table.astype(bf16)
+
+
+def route(added, rows, gain, router, ids, slots):
+    count, half = rows.shape
+    return pl.pallas_call(
+        route_kernel,
+        out_shape=(
+            jax.ShapeDtypeStruct((count, half), f32),
+            jax.ShapeDtypeStruct((count, half + EXTRA), bf16),
+        ),
+        in_specs=[vmem()] * 9,
+        out_specs=[vmem()] * 2,
+        compiler_params=params(4),
+        cost_estimate=cost(4 * count * half * EXPERTS, 20 * count * half),
+        name="route",
+    )(*added, rows, gain, router, ids, slots)
+
+
+def finish_kernel(hidden, first, one, two, three, out):
+    seqs, steps, _ = out.shape
+    half = hidden.shape[1]
+    total = first[...] + one[...].astype(f32) + two[...].astype(f32) + three[...].astype(f32)
+    total = (hidden[...] + total).astype(bf16)
+    for c in range(HALVES):
+        for b in range(seqs):
+            at = (c * seqs + b) * steps
+            out[b, :, pl.ds(c * half, half)] = total[at : at + steps]
+
+
+def finish(hidden, added, shape):
+    return pl.pallas_call(
+        finish_kernel,
+        out_shape=jax.ShapeDtypeStruct(shape, bf16),
+        in_specs=[vmem()] * 5,
+        out_specs=vmem(),
+        compiler_params=params(4),
+        cost_estimate=cost(5 * hidden.size, 14 * hidden.size),
+        name="finish",
+    )(hidden, *added)
+
+
 def reduce_z(own, right, left, ahead, behind):
     right = shift_z(right, 1)
     left = shift_z(left, -1)
     ahead = shift_z(ahead, 2)
     behind = shift_z(behind, -2)
-    out, *sent = merge(own, right, left, ahead, behind)
-    for k, rows in enumerate(sent):
-        step = NEAR * (k + 1)
-        out = out + shift_z(rows, step if step <= RING // 2 else step - RING).astype(f32)
-    return out
+    first, *sent = merge(own, right, left, ahead, behind)
+    others = [shift_z(sent[0], NEAR), shift_z(sent[1], 2 * NEAR), shift_z(sent[2], -NEAR)]
+    return first, *others
 
 
 def layer(
@@ -501,38 +577,19 @@
     for pair in ((top_left, low_left), (top_right, low_right)):
         near += [*pair, *map(swap_core, pair)]
     beyond = [top_far, low_far, swap_core(top_far), swap_core(low_far)]
-    weights = stage((w_gate, swap_core(w_gate), w_up, swap_core(w_up), w_down, swap_core(w_down)))
+    others = [swap_core(w) for w in (w_gate, w_up, w_down)]
+    weights = stage((w_gate, others[0], w_up, others[1], w_down, others[2]))
     arrived = arrived.reshape(RING * nx * tok, LAT)
     most = attend_part(where, nx, arrived, near, tok, 0, None)
-    attended = reduce_z(*attend_part(where, nx, arrived, beyond, tok, nx - 1, most))
+    added = reduce_z(*attend_part(where, nx, arrived, beyond, tok, nx - 1, most))
 
     half = D // HALVES
     rows = resid.reshape(tok, HALVES, half).swapaxes(0, 1).reshape(HALVES * tok, half)
-    hidden = rows.astype(f32) + attended
-    square = jnp.sum(hidden * hidden, axis=-1).reshape(HALVES, tok)
-    scale = lax.rsqrt(jnp.sum(square, axis=0) / D + norm_eps)
     gain = jnp.repeat(norm_gain.astype(f32).reshape(HALVES, half), tok, axis=0)
-    normed = (hidden * jnp.tile(scale, HALVES)[:, None] * gain).astype(bf16)
-
-    route_ids = expert_ids.reshape(tok, TOP)
-    route_slots = slots.reshape(tok, TOP)
-    wide_router = router.reshape(HALVES, half, EXPERTS).swapaxes(0, 1).reshape(half, HALVES * EXPERTS)
-    logits = jnp.dot(normed, wide_router, preferred_element_type=f32).reshape(HALVES, tok, HALVES, EXPERTS)
-    logits = sum(logits[c, :, c] for c in range(HALVES))
-    is_pick = route_ids[:, :, None] == jnp.arange(EXPERTS, dtype=jnp.int32)[None, None, :]
-    picked = jnp.sum(jnp.where(is_pick, logits[:, None, :], 0.0), axis=-1)
-    gates = jax.nn.sigmoid(picked)
-    gates = route_scale * gates / jnp.sum(gates, axis=1, keepdims=True)
-    share = jnp.sum(jnp.where(is_pick, gates[:, :, None], 0.0), axis=1)
-    slot = jnp.sum(jnp.where(is_pick, route_slots[:, :, None] + 1, 0), axis=1)
-    places = [(slot == s + 1).astype(bf16) for s in range(CAP)]
-    high = share.astype(bf16)
-    rest = share - high.astype(f32)
-    middle = rest.astype(bf16)
-    low = (rest - middle.astype(f32)).astype(bf16)
-    extra = jnp.concatenate(places + [high, middle, low], axis=1)
-    extra = jnp.pad(extra, ((0, 0), (0, EXTRA - extra.shape[1])))
-    payload = jnp.concatenate([normed, jnp.tile(extra, (HALVES, 1))], axis=1)
+    ids, places = [
+        jnp.tile(a.reshape(tok, TOP).astype(jnp.int32), (HALVES, 1)) for a in (expert_ids, slots)
+    ]
+    hidden, payload = route(added, rows, gain, router.T, ids, places)
 
     ring = lax.all_gather(payload, ZAX, axis=0, tiled=True)
     *sent, spread = dispatch(where, nx, ring, tok)
@@ -544,9 +601,8 @@
     back_right = shift_x(done[2], -1)
     (far_done,) = expert_part(where, (from_far,), weights)
     back_far = shift_x(far_done, 2)
-    expert_mix = reduce_z(*collect(spread, (done[0], back_left, back_right, back_far)))
-    mixed = (hidden + expert_mix).astype(bf16).reshape(HALVES, tok, half)
-    return mixed.swapaxes(0, 1).reshape(resid.shape)
+    added = reduce_z(*collect(spread, (done[0], back_left, back_right, back_far)))
+    return finish(hidden, added, resid.shape)
 
 
 def solution(mesh):

time: 212 us -> 235 us (1.11)
  the two profiles are of different devices: /device:TPU:164 before, /device:TPU:40 now
where the time goes in v6:
time: 235 us
  starting transfers between devices  94.6 us (40%)
  waiting for transfers between devices  74.4 us (32%)
  blocking collectives  37.9 us (16%)
  Pallas kernels  25.2 us (11%)
    ppermute x12, waiting for transfers between devices, shift_x(): return lax.ppermute(a, 'x', [(i, (i + step) % n) for i in range(n)])  50.4 us
    ppermute x14, starting transfers between devices, shift_z(): return lax.ppermute(a, ZAX, [(i, (i + step) % RING) for i in range(RING)])  48.9 us
    all_gather x1, blocking collectives, layer(): ring = lax.all_gather(payload, ZAX, axis=0, tiled=True)  37.9 us
    all_to_all x1, starting transfers between devices, layer(): lax.all_to_all(outgoing.reshape(RING, nx * tok, LAT), ZAX, split_axis=0,...  24 us
    ppermute x12, starting transfers between devices, shift_x(): return lax.ppermute(a, 'x', [(i, (i + step) % n) for i in range(n)])  20.3 us
    ppermute x14, waiting for transfers between devices, shift_z(): return lax.ppermute(a, ZAX, [(i, (i + step) % RING) for i in range(RING)])  20.2 us
    pallas_call x1, Pallas kernels, context_rows(): pl.pallas_call(functools.partial(context_kernel, nx), grid=(seqs,), out_s...  5.9 us
    pallas_call x2, Pallas kernels, attend_part(): pl.pallas_call(functools.partial(attend_kernel, tok, nx, count, first, la...  5.41 us
  transfers between devices with their start and end apart: 38, of which 17 were waited for; matrix products, arithmetic and copies ran while one was open for 0% of the time, Pallas kernels for 10%

profile of v6, /device:TPU:40, one launch (start us, length us, event | category | flops | bytes accessed | tf_op | source)
XLA Modules:
  0.0 235.0 jit_solution(7835982416785616526)
XLA Ops:
  0.0 1.2 pack.1
  1.2 3.3 %collective-permute-start.11 = (bf16[32,7680]{1,0:T(8,128)(2,1)S(1)}, bf16[32,7680]{1,0:T(8,128)(2,1)S(1)}, u32[]{:S(2)}, u32[]{:S(2)}) collective-permute-start(bf16[32,7680]{1,0:T(8,128)(2,1)S(1)} %get-tuple-element.37.refs_0_), channel_id=1, source_target_pairs={{0,96},{32,0},{64,32},{96,64},{1,97},{33,1},{65,33},{97,65},{2,98}... | collective-permute-start | bytes 1474568 | tf_op jit(solution)/shard_map/ppermute | solution.py:39
  4.5 0.5 collective-permute-start.8
  5.0 0.0 collective-permute-start.7
  5.0 10.0 %collective-permute-done.11.refs_8_ = bf16[32,7680]{1,0:T(8,128)(2,1)S(1)} collective-permute-done((bf16[32,7680]{1,0:T(8,128)(2,1)S(1)}, bf16[32,7680]{1,0:T(8,128)(2,1)S(1)}, u32[]{:S(2)}, u32[]{:S(2)}) %collective-permute-start.11) | collective-permute-done | bytes 491552 | tf_op jit(solution)/shard_map/ppermute | solution.py:39
  15.0 3.7 %collective-permute-start.2 = (bf16[32,7680]{1,0:T(8,128)(2,1)S(1)}, bf16[32,7680]{1,0:T(8,128)(2,1)}, u32[]{:S(2)}, u32[]{:S(2)}) collective-permute-start(bf16[32,7680]{1,0:T(8,128)(2,1)S(1)} %get-tuple-element.38.refs_1_), channel_id=1, source_target_pairs={{0,96},{32,0},{64,32},{96,64},{1,97},{33,1},{65,33},{97,65},{2,98}... | collective-permute-start | bytes 1474568 | tf_op jit(solution)/shard_map/ppermute | solution.py:39
  18.7 1.1 collective-permute-done.refs_4_
  19.8 10.1 %collective-permute-done.8.refs_5_ = bf16[32,7680]{1,0:T(8,128)(2,1)S(1)} collective-permute-done((bf16[32,7680]{1,0:T(8,128)(2,1)S(1)}, bf16[32,7680]{1,0:T(8,128)(2,1)S(1)}, u32[]{:S(2)}, u32[]{:S(2)}) %collective-permute-start.8) | collective-permute-done | bytes 491552 | tf_op jit(solution)/shard_map/ppermute | solution.py:39
  29.9 0.0 collective-permute-start.10
  29.9 0.7 pad_add_fusion.where_ref
  30.6 5.9 %context_rows.1 = bf16[256,512]{1,0:T(8,128)(2,1)} custom-call(s32[5]{0:T(128)S(1)} %pad_add_fusion.where_ref, bf16[2,576,2048]{2,1,0:T(8,128)(2,1)} %bitcast.20, bf16[2,2,64,576]{3,2,1,0:T(8,128)(2,1)} %queries.1, bf16[2,2,576]{2,1,0:T(2,128)(2,1)} %new.1), custom_call_target="tpu_custom_call" | custom-call | flops 1140850688 | bytes 4718592 | tf_op jit(solution)/shard_map/context_rows/pallas_call | solution.py:146
  36.5 24.0 %all-to-all-start = ((bf16[16,16,512]{2,1,0:T(8,128)(2,1)}), bf16[16,16,512]{2,1,0:T(8,128)(2,1)S(1)}, u32[]{:S(2)}, u32[]{:S(2)}) async-start(bf16[16,16,512]{2,1,0:T(8,128)(2,1)} %bitcast.4), calls=%async_computation | async-start | bytes 524288 | tf_op jit(solution)/shard_map/all_to_all | solution.py:571
  60.5 0.3 collective-permute-start.13
  60.9 3.2 %collective-permute-start.3 = (bf16[32,7680]{1,0:T(8,128)(2,1)}, bf16[32,7680]{1,0:T(8,128)(2,1)}, u32[]{:S(2)}, u32[]{:S(2)}) collective-permute-start(bf16[32,7680]{1,0:T(8,128)(2,1)} %collective-permute-done.2.refs_9_), channel_id=1, source_target_pairs={{0,96},{32,0},{64,32},{96,64},{1,97},{33,1},{65,33},{97,65},{2,98}... | collective-permute-start | bytes 1474568 | tf_op jit(solution)/shard_map/ppermute | solution.py:39
  64.1 0.5 collective-permute-start.24
  64.6 0.3 collective-permute-start.25
  65.0 0.8 copy-done
  65.7 0.2 collective-permute-start.4
  65.9 9.4 %collective-permute-done.3.refs_1_ = bf16[32,7680]{1,0:T(8,128)(2,1)} collective-permute-done((bf16[32,7680]{1,0:T(8,128)(2,1)}, bf16[32,7680]{1,0:T(8,128)(2,1)}, u32[]{:S(2)}, u32[]{:S(2)}) %collective-permute-start.3) | collective-permute-done | bytes 491552 | tf_op jit(solution)/shard_map/ppermute | solution.py:39
  75.4 3.8 %all-to-all-done = bf16[16,16,512]{2,1,0:T(8,128)(2,1)S(1)} async-done(((bf16[16,16,512]{2,1,0:T(8,128)(2,1)}), bf16[16,16,512]{2,1,0:T(8,128)(2,1)S(1)}, u32[]{:S(2)}, u32[]{:S(2)}) %all-to-all-start) | async-done | bytes 262176 | tf_op jit(solution)/shard_map/all_to_all | solution.py:571
  79.2 1.0 copy-done.1
  80.2 3.0 %attend_part.2.refs_4_ = f32[128,3584]{1,0:T(8,128)S(1)} custom-call(s32[5]{0:T(128)S(1)} %pad_add_fusion.where_ref, bf16[256,512]{1,0:T(8,128)(2,1)S(1)} %bitcast.15, bf16[32,7680]{1,0:T(8,128)(2,1)S(1)} %get-tuple-element.37.refs_0_, bf16[32,7680]{1,0:T(8,128)(2,1)S(1)} %get-tuple-element.38.refs_1_, bf16[32,7680]{1,0:T(8,128)(2,1)S(1)} %collective-permute-done.6.refs_2_, ...), custom_call_target="tpu_custom_call" | custom-call | flops 1409286144 | bytes 5505024 | tf_op jit(solution)/shard_map/attend_part/pallas_call | solution.py:260
  83.2 2.4 %attend_part.3 = (f32[32,3584]{1,0:T(8,128)S(1)}, bf16[32,3584]{1,0:T(8,128)(2,1)S(1)}, bf16[32,3584]{1,0:T(8,128)(2,1)S(1)}, bf16[32,1792]{1,0:T(8,128)(2,1)S(1)}, bf16[32,1792]{1,0:T(8,128)(2,1)S(1)}) custom-call(s32[5]{0:T(128)S(1)} %pad_add_fusion.where_ref, bf16[256,512]{1,0:T(8,128)(2,1)S(1)} %bitcast.16, ...), custom_call_target="tpu_custom_call" | custom-call | flops 469762048 | bytes 1835008 | tf_op jit(solution)/shard_map/attend_part/pallas_call | solution.py:260
  85.7 0.6 collective-permute-start.16
  86.3 3.6 %collective-permute-start.17 = (bf16[32,1792]{1,0:T(8,128)(2,1)S(1)}, bf16[32,1792]{1,0:T(8,128)(2,1)S(1)}, u32[]{:S(2)}, u32[]{:S(2)}) collective-permute-start(bf16[32,1792]{1,0:T(8,128)(2,1)S(1)} %get-tuple-element.43), channel_id=1, source_target_pairs={{0,28},{2,30},{4,0},{6,2},{8,4},{10,6},{12,8},{14,10},{16,12},{18,... | collective-permute-start | bytes 344072 | tf_op jit(solution)/shard_map/ppermute | solution.py:43
  89.9 2.8 %collective-permute-done.16.ahead = bf16[32,1792]{1,0:T(8,128)(2,1)S(1)} collective-permute-done((bf16[32,1792]{1,0:T(8,128)(2,1)S(1)}, bf16[32,1792]{1,0:T(8,128)(2,1)S(1)}, u32[]{:S(2)}, u32[]{:S(2)}) %collective-permute-start.16) | collective-permute-done | bytes 114720 | tf_op jit(solution)/shard_map/ppermute | solution.py:43
  92.7 3.0 %collective-permute-start.14 = (bf16[32,3584]{1,0:T(8,128)(2,1)S(1)}, bf16[32,3584]{1,0:T(8,128)(2,1)S(1)}, u32[]{:S(2)}, u32[]{:S(2)}) collective-permute-start(bf16[32,3584]{1,0:T(8,128)(2,1)S(1)} %get-tuple-element.40), channel_id=1, source_target_pairs={{0,2},{2,4},{4,6},{6,8},{8,10},{10,12},{12,14},{14,16},{16,18},{18... | collective-permute-start | bytes 688136 | tf_op jit(solution)/shard_map/ppermute | solution.py:43
  95.7 1.6 collective-permute-start.15
  97.3 3.3 %collective-permute-done.14.right = bf16[32,3584]{1,0:T(8,128)(2,1)S(1)} collective-permute-done((bf16[32,3584]{1,0:T(8,128)(2,1)S(1)}, bf16[32,3584]{1,0:T(8,128)(2,1)S(1)}, u32[]{:S(2)}, u32[]{:S(2)}) %collective-permute-start.14) | collective-permute-done | bytes 229408 | tf_op jit(solution)/shard_map/ppermute | solution.py:43
  100.7 1.4 collective-permute-done.15.left
  102.1 0.1 merge.2
  102.2 5.2 %collective-permute-start.18 = (bf16[8,3584]{1,0:T(8,128)(2,1)S(1)}, bf16[8,3584]{1,0:T(8,128)(2,1)S(1)}, u32[]{:S(2)}, u32[]{:S(2)}) collective-permute-start(bf16[8,3584]{1,0:T(8,128)(2,1)S(1)} %get-tuple-element.45), channel_id=1, source_target_pairs={{0,8},{2,10},{4,12},{6,14},{8,16},{10,18},{12,20},{14,22},{16,24},... | collective-permute-start | bytes 172040 | tf_op jit(solution)/shard_map/ppermute | solution.py:43
  107.4 4.9 %collective-permute-start.19 = (bf16[8,3584]{1,0:T(8,128)(2,1)S(1)}, bf16[8,3584]{1,0:T(8,128)(2,1)S(1)}, u32[]{:S(2)}, u32[]{:S(2)}) collective-permute-start(bf16[8,3584]{1,0:T(8,128)(2,1)S(1)} %get-tuple-element.46), channel_id=1, source_target_pairs={{0,16},{2,18},{4,20},{6,22},{8,24},{10,26},{12,28},{14,30},{16,0},... | collective-permute-start | bytes 172040 | tf_op jit(solution)/shard_map/ppermute | solution.py:43
  112.3 6.6 %collective-permute-start.20 = (bf16[8,3584]{1,0:T(8,128)(2,1)S(1)}, bf16[8,3584]{1,0:T(8,128)(2,1)S(1)}, u32[]{:S(2)}, u32[]{:S(2)}) collective-permute-start(bf16[8,3584]{1,0:T(8,128)(2,1)S(1)} %get-tuple-element.47), channel_id=1, source_target_pairs={{0,24},{2,26},{4,28},{6,30},{8,0},{10,2},{12,4},{14,6},{16,8},{18,... | collective-permute-start | bytes 172040 | tf_op jit(solution)/shard_map/ppermute | solution.py:43
  119.1 2.7 %collective-permute-done.19.two = bf16[8,3584]{1,0:T(8,128)(2,1)S(1)} collective-permute-done((bf16[8,3584]{1,0:T(8,128)(2,1)S(1)}, bf16[8,3584]{1,0:T(8,128)(2,1)S(1)}, u32[]{:S(2)}, u32[]{:S(2)}) %collective-permute-start.19) | collective-permute-done | bytes 57376 | tf_op jit(solution)/shard_map/ppermute | solution.py:43
  121.8 0.7 collective-permute-done.20.three
  122.6 0.6 route.1
  123.2 37.9 %all_gather.3.tokens = bf16[128,3712]{1,0:T(8,128)(2,1)S(1)} all-gather(bf16[8,3712]{1,0:T(8,128)(2,1)S(1)} %get-tuple-element.49), channel_id=1, replica_groups=mesh['rep'=2,'x'=4,'zb'=4,'j'=4,'c'=2] {'zb','j'}, dimensions={0}, use_global_device_ids=true | all-gather | bytes 1009664 | tf_op jit(solution)/shard_map/all_gather | solution.py:594
  161.0 1.3 dispatch.1
  162.4 2.2 collective-permute-start.21
  164.6 1.6 collective-permute-start.28
  166.2 4.3 %stage.1 = (bf16[7168,512]{1,0:T(8,128)(2,1)S(1)}, bf16[256,7168]{1,0:T(8,128)(2,1)S(1)}) custom-call(bf16[7168,128]{1,0:T(8,128)(2,1)} %gate_a.1, bf16[7168,128]{1,0:T(8,128)(2,1)} %collective-permute-done.23.gate_b, bf16[7168,128]{1,0:T(8,128)(2,1)} %up_a.1, bf16[7168,128]{1,0:T(8,128)(2,1)} %collective-permute-done.24.up_b, bf16[128,7168]{1,0:T(8,128)(2,1)} %down_a.1, ...), custom_call_target="tpu_custom_call" | custom-call | flops 3670016000 | bytes 11010048 | tf_op jit(solution)/shard_map/stage/pallas_call | solution.py:349
  170.4 8.5 %collective-permute-done.21.refs_1_ = bf16[32,7296]{1,0:T(8,128)(2,1)S(1)} collective-permute-done((bf16[32,7296]{1,0:T(8,128)(2,1)S(1)}, bf16[32,7296]{1,0:T(8,128)(2,1)S(1)}, u32[]{:S(2)}, u32[]{:S(2)}) %collective-permute-start.21) | collective-permute-done | bytes 466976 | tf_op jit(solution)/shard_map/ppermute | solution.py:39
  179.0 3.7 %collective-permute-done.22.refs_2_ = bf16[32,7296]{1,0:T(8,128)(2,1)S(1)} collective-permute-done((bf16[32,7296]{1,0:T(8,128)(2,1)S(1)}, bf16[32,7296]{1,0:T(8,128)(2,1)S(1)}, u32[]{:S(2)}, u32[]{:S(2)}) %collective-permute-start.22) | collective-permute-done | bytes 466976 | tf_op jit(solution)/shard_map/ppermute | solution.py:39
  182.7 2.5 %expert_part.2 = (bf16[32,7168]{1,0:T(8,128)(2,1)S(1)}, bf16[32,7168]{1,0:T(8,128)(2,1)S(1)}, bf16[32,7168]{1,0:T(8,128)(2,1)S(1)}) custom-call(s32[5]{0:T(128)S(1)} %pad_add_fusion.where_ref, bf16[32,7296]{1,0:T(8,128)(2,1)S(1)} %get-tuple-element.51.refs_0_, bf16[32,7296]{1,0:T(8,128)(2,1)S(1)} %collective-permute-done.21.refs_1_, ...), custom_call_target="tpu_custom_call" | custom-call | flops 2113929216 | bytes 1376256 | tf_op jit(solution)/shard_map/expert_part/pallas_call | solution.py:396
  185.2 1.0 collective-permute-start.26
  186.2 2.3 collective-permute-start.27
  188.6 2.6 %expert_part.3 = bf16[32,7168]{1,0:T(8,128)(2,1)S(1)} custom-call(s32[5]{0:T(128)S(1)} %pad_add_fusion.where_ref, bf16[32,7296]{1,0:T(8,128)(2,1)S(1)} %collective-permute-done.28.refs_0_, bf16[7168,512]{1,0:T(8,128)(2,1)S(1)} %get-tuple-element.54.refs_3_.refs_1_, bf16[256,7168]{1,0:T(8,128)(2,1)S(1)} %get-tuple-element.55.refs_4_.refs_2_), custom_call_target="tpu_custom_call" | custom-call | flops 704643072 | bytes 458752 | tf_op jit(solution)/shard_map/expert_part/pallas_call | solution.py:396
  191.2 2.5 %collective-permute-start.29 = (bf16[32,7168]{1,0:T(8,128)(2,1)S(1)}, bf16[32,7168]{1,0:T(8,128)(2,1)S(1)}, u32[]{:S(2)}, u32[]{:S(2)}) collective-permute-start(bf16[32,7168]{1,0:T(8,128)(2,1)S(1)} %expert_part.3), channel_id=1, source_target_pairs={{0,64},{32,96},{64,0},{96,32},{1,65},{33,97},{65,1},{97,33},{2,66}... | collective-permute-start | bytes 1376264 | tf_op jit(solution)/shard_map/ppermute | solution.py:39
  193.7 2.6 %collective-permute-done.26.refs_1_ = bf16[32,7168]{1,0:T(8,128)(2,1)S(1)} collective-permute-done((bf16[32,7168]{1,0:T(8,128)(2,1)S(1)}, bf16[32,7168]{1,0:T(8,128)(2,1)S(1)}, u32[]{:S(2)}, u32[]{:S(2)}) %collective-permute-start.26) | collective-permute-done | bytes 458784 | tf_op jit(solution)/shard_map/ppermute | solution.py:39
  196.2 5.0 %collective-permute-done.29.refs_3_ = bf16[32,7168]{1,0:T(8,128)(2,1)S(1)} collective-permute-done((bf16[32,7168]{1,0:T(8,128)(2,1)S(1)}, bf16[32,7168]{1,0:T(8,128)(2,1)S(1)}, u32[]{:S(2)}, u32[]{:S(2)}) %collective-permute-start.29) | collective-permute-done | bytes 458784 | tf_op jit(solution)/shard_map/ppermute | solution.py:39
  201.3 0.4 collect.1
  201.7 0.1 collective-permute-start.30
  201.8 3.2 %collective-permute-start.31 = (bf16[32,3584]{1,0:T(8,128)(2,1)S(1)}, bf16[32,3584]{1,0:T(8,128)(2,1)S(1)}, u32[]{:S(2)}, u32[]{:S(2)}) collective-permute-start(bf16[32,3584]{1,0:T(8,128)(2,1)S(1)} %get-tuple-element.62), channel_id=1, source_target_pairs={{0,30},{2,0},{4,2},{6,4},{8,6},{10,8},{12,10},{14,12},{16,14},{18,... | collective-permute-start | bytes 688136 | tf_op jit(solution)/shard_map/ppermute | solution.py:43
  205.0 0.4 collective-permute-start.32
  205.5 3.7 %collective-permute-start.33 = (bf16[32,1792]{1,0:T(8,128)(2,1)S(1)}, bf16[32,1792]{1,0:T(8,128)(2,1)S(1)}, u32[]{:S(2)}, u32[]{:S(2)}) collective-permute-start(bf16[32,1792]{1,0:T(8,128)(2,1)S(1)} %get-tuple-element.64), channel_id=1, source_target_pairs={{0,28},{2,30},{4,0},{6,2},{8,4},{10,6},{12,8},{14,10},{16,12},{18,... | collective-permute-start | bytes 344072 | tf_op jit(solution)/shard_map/ppermute | solution.py:43
  209.2 4.8 %collective-permute-done.32.ahead = bf16[32,1792]{1,0:T(8,128)(2,1)S(1)} collective-permute-done((bf16[32,1792]{1,0:T(8,128)(2,1)S(1)}, bf16[32,1792]{1,0:T(8,128)(2,1)S(1)}, u32[]{:S(2)}, u32[]{:S(2)}) %collective-permute-start.32) | collective-permute-done | bytes 114720 | tf_op jit(solution)/shard_map/ppermute | solution.py:43
  213.9 0.7 collective-permute-done.33.behind
  214.7 0.1 merge.3
  214.8 5.7 %collective-permute-start.34 = (bf16[8,3584]{1,0:T(8,128)(2,1)S(1)}, bf16[8,3584]{1,0:T(8,128)(2,1)S(1)}, u32[]{:S(2)}, u32[]{:S(2)}) collective-permute-start(bf16[8,3584]{1,0:T(8,128)(2,1)S(1)} %get-tuple-element.66), channel_id=1, source_target_pairs={{0,8},{2,10},{4,12},{6,14},{8,16},{10,18},{12,20},{14,22},{16,24},... | collective-permute-start | bytes 172040 | tf_op jit(solution)/shard_map/ppermute | solution.py:43
  220.5 4.3 %collective-permute-start.35 = (bf16[8,3584]{1,0:T(8,128)(2,1)S(1)}, bf16[8,3584]{1,0:T(8,128)(2,1)S(1)}, u32[]{:S(2)}, u32[]{:S(2)}) collective-permute-start(bf16[8,3584]{1,0:T(8,128)(2,1)S(1)} %get-tuple-element.67), channel_id=1, source_target_pairs={{0,16},{2,18},{4,20},{6,22},{8,24},{10,26},{12,28},{14,30},{16,0},... | collective-permute-start | bytes 172040 | tf_op jit(solution)/shard_map/ppermute | solution.py:43
  224.8 5.8 %collective-permute-start.36 = (bf16[8,3584]{1,0:T(8,128)(2,1)S(1)}, bf16[8,3584]{1,0:T(8,128)(2,1)S(1)}, u32[]{:S(2)}, u32[]{:S(2)}) collective-permute-start(bf16[8,3584]{1,0:T(8,128)(2,1)S(1)} %get-tuple-element.68), channel_id=1, source_target_pairs={{0,24},{2,26},{4,28},{6,30},{8,0},{10,2},{12,4},{14,6},{16,8},{18,... | collective-permute-start | bytes 172040 | tf_op jit(solution)/shard_map/ppermute | solution.py:43
  230.6 3.8 %collective-permute-done.35.two = bf16[8,3584]{1,0:T(8,128)(2,1)S(1)} collective-permute-done((bf16[8,3584]{1,0:T(8,128)(2,1)S(1)}, bf16[8,3584]{1,0:T(8,128)(2,1)S(1)}, u32[]{:S(2)}, u32[]{:S(2)}) %collective-permute-start.35) | collective-permute-done | bytes 57376 | tf_op jit(solution)/shard_map/ppermute | solution.py:43
  234.4 0.7 finish.1
  (49 shorter events, 0.3 us)
Async XLA Ops:
  1.2 13.8 %collective-permute-start.11 = (bf16[32,7680]{1,0:T(8,128)(2,1)S(1)}, bf16[32,7680]{1,0:T(8,128)(2,1)S(1)}, u32[]{:S(2)}, u32[]{:S(2)}) collective-permute-start(bf16[32,7680]{1,0:T(8,128)(2,1)S(1)} %get-tuple-element.37.refs_0_), channel_id=1, source_target_pairs={{0,96},{32,0},{64,32},{96,64},{1,97},{33,1},{65,33},{97,65},{2,98}... | collective-permute-start | bytes 1474568 | tf_op jit(solution)/shard_map/ppermute | solution.py:39
  4.5 14.2 %collective-permute-start.6 = (bf16[32,7680]{1,0:T(8,128)(2,1)S(1)}, bf16[32,7680]{1,0:T(8,128)(2,1)S(1)}, u32[]{:S(2)}, u32[]{:S(2)}) collective-permute-start(bf16[32,7680]{1,0:T(8,128)(2,1)S(1)} %get-tuple-element.37.refs_0_), channel_id=1, source_target_pairs={{0,1},{1,0},{2,3},{3,2},{4,5},{5,4},{6,7},{7,6},{8,9},{9,8},{10,11... | collective-permute-start | bytes 1474568 | tf_op jit(solution)/shard_map/ppermute | solution.py:47
  4.5 15.3 %collective-permute-start = (bf16[32,7680]{1,0:T(8,128)(2,1)S(1)}, bf16[32,7680]{1,0:T(8,128)(2,1)S(1)}, u32[]{:S(2)}, u32[]{:S(2)}) collective-permute-start(bf16[32,7680]{1,0:T(8,128)(2,1)S(1)} %get-tuple-element.37.refs_0_), channel_id=1, source_target_pairs={{0,32},{32,64},{64,96},{96,0},{1,33},{33,65},{65,97},{97,1},{2,34}... | collective-permute-start | bytes 1474568 | tf_op jit(solution)/shard_map/ppermute | solution.py:39
  4.5 25.4 %collective-permute-start.8 = (bf16[32,7680]{1,0:T(8,128)(2,1)S(1)}, bf16[32,7680]{1,0:T(8,128)(2,1)S(1)}, u32[]{:S(2)}, u32[]{:S(2)}) collective-permute-start(bf16[32,7680]{1,0:T(8,128)(2,1)S(1)} %get-tuple-element.38.refs_1_), channel_id=1, source_target_pairs={{0,32},{32,64},{64,96},{96,0},{1,33},{33,65},{65,97},{97,1},{2,34}... | collective-permute-start | bytes 1474568 | tf_op jit(solution)/shard_map/ppermute | solution.py:39
  5.0 24.9 %collective-permute-start.7 = (bf16[32,7680]{1,0:T(8,128)(2,1)S(1)}, bf16[32,7680]{1,0:T(8,128)(2,1)}, u32[]{:S(2)}, u32[]{:S(2)}) collective-permute-start(bf16[32,7680]{1,0:T(8,128)(2,1)S(1)} %get-tuple-element.38.refs_1_), channel_id=1, source_target_pairs={{0,1},{1,0},{2,3},{3,2},{4,5},{5,4},{6,7},{7,6},{8,9},{9,8},{10,11... | collective-permute-start | bytes 1474568 | tf_op jit(solution)/shard_map/ppermute | solution.py:47
  15.0 45.5 %collective-permute-start.2 = (bf16[32,7680]{1,0:T(8,128)(2,1)S(1)}, bf16[32,7680]{1,0:T(8,128)(2,1)}, u32[]{:S(2)}, u32[]{:S(2)}) collective-permute-start(bf16[32,7680]{1,0:T(8,128)(2,1)S(1)} %get-tuple-element.38.refs_1_), channel_id=1, source_target_pairs={{0,96},{32,0},{64,32},{96,64},{1,97},{33,1},{65,33},{97,65},{2,98}... | collective-permute-start | bytes 1474568 | tf_op jit(solution)/shard_map/ppermute | solution.py:39
  18.7 42.1 %collective-permute-start.12 = (bf16[32,7680]{1,0:T(8,128)(2,1)S(1)}, bf16[32,7680]{1,0:T(8,128)(2,1)}, u32[]{:S(2)}, u32[]{:S(2)}) collective-permute-start(bf16[32,7680]{1,0:T(8,128)(2,1)S(1)} %collective-permute-done.11.refs_8_), channel_id=1, source_target_pairs={{0,1},{1,0},{2,3},{3,2},{4,5},{5,4},{6,7},{7,6},{8,9},{9,8},{10,11... | collective-permute-start | bytes 1474568 | tf_op jit(solution)/shard_map/ppermute | solution.py:47
  19.8 44.3 %collective-permute-start.9 = (bf16[32,7680]{1,0:T(8,128)(2,1)S(1)}, bf16[32,7680]{1,0:T(8,128)(2,1)}, u32[]{:S(2)}, u32[]{:S(2)}) collective-permute-start(bf16[32,7680]{1,0:T(8,128)(2,1)S(1)} %collective-permute-done.refs_4_), channel_id=1, source_target_pairs={{0,1},{1,0},{2,3},{3,2},{4,5},{5,4},{6,7},{7,6},{8,9},{9,8},{10,11... | collective-permute-start | bytes 1474568 | tf_op jit(solution)/shard_map/ppermute | solution.py:47
  29.9 34.2 %collective-permute-start.1 = (bf16[32,7680]{1,0:T(8,128)(2,1)S(1)}, bf16[32,7680]{1,0:T(8,128)(2,1)}, u32[]{:S(2)}, u32[]{:S(2)}) collective-permute-start(bf16[32,7680]{1,0:T(8,128)(2,1)S(1)} %collective-permute-done.refs_4_), channel_id=1, source_target_pairs={{0,32},{32,64},{64,96},{96,0},{1,33},{33,65},{65,97},{97,1},{2,34}... | collective-permute-start | bytes 1474568 | tf_op jit(solution)/shard_map/ppermute | solution.py:39
  29.9 34.8 %collective-permute-start.10 = (bf16[32,7680]{1,0:T(8,128)(2,1)S(1)}, bf16[32,7680]{1,0:T(8,128)(2,1)}, u32[]{:S(2)}, u32[]{:S(2)}) collective-permute-start(bf16[32,7680]{1,0:T(8,128)(2,1)S(1)} %collective-permute-done.8.refs_5_), channel_id=1, source_target_pairs={{0,1},{1,0},{2,3},{3,2},{4,5},{5,4},{6,7},{7,6},{8,9},{9,8},{10,11... | collective-permute-start | bytes 1474568 | tf_op jit(solution)/shard_map/ppermute | solution.py:47
  36.5 42.6 %all-to-all-start = ((bf16[16,16,512]{2,1,0:T(8,128)(2,1)}), bf16[16,16,512]{2,1,0:T(8,128)(2,1)S(1)}, u32[]{:S(2)}, u32[]{:S(2)}) async-start(bf16[16,16,512]{2,1,0:T(8,128)(2,1)} %bitcast.4), calls=%async_computation | async-start | bytes 524288 | tf_op jit(solution)/shard_map/all_to_all | solution.py:571
  60.5 4.4 %collective-permute-start.13 = (bf16[32,7680]{1,0:T(8,128)(2,1)}, bf16[32,7680]{1,0:T(8,128)(2,1)S(1)}, u32[]{:S(2)}, u32[]{:S(2)}) collective-permute-start(bf16[32,7680]{1,0:T(8,128)(2,1)} %collective-permute-done.2.refs_9_), channel_id=1, source_target_pairs={{0,1},{1,0},{2,3},{3,2},{4,5},{5,4},{6,7},{7,6},{8,9},{9,8},{10,11... | collective-permute-start | bytes 1474568 | tf_op jit(solution)/shard_map/ppermute | solution.py:47
  60.9 14.5 %collective-permute-start.3 = (bf16[32,7680]{1,0:T(8,128)(2,1)}, bf16[32,7680]{1,0:T(8,128)(2,1)}, u32[]{:S(2)}, u32[]{:S(2)}) collective-permute-start(bf16[32,7680]{1,0:T(8,128)(2,1)} %collective-permute-done.2.refs_9_), channel_id=1, source_target_pairs={{0,96},{32,0},{64,32},{96,64},{1,97},{33,1},{65,33},{97,65},{2,98}... | collective-permute-start | bytes 1474568 | tf_op jit(solution)/shard_map/ppermute | solution.py:39
  64.1 100.5 %collective-permute-start.23 = (bf16[7168,128]{1,0:T(8,128)(2,1)}, bf16[7168,128]{1,0:T(8,128)(2,1)}, u32[]{:S(2)}, u32[]{:S(2)}) collective-permute-start(bf16[7168,128]{1,0:T(8,128)(2,1)} %gate_a.1), channel_id=1, source_target_pairs={{0,1},{1,0},{2,3},{3,2},{4,5},{5,4},{6,7},{7,6},{8,9},{9,8},{10,11... | collective-permute-start | bytes 5505032 | tf_op jit(solution)/shard_map/ppermute | solution.py:47
  64.1 102.0 %collective-permute-start.24 = (bf16[7168,128]{1,0:T(8,128)(2,1)}, bf16[7168,128]{1,0:T(8,128)(2,1)}, u32[]{:S(2)}, u32[]{:S(2)}) collective-permute-start(bf16[7168,128]{1,0:T(8,128)(2,1)} %up_a.1), channel_id=1, source_target_pairs={{0,1},{1,0},{2,3},{3,2},{4,5},{5,4},{6,7},{7,6},{8,9},{9,8},{10,11... | collective-permute-start | bytes 5505032 | tf_op jit(solution)/shard_map/ppermute | solution.py:47
  64.6 101.5 %collective-permute-start.25 = (bf16[128,7168]{1,0:T(8,128)(2,1)}, bf16[128,7168]{1,0:T(8,128)(2,1)}, u32[]{:S(2)}, u32[]{:S(2)}) collective-permute-start(bf16[128,7168]{1,0:T(8,128)(2,1)} %down_a.1), channel_id=1, source_target_pairs={{0,1},{1,0},{2,3},{3,2},{4,5},{5,4},{6,7},{7,6},{8,9},{9,8},{10,11... | collective-permute-start | bytes 5505032 | tf_op jit(solution)/shard_map/ppermute | solution.py:47
  64.9 0.8 copy-start
  65.7 17.5 %collective-permute-start.4 = (bf16[32,7680]{1,0:T(8,128)(2,1)}, bf16[32,7680]{1,0:T(8,128)(2,1)}, u32[]{:S(2)}, u32[]{:S(2)}) collective-permute-start(bf16[32,7680]{1,0:T(8,128)(2,1)} %collective-permute-done.1.refs_0_), channel_id=1, source_target_pairs={{0,1},{1,0},{2,3},{3,2},{4,5},{5,4},{6,7},{7,6},{8,9},{9,8},{10,11... | collective-permute-start | bytes 1474568 | tf_op jit(solution)/shard_map/ppermute | solution.py:47
  75.4 7.9 %collective-permute-start.5 = (bf16[32,7680]{1,0:T(8,128)(2,1)}, bf16[32,7680]{1,0:T(8,128)(2,1)}, u32[]{:S(2)}, u32[]{:S(2)}) collective-permute-start(bf16[32,7680]{1,0:T(8,128)(2,1)} %collective-permute-done.3.refs_1_), channel_id=1, source_target_pairs={{0,1},{1,0},{2,3},{3,2},{4,5},{5,4},{6,7},{7,6},{8,9},{9,8},{10,11... | collective-permute-start | bytes 1474568 | tf_op jit(solution)/shard_map/ppermute | solution.py:47
  79.1 1.0 copy-start.1
  83.2 35.7 %copy-start.4 = (bf16[7168]{0:T(1024)(128)(2,1)S(1)}, bf16[7168]{0:T(1024)(128)(2,1)}, u32[]{:S(2)}) copy-start(bf16[7168]{0:T(1024)(128)(2,1)} %param.21) | copy-start | bytes 43012
  83.2 35.7 %copy-start.3 = (bf16[2,2,7168]{2,1,0:T(2,128)(2,1)S(1)}, bf16[2,2,7168]{2,1,0:T(2,128)(2,1)}, u32[]{:S(2)}) copy-start(bf16[2,2,7168]{2,1,0:T(2,128)(2,1)} %param.18) | copy-start | bytes 172036
  85.6 36.9 %copy-start.5 = (s32[2,2,8]{2,1,0:T(2,128)S(1)}, s32[2,2,8]{2,1,0:T(2,128)}, u32[]{:S(2)}) copy-start(s32[2,2,8]{2,1,0:T(2,128)} %param.23) | copy-start | bytes 388
  85.7 36.9 %copy-start.6 = (s32[2,2,8]{2,1,0:T(2,128)S(1)}, s32[2,2,8]{2,1,0:T(2,128)}, u32[]{:S(2)}) copy-start(s32[2,2,8]{2,1,0:T(2,128)} %param.24) | copy-start | bytes 388
  85.7 36.9 %copy-start.2 = (bf16[7168,16]{0,1:T(8,128)(2,1)S(1)}, bf16[7168,16]{0,1:T(8,128)(2,1)}, u32[]{:S(2)}) copy-start(bf16[7168,16]{0,1:T(8,128)(2,1)} %param.22) | copy-start | bytes 688132
  85.7 7.0 %collective-permute-start.16 = (bf16[32,1792]{1,0:T(8,128)(2,1)S(1)}, bf16[32,1792]{1,0:T(8,128)(2,1)S(1)}, u32[]{:S(2)}, u32[]{:S(2)}) collective-permute-start(bf16[32,1792]{1,0:T(8,128)(2,1)S(1)} %get-tuple-element.42), channel_id=1, source_target_pairs={{0,4},{2,6},{4,8},{6,10},{8,12},{10,14},{12,16},{14,18},{16,20},{1... | collective-permute-start | bytes 344072 | tf_op jit(solution)/shard_map/ppermute | solution.py:43
  86.3 9.4 %collective-permute-start.17 = (bf16[32,1792]{1,0:T(8,128)(2,1)S(1)}, bf16[32,1792]{1,0:T(8,128)(2,1)S(1)}, u32[]{:S(2)}, u32[]{:S(2)}) collective-permute-start(bf16[32,1792]{1,0:T(8,128)(2,1)S(1)} %get-tuple-element.43), channel_id=1, source_target_pairs={{0,28},{2,30},{4,0},{6,2},{8,4},{10,6},{12,8},{14,10},{16,12},{18,... | collective-permute-start | bytes 344072 | tf_op jit(solution)/shard_map/ppermute | solution.py:43
  92.7 8.0 %collective-permute-start.14 = (bf16[32,3584]{1,0:T(8,128)(2,1)S(1)}, bf16[32,3584]{1,0:T(8,128)(2,1)S(1)}, u32[]{:S(2)}, u32[]{:S(2)}) collective-permute-start(bf16[32,3584]{1,0:T(8,128)(2,1)S(1)} %get-tuple-element.40), channel_id=1, source_target_pairs={{0,2},{2,4},{4,6},{6,8},{8,10},{10,12},{12,14},{14,16},{16,18},{18... | collective-permute-start | bytes 688136 | tf_op jit(solution)/shard_map/ppermute | solution.py:43
  95.7 6.4 %collective-permute-start.15 = (bf16[32,3584]{1,0:T(8,128)(2,1)S(1)}, bf16[32,3584]{1,0:T(8,128)(2,1)S(1)}, u32[]{:S(2)}, u32[]{:S(2)}) collective-permute-start(bf16[32,3584]{1,0:T(8,128)(2,1)S(1)} %get-tuple-element.41), channel_id=1, source_target_pairs={{0,30},{2,0},{4,2},{6,4},{8,6},{10,8},{12,10},{14,12},{16,14},{18,... | collective-permute-start | bytes 688136 | tf_op jit(solution)/shard_map/ppermute | solution.py:43
  102.2 10.1 %collective-permute-start.18 = (bf16[8,3584]{1,0:T(8,128)(2,1)S(1)}, bf16[8,3584]{1,0:T(8,128)(2,1)S(1)}, u32[]{:S(2)}, u32[]{:S(2)}) collective-permute-start(bf16[8,3584]{1,0:T(8,128)(2,1)S(1)} %get-tuple-element.45), channel_id=1, source_target_pairs={{0,8},{2,10},{4,12},{6,14},{8,16},{10,18},{12,20},{14,22},{16,24},... | collective-permute-start | bytes 172040 | tf_op jit(solution)/shard_map/ppermute | solution.py:43
  107.4 14.4 %collective-permute-start.19 = (bf16[8,3584]{1,0:T(8,128)(2,1)S(1)}, bf16[8,3584]{1,0:T(8,128)(2,1)S(1)}, u32[]{:S(2)}, u32[]{:S(2)}) collective-permute-start(bf16[8,3584]{1,0:T(8,128)(2,1)S(1)} %get-tuple-element.46), channel_id=1, source_target_pairs={{0,16},{2,18},{4,20},{6,22},{8,24},{10,26},{12,28},{14,30},{16,0},... | collective-permute-start | bytes 172040 | tf_op jit(solution)/shard_map/ppermute | solution.py:43
  112.3 10.2 %collective-permute-start.20 = (bf16[8,3584]{1,0:T(8,128)(2,1)S(1)}, bf16[8,3584]{1,0:T(8,128)(2,1)S(1)}, u32[]{:S(2)}, u32[]{:S(2)}) collective-permute-start(bf16[8,3584]{1,0:T(8,128)(2,1)S(1)} %get-tuple-element.47), channel_id=1, source_target_pairs={{0,24},{2,26},{4,28},{6,30},{8,0},{10,2},{12,4},{14,6},{16,8},{18,... | collective-permute-start | bytes 172040 | tf_op jit(solution)/shard_map/ppermute | solution.py:43
  162.4 16.6 %collective-permute-start.21 = (bf16[32,7296]{1,0:T(8,128)(2,1)S(1)}, bf16[32,7296]{1,0:T(8,128)(2,1)S(1)}, u32[]{:S(2)}, u32[]{:S(2)}) collective-permute-start(bf16[32,7296]{1,0:T(8,128)(2,1)S(1)} %get-tuple-element.52), channel_id=1, source_target_pairs={{0,96},{32,0},{64,32},{96,64},{1,97},{33,1},{65,33},{97,65},{2,98}... | collective-permute-start | bytes 1400840 | tf_op jit(solution)/shard_map/ppermute | solution.py:39
  164.6 18.1 %collective-permute-start.22 = (bf16[32,7296]{1,0:T(8,128)(2,1)S(1)}, bf16[32,7296]{1,0:T(8,128)(2,1)S(1)}, u32[]{:S(2)}, u32[]{:S(2)}) collective-permute-start(bf16[32,7296]{1,0:T(8,128)(2,1)S(1)} %get-tuple-element.53), channel_id=1, source_target_pairs={{0,32},{32,64},{64,96},{96,0},{1,33},{33,65},{65,97},{97,1},{2,34}... | collective-permute-start | bytes 1400840 | tf_op jit(solution)/shard_map/ppermute | solution.py:39
  164.6 24.0 %collective-permute-start.28 = (bf16[32,7296]{1,0:T(8,128)(2,1)S(1)}, bf16[32,7296]{1,0:T(8,128)(2,1)S(1)}, u32[]{:S(2)}, u32[]{:S(2)}) collective-permute-start(bf16[32,7296]{1,0:T(8,128)(2,1)S(1)} %get-tuple-element.59), channel_id=1, source_target_pairs={{0,64},{32,96},{64,0},{96,32},{1,65},{33,97},{65,1},{97,33},{2,66}... | collective-permute-start | bytes 1400840 | tf_op jit(solution)/shard_map/ppermute | solution.py:39
  185.2 11.0 %collective-permute-start.26 = (bf16[32,7168]{1,0:T(8,128)(2,1)S(1)}, bf16[32,7168]{1,0:T(8,128)(2,1)S(1)}, u32[]{:S(2)}, u32[]{:S(2)}) collective-permute-start(bf16[32,7168]{1,0:T(8,128)(2,1)S(1)} %get-tuple-element.57), channel_id=1, source_target_pairs={{0,32},{32,64},{64,96},{96,0},{1,33},{33,65},{65,97},{97,1},{2,34}... | collective-permute-start | bytes 1376264 | tf_op jit(solution)/shard_map/ppermute | solution.py:39
  186.2 10.0 %collective-permute-start.27 = (bf16[32,7168]{1,0:T(8,128)(2,1)S(1)}, bf16[32,7168]{1,0:T(8,128)(2,1)S(1)}, u32[]{:S(2)}, u32[]{:S(2)}) collective-permute-start(bf16[32,7168]{1,0:T(8,128)(2,1)S(1)} %get-tuple-element.58), channel_id=1, source_target_pairs={{0,96},{32,0},{64,32},{96,64},{1,97},{33,1},{65,33},{97,65},{2,98}... | collective-permute-start | bytes 1376264 | tf_op jit(solution)/shard_map/ppermute | solution.py:39
  191.2 10.1 %collective-permute-start.29 = (bf16[32,7168]{1,0:T(8,128)(2,1)S(1)}, bf16[32,7168]{1,0:T(8,128)(2,1)S(1)}, u32[]{:S(2)}, u32[]{:S(2)}) collective-permute-start(bf16[32,7168]{1,0:T(8,128)(2,1)S(1)} %expert_part.3), channel_id=1, source_target_pairs={{0,64},{32,96},{64,0},{96,32},{1,65},{33,97},{65,1},{97,33},{2,66}... | collective-permute-start | bytes 1376264 | tf_op jit(solution)/shard_map/ppermute | solution.py:39
  201.7 13.0 %collective-permute-start.30 = (bf16[32,3584]{1,0:T(8,128)(2,1)S(1)}, bf16[32,3584]{1,0:T(8,128)(2,1)S(1)}, u32[]{:S(2)}, u32[]{:S(2)}) collective-permute-start(bf16[32,3584]{1,0:T(8,128)(2,1)S(1)} %get-tuple-element.61), channel_id=1, source_target_pairs={{0,2},{2,4},{4,6},{6,8},{8,10},{10,12},{12,14},{14,16},{16,18},{18... | collective-permute-start | bytes 688136 | tf_op jit(solution)/shard_map/ppermute | solution.py:43
  201.8 12.8 %collective-permute-start.31 = (bf16[32,3584]{1,0:T(8,128)(2,1)S(1)}, bf16[32,3584]{1,0:T(8,128)(2,1)S(1)}, u32[]{:S(2)}, u32[]{:S(2)}) collective-permute-start(bf16[32,3584]{1,0:T(8,128)(2,1)S(1)} %get-tuple-element.62), channel_id=1, source_target_pairs={{0,30},{2,0},{4,2},{6,4},{8,6},{10,8},{12,10},{14,12},{16,14},{18,... | collective-permute-start | bytes 688136 | tf_op jit(solution)/shard_map/ppermute | solution.py:43
  205.0 8.9 %collective-permute-start.32 = (bf16[32,1792]{1,0:T(8,128)(2,1)S(1)}, bf16[32,1792]{1,0:T(8,128)(2,1)S(1)}, u32[]{:S(2)}, u32[]{:S(2)}) collective-permute-start(bf16[32,1792]{1,0:T(8,128)(2,1)S(1)} %get-tuple-element.63), channel_id=1, source_target_pairs={{0,4},{2,6},{4,8},{6,10},{8,12},{10,14},{12,16},{14,18},{16,20},{1... | collective-permute-start | bytes 344072 | tf_op jit(solution)/shard_map/ppermute | solution.py:43
  205.5 9.2 %collective-permute-start.33 = (bf16[32,1792]{1,0:T(8,128)(2,1)S(1)}, bf16[32,1792]{1,0:T(8,128)(2,1)S(1)}, u32[]{:S(2)}, u32[]{:S(2)}) collective-permute-start(bf16[32,1792]{1,0:T(8,128)(2,1)S(1)} %get-tuple-element.64), channel_id=1, source_target_pairs={{0,28},{2,30},{4,0},{6,2},{8,4},{10,6},{12,8},{14,10},{16,12},{18,... | collective-permute-start | bytes 344072 | tf_op jit(solution)/shard_map/ppermute | solution.py:43
  214.8 15.8 %collective-permute-start.34 = (bf16[8,3584]{1,0:T(8,128)(2,1)S(1)}, bf16[8,3584]{1,0:T(8,128)(2,1)S(1)}, u32[]{:S(2)}, u32[]{:S(2)}) collective-permute-start(bf16[8,3584]{1,0:T(8,128)(2,1)S(1)} %get-tuple-element.66), channel_id=1, source_target_pairs={{0,8},{2,10},{4,12},{6,14},{8,16},{10,18},{12,20},{14,22},{16,24},... | collective-permute-start | bytes 172040 | tf_op jit(solution)/shard_map/ppermute | solution.py:43
  220.5 13.9 %collective-permute-start.35 = (bf16[8,3584]{1,0:T(8,128)(2,1)S(1)}, bf16[8,3584]{1,0:T(8,128)(2,1)S(1)}, u32[]{:S(2)}, u32[]{:S(2)}) collective-permute-start(bf16[8,3584]{1,0:T(8,128)(2,1)S(1)} %get-tuple-element.67), channel_id=1, source_target_pairs={{0,16},{2,18},{4,20},{6,22},{8,24},{10,26},{12,28},{14,30},{16,0},... | collective-permute-start | bytes 172040 | tf_op jit(solution)/shard_map/ppermute | solution.py:43
  224.8 9.5 %collective-permute-start.36 = (bf16[8,3584]{1,0:T(8,128)(2,1)S(1)}, bf16[8,3584]{1,0:T(8,128)(2,1)S(1)}, u32[]{:S(2)}, u32[]{:S(2)}) collective-permute-start(bf16[8,3584]{1,0:T(8,128)(2,1)S(1)} %get-tuple-element.68), channel_id=1, source_target_pairs={{0,24},{2,26},{4,28},{6,30},{8,0},{10,2},{12,4},{14,6},{16,8},{18,... | collective-permute-start | bytes 172040 | tf_op jit(solution)/shard_map/ppermute | solution.py:43

commit v7 on v6

--- a/solution.py
+++ b/solution.py
@@ -34,17 +34,20 @@
 NT = (((1,), (1,)), ((), ()))
 
 
-def shift_x(a, step):
-    n = lax.axis_size("x")
-    return lax.ppermute(a, "x", [(i, (i + step) % n) for i in range(n)])
+def swap_x(a, bits):
+    return lax.ppermute(a, "x", [(i, i ^ bits) for i in range(lax.axis_size("x"))])
 
 
 def shift_z(a, step):
     return lax.ppermute(a, ZAX, [(i, (i + step) % RING) for i in range(RING)])
 
 
+def swap_far(a, bits):
+    return lax.ppermute(a, "zb", [(i, i ^ bits) for i in range(FAR)])
+
+
 def swap_core(a):
-    return lax.ppermute(a, "c", [(i, (i + 1) % CORES) for i in range(CORES)])
+    return lax.ppermute(a, "c", [(i, i ^ 1) for i in range(CORES)])
 
 
 def iota(shape, axis):
@@ -55,15 +58,30 @@
     return jnp.where(mask, 1.0, 0.0).astype(bf16)
 
 
-def column(hop, x, nx):
-    step = jnp.where(hop == 1, nx - 1, jnp.where(hop == 2, 1, jnp.where(hop == 3, 2, 0)))
-    return lax.rem(x + step, nx)
+COLUMNS = (0, 1, 3, 2)
+
+
+def column(index, x):
+    return x ^ jnp.where(index == 2, 3, jnp.where(index == 3, 2, index))
+
+
+STEPS = (0, 1, RING - 1, 2, RING - 2)
 
 
 def chip_at(place, where_ref):
-    group, block = place // FAR, lax.rem(place, FAR)
-    step = jnp.where(group == 2, RING - 1, jnp.where(group == 3, 2, group))
-    return lax.rem(NEAR * where_ref[1] + where_ref[2] + step + NEAR * block, RING)
+    group, bits = place // FAR, lax.rem(place, FAR)
+    step = 0
+    for i, value in enumerate(STEPS):
+        step = jnp.where(group == i, value, step)
+    chip = lax.rem(NEAR * where_ref[1] + where_ref[2] + step, RING)
+    return NEAR * ((chip // NEAR) ^ bits) + lax.rem(chip, NEAR)
+
+
+def of_tile(rows, n, tiles):
+    size = rows.shape[0] // len(STEPS)
+    if n < tiles // 2:
+        return rows[: 4 * size]
+    return jnp.concatenate([rows[: 3 * size], rows[4 * size :]], axis=0)
 
 
 def smem():
@@ -133,7 +151,7 @@
         shape = (rows, rows)
         to, source = iota(shape, 0), iota(shape, 1)
         hop = lax.rem(to // tok, nx)
-        head = column(hop, where_ref[0], nx) * RING + to // (tok * nx)
+        head = column(hop, where_ref[0]) * RING + to // (tok * nx)
         take = (lax.rem(to, tok) == source // heads) & (head == lax.rem(source, heads))
         out[...] = jnp.dot(one_hot(take), held[...], preferred_element_type=f32).astype(bf16)
 
@@ -199,13 +217,8 @@
     own[:, cols] = got[:size]
     right[:, cols] = got[size : 2 * size].astype(bf16)
     left[:, cols] = got[2 * size : 3 * size].astype(bf16)
-    rows = got[3 * size :].astype(bf16)
-    if n * TILE < width:
-        ahead[:, cols] = rows
-    else:
-        block, cols = size // FAR, pl.ds(n * TILE - width, TILE)
-        behind[pl.ds(block, size - block), cols] = rows[: size - block]
-        behind[pl.ds(0, block), cols] = rows[size - block :]
+    last, at = (ahead, n * TILE) if n * TILE < width else (behind, n * TILE - width)
+    last[:, pl.ds(at, TILE)] = got[3 * size :].astype(bf16)
 
 
 def row_shapes(size, width):
@@ -232,7 +245,7 @@
     values = lax.dot_general(arrived[...], up, NT, preferred_element_type=f32)
     hop = lax.rem(iota(values.shape, 0) // tok, nx)
     values = jnp.where(hop == first + iota(values.shape, 1) // VH, values, 0.0).astype(bf16)
-    shape = (RING * HALVES * tok, arrived.shape[0])
+    shape = (len(STEPS) * FAR * HALVES * tok, arrived.shape[0])
     row, source = iota(shape, 0), iota(shape, 1)
     chip = chip_at(row // (HALVES * tok), where_ref)
     take = (source // (tok * nx) == chip) & (lax.rem(source, tok) == lax.rem(row, tok))
@@ -242,8 +255,9 @@
         for c in range(HALVES)
     ]
     values = jnp.concatenate(taken, axis=1)
-    for n in range(outs[0].shape[1] // TILE):
-        got = jnp.dot(values, tiles_of(pieces, LAT, n), preferred_element_type=f32)
+    tiles = outs[0].shape[1] // TILE
+    for n in range(tiles):
+        got = jnp.dot(of_tile(values, n, tiles), tiles_of(pieces, LAT, n), preferred_element_type=f32)
         cols = pl.ds(n * TILE, TILE)
         if last:
             put_rows(before[:, cols] + got, outs, n)
@@ -278,7 +292,7 @@
     table = tokens[:, pl.ds(half, EXTRA)]
     shape = (nx * CAP, EXTRA)
     row, place = iota(shape, 0), iota(shape, 1)
-    expert = FAR * column(row // CAP, where_ref[0], nx) + where_ref[1]
+    expert = FAR * column(row // CAP, where_ref[0]) + where_ref[1]
     hot = one_hot(place == lax.rem(row, CAP) * EXPERTS + expert)
     got = lax.dot_general(hot, table, NT, preferred_element_type=f32)
     shape = (SLOTS, count)
@@ -301,7 +315,7 @@
     got = jnp.dot(sels[0], table, preferred_element_type=f32).astype(bf16)
     for r in range(nx):
         outs[r][:, pl.ds(HALVES * half, EXTRA)] = got[r * SLOTS : (r + 1) * SLOTS]
-    shape = (count, count)
+    shape = (spread.shape[0], count)
     row, token = iota(shape, 0), iota(shape, 1)
     chip = chip_at(row // (HALVES * tok), where_ref)
     take = (token // (HALVES * tok) == chip) & (lax.rem(token, HALVES * tok) == lax.rem(row, HALVES * tok))
@@ -316,7 +330,7 @@
     return pl.pallas_call(
         functools.partial(dispatch_kernel, tok, nx),
         out_shape=(jax.ShapeDtypeStruct((SLOTS, full), bf16),) * nx
-        + (jax.ShapeDtypeStruct((count, HALVES * nx * SLOTS), bf16),),
+        + (jax.ShapeDtypeStruct((count // NEAR * len(STEPS), HALVES * nx * SLOTS), bf16),),
         in_specs=[smem(), vmem()],
         out_specs=[vmem()] * (nx + 1),
         compiler_params=params(12),
@@ -407,8 +421,10 @@
 
 def collect_kernel(count, spread, *refs):
     parts, outs = refs[:count], refs[count:]
-    for n in range(outs[0].shape[1] // TILE):
-        put_rows(jnp.dot(spread[...], tiles_of(parts, 0, n), preferred_element_type=f32), outs, n)
+    tiles = outs[0].shape[1] // TILE
+    for n in range(tiles):
+        got = jnp.dot(of_tile(spread[...], n, tiles), tiles_of(parts, 0, n), preferred_element_type=f32)
+        put_rows(got, outs, n)
 
 
 def collect(spread, parts):
@@ -416,7 +432,7 @@
     count = len(parts)
     return pl.pallas_call(
         functools.partial(collect_kernel, count),
-        out_shape=row_shapes(spread.shape[0] // NEAR, width),
+        out_shape=row_shapes(spread.shape[0] // len(STEPS), width),
         in_specs=[vmem()] * (count + 1),
         out_specs=[vmem()] * 5,
         compiler_params=params(12),
@@ -535,7 +551,7 @@
     ahead = shift_z(ahead, 2)
     behind = shift_z(behind, -2)
     first, *sent = merge(own, right, left, ahead, behind)
-    others = [shift_z(sent[0], NEAR), shift_z(sent[1], 2 * NEAR), shift_z(sent[2], -NEAR)]
+    others = [swap_far(rows, k + 1) for k, rows in enumerate(sent)]
     return first, *others
 
 
@@ -562,17 +578,17 @@
     where = jnp.concatenate([where, lengths.astype(jnp.int32)])
 
     tops, lows = pack(value_up.T, out_proj)
-    top_left = shift_x(tops, 1)
-    low_right = shift_x(lows, -1)
-    low_left = shift_x(lows, 1)
-    top_right = shift_x(tops, -1)
+    top_left = swap_x(tops, 1)
+    low_right = swap_x(lows, 3)
+    low_left = swap_x(lows, 1)
+    top_right = swap_x(tops, 3)
 
     outgoing = context_rows(where, nx, cache_kv, new_kv, queries)
     arrived = lax.all_to_all(
         outgoing.reshape(RING, nx * tok, LAT), ZAX, split_axis=0, concat_axis=0, tiled=True
     )
-    top_far = shift_x(top_left, 1)
-    low_far = shift_x(low_right, -1)
+    top_far = swap_x(top_left, 3)
+    low_far = swap_x(low_right, 1)
     near = [tops, lows, swap_core(tops), swap_core(lows)]
     for pair in ((top_left, low_left), (top_right, low_right)):
         near += [*pair, *map(swap_core, pair)]
@@ -593,15 +609,12 @@
 
     ring = lax.all_gather(payload, ZAX, axis=0, tiled=True)
     *sent, spread = dispatch(where, nx, ring, tok)
-    from_right = shift_x(sent[1], -1)
-    from_left = shift_x(sent[2], 1)
-    from_far = shift_x(sent[3], 2)
-    done = expert_part(where, (sent[0], from_right, from_left), weights)
-    back_left = shift_x(done[1], 1)
-    back_right = shift_x(done[2], -1)
-    (far_done,) = expert_part(where, (from_far,), weights)
-    back_far = shift_x(far_done, 2)
-    added = reduce_z(*collect(spread, (done[0], back_left, back_right, back_far)))
+    from_one, from_three, from_two = [swap_x(sent[i], COLUMNS[i]) for i in (1, 2, 3)]
+    done = expert_part(where, (sent[0], from_one, from_three), weights)
+    back_one, back_three = swap_x(done[1], 1), swap_x(done[2], 3)
+    (far_done,) = expert_part(where, (from_two,), weights)
+    back_two = swap_x(far_done, 2)
+    added = reduce_z(*collect(spread, (done[0], back_one, back_three, back_two)))
     return finish(hidden, added, resid.shape)
 
 

time: 235 us -> 230 us (0.979)
  the two profiles are of different devices: /device:TPU:40 before, /device:TPU:164 now
where the time goes in v7:
time: 230 us; the launch traced here: 228 us
  waiting for transfers between devices  82.7 us (36%)
  starting transfers between devices  82.3 us (36%)
  blocking collectives  34.5 us (15%)
  Pallas kernels  25.2 us (11%)
    ppermute x12, waiting for transfers between devices, swap_x(): lax.ppermute(a, 'x', [(i, i ^ bits) for i in range(lax.axis_size('x'))])  49.3 us
    all_gather x1, blocking collectives, layer(): ring = lax.all_gather(payload, ZAX, axis=0, tiled=True)  34.5 us
    ppermute x6, starting transfers between devices, swap_far(): return lax.ppermute(a, 'zb', [(i, i ^ bits) for i in range(FAR)])  27.6 us
    all_to_all x1, starting transfers between devices, layer(): lax.all_to_all(outgoing.reshape(RING, nx * tok, LAT), ZAX, split_axis=0,...  22.9 us
    ppermute x12, starting transfers between devices, swap_x(): lax.ppermute(a, 'x', [(i, i ^ bits) for i in range(lax.axis_size('x'))])  18.1 us
    ppermute x6, waiting for transfers between devices, swap_far(): return lax.ppermute(a, 'zb', [(i, i ^ bits) for i in range(FAR)])  16.8 us
    ppermute x8, starting transfers between devices, shift_z(): return lax.ppermute(a, ZAX, [(i, (i + step) % RING) for i in range(RING)])  12.5 us
    ppermute x8, waiting for transfers between devices, shift_z(): return lax.ppermute(a, ZAX, [(i, (i + step) % RING) for i in range(RING)])  12.5 us
  transfers between devices with their start and end apart: 38, of which 16 were waited for; matrix products, arithmetic and copies ran while one was open for 0% of the time, Pallas kernels for 10%

profile of v7, /device:TPU:164, one launch (start us, length us, event | category | flops | bytes accessed | tf_op | source)
XLA Modules:
  0.0 227.7 jit_solution(544113890613354999)
XLA Ops:
  0.0 1.2 pack.1
  1.2 0.5 collective-permute-start.11
  1.7 1.2 collective-permute-start
  3.0 0.8 collective-permute-start.8
  3.8 10.6 %collective-permute-done.11.refs_8_ = bf16[32,7680]{1,0:T(8,128)(2,1)S(1)} collective-permute-done((bf16[32,7680]{1,0:T(8,128)(2,1)S(1)}, bf16[32,7680]{1,0:T(8,128)(2,1)S(1)}, u32[]{:S(2)}, u32[]{:S(2)}) %collective-permute-start.11) | collective-permute-done | bytes 491552 | tf_op jit(solution)/shard_map/ppermute | solution.py:38
  14.4 0.4 collective-permute-start.2
  14.8 1.1 collective-permute-done.refs_4_
  15.8 10.1 %collective-permute-done.8.refs_5_ = bf16[32,7680]{1,0:T(8,128)(2,1)S(1)} collective-permute-done((bf16[32,7680]{1,0:T(8,128)(2,1)S(1)}, bf16[32,7680]{1,0:T(8,128)(2,1)S(1)}, u32[]{:S(2)}, u32[]{:S(2)}) %collective-permute-start.8) | collective-permute-done | bytes 491552 | tf_op jit(solution)/shard_map/ppermute | solution.py:38
  25.9 1.8 collective-permute-start.1
  27.7 0.7 pad_add_fusion.where_ref
  28.5 5.9 %context_rows.1 = bf16[256,512]{1,0:T(8,128)(2,1)} custom-call(s32[5]{0:T(128)S(1)} %pad_add_fusion.where_ref, bf16[2,576,2048]{2,1,0:T(8,128)(2,1)} %bitcast.20, bf16[2,2,64,576]{3,2,1,0:T(8,128)(2,1)} %queries.1, bf16[2,2,576]{2,1,0:T(2,128)(2,1)} %new.1), custom_call_target="tpu_custom_call" | custom-call | flops 1140850688 | bytes 4718592 | tf_op jit(solution)/shard_map/context_rows/pallas_call | solution.py:164
  34.4 22.9 %all-to-all-start = ((bf16[16,16,512]{2,1,0:T(8,128)(2,1)}), bf16[16,16,512]{2,1,0:T(8,128)(2,1)S(1)}, u32[]{:S(2)}, u32[]{:S(2)}) async-start(bf16[16,16,512]{2,1,0:T(8,128)(2,1)} %bitcast.4), calls=%async_computation | async-start | bytes 524288 | tf_op jit(solution)/shard_map/all_to_all | solution.py:587
  57.3 0.1 collective-permute-start.13
  57.5 2.5 %collective-permute-start.3 = (bf16[32,7680]{1,0:T(8,128)(2,1)}, bf16[32,7680]{1,0:T(8,128)(2,1)}, u32[]{:S(2)}, u32[]{:S(2)}) collective-permute-start(bf16[32,7680]{1,0:T(8,128)(2,1)} %collective-permute-done.2.refs_9_), channel_id=1, source_target_pairs={{0,32},{32,0},{64,96},{96,64},{1,33},{33,1},{65,97},{97,65},{2,34}... | collective-permute-start | bytes 1474568 | tf_op jit(solution)/shard_map/ppermute | solution.py:38
  59.9 0.1 collective-permute-start.23
  60.0 0.4 collective-permute-start.24
  60.4 0.1 collective-permute-start.25
  60.6 0.8 copy-done
  61.4 0.4 collective-permute-start.4
  61.7 10.2 %collective-permute-done.3.refs_1_ = bf16[32,7680]{1,0:T(8,128)(2,1)} collective-permute-done((bf16[32,7680]{1,0:T(8,128)(2,1)}, bf16[32,7680]{1,0:T(8,128)(2,1)}, u32[]{:S(2)}, u32[]{:S(2)}) %collective-permute-start.3) | collective-permute-done | bytes 491552 | tf_op jit(solution)/shard_map/ppermute | solution.py:38
  72.0 4.1 %all-to-all-done = bf16[16,16,512]{2,1,0:T(8,128)(2,1)S(1)} async-done(((bf16[16,16,512]{2,1,0:T(8,128)(2,1)}), bf16[16,16,512]{2,1,0:T(8,128)(2,1)S(1)}, u32[]{:S(2)}, u32[]{:S(2)}) %all-to-all-start) | async-done | bytes 262176 | tf_op jit(solution)/shard_map/all_to_all | solution.py:587
  76.0 1.0 copy-done.1
  77.1 3.0 %attend_part.2.refs_4_ = f32[128,3584]{1,0:T(8,128)S(1)} custom-call(s32[5]{0:T(128)S(1)} %pad_add_fusion.where_ref, bf16[256,512]{1,0:T(8,128)(2,1)S(1)} %bitcast.15, bf16[32,7680]{1,0:T(8,128)(2,1)S(1)} %get-tuple-element.37.refs_0_, bf16[32,7680]{1,0:T(8,128)(2,1)S(1)} %get-tuple-element.38.refs_1_, bf16[32,7680]{1,0:T(8,128)(2,1)S(1)} %collective-permute-done.6.refs_2_, ...), custom_call_target="tpu_custom_call" | custom-call | flops 1409286144 | bytes 5505024 | tf_op jit(solution)/shard_map/attend_part/pallas_call | solution.py:274
  80.2 2.4 %attend_part.3 = (f32[32,3584]{1,0:T(8,128)S(1)}, bf16[32,3584]{1,0:T(8,128)(2,1)S(1)}, bf16[32,3584]{1,0:T(8,128)(2,1)S(1)}, bf16[32,1792]{1,0:T(8,128)(2,1)S(1)}, bf16[32,1792]{1,0:T(8,128)(2,1)S(1)}) custom-call(s32[5]{0:T(128)S(1)} %pad_add_fusion.where_ref, bf16[256,512]{1,0:T(8,128)(2,1)S(1)} %bitcast.16, ...), custom_call_target="tpu_custom_call" | custom-call | flops 469762048 | bytes 1835008 | tf_op jit(solution)/shard_map/attend_part/pallas_call | solution.py:274
  82.6 0.0 copy-start.5
  82.6 2.3 %collective-permute-start.16 = (bf16[32,1792]{1,0:T(8,128)(2,1)S(1)}, bf16[32,1792]{1,0:T(8,128)(2,1)S(1)}, u32[]{:S(2)}, u32[]{:S(2)}) collective-permute-start(bf16[32,1792]{1,0:T(8,128)(2,1)S(1)} %get-tuple-element.42), channel_id=1, source_target_pairs={{0,4},{2,6},{4,8},{6,10},{8,12},{10,14},{12,16},{14,18},{16,20},{1... | collective-permute-start | bytes 344072 | tf_op jit(solution)/shard_map/ppermute | solution.py:42
  84.9 1.9 collective-permute-start.17
  86.8 4.0 %collective-permute-done.16.ahead = bf16[32,1792]{1,0:T(8,128)(2,1)S(1)} collective-permute-done((bf16[32,1792]{1,0:T(8,128)(2,1)S(1)}, bf16[32,1792]{1,0:T(8,128)(2,1)S(1)}, u32[]{:S(2)}, u32[]{:S(2)}) %collective-permute-start.16) | collective-permute-done | bytes 114720 | tf_op jit(solution)/shard_map/ppermute | solution.py:42
  90.8 2.0 collective-permute-start.15
  92.8 4.6 %collective-permute-done.14.right = bf16[32,3584]{1,0:T(8,128)(2,1)S(1)} collective-permute-done((bf16[32,3584]{1,0:T(8,128)(2,1)S(1)}, bf16[32,3584]{1,0:T(8,128)(2,1)S(1)}, u32[]{:S(2)}, u32[]{:S(2)}) %collective-permute-start.14) | collective-permute-done | bytes 229408 | tf_op jit(solution)/shard_map/ppermute | solution.py:42
  97.5 0.0 collective-permute-done.15.left
  97.5 0.1 merge.2
  97.6 5.9 %collective-permute-start.18 = (bf16[8,3584]{1,0:T(8,128)(2,1)S(1)}, bf16[8,3584]{1,0:T(8,128)(2,1)S(1)}, u32[]{:S(2)}, u32[]{:S(2)}) collective-permute-start(bf16[8,3584]{1,0:T(8,128)(2,1)S(1)} %get-tuple-element.45), channel_id=1, source_target_pairs={{0,8},{8,0},{16,24},{24,16},{1,9},{9,1},{17,25},{25,17},{2,10},{10... | collective-permute-start | bytes 172040 | tf_op jit(solution)/shard_map/ppermute | solution.py:46
  103.5 4.6 %collective-permute-start.19 = (bf16[8,3584]{1,0:T(8,128)(2,1)S(1)}, bf16[8,3584]{1,0:T(8,128)(2,1)S(1)}, u32[]{:S(2)}, u32[]{:S(2)}) collective-permute-start(bf16[8,3584]{1,0:T(8,128)(2,1)S(1)} %get-tuple-element.46), channel_id=1, source_target_pairs={{0,16},{8,24},{16,0},{24,8},{1,17},{9,25},{17,1},{25,9},{2,18},{10... | collective-permute-start | bytes 172040 | tf_op jit(solution)/shard_map/ppermute | solution.py:46
  108.1 2.8 %collective-permute-start.20 = (bf16[8,3584]{1,0:T(8,128)(2,1)S(1)}, bf16[8,3584]{1,0:T(8,128)(2,1)S(1)}, u32[]{:S(2)}, u32[]{:S(2)}) collective-permute-start(bf16[8,3584]{1,0:T(8,128)(2,1)S(1)} %get-tuple-element.47), channel_id=1, source_target_pairs={{0,24},{8,16},{16,8},{24,0},{1,25},{9,17},{17,9},{25,1},{2,26},{10... | collective-permute-start | bytes 172040 | tf_op jit(solution)/shard_map/ppermute | solution.py:46
  111.1 8.1 %collective-permute-done.19.two = bf16[8,3584]{1,0:T(8,128)(2,1)S(1)} collective-permute-done((bf16[8,3584]{1,0:T(8,128)(2,1)S(1)}, bf16[8,3584]{1,0:T(8,128)(2,1)S(1)}, u32[]{:S(2)}, u32[]{:S(2)}) %collective-permute-start.19) | collective-permute-done | bytes 57376 | tf_op jit(solution)/shard_map/ppermute | solution.py:46
  119.3 0.6 route.1
  119.9 34.5 %all_gather.3.tokens = bf16[128,3712]{1,0:T(8,128)(2,1)S(1)} all-gather(bf16[8,3712]{1,0:T(8,128)(2,1)S(1)} %get-tuple-element.49), channel_id=1, replica_groups=mesh['rep'=2,'x'=4,'zb'=4,'j'=4,'c'=2] {'zb','j'}, dimensions={0}, use_global_device_ids=true | all-gather | bytes 1009664 | tf_op jit(solution)/shard_map/all_gather | solution.py:610
  154.4 1.3 dispatch.1
  155.7 4.3 %collective-permute-start.21 = (bf16[32,7296]{1,0:T(8,128)(2,1)S(1)}, bf16[32,7296]{1,0:T(8,128)(2,1)S(1)}, u32[]{:S(2)}, u32[]{:S(2)}) collective-permute-start(bf16[32,7296]{1,0:T(8,128)(2,1)S(1)} %get-tuple-element.52), channel_id=1, source_target_pairs={{0,32},{32,0},{64,96},{96,64},{1,33},{33,1},{65,97},{97,65},{2,34}... | collective-permute-start | bytes 1400840 | tf_op jit(solution)/shard_map/ppermute | solution.py:38
  160.1 2.2 collective-permute-start.28
  162.3 4.3 %stage.1 = (bf16[7168,512]{1,0:T(8,128)(2,1)S(1)}, bf16[256,7168]{1,0:T(8,128)(2,1)S(1)}) custom-call(bf16[7168,128]{1,0:T(8,128)(2,1)} %gate_a.1, bf16[7168,128]{1,0:T(8,128)(2,1)} %collective-permute-done.23.gate_b, bf16[7168,128]{1,0:T(8,128)(2,1)} %up_a.1, bf16[7168,128]{1,0:T(8,128)(2,1)} %collective-permute-done.24.up_b, bf16[128,7168]{1,0:T(8,128)(2,1)} %down_a.1, ...), custom_call_target="tpu_custom_call" | custom-call | flops 3670016000 | bytes 11010048 | tf_op jit(solution)/shard_map/stage/pallas_call | solution.py:363
  166.6 0.8 collective-permute-done.21.refs_1_
  167.4 7.5 %collective-permute-done.22.refs_2_ = bf16[32,7296]{1,0:T(8,128)(2,1)S(1)} collective-permute-done((bf16[32,7296]{1,0:T(8,128)(2,1)S(1)}, bf16[32,7296]{1,0:T(8,128)(2,1)S(1)}, u32[]{:S(2)}, u32[]{:S(2)}) %collective-permute-start.22) | collective-permute-done | bytes 466976 | tf_op jit(solution)/shard_map/ppermute | solution.py:38
  174.8 2.5 %expert_part.2 = (bf16[32,7168]{1,0:T(8,128)(2,1)S(1)}, bf16[32,7168]{1,0:T(8,128)(2,1)S(1)}, bf16[32,7168]{1,0:T(8,128)(2,1)S(1)}) custom-call(s32[5]{0:T(128)S(1)} %pad_add_fusion.where_ref, bf16[32,7296]{1,0:T(8,128)(2,1)S(1)} %get-tuple-element.51.refs_0_, bf16[32,7296]{1,0:T(8,128)(2,1)S(1)} %collective-permute-done.21.refs_1_, ...), custom_call_target="tpu_custom_call" | custom-call | flops 2113929216 | bytes 1376256 | tf_op jit(solution)/shard_map/expert_part/pallas_call | solution.py:410
  177.4 0.1 collective-permute-start.26
  177.5 0.4 collective-permute-start.27
  177.9 2.6 %expert_part.3 = bf16[32,7168]{1,0:T(8,128)(2,1)S(1)} custom-call(s32[5]{0:T(128)S(1)} %pad_add_fusion.where_ref, bf16[32,7296]{1,0:T(8,128)(2,1)S(1)} %collective-permute-done.28.refs_0_, bf16[7168,512]{1,0:T(8,128)(2,1)S(1)} %get-tuple-element.54.refs_3_.refs_1_, bf16[256,7168]{1,0:T(8,128)(2,1)S(1)} %get-tuple-element.55.refs_4_.refs_2_), custom_call_target="tpu_custom_call" | custom-call | flops 704643072 | bytes 458752 | tf_op jit(solution)/shard_map/expert_part/pallas_call | solution.py:410
  180.5 3.8 %collective-permute-start.29 = (bf16[32,7168]{1,0:T(8,128)(2,1)S(1)}, bf16[32,7168]{1,0:T(8,128)(2,1)S(1)}, u32[]{:S(2)}, u32[]{:S(2)}) collective-permute-start(bf16[32,7168]{1,0:T(8,128)(2,1)S(1)} %expert_part.3), channel_id=1, source_target_pairs={{0,64},{32,96},{64,0},{96,32},{1,65},{33,97},{65,1},{97,33},{2,66}... | collective-permute-start | bytes 1376264 | tf_op jit(solution)/shard_map/ppermute | solution.py:38
  184.3 2.9 %collective-permute-done.26.refs_1_ = bf16[32,7168]{1,0:T(8,128)(2,1)S(1)} collective-permute-done((bf16[32,7168]{1,0:T(8,128)(2,1)S(1)}, bf16[32,7168]{1,0:T(8,128)(2,1)S(1)}, u32[]{:S(2)}, u32[]{:S(2)}) %collective-permute-start.26) | collective-permute-done | bytes 458784 | tf_op jit(solution)/shard_map/ppermute | solution.py:38
  187.2 6.2 %collective-permute-done.27.refs_2_ = bf16[32,7168]{1,0:T(8,128)(2,1)S(1)} collective-permute-done((bf16[32,7168]{1,0:T(8,128)(2,1)S(1)}, bf16[32,7168]{1,0:T(8,128)(2,1)S(1)}, u32[]{:S(2)}, u32[]{:S(2)}) %collective-permute-start.27) | collective-permute-done | bytes 458784 | tf_op jit(solution)/shard_map/ppermute | solution.py:38
  193.4 0.4 collect.1
  193.8 0.1 collective-permute-start.30
  194.0 2.0 collective-permute-start.31
  196.0 0.8 collective-permute-start.32
  196.8 3.3 %collective-permute-start.33 = (bf16[32,1792]{1,0:T(8,128)(2,1)S(1)}, bf16[32,1792]{1,0:T(8,128)(2,1)S(1)}, u32[]{:S(2)}, u32[]{:S(2)}) collective-permute-start(bf16[32,1792]{1,0:T(8,128)(2,1)S(1)} %get-tuple-element.64), channel_id=1, source_target_pairs={{0,28},{2,30},{4,0},{6,2},{8,4},{10,6},{12,8},{14,10},{16,12},{18,... | collective-permute-start | bytes 344072 | tf_op jit(solution)/shard_map/ppermute | solution.py:42
  200.1 3.0 %collective-permute-done.32.ahead = bf16[32,1792]{1,0:T(8,128)(2,1)S(1)} collective-permute-done((bf16[32,1792]{1,0:T(8,128)(2,1)S(1)}, bf16[32,1792]{1,0:T(8,128)(2,1)S(1)}, u32[]{:S(2)}, u32[]{:S(2)}) %collective-permute-start.32) | collective-permute-done | bytes 114720 | tf_op jit(solution)/shard_map/ppermute | solution.py:42
  203.1 0.9 collective-permute-done.33.behind
  204.0 0.1 merge.3
  204.1 5.4 %collective-permute-start.34 = (bf16[8,3584]{1,0:T(8,128)(2,1)S(1)}, bf16[8,3584]{1,0:T(8,128)(2,1)S(1)}, u32[]{:S(2)}, u32[]{:S(2)}) collective-permute-start(bf16[8,3584]{1,0:T(8,128)(2,1)S(1)} %get-tuple-element.66), channel_id=1, source_target_pairs={{0,8},{8,0},{16,24},{24,16},{1,9},{9,1},{17,25},{25,17},{2,10},{10... | collective-permute-start | bytes 172040 | tf_op jit(solution)/shard_map/ppermute | solution.py:46
  209.5 8.9 %collective-permute-start.35 = (bf16[8,3584]{1,0:T(8,128)(2,1)S(1)}, bf16[8,3584]{1,0:T(8,128)(2,1)S(1)}, u32[]{:S(2)}, u32[]{:S(2)}) collective-permute-start(bf16[8,3584]{1,0:T(8,128)(2,1)S(1)} %get-tuple-element.67), channel_id=1, source_target_pairs={{0,16},{8,24},{16,0},{24,8},{1,17},{9,25},{17,1},{25,9},{2,18},{10... | collective-permute-start | bytes 172040 | tf_op jit(solution)/shard_map/ppermute | solution.py:46
  218.5 5.2 %collective-permute-done.35.two = bf16[8,3584]{1,0:T(8,128)(2,1)S(1)} collective-permute-done((bf16[8,3584]{1,0:T(8,128)(2,1)S(1)}, bf16[8,3584]{1,0:T(8,128)(2,1)S(1)}, u32[]{:S(2)}, u32[]{:S(2)}) %collective-permute-start.35) | collective-permute-done | bytes 57376 | tf_op jit(solution)/shard_map/ppermute | solution.py:46
  223.6 3.4 %collective-permute-done.36.three = bf16[8,3584]{1,0:T(8,128)(2,1)S(1)} collective-permute-done((bf16[8,3584]{1,0:T(8,128)(2,1)S(1)}, bf16[8,3584]{1,0:T(8,128)(2,1)S(1)}, u32[]{:S(2)}, u32[]{:S(2)}) %collective-permute-start.36) | collective-permute-done | bytes 57376 | tf_op jit(solution)/shard_map/ppermute | solution.py:46
  227.1 0.7 finish.1
  (49 shorter events, 0.3 us)
Async XLA Ops:
  1.2 13.2 %collective-permute-start.11 = (bf16[32,7680]{1,0:T(8,128)(2,1)S(1)}, bf16[32,7680]{1,0:T(8,128)(2,1)S(1)}, u32[]{:S(2)}, u32[]{:S(2)}) collective-permute-start(bf16[32,7680]{1,0:T(8,128)(2,1)S(1)} %get-tuple-element.37.refs_0_), channel_id=1, source_target_pairs={{0,96},{32,64},{64,32},{96,0},{1,97},{33,65},{65,33},{97,1},{2,98}... | collective-permute-start | bytes 1474568 | tf_op jit(solution)/shard_map/ppermute | solution.py:38
  1.7 13.0 %collective-permute-start.6 = (bf16[32,7680]{1,0:T(8,128)(2,1)S(1)}, bf16[32,7680]{1,0:T(8,128)(2,1)S(1)}, u32[]{:S(2)}, u32[]{:S(2)}) collective-permute-start(bf16[32,7680]{1,0:T(8,128)(2,1)S(1)} %get-tuple-element.37.refs_0_), channel_id=1, source_target_pairs={{0,1},{1,0},{2,3},{3,2},{4,5},{5,4},{6,7},{7,6},{8,9},{9,8},{10,11... | collective-permute-start | bytes 1474568 | tf_op jit(solution)/shard_map/ppermute | solution.py:50
  1.7 14.1 %collective-permute-start = (bf16[32,7680]{1,0:T(8,128)(2,1)S(1)}, bf16[32,7680]{1,0:T(8,128)(2,1)S(1)}, u32[]{:S(2)}, u32[]{:S(2)}) collective-permute-start(bf16[32,7680]{1,0:T(8,128)(2,1)S(1)} %get-tuple-element.37.refs_0_), channel_id=1, source_target_pairs={{0,32},{32,0},{64,96},{96,64},{1,33},{33,1},{65,97},{97,65},{2,34}... | collective-permute-start | bytes 1474568 | tf_op jit(solution)/shard_map/ppermute | solution.py:38
  3.0 22.9 %collective-permute-start.8 = (bf16[32,7680]{1,0:T(8,128)(2,1)S(1)}, bf16[32,7680]{1,0:T(8,128)(2,1)S(1)}, u32[]{:S(2)}, u32[]{:S(2)}) collective-permute-start(bf16[32,7680]{1,0:T(8,128)(2,1)S(1)} %get-tuple-element.38.refs_1_), channel_id=1, source_target_pairs={{0,32},{32,0},{64,96},{96,64},{1,33},{33,1},{65,97},{97,65},{2,34}... | collective-permute-start | bytes 1474568 | tf_op jit(solution)/shard_map/ppermute | solution.py:38
  3.8 24.0 %collective-permute-start.7 = (bf16[32,7680]{1,0:T(8,128)(2,1)S(1)}, bf16[32,7680]{1,0:T(8,128)(2,1)}, u32[]{:S(2)}, u32[]{:S(2)}) collective-permute-start(bf16[32,7680]{1,0:T(8,128)(2,1)S(1)} %get-tuple-element.38.refs_1_), channel_id=1, source_target_pairs={{0,1},{1,0},{2,3},{3,2},{4,5},{5,4},{6,7},{7,6},{8,9},{9,8},{10,11... | collective-permute-start | bytes 1474568 | tf_op jit(solution)/shard_map/ppermute | solution.py:50
  14.4 42.9 %collective-permute-start.2 = (bf16[32,7680]{1,0:T(8,128)(2,1)S(1)}, bf16[32,7680]{1,0:T(8,128)(2,1)}, u32[]{:S(2)}, u32[]{:S(2)}) collective-permute-start(bf16[32,7680]{1,0:T(8,128)(2,1)S(1)} %get-tuple-element.38.refs_1_), channel_id=1, source_target_pairs={{0,96},{32,64},{64,32},{96,0},{1,97},{33,65},{65,33},{97,1},{2,98}... | collective-permute-start | bytes 1474568 | tf_op jit(solution)/shard_map/ppermute | solution.py:38
  14.8 42.7 %collective-permute-start.12 = (bf16[32,7680]{1,0:T(8,128)(2,1)S(1)}, bf16[32,7680]{1,0:T(8,128)(2,1)}, u32[]{:S(2)}, u32[]{:S(2)}) collective-permute-start(bf16[32,7680]{1,0:T(8,128)(2,1)S(1)} %collective-permute-done.11.refs_8_), channel_id=1, source_target_pairs={{0,1},{1,0},{2,3},{3,2},{4,5},{5,4},{6,7},{7,6},{8,9},{9,8},{10,11... | collective-permute-start | bytes 1474568 | tf_op jit(solution)/shard_map/ppermute | solution.py:50
  15.8 44.1 %collective-permute-start.9 = (bf16[32,7680]{1,0:T(8,128)(2,1)S(1)}, bf16[32,7680]{1,0:T(8,128)(2,1)}, u32[]{:S(2)}, u32[]{:S(2)}) collective-permute-start(bf16[32,7680]{1,0:T(8,128)(2,1)S(1)} %collective-permute-done.refs_4_), channel_id=1, source_target_pairs={{0,1},{1,0},{2,3},{3,2},{4,5},{5,4},{6,7},{7,6},{8,9},{9,8},{10,11... | collective-permute-start | bytes 1474568 | tf_op jit(solution)/shard_map/ppermute | solution.py:50
  25.9 34.1 %collective-permute-start.1 = (bf16[32,7680]{1,0:T(8,128)(2,1)S(1)}, bf16[32,7680]{1,0:T(8,128)(2,1)}, u32[]{:S(2)}, u32[]{:S(2)}) collective-permute-start(bf16[32,7680]{1,0:T(8,128)(2,1)S(1)} %collective-permute-done.refs_4_), channel_id=1, source_target_pairs={{0,96},{32,64},{64,32},{96,0},{1,97},{33,65},{65,33},{97,1},{2,98}... | collective-permute-start | bytes 1474568 | tf_op jit(solution)/shard_map/ppermute | solution.py:38
  27.7 32.7 %collective-permute-start.10 = (bf16[32,7680]{1,0:T(8,128)(2,1)S(1)}, bf16[32,7680]{1,0:T(8,128)(2,1)}, u32[]{:S(2)}, u32[]{:S(2)}) collective-permute-start(bf16[32,7680]{1,0:T(8,128)(2,1)S(1)} %collective-permute-done.8.refs_5_), channel_id=1, source_target_pairs={{0,1},{1,0},{2,3},{3,2},{4,5},{5,4},{6,7},{7,6},{8,9},{9,8},{10,11... | collective-permute-start | bytes 1474568 | tf_op jit(solution)/shard_map/ppermute | solution.py:50
  34.4 41.7 %all-to-all-start = ((bf16[16,16,512]{2,1,0:T(8,128)(2,1)}), bf16[16,16,512]{2,1,0:T(8,128)(2,1)S(1)}, u32[]{:S(2)}, u32[]{:S(2)}) async-start(bf16[16,16,512]{2,1,0:T(8,128)(2,1)} %bitcast.4), calls=%async_computation | async-start | bytes 524288 | tf_op jit(solution)/shard_map/all_to_all | solution.py:587
  57.3 3.3 %collective-permute-start.13 = (bf16[32,7680]{1,0:T(8,128)(2,1)}, bf16[32,7680]{1,0:T(8,128)(2,1)S(1)}, u32[]{:S(2)}, u32[]{:S(2)}) collective-permute-start(bf16[32,7680]{1,0:T(8,128)(2,1)} %collective-permute-done.2.refs_9_), channel_id=1, source_target_pairs={{0,1},{1,0},{2,3},{3,2},{4,5},{5,4},{6,7},{7,6},{8,9},{9,8},{10,11... | collective-permute-start | bytes 1474568 | tf_op jit(solution)/shard_map/ppermute | solution.py:50
  57.5 14.5 %collective-permute-start.3 = (bf16[32,7680]{1,0:T(8,128)(2,1)}, bf16[32,7680]{1,0:T(8,128)(2,1)}, u32[]{:S(2)}, u32[]{:S(2)}) collective-permute-start(bf16[32,7680]{1,0:T(8,128)(2,1)} %collective-permute-done.2.refs_9_), channel_id=1, source_target_pairs={{0,32},{32,0},{64,96},{96,64},{1,33},{33,1},{65,97},{97,65},{2,34}... | collective-permute-start | bytes 1474568 | tf_op jit(solution)/shard_map/ppermute | solution.py:38
  59.9 100.1 %collective-permute-start.23 = (bf16[7168,128]{1,0:T(8,128)(2,1)}, bf16[7168,128]{1,0:T(8,128)(2,1)}, u32[]{:S(2)}, u32[]{:S(2)}) collective-permute-start(bf16[7168,128]{1,0:T(8,128)(2,1)} %gate_a.1), channel_id=1, source_target_pairs={{0,1},{1,0},{2,3},{3,2},{4,5},{5,4},{6,7},{7,6},{8,9},{9,8},{10,11... | collective-permute-start | bytes 5505032 | tf_op jit(solution)/shard_map/ppermute | solution.py:50
  60.0 102.3 %collective-permute-start.24 = (bf16[7168,128]{1,0:T(8,128)(2,1)}, bf16[7168,128]{1,0:T(8,128)(2,1)}, u32[]{:S(2)}, u32[]{:S(2)}) collective-permute-start(bf16[7168,128]{1,0:T(8,128)(2,1)} %up_a.1), channel_id=1, source_target_pairs={{0,1},{1,0},{2,3},{3,2},{4,5},{5,4},{6,7},{7,6},{8,9},{9,8},{10,11... | collective-permute-start | bytes 5505032 | tf_op jit(solution)/shard_map/ppermute | solution.py:50
  60.4 101.8 %collective-permute-start.25 = (bf16[128,7168]{1,0:T(8,128)(2,1)}, bf16[128,7168]{1,0:T(8,128)(2,1)}, u32[]{:S(2)}, u32[]{:S(2)}) collective-permute-start(bf16[128,7168]{1,0:T(8,128)(2,1)} %down_a.1), channel_id=1, source_target_pairs={{0,1},{1,0},{2,3},{3,2},{4,5},{5,4},{6,7},{7,6},{8,9},{9,8},{10,11... | collective-permute-start | bytes 5505032 | tf_op jit(solution)/shard_map/ppermute | solution.py:50
  60.6 0.8 copy-start
  61.4 18.8 %collective-permute-start.4 = (bf16[32,7680]{1,0:T(8,128)(2,1)}, bf16[32,7680]{1,0:T(8,128)(2,1)}, u32[]{:S(2)}, u32[]{:S(2)}) collective-permute-start(bf16[32,7680]{1,0:T(8,128)(2,1)} %collective-permute-done.1.refs_0_), channel_id=1, source_target_pairs={{0,1},{1,0},{2,3},{3,2},{4,5},{5,4},{6,7},{7,6},{8,9},{9,8},{10,11... | collective-permute-start | bytes 1474568 | tf_op jit(solution)/shard_map/ppermute | solution.py:50
  72.0 8.2 %collective-permute-start.5 = (bf16[32,7680]{1,0:T(8,128)(2,1)}, bf16[32,7680]{1,0:T(8,128)(2,1)}, u32[]{:S(2)}, u32[]{:S(2)}) collective-permute-start(bf16[32,7680]{1,0:T(8,128)(2,1)} %collective-permute-done.3.refs_1_), channel_id=1, source_target_pairs={{0,1},{1,0},{2,3},{3,2},{4,5},{5,4},{6,7},{7,6},{8,9},{9,8},{10,11... | collective-permute-start | bytes 1474568 | tf_op jit(solution)/shard_map/ppermute | solution.py:50
  76.0 1.0 copy-start.1
  80.1 30.8 %copy-start.4 = (bf16[7168]{0:T(1024)(128)(2,1)S(1)}, bf16[7168]{0:T(1024)(128)(2,1)}, u32[]{:S(2)}) copy-start(bf16[7168]{0:T(1024)(128)(2,1)} %param.21) | copy-start | bytes 43012
  80.1 30.8 %copy-start.3 = (bf16[2,2,7168]{2,1,0:T(2,128)(2,1)S(1)}, bf16[2,2,7168]{2,1,0:T(2,128)(2,1)}, u32[]{:S(2)}) copy-start(bf16[2,2,7168]{2,1,0:T(2,128)(2,1)} %param.18) | copy-start | bytes 172036
  82.6 36.7 %copy-start.5 = (s32[2,2,8]{2,1,0:T(2,128)S(1)}, s32[2,2,8]{2,1,0:T(2,128)}, u32[]{:S(2)}) copy-start(s32[2,2,8]{2,1,0:T(2,128)} %param.23) | copy-start | bytes 388
  82.6 36.7 %copy-start.6 = (s32[2,2,8]{2,1,0:T(2,128)S(1)}, s32[2,2,8]{2,1,0:T(2,128)}, u32[]{:S(2)}) copy-start(s32[2,2,8]{2,1,0:T(2,128)} %param.24) | copy-start | bytes 388
  82.6 36.7 %copy-start.2 = (bf16[7168,16]{0,1:T(8,128)(2,1)S(1)}, bf16[7168,16]{0,1:T(8,128)(2,1)}, u32[]{:S(2)}) copy-start(bf16[7168,16]{0,1:T(8,128)(2,1)} %param.22) | copy-start | bytes 688132
  82.6 8.2 %collective-permute-start.16 = (bf16[32,1792]{1,0:T(8,128)(2,1)S(1)}, bf16[32,1792]{1,0:T(8,128)(2,1)S(1)}, u32[]{:S(2)}, u32[]{:S(2)}) collective-permute-start(bf16[32,1792]{1,0:T(8,128)(2,1)S(1)} %get-tuple-element.42), channel_id=1, source_target_pairs={{0,4},{2,6},{4,8},{6,10},{8,12},{10,14},{12,16},{14,18},{16,20},{1... | collective-permute-start | bytes 344072 | tf_op jit(solution)/shard_map/ppermute | solution.py:42
  84.9 5.9 %collective-permute-start.17 = (bf16[32,1792]{1,0:T(8,128)(2,1)S(1)}, bf16[32,1792]{1,0:T(8,128)(2,1)S(1)}, u32[]{:S(2)}, u32[]{:S(2)}) collective-permute-start(bf16[32,1792]{1,0:T(8,128)(2,1)S(1)} %get-tuple-element.43), channel_id=1, source_target_pairs={{0,28},{2,30},{4,0},{6,2},{8,4},{10,6},{12,8},{14,10},{16,12},{18,... | collective-permute-start | bytes 344072 | tf_op jit(solution)/shard_map/ppermute | solution.py:42
  90.8 6.7 %collective-permute-start.14 = (bf16[32,3584]{1,0:T(8,128)(2,1)S(1)}, bf16[32,3584]{1,0:T(8,128)(2,1)S(1)}, u32[]{:S(2)}, u32[]{:S(2)}) collective-permute-start(bf16[32,3584]{1,0:T(8,128)(2,1)S(1)} %get-tuple-element.40), channel_id=1, source_target_pairs={{0,2},{2,4},{4,6},{6,8},{8,10},{10,12},{12,14},{14,16},{16,18},{18... | collective-permute-start | bytes 688136 | tf_op jit(solution)/shard_map/ppermute | solution.py:42
  90.8 6.7 %collective-permute-start.15 = (bf16[32,3584]{1,0:T(8,128)(2,1)S(1)}, bf16[32,3584]{1,0:T(8,128)(2,1)S(1)}, u32[]{:S(2)}, u32[]{:S(2)}) collective-permute-start(bf16[32,3584]{1,0:T(8,128)(2,1)S(1)} %get-tuple-element.41), channel_id=1, source_target_pairs={{0,30},{2,0},{4,2},{6,4},{8,6},{10,8},{12,10},{14,12},{16,14},{18,... | collective-permute-start | bytes 688136 | tf_op jit(solution)/shard_map/ppermute | solution.py:42
  97.6 10.4 %collective-permute-start.18 = (bf16[8,3584]{1,0:T(8,128)(2,1)S(1)}, bf16[8,3584]{1,0:T(8,128)(2,1)S(1)}, u32[]{:S(2)}, u32[]{:S(2)}) collective-permute-start(bf16[8,3584]{1,0:T(8,128)(2,1)S(1)} %get-tuple-element.45), channel_id=1, source_target_pairs={{0,8},{8,0},{16,24},{24,16},{1,9},{9,1},{17,25},{25,17},{2,10},{10... | collective-permute-start | bytes 172040 | tf_op jit(solution)/shard_map/ppermute | solution.py:46
  103.5 15.8 %collective-permute-start.19 = (bf16[8,3584]{1,0:T(8,128)(2,1)S(1)}, bf16[8,3584]{1,0:T(8,128)(2,1)S(1)}, u32[]{:S(2)}, u32[]{:S(2)}) collective-permute-start(bf16[8,3584]{1,0:T(8,128)(2,1)S(1)} %get-tuple-element.46), channel_id=1, source_target_pairs={{0,16},{8,24},{16,0},{24,8},{1,17},{9,25},{17,1},{25,9},{2,18},{10... | collective-permute-start | bytes 172040 | tf_op jit(solution)/shard_map/ppermute | solution.py:46
  108.1 11.2 %collective-permute-start.20 = (bf16[8,3584]{1,0:T(8,128)(2,1)S(1)}, bf16[8,3584]{1,0:T(8,128)(2,1)S(1)}, u32[]{:S(2)}, u32[]{:S(2)}) collective-permute-start(bf16[8,3584]{1,0:T(8,128)(2,1)S(1)} %get-tuple-element.47), channel_id=1, source_target_pairs={{0,24},{8,16},{16,8},{24,0},{1,25},{9,17},{17,9},{25,1},{2,26},{10... | collective-permute-start | bytes 172040 | tf_op jit(solution)/shard_map/ppermute | solution.py:46
  155.7 11.6 %collective-permute-start.21 = (bf16[32,7296]{1,0:T(8,128)(2,1)S(1)}, bf16[32,7296]{1,0:T(8,128)(2,1)S(1)}, u32[]{:S(2)}, u32[]{:S(2)}) collective-permute-start(bf16[32,7296]{1,0:T(8,128)(2,1)S(1)} %get-tuple-element.52), channel_id=1, source_target_pairs={{0,32},{32,0},{64,96},{96,64},{1,33},{33,1},{65,97},{97,65},{2,34}... | collective-permute-start | bytes 1400840 | tf_op jit(solution)/shard_map/ppermute | solution.py:38
  160.1 14.8 %collective-permute-start.22 = (bf16[32,7296]{1,0:T(8,128)(2,1)S(1)}, bf16[32,7296]{1,0:T(8,128)(2,1)S(1)}, u32[]{:S(2)}, u32[]{:S(2)}) collective-permute-start(bf16[32,7296]{1,0:T(8,128)(2,1)S(1)} %get-tuple-element.53), channel_id=1, source_target_pairs={{0,96},{32,64},{64,32},{96,0},{1,97},{33,65},{65,33},{97,1},{2,98}... | collective-permute-start | bytes 1400840 | tf_op jit(solution)/shard_map/ppermute | solution.py:38
  160.1 17.8 %collective-permute-start.28 = (bf16[32,7296]{1,0:T(8,128)(2,1)S(1)}, bf16[32,7296]{1,0:T(8,128)(2,1)S(1)}, u32[]{:S(2)}, u32[]{:S(2)}) collective-permute-start(bf16[32,7296]{1,0:T(8,128)(2,1)S(1)} %get-tuple-element.59), channel_id=1, source_target_pairs={{0,64},{32,96},{64,0},{96,32},{1,65},{33,97},{65,1},{97,33},{2,66}... | collective-permute-start | bytes 1400840 | tf_op jit(solution)/shard_map/ppermute | solution.py:38
  177.4 9.8 %collective-permute-start.26 = (bf16[32,7168]{1,0:T(8,128)(2,1)S(1)}, bf16[32,7168]{1,0:T(8,128)(2,1)S(1)}, u32[]{:S(2)}, u32[]{:S(2)}) collective-permute-start(bf16[32,7168]{1,0:T(8,128)(2,1)S(1)} %get-tuple-element.57), channel_id=1, source_target_pairs={{0,32},{32,0},{64,96},{96,64},{1,33},{33,1},{65,97},{97,65},{2,34}... | collective-permute-start | bytes 1376264 | tf_op jit(solution)/shard_map/ppermute | solution.py:38
  177.5 15.9 %collective-permute-start.27 = (bf16[32,7168]{1,0:T(8,128)(2,1)S(1)}, bf16[32,7168]{1,0:T(8,128)(2,1)S(1)}, u32[]{:S(2)}, u32[]{:S(2)}) collective-permute-start(bf16[32,7168]{1,0:T(8,128)(2,1)S(1)} %get-tuple-element.58), channel_id=1, source_target_pairs={{0,96},{32,64},{64,32},{96,0},{1,97},{33,65},{65,33},{97,1},{2,98}... | collective-permute-start | bytes 1376264 | tf_op jit(solution)/shard_map/ppermute | solution.py:38
  180.5 12.9 %collective-permute-start.29 = (bf16[32,7168]{1,0:T(8,128)(2,1)S(1)}, bf16[32,7168]{1,0:T(8,128)(2,1)S(1)}, u32[]{:S(2)}, u32[]{:S(2)}) collective-permute-start(bf16[32,7168]{1,0:T(8,128)(2,1)S(1)} %expert_part.3), channel_id=1, source_target_pairs={{0,64},{32,96},{64,0},{96,32},{1,65},{33,97},{65,1},{97,33},{2,66}... | collective-permute-start | bytes 1376264 | tf_op jit(solution)/shard_map/ppermute | solution.py:38
  193.8 10.1 %collective-permute-start.30 = (bf16[32,3584]{1,0:T(8,128)(2,1)S(1)}, bf16[32,3584]{1,0:T(8,128)(2,1)S(1)}, u32[]{:S(2)}, u32[]{:S(2)}) collective-permute-start(bf16[32,3584]{1,0:T(8,128)(2,1)S(1)} %get-tuple-element.61), channel_id=1, source_target_pairs={{0,2},{2,4},{4,6},{6,8},{8,10},{10,12},{12,14},{14,16},{16,18},{18... | collective-permute-start | bytes 688136 | tf_op jit(solution)/shard_map/ppermute | solution.py:42
  194.0 10.0 %collective-permute-start.31 = (bf16[32,3584]{1,0:T(8,128)(2,1)S(1)}, bf16[32,3584]{1,0:T(8,128)(2,1)S(1)}, u32[]{:S(2)}, u32[]{:S(2)}) collective-permute-start(bf16[32,3584]{1,0:T(8,128)(2,1)S(1)} %get-tuple-element.62), channel_id=1, source_target_pairs={{0,30},{2,0},{4,2},{6,4},{8,6},{10,8},{12,10},{14,12},{16,14},{18,... | collective-permute-start | bytes 688136 | tf_op jit(solution)/shard_map/ppermute | solution.py:42
  196.0 7.2 %collective-permute-start.32 = (bf16[32,1792]{1,0:T(8,128)(2,1)S(1)}, bf16[32,1792]{1,0:T(8,128)(2,1)S(1)}, u32[]{:S(2)}, u32[]{:S(2)}) collective-permute-start(bf16[32,1792]{1,0:T(8,128)(2,1)S(1)} %get-tuple-element.63), channel_id=1, source_target_pairs={{0,4},{2,6},{4,8},{6,10},{8,12},{10,14},{12,16},{14,18},{16,20},{1... | collective-permute-start | bytes 344072 | tf_op jit(solution)/shard_map/ppermute | solution.py:42
  196.8 7.2 %collective-permute-start.33 = (bf16[32,1792]{1,0:T(8,128)(2,1)S(1)}, bf16[32,1792]{1,0:T(8,128)(2,1)S(1)}, u32[]{:S(2)}, u32[]{:S(2)}) collective-permute-start(bf16[32,1792]{1,0:T(8,128)(2,1)S(1)} %get-tuple-element.64), channel_id=1, source_target_pairs={{0,28},{2,30},{4,0},{6,2},{8,4},{10,6},{12,8},{14,10},{16,12},{18,... | collective-permute-start | bytes 344072 | tf_op jit(solution)/shard_map/ppermute | solution.py:42
  204.1 14.4 %collective-permute-start.34 = (bf16[8,3584]{1,0:T(8,128)(2,1)S(1)}, bf16[8,3584]{1,0:T(8,128)(2,1)S(1)}, u32[]{:S(2)}, u32[]{:S(2)}) collective-permute-start(bf16[8,3584]{1,0:T(8,128)(2,1)S(1)} %get-tuple-element.66), channel_id=1, source_target_pairs={{0,8},{8,0},{16,24},{24,16},{1,9},{9,1},{17,25},{25,17},{2,10},{10... | collective-permute-start | bytes 172040 | tf_op jit(solution)/shard_map/ppermute | solution.py:46
  209.5 14.1 %collective-permute-start.35 = (bf16[8,3584]{1,0:T(8,128)(2,1)S(1)}, bf16[8,3584]{1,0:T(8,128)(2,1)S(1)}, u32[]{:S(2)}, u32[]{:S(2)}) collective-permute-start(bf16[8,3584]{1,0:T(8,128)(2,1)S(1)} %get-tuple-element.67), channel_id=1, source_target_pairs={{0,16},{8,24},{16,0},{24,8},{1,17},{9,25},{17,1},{25,9},{2,18},{10... | collective-permute-start | bytes 172040 | tf_op jit(solution)/shard_map/ppermute | solution.py:46
  218.5 8.6 %collective-permute-start.36 = (bf16[8,3584]{1,0:T(8,128)(2,1)S(1)}, bf16[8,3584]{1,0:T(8,128)(2,1)S(1)}, u32[]{:S(2)}, u32[]{:S(2)}) collective-permute-start(bf16[8,3584]{1,0:T(8,128)(2,1)S(1)} %get-tuple-element.68), channel_id=1, source_target_pairs={{0,24},{8,16},{16,8},{24,0},{1,25},{9,17},{17,9},{25,1},{2,26},{10... | collective-permute-start | bytes 172040 | tf_op jit(solution)/shard_map/ppermute | solution.py:46

commit v8 on v7

--- a/solution.py
+++ b/solution.py
@@ -23,6 +23,8 @@
 FAR = 4
 RING = NEAR * FAR
 SLOTS = RING * CAP
+TURNS = (1, NEAR - 1, 2, 0)
+PARTS = (2 * FAR * CAP, FAR * CAP, FAR * CAP)
 EXTRA = 128
 
 route_scale = 2.827
@@ -285,11 +287,8 @@
 SEND_TILE = 512
 
 
-def dispatch_kernel(tok, nx, where_ref, tokens, *refs):
-    outs, spread = refs[:nx], refs[nx]
-    count, width = tokens.shape
-    half = width - EXTRA
-    table = tokens[:, pl.ds(half, EXTRA)]
+def slot_rows(tok, nx, where_ref, table):
+    count = table.shape[0]
     shape = (nx * CAP, EXTRA)
     row, place = iota(shape, 0), iota(shape, 1)
     expert = FAR * column(row // CAP, where_ref[0]) + where_ref[1]
@@ -297,14 +296,22 @@
     got = lax.dot_general(hot, table, NT, preferred_element_type=f32)
     shape = (SLOTS, count)
     slot, token = iota(shape, 0), iota(shape, 1)
-    parts = []
+    source = slot // CAP
+    turn = sum(jnp.where(source // FAR == i, value, 0) for i, value in enumerate(TURNS))
+    chip = NEAR * lax.rem(source, FAR) + lax.rem(where_ref[2] + turn, NEAR)
+    same = chip == token // (HALVES * tok)
+    half = lax.rem(token // tok, HALVES)
+    rows = []
     for r in range(nx):
         sel = jnp.where(lax.rem(slot, CAP) == 0, got[CAP * r : CAP * r + 1], got[CAP * r + 1 : CAP * r + 2])
-        parts.append(jnp.where(slot // CAP == token // (HALVES * tok), sel, 0.0))
-    sel = jnp.concatenate(parts, axis=0)
-    of_half = lax.rem(iota(sel.shape, 1) // tok, HALVES)
-    sels = [jnp.where(of_half == c, sel, 0.0).astype(bf16) for c in range(HALVES)]
-    both = jnp.concatenate(sels, axis=0)
+        rows.append(jnp.where(same, sel, 0.0))
+    return [[jnp.where(half == c, sel, 0.0) for sel in rows] for c in range(HALVES)]
+
+
+def dispatch_kernel(tok, nx, where_ref, tokens, *outs):
+    half = tokens.shape[1] - EXTRA
+    table = tokens[:, pl.ds(half, EXTRA)]
+    both = jnp.concatenate(sum(slot_rows(tok, nx, where_ref, table), []), axis=0).astype(bf16)
     rows = nx * SLOTS
     for n in range(half // SEND_TILE):
         got = jnp.dot(both, tokens[:, pl.ds(n * SEND_TILE, SEND_TILE)], preferred_element_type=f32).astype(bf16)
@@ -312,16 +319,9 @@
             for r in range(nx):
                 at = c * rows + r * SLOTS
                 outs[r][:, pl.ds(c * half + n * SEND_TILE, SEND_TILE)] = got[at : at + SLOTS]
-    got = jnp.dot(sels[0], table, preferred_element_type=f32).astype(bf16)
+    got = jnp.dot(both[:rows], table, preferred_element_type=f32).astype(bf16)
     for r in range(nx):
         outs[r][:, pl.ds(HALVES * half, EXTRA)] = got[r * SLOTS : (r + 1) * SLOTS]
-    shape = (spread.shape[0], count)
-    row, token = iota(shape, 0), iota(shape, 1)
-    chip = chip_at(row // (HALVES * tok), where_ref)
-    take = (token // (HALVES * tok) == chip) & (lax.rem(token, HALVES * tok) == lax.rem(row, HALVES * tok))
-    for c in range(HALVES):
-        got = lax.dot_general(one_hot(take), sels[c], NT, preferred_element_type=f32)
-        spread[:, pl.ds(c * rows, rows)] = got.astype(bf16)
 
 
 def dispatch(where, nx, tokens, tok):
@@ -329,13 +329,42 @@
     full = HALVES * (width - EXTRA) + EXTRA
     return pl.pallas_call(
         functools.partial(dispatch_kernel, tok, nx),
-        out_shape=(jax.ShapeDtypeStruct((SLOTS, full), bf16),) * nx
-        + (jax.ShapeDtypeStruct((count // NEAR * len(STEPS), HALVES * nx * SLOTS), bf16),),
+        out_shape=(jax.ShapeDtypeStruct((SLOTS, full), bf16),) * nx,
         in_specs=[smem(), vmem()],
-        out_specs=[vmem()] * (nx + 1),
+        out_specs=[vmem()] * nx,
         compiler_params=params(12),
         cost_estimate=cost(2 * nx * SLOTS * count * full, 4 * count * width),
         name="dispatch",
+    )(where, tokens)
+
+
+def plan_kernel(tok, nx, where_ref, tokens, *outs):
+    count, width = tokens.shape
+    halves = slot_rows(tok, nx, where_ref, tokens[:, pl.ds(width - EXTRA, EXTRA)])
+    unit = HALVES * tok
+    at = 0
+    for out, group, size in zip(outs, (1, 3, 0), PARTS):
+        shape = (out.shape[0], count)
+        row, token = iota(shape, 0), iota(shape, 1)
+        take = token // unit == chip_at(group * FAR + row // unit, where_ref)
+        take = take & (lax.rem(token, unit) == lax.rem(row, unit))
+        sel = jnp.concatenate([sel[at : at + size] for rows in halves for sel in rows], axis=0).astype(bf16)
+        out[...] = lax.dot_general(one_hot(take), sel, NT, preferred_element_type=f32).astype(bf16)
+        at += size
+
+
+def plan(where, nx, tokens, tok):
+    count, _ = tokens.shape
+    near = count // NEAR
+    shapes = [(rows * near, HALVES * nx * size) for rows, size in zip((2, 2, 1), PARTS)]
+    return pl.pallas_call(
+        functools.partial(plan_kernel, tok, nx),
+        out_shape=[jax.ShapeDtypeStruct(shape, bf16) for shape in shapes],
+        in_specs=[smem(), vmem()],
+        out_specs=[vmem()] * len(PARTS),
+        compiler_params=params(6),
+        cost_estimate=cost(2 * count * SLOTS * count, 4 * count * SLOTS),
+        name="plan",
     )(where, tokens)
 
 
@@ -378,8 +407,8 @@
 def expert_kernel(groups, where_ref, *refs):
     tokens = refs[:groups]
     wide, deep = refs[groups : groups + 2]
-    outs = refs[groups + 2 : 2 * groups + 2]
-    held = refs[2 * groups + 2] if groups > 1 else tokens[0]
+    outs = refs[groups + 2 : groups + 2 + len(PARTS) * groups]
+    held = refs[-1] if groups > 1 else tokens[0]
     dim = wide.shape[0]
     part = wide.shape[1] // 2
     chunk = dim // CHUNKS
@@ -398,7 +427,10 @@
         cols = pl.ds(k * chunk, chunk)
         got = jnp.dot(act, deep[:, cols], preferred_element_type=f32) * share
         for g in range(groups):
-            outs[g][:, cols] = got[g * SLOTS : (g + 1) * SLOTS].astype(bf16)
+            at = g * SLOTS
+            for n, size in enumerate(PARTS):
+                outs[n * groups + g][:, cols] = got[at : at + size].astype(bf16)
+                at += size
 
 
 def expert_part(where, tokens, weights):
@@ -409,9 +441,9 @@
     held = [pltpu.VMEM((rows, dim + EXTRA), bf16)] if groups > 1 else []
     return pl.pallas_call(
         functools.partial(expert_kernel, groups),
-        out_shape=(jax.ShapeDtypeStruct((SLOTS, dim), bf16),) * groups,
+        out_shape=[jax.ShapeDtypeStruct((size, dim), bf16) for size in PARTS for _ in range(groups)],
         in_specs=[smem()] + [vmem()] * (groups + 2),
-        out_specs=[vmem()] * groups,
+        out_specs=[vmem()] * (len(PARTS) * groups),
         scratch_shapes=held,
         compiler_params=params(8),
         cost_estimate=cost(6 * rows * wide.size, 2 * rows * dim),
@@ -421,50 +453,60 @@
 
 def collect_kernel(count, spread, *refs):
     parts, outs = refs[:count], refs[count:]
-    tiles = outs[0].shape[1] // TILE
-    for n in range(tiles):
-        got = jnp.dot(of_tile(spread[...], n, tiles), tiles_of(parts, 0, n), preferred_element_type=f32)
-        put_rows(got, outs, n)
-
-
-def collect(spread, parts):
-    width = parts[0].shape[1] // HALVES
-    count = len(parts)
+    half = spread.shape[0] // len(outs)
+    width = outs[0].shape[1]
+    whole = parts[0].shape[1] // HALVES == width
+    for n in range(parts[0].shape[1] // HALVES // TILE):
+        place, at = n * TILE // width, n * TILE % width
+        rows = spread[...] if whole else spread[pl.ds(place * half, half), :]
+        got = jnp.dot(rows, tiles_of(parts, 0, n), preferred_element_type=f32).astype(bf16)
+        for i, out in enumerate(outs if whole else (outs[place],)):
+            out[:, pl.ds(at, TILE)] = got[i * half : (i + 1) * half]
+
+
+def collect(spread, parts, width):
+    rows, count = spread.shape[0] // 2, len(parts)
     return pl.pallas_call(
         functools.partial(collect_kernel, count),
-        out_shape=row_shapes(spread.shape[0] // len(STEPS), width),
+        out_shape=(jax.ShapeDtypeStruct((rows, width), bf16),) * 2,
         in_specs=[vmem()] * (count + 1),
-        out_specs=[vmem()] * 5,
+        out_specs=[vmem()] * 2,
         compiler_params=params(12),
         cost_estimate=cost(2 * spread.size * width, 4 * spread.shape[0] * width),
         name="collect",
     )(spread, *parts)
 
 
-def merge_kernel(own, right, left, ahead, behind, first, *rest):
+def merge_kernel(count, *refs):
+    mine, (right, left, ahead, behind, first), rest = refs[:count], refs[count : count + 5], refs[count + 5 :]
     block = first.shape[0]
-    width = ahead.shape[1]
-    for c, last in enumerate((ahead, behind)):
-        cols = pl.ds(c * width, width)
-        total = own[:, cols] + right[:, cols].astype(f32) + left[:, cols].astype(f32)
-        total = total + last[...].astype(f32)
+    tiles = first.shape[1] // TILE
+    for n in range(tiles):
+        cols = pl.ds(n * TILE, TILE)
+        if count == 1:
+            total = mine[0][:, cols]
+        else:
+            total = jnp.dot(mine[0][...], tiles_of(mine[1:], 0, n), preferred_element_type=f32)
+        last, at = (ahead, n * TILE) if n < tiles // 2 else (behind, (n - tiles // 2) * TILE)
+        total = total + right[:, cols].astype(f32) + left[:, cols].astype(f32)
+        total = total + last[:, pl.ds(at, TILE)].astype(f32)
         first[:, cols] = total[:block]
         for k, out in enumerate(rest):
             out[:, cols] = total[(k + 1) * block : (k + 2) * block].astype(bf16)
 
 
-def merge(own, *others):
-    size, width = own.shape
+def merge(mine, others):
+    size, width = others[0].shape
     block = (size // FAR, width)
     return pl.pallas_call(
-        merge_kernel,
+        functools.partial(merge_kernel, len(mine)),
         out_shape=(jax.ShapeDtypeStruct(block, f32),) + (jax.ShapeDtypeStruct(block, bf16),) * (FAR - 1),
-        in_specs=[vmem()] * 5,
+        in_specs=[vmem()] * (len(mine) + 4),
         out_specs=[vmem()] * FAR,
         compiler_params=params(4),
         cost_estimate=cost(4 * size * width, 12 * size * width),
         name="merge",
-    )(own, *others)
+    )(*mine, *others)
 
 
 def half_swap(a):
@@ -545,12 +587,16 @@
     )(hidden, *added)
 
 
-def reduce_z(own, right, left, ahead, behind):
-    right = shift_z(right, 1)
-    left = shift_z(left, -1)
-    ahead = shift_z(ahead, 2)
-    behind = shift_z(behind, -2)
-    first, *sent = merge(own, right, left, ahead, behind)
+def one_on(right, left):
+    return shift_z(right, 1), shift_z(left, -1)
+
+
+def two_on(ahead, behind):
+    return shift_z(ahead, 2), shift_z(behind, -2)
+
+
+def far_on(mine, others):
+    first, *sent = merge(mine, others)
     others = [swap_far(rows, k + 1) for k, rows in enumerate(sent)]
     return first, *others
 
@@ -597,7 +643,8 @@
     weights = stage((w_gate, others[0], w_up, others[1], w_down, others[2]))
     arrived = arrived.reshape(RING * nx * tok, LAT)
     most = attend_part(where, nx, arrived, near, tok, 0, None)
-    added = reduce_z(*attend_part(where, nx, arrived, beyond, tok, nx - 1, most))
+    own, *rows = attend_part(where, nx, arrived, beyond, tok, nx - 1, most)
+    added = far_on((own,), one_on(*rows[:2]) + two_on(*rows[2:]))
 
     half = D // HALVES
     rows = resid.reshape(tok, HALVES, half).swapaxes(0, 1).reshape(HALVES * tok, half)
@@ -608,13 +655,19 @@
     hidden, payload = route(added, rows, gain, router.T, ids, places)
 
     ring = lax.all_gather(payload, ZAX, axis=0, tiled=True)
-    *sent, spread = dispatch(where, nx, ring, tok)
-    from_one, from_three, from_two = [swap_x(sent[i], COLUMNS[i]) for i in (1, 2, 3)]
-    done = expert_part(where, (sent[0], from_one, from_three), weights)
-    back_one, back_three = swap_x(done[1], 1), swap_x(done[2], 3)
-    (far_done,) = expert_part(where, (from_two,), weights)
-    back_two = swap_x(far_done, 2)
-    added = reduce_z(*collect(spread, (done[0], back_one, back_three, back_two)))
+    sent = dispatch(where, nx, ring, tok)
+    got = [swap_x(sent[i], COLUMNS[i]) for i in range(1, nx)]
+    spreads = plan(where, nx, ring, tok)
+    done = expert_part(where, (sent[0], *got[: nx - 2]), weights)
+    last = expert_part(where, got[nx - 2 :], weights)
+    backs = []
+    for n in range(len(PARTS)):
+        rows = [*done[n * (nx - 1) : (n + 1) * (nx - 1)], last[n]]
+        backs.append(rows[:1] + [swap_x(rows[i], COLUMNS[i]) for i in range(1, nx)])
+    near = one_on(*collect(spreads[0], backs[0], half))
+    two = collect(spreads[1], backs[1], half // 2)
+    near += two_on(*two)
+    added = far_on((spreads[2], *backs[2]), near)
     return finish(hidden, added, resid.shape)
 
 

time: 230 us -> 233 us (1.013)
  starting transfers between devices: 82.3 us -> 91.1 us
  waiting for transfers between devices: 82.7 us -> 75.9 us
    ppermute x12 -> x18, starting transfers between devices: 18.1 us -> 29.7 us  [swap_x(): lax.ppermute(a, 'x', [(i, i ^ bits) for i in range(lax.axis_size('x'))])]
    ppermute x12 -> x18, waiting for transfers between devices: 49.3 us -> 42 us  [swap_x(): lax.ppermute(a, 'x', [(i, i ^ bits) for i in range(lax.axis_size('x'))])]
    ppermute x8, waiting for transfers between devices: 12.5 us -> 17.2 us  [shift_z(): return lax.ppermute(a, ZAX, [(i, (i + step) % RING) for i in range(RING)])]
    ppermute x6, waiting for transfers between devices: 16.8 us -> 12.6 us  [swap_far(): return lax.ppermute(a, 'zb', [(i, i ^ bits) for i in range(FAR)])]
    ppermute x6, starting transfers between devices: 27.6 us -> 24.7 us  [swap_far(): return lax.ppermute(a, 'zb', [(i, i ^ bits) for i in range(FAR)])]
    pallas_call x5 -> x7, Pallas kernels: 5.79 us -> 6.85 us  [the longest x2 5.15 us: expert_part(): pl.pallas_call(functools.partial(expert_kernel, groups), out_shape=[jax.S...]
  transfers between devices with their start and end apart: 38 -> 44, of which waited for: 16 -> 15; matrix products, arithmetic and copies ran while one was open for 0% -> 0% of each run, Pallas kernels for 10% -> 10%
where the time goes in v8:
time: 233 us; the launch traced here: 231 us
  starting transfers between devices  91.1 us (39%)
  waiting for transfers between devices  75.9 us (33%)
  blocking collectives  34.5 us (15%)
  Pallas kernels  26.2 us (11%)
    ppermute x18, waiting for transfers between devices, swap_x(): lax.ppermute(a, 'x', [(i, i ^ bits) for i in range(lax.axis_size('x'))])  42 us
    all_gather x1, blocking collectives, layer(): ring = lax.all_gather(payload, ZAX, axis=0, tiled=True)  34.5 us
    ppermute x18, starting transfers between devices, swap_x(): lax.ppermute(a, 'x', [(i, i ^ bits) for i in range(lax.axis_size('x'))])  29.7 us
    ppermute x6, starting transfers between devices, swap_far(): return lax.ppermute(a, 'zb', [(i, i ^ bits) for i in range(FAR)])  24.7 us
    all_to_all x1, starting transfers between devices, layer(): lax.all_to_all(outgoing.reshape(RING, nx * tok, LAT), ZAX, split_axis=0,...  22.9 us
    ppermute x8, waiting for transfers between devices, shift_z(): return lax.ppermute(a, ZAX, [(i, (i + step) % RING) for i in range(RING)])  17.2 us
    ppermute x8, starting transfers between devices, shift_z(): return lax.ppermute(a, ZAX, [(i, (i + step) % RING) for i in range(RING)])  12.6 us
    ppermute x6, waiting for transfers between devices, swap_far(): return lax.ppermute(a, 'zb', [(i, i ^ bits) for i in range(FAR)])  12.6 us
  transfers between devices with their start and end apart: 44, of which 15 were waited for; matrix products, arithmetic and copies ran while one was open for 0% of the time, Pallas kernels for 10%

profile of v8, /device:TPU:164, one launch (start us, length us, event | category | flops | bytes accessed | tf_op | source)
XLA Modules:
  0.0 230.7 jit_solution(14071738428401895045)
XLA Ops:
  0.0 1.2 pack.1
  1.2 0.5 collective-permute-start.11
  1.7 1.2 collective-permute-start
  3.0 0.8 collective-permute-start.8
  3.8 10.6 %collective-permute-done.11.refs_8_ = bf16[32,7680]{1,0:T(8,128)(2,1)S(1)} collective-permute-done((bf16[32,7680]{1,0:T(8,128)(2,1)S(1)}, bf16[32,7680]{1,0:T(8,128)(2,1)S(1)}, u32[]{:S(2)}, u32[]{:S(2)}) %collective-permute-start.11) | collective-permute-done | bytes 491552 | tf_op jit(solution)/shard_map/ppermute | solution.py:40
  14.4 0.4 collective-permute-start.2
  14.8 1.1 collective-permute-done.refs_4_
  15.8 10.1 %collective-permute-done.8.refs_5_ = bf16[32,7680]{1,0:T(8,128)(2,1)S(1)} collective-permute-done((bf16[32,7680]{1,0:T(8,128)(2,1)S(1)}, bf16[32,7680]{1,0:T(8,128)(2,1)S(1)}, u32[]{:S(2)}, u32[]{:S(2)}) %collective-permute-start.8) | collective-permute-done | bytes 491552 | tf_op jit(solution)/shard_map/ppermute | solution.py:40
  25.9 1.8 collective-permute-start.1
  27.7 0.7 pad_add_fusion.where_ref
  28.5 5.9 %context_rows.1 = bf16[256,512]{1,0:T(8,128)(2,1)} custom-call(s32[5]{0:T(128)S(1)} %pad_add_fusion.where_ref, bf16[2,576,2048]{2,1,0:T(8,128)(2,1)} %bitcast.20, bf16[2,2,64,576]{3,2,1,0:T(8,128)(2,1)} %queries.1, bf16[2,2,576]{2,1,0:T(2,128)(2,1)} %new.1), custom_call_target="tpu_custom_call" | custom-call | flops 1140850688 | bytes 4718592 | tf_op jit(solution)/shard_map/context_rows/pallas_call | solution.py:166
  34.3 22.9 %all-to-all-start = ((bf16[16,16,512]{2,1,0:T(8,128)(2,1)}), bf16[16,16,512]{2,1,0:T(8,128)(2,1)S(1)}, u32[]{:S(2)}, u32[]{:S(2)}) async-start(bf16[16,16,512]{2,1,0:T(8,128)(2,1)} %bitcast.4), calls=%async_computation | async-start | bytes 524288 | tf_op jit(solution)/shard_map/all_to_all | solution.py:633
  57.5 2.5 %collective-permute-start.3 = (bf16[32,7680]{1,0:T(8,128)(2,1)}, bf16[32,7680]{1,0:T(8,128)(2,1)}, u32[]{:S(2)}, u32[]{:S(2)}) collective-permute-start(bf16[32,7680]{1,0:T(8,128)(2,1)} %collective-permute-done.2.refs_9_), channel_id=1, source_target_pairs={{0,32},{32,0},{64,96},{96,64},{1,33},{33,1},{65,97},{97,65},{2,34}... | collective-permute-start | bytes 1474568 | tf_op jit(solution)/shard_map/ppermute | solution.py:40
  60.0 0.4 collective-permute-start.24
  60.6 0.8 copy-done
  61.4 0.4 collective-permute-start.4
  61.7 10.2 %collective-permute-done.3.refs_1_ = bf16[32,7680]{1,0:T(8,128)(2,1)} collective-permute-done((bf16[32,7680]{1,0:T(8,128)(2,1)}, bf16[32,7680]{1,0:T(8,128)(2,1)}, u32[]{:S(2)}, u32[]{:S(2)}) %collective-permute-start.3) | collective-permute-done | bytes 491552 | tf_op jit(solution)/shard_map/ppermute | solution.py:40
  72.0 4.1 %all-to-all-done = bf16[16,16,512]{2,1,0:T(8,128)(2,1)S(1)} async-done(((bf16[16,16,512]{2,1,0:T(8,128)(2,1)}), bf16[16,16,512]{2,1,0:T(8,128)(2,1)S(1)}, u32[]{:S(2)}, u32[]{:S(2)}) %all-to-all-start) | async-done | bytes 262176 | tf_op jit(solution)/shard_map/all_to_all | solution.py:633
  76.0 1.0 copy-done.1
  77.1 3.0 %attend_part.2.refs_4_ = f32[128,3584]{1,0:T(8,128)S(1)} custom-call(s32[5]{0:T(128)S(1)} %pad_add_fusion.where_ref, bf16[256,512]{1,0:T(8,128)(2,1)S(1)} %bitcast.15, bf16[32,7680]{1,0:T(8,128)(2,1)S(1)} %get-tuple-element.47.refs_0_, bf16[32,7680]{1,0:T(8,128)(2,1)S(1)} %get-tuple-element.48.refs_1_, bf16[32,7680]{1,0:T(8,128)(2,1)S(1)} %collective-permute-done.6.refs_2_, ...), custom_call_target="tpu_custom_call" | custom-call | flops 1409286144 | bytes 5505024 | tf_op jit(solution)/shard_map/attend_part/pallas_call | solution.py:276
  80.1 2.4 %attend_part.3 = (f32[32,3584]{1,0:T(8,128)S(1)}, bf16[32,3584]{1,0:T(8,128)(2,1)S(1)}, bf16[32,3584]{1,0:T(8,128)(2,1)S(1)}, bf16[32,1792]{1,0:T(8,128)(2,1)S(1)}, bf16[32,1792]{1,0:T(8,128)(2,1)S(1)}) custom-call(s32[5]{0:T(128)S(1)} %pad_add_fusion.where_ref, bf16[256,512]{1,0:T(8,128)(2,1)S(1)} %bitcast.16, ...), custom_call_target="tpu_custom_call" | custom-call | flops 469762048 | bytes 1835008 | tf_op jit(solution)/shard_map/attend_part/pallas_call | solution.py:276
  82.5 2.3 %collective-permute-start.16 = (bf16[32,1792]{1,0:T(8,128)(2,1)S(1)}, bf16[32,1792]{1,0:T(8,128)(2,1)S(1)}, u32[]{:S(2)}, u32[]{:S(2)}) collective-permute-start(bf16[32,1792]{1,0:T(8,128)(2,1)S(1)} %get-tuple-element.52), channel_id=1, source_target_pairs={{0,4},{2,6},{4,8},{6,10},{8,12},{10,14},{12,16},{14,18},{16,20},{1... | collective-permute-start | bytes 344072 | tf_op jit(solution)/shard_map/ppermute | solution.py:44
  84.9 1.9 collective-permute-start.17
  86.8 4.0 %collective-permute-done.16.refs_3_ = bf16[32,1792]{1,0:T(8,128)(2,1)S(1)} collective-permute-done((bf16[32,1792]{1,0:T(8,128)(2,1)S(1)}, bf16[32,1792]{1,0:T(8,128)(2,1)S(1)}, u32[]{:S(2)}, u32[]{:S(2)}) %collective-permute-start.16) | collective-permute-done | bytes 114720 | tf_op jit(solution)/shard_map/ppermute | solution.py:44
  90.8 2.0 collective-permute-start.15
  92.8 4.7 %collective-permute-done.14.refs_1_ = bf16[32,3584]{1,0:T(8,128)(2,1)S(1)} collective-permute-done((bf16[32,3584]{1,0:T(8,128)(2,1)S(1)}, bf16[32,3584]{1,0:T(8,128)(2,1)S(1)}, u32[]{:S(2)}, u32[]{:S(2)}) %collective-permute-start.14) | collective-permute-done | bytes 229408 | tf_op jit(solution)/shard_map/ppermute | solution.py:44
  97.6 5.9 %collective-permute-start.18 = (bf16[8,3584]{1,0:T(8,128)(2,1)S(1)}, bf16[8,3584]{1,0:T(8,128)(2,1)S(1)}, u32[]{:S(2)}, u32[]{:S(2)}) collective-permute-start(bf16[8,3584]{1,0:T(8,128)(2,1)S(1)} %get-tuple-element.55), channel_id=1, source_target_pairs={{0,8},{8,0},{16,24},{24,16},{1,9},{9,1},{17,25},{25,17},{2,10},{10... | collective-permute-start | bytes 172040 | tf_op jit(solution)/shard_map/ppermute | solution.py:48
  103.4 4.6 %collective-permute-start.19 = (bf16[8,3584]{1,0:T(8,128)(2,1)S(1)}, bf16[8,3584]{1,0:T(8,128)(2,1)S(1)}, u32[]{:S(2)}, u32[]{:S(2)}) collective-permute-start(bf16[8,3584]{1,0:T(8,128)(2,1)S(1)} %get-tuple-element.56), channel_id=1, source_target_pairs={{0,16},{8,24},{16,0},{24,8},{1,17},{9,25},{17,1},{25,9},{2,18},{10... | collective-permute-start | bytes 172040 | tf_op jit(solution)/shard_map/ppermute | solution.py:48
  108.0 2.8 %collective-permute-start.20 = (bf16[8,3584]{1,0:T(8,128)(2,1)S(1)}, bf16[8,3584]{1,0:T(8,128)(2,1)S(1)}, u32[]{:S(2)}, u32[]{:S(2)}) collective-permute-start(bf16[8,3584]{1,0:T(8,128)(2,1)S(1)} %get-tuple-element.57), channel_id=1, source_target_pairs={{0,24},{8,16},{16,8},{24,0},{1,25},{9,17},{17,9},{25,1},{2,26},{10... | collective-permute-start | bytes 172040 | tf_op jit(solution)/shard_map/ppermute | solution.py:48
  111.0 8.2 %collective-permute-done.19.two = bf16[8,3584]{1,0:T(8,128)(2,1)S(1)} collective-permute-done((bf16[8,3584]{1,0:T(8,128)(2,1)S(1)}, bf16[8,3584]{1,0:T(8,128)(2,1)S(1)}, u32[]{:S(2)}, u32[]{:S(2)}) %collective-permute-start.19) | collective-permute-done | bytes 57376 | tf_op jit(solution)/shard_map/ppermute | solution.py:48
  119.2 0.6 route.1
  119.8 34.5 %all_gather.3.tokens = bf16[128,3712]{1,0:T(8,128)(2,1)S(1)} all-gather(bf16[8,3712]{1,0:T(8,128)(2,1)S(1)} %get-tuple-element.59), channel_id=1, replica_groups=mesh['rep'=2,'x'=4,'zb'=4,'j'=4,'c'=2] {'zb','j'}, dimensions={0}, use_global_device_ids=true | all-gather | bytes 1009664 | tf_op jit(solution)/shard_map/all_gather | solution.py:657
  154.3 1.3 dispatch.1
  155.6 4.4 %collective-permute-start.21 = (bf16[32,7296]{1,0:T(8,128)(2,1)S(1)}, bf16[32,7296]{1,0:T(8,128)(2,1)S(1)}, u32[]{:S(2)}, u32[]{:S(2)}) collective-permute-start(bf16[32,7296]{1,0:T(8,128)(2,1)S(1)} %get-tuple-element.62), channel_id=1, source_target_pairs={{0,32},{32,0},{64,96},{96,64},{1,33},{33,1},{65,97},{97,65},{2,34}... | collective-permute-start | bytes 1400840 | tf_op jit(solution)/shard_map/ppermute | solution.py:40
  160.0 2.2 collective-permute-start.28
  162.2 4.2 %stage.1 = (bf16[7168,512]{1,0:T(8,128)(2,1)S(1)}, bf16[256,7168]{1,0:T(8,128)(2,1)S(1)}) custom-call(bf16[7168,128]{1,0:T(8,128)(2,1)} %gate_a.1, bf16[7168,128]{1,0:T(8,128)(2,1)} %collective-permute-done.23.gate_b, bf16[7168,128]{1,0:T(8,128)(2,1)} %up_a.1, bf16[7168,128]{1,0:T(8,128)(2,1)} %collective-permute-done.24.up_b, bf16[128,7168]{1,0:T(8,128)(2,1)} %down_a.1, ...), custom_call_target="tpu_custom_call" | custom-call | flops 3670016000 | bytes 11010048 | tf_op jit(solution)/shard_map/stage/pallas_call | solution.py:392
  166.5 0.8 collective-permute-done.21.refs_1_
  167.3 7.5 %collective-permute-done.22.refs_2_ = bf16[32,7296]{1,0:T(8,128)(2,1)S(1)} collective-permute-done((bf16[32,7296]{1,0:T(8,128)(2,1)S(1)}, bf16[32,7296]{1,0:T(8,128)(2,1)S(1)}, u32[]{:S(2)}, u32[]{:S(2)}) %collective-permute-start.22) | collective-permute-done | bytes 466976 | tf_op jit(solution)/shard_map/ppermute | solution.py:40
  174.8 2.5 %expert_part.2 = (bf16[16,7168]{1,0:T(8,128)(2,1)S(1)}, bf16[16,7168]{1,0:T(8,128)(2,1)S(1)}, bf16[16,7168]{1,0:T(8,128)(2,1)S(1)}, bf16[8,7168]{1,0:T(8,128)(2,...) custom-call(s32[5]{0:T(128)S(1)} %pad_add_fusion.where_ref, ...), custom_call_target="tpu_custom_call" | custom-call | flops 2113929216 | bytes 1376256 | tf_op jit(solution)/shard_map/expert_part/pallas_call | solution.py:442
  177.5 0.4 collective-permute-start.31
  177.9 2.6 %expert_part.3 = (bf16[16,7168]{1,0:T(8,128)(2,1)S(1)}, bf16[8,7168]{1,0:T(8,128)(2,1)S(1)}, bf16[8,7168]{1,0:T(8,128)(2,1)S(1)}) custom-call(s32[5]{0:T(128)S(1)} %pad_add_fusion.where_ref, bf16[32,7296]{1,0:T(8,128)(2,1)S(1)} %collective-permute-done.28.refs_0_, bf16[7168,512]{1,0:T(8,128)(2,1)S(1)} %get-tuple-element.64.refs_3_.refs_1_, ...), custom_call_target="tpu_custom_call" | custom-call | flops 704643072 | bytes 458752 | tf_op jit(solution)/shard_map/expert_part/pallas_call | solution.py:442
  180.5 3.8 %collective-permute-start.32 = (bf16[16,7168]{1,0:T(8,128)(2,1)S(1)}, bf16[16,7168]{1,0:T(8,128)(2,1)S(1)}, u32[]{:S(2)}, u32[]{:S(2)}) collective-permute-start(bf16[16,7168]{1,0:T(8,128)(2,1)S(1)} %get-tuple-element.75), channel_id=1, source_target_pairs={{0,64},{32,96},{64,0},{96,32},{1,65},{33,97},{65,1},{97,33},{2,66}... | collective-permute-start | bytes 688136 | tf_op jit(solution)/shard_map/ppermute | solution.py:40
  184.3 0.4 collective-permute-start.35
  184.6 0.3 collective-permute-start.36
  185.0 0.9 plan.1
  185.9 1.6 collective-permute-start.26
  187.5 1.4 collective-permute-done.31.refs_2_
  188.8 1.1 collective-permute-start.27
  189.9 4.6 %collective-permute-start.37 = (bf16[8,7168]{1,0:T(8,128)(2,1)S(1)}, bf16[8,7168]{1,0:T(8,128)(2,1)S(1)}, u32[]{:S(2)}, u32[]{:S(2)}) collective-permute-start(bf16[8,7168]{1,0:T(8,128)(2,1)S(1)} %get-tuple-element.82), channel_id=1, source_target_pairs={{0,64},{32,96},{64,0},{96,32},{1,65},{33,97},{65,1},{97,33},{2,66}... | collective-permute-start | bytes 344072 | tf_op jit(solution)/shard_map/ppermute | solution.py:40
  194.6 0.3 collect.2
  195.0 2.0 collective-permute-start.34
  197.0 0.3 collective-permute-done.37.refs_3_
  197.3 3.5 %collective-permute-start.29 = (bf16[8,7168]{1,0:T(8,128)(2,1)S(1)}, bf16[8,7168]{1,0:T(8,128)(2,1)S(1)}, u32[]{:S(2)}, u32[]{:S(2)}) collective-permute-start(bf16[8,7168]{1,0:T(8,128)(2,1)S(1)} %get-tuple-element.70), channel_id=1, source_target_pairs={{0,64},{32,96},{64,0},{96,32},{1,65},{33,97},{65,1},{97,33},{2,66}... | collective-permute-start | bytes 344072 | tf_op jit(solution)/shard_map/ppermute | solution.py:40
  200.9 0.2 collect.3
  201.1 1.5 collective-permute-start.38
  202.5 2.8 %collective-permute-start.39 = (bf16[32,1792]{1,0:T(8,128)(2,1)S(1)}, bf16[32,1792]{1,0:T(8,128)(2,1)S(1)}, u32[]{:S(2)}, u32[]{:S(2)}) collective-permute-start(bf16[32,1792]{1,0:T(8,128)(2,1)S(1)} %get-tuple-element.84), channel_id=1, source_target_pairs={{0,28},{2,30},{4,0},{6,2},{8,4},{10,6},{12,8},{14,10},{16,12},{18,... | collective-permute-start | bytes 344072 | tf_op jit(solution)/shard_map/ppermute | solution.py:44
  205.3 8.6 %collective-permute-done.38.refs_7_ = bf16[32,1792]{1,0:T(8,128)(2,1)S(1)} collective-permute-done((bf16[32,1792]{1,0:T(8,128)(2,1)S(1)}, bf16[32,1792]{1,0:T(8,128)(2,1)S(1)}, u32[]{:S(2)}, u32[]{:S(2)}) %collective-permute-start.38) | collective-permute-done | bytes 114720 | tf_op jit(solution)/shard_map/ppermute | solution.py:44
  214.0 0.2 merge.3
  214.2 0.1 collective-permute-start.40
  214.3 6.3 %collective-permute-start.41 = (bf16[8,3584]{1,0:T(8,128)(2,1)S(1)}, bf16[8,3584]{1,0:T(8,128)(2,1)S(1)}, u32[]{:S(2)}, u32[]{:S(2)}) collective-permute-start(bf16[8,3584]{1,0:T(8,128)(2,1)S(1)} %get-tuple-element.87), channel_id=1, source_target_pairs={{0,16},{8,24},{16,0},{24,8},{1,17},{9,25},{17,1},{25,9},{2,18},{10... | collective-permute-start | bytes 172040 | tf_op jit(solution)/shard_map/ppermute | solution.py:48
  220.7 4.9 %collective-permute-start.42 = (bf16[8,3584]{1,0:T(8,128)(2,1)S(1)}, bf16[8,3584]{1,0:T(8,128)(2,1)S(1)}, u32[]{:S(2)}, u32[]{:S(2)}) collective-permute-start(bf16[8,3584]{1,0:T(8,128)(2,1)S(1)} %get-tuple-element.88), channel_id=1, source_target_pairs={{0,24},{8,16},{16,8},{24,0},{1,25},{9,17},{17,9},{25,1},{2,26},{10... | collective-permute-start | bytes 172040 | tf_op jit(solution)/shard_map/ppermute | solution.py:48
  225.6 1.7 collective-permute-done.41.two
  227.4 2.7 %collective-permute-done.42.three = bf16[8,3584]{1,0:T(8,128)(2,1)S(1)} collective-permute-done((bf16[8,3584]{1,0:T(8,128)(2,1)S(1)}, bf16[8,3584]{1,0:T(8,128)(2,1)S(1)}, u32[]{:S(2)}, u32[]{:S(2)}) %collective-permute-start.42) | collective-permute-done | bytes 57376 | tf_op jit(solution)/shard_map/ppermute | solution.py:48
  230.0 0.7 finish.1
  (63 shorter events, 1.0 us)
Async XLA Ops:
  1.2 13.2 %collective-permute-start.11 = (bf16[32,7680]{1,0:T(8,128)(2,1)S(1)}, bf16[32,7680]{1,0:T(8,128)(2,1)S(1)}, u32[]{:S(2)}, u32[]{:S(2)}) collective-permute-start(bf16[32,7680]{1,0:T(8,128)(2,1)S(1)} %get-tuple-element.47.refs_0_), channel_id=1, source_target_pairs={{0,96},{32,64},{64,32},{96,0},{1,97},{33,65},{65,33},{97,1},{2,98}... | collective-permute-start | bytes 1474568 | tf_op jit(solution)/shard_map/ppermute | solution.py:40
  1.7 13.0 %collective-permute-start.6 = (bf16[32,7680]{1,0:T(8,128)(2,1)S(1)}, bf16[32,7680]{1,0:T(8,128)(2,1)S(1)}, u32[]{:S(2)}, u32[]{:S(2)}) collective-permute-start(bf16[32,7680]{1,0:T(8,128)(2,1)S(1)} %get-tuple-element.47.refs_0_), channel_id=1, source_target_pairs={{0,1},{1,0},{2,3},{3,2},{4,5},{5,4},{6,7},{7,6},{8,9},{9,8},{10,11... | collective-permute-start | bytes 1474568 | tf_op jit(solution)/shard_map/ppermute | solution.py:52
  1.7 14.1 %collective-permute-start = (bf16[32,7680]{1,0:T(8,128)(2,1)S(1)}, bf16[32,7680]{1,0:T(8,128)(2,1)S(1)}, u32[]{:S(2)}, u32[]{:S(2)}) collective-permute-start(bf16[32,7680]{1,0:T(8,128)(2,1)S(1)} %get-tuple-element.47.refs_0_), channel_id=1, source_target_pairs={{0,32},{32,0},{64,96},{96,64},{1,33},{33,1},{65,97},{97,65},{2,34}... | collective-permute-start | bytes 1474568 | tf_op jit(solution)/shard_map/ppermute | solution.py:40
  3.0 22.9 %collective-permute-start.8 = (bf16[32,7680]{1,0:T(8,128)(2,1)S(1)}, bf16[32,7680]{1,0:T(8,128)(2,1)S(1)}, u32[]{:S(2)}, u32[]{:S(2)}) collective-permute-start(bf16[32,7680]{1,0:T(8,128)(2,1)S(1)} %get-tuple-element.48.refs_1_), channel_id=1, source_target_pairs={{0,32},{32,0},{64,96},{96,64},{1,33},{33,1},{65,97},{97,65},{2,34}... | collective-permute-start | bytes 1474568 | tf_op jit(solution)/shard_map/ppermute | solution.py:40
  3.8 24.0 %collective-permute-start.7 = (bf16[32,7680]{1,0:T(8,128)(2,1)S(1)}, bf16[32,7680]{1,0:T(8,128)(2,1)}, u32[]{:S(2)}, u32[]{:S(2)}) collective-permute-start(bf16[32,7680]{1,0:T(8,128)(2,1)S(1)} %get-tuple-element.48.refs_1_), channel_id=1, source_target_pairs={{0,1},{1,0},{2,3},{3,2},{4,5},{5,4},{6,7},{7,6},{8,9},{9,8},{10,11... | collective-permute-start | bytes 1474568 | tf_op jit(solution)/shard_map/ppermute | solution.py:52
  14.4 42.9 %collective-permute-start.2 = (bf16[32,7680]{1,0:T(8,128)(2,1)S(1)}, bf16[32,7680]{1,0:T(8,128)(2,1)}, u32[]{:S(2)}, u32[]{:S(2)}) collective-permute-start(bf16[32,7680]{1,0:T(8,128)(2,1)S(1)} %get-tuple-element.48.refs_1_), channel_id=1, source_target_pairs={{0,96},{32,64},{64,32},{96,0},{1,97},{33,65},{65,33},{97,1},{2,98}... | collective-permute-start | bytes 1474568 | tf_op jit(solution)/shard_map/ppermute | solution.py:40
  14.8 42.7 %collective-permute-start.12 = (bf16[32,7680]{1,0:T(8,128)(2,1)S(1)}, bf16[32,7680]{1,0:T(8,128)(2,1)}, u32[]{:S(2)}, u32[]{:S(2)}) collective-permute-start(bf16[32,7680]{1,0:T(8,128)(2,1)S(1)} %collective-permute-done.11.refs_8_), channel_id=1, source_target_pairs={{0,1},{1,0},{2,3},{3,2},{4,5},{5,4},{6,7},{7,6},{8,9},{9,8},{10,11... | collective-permute-start | bytes 1474568 | tf_op jit(solution)/shard_map/ppermute | solution.py:52
  15.8 44.1 %collective-permute-start.9 = (bf16[32,7680]{1,0:T(8,128)(2,1)S(1)}, bf16[32,7680]{1,0:T(8,128)(2,1)}, u32[]{:S(2)}, u32[]{:S(2)}) collective-permute-start(bf16[32,7680]{1,0:T(8,128)(2,1)S(1)} %collective-permute-done.refs_4_), channel_id=1, source_target_pairs={{0,1},{1,0},{2,3},{3,2},{4,5},{5,4},{6,7},{7,6},{8,9},{9,8},{10,11... | collective-permute-start | bytes 1474568 | tf_op jit(solution)/shard_map/ppermute | solution.py:52
  25.9 34.1 %collective-permute-start.1 = (bf16[32,7680]{1,0:T(8,128)(2,1)S(1)}, bf16[32,7680]{1,0:T(8,128)(2,1)}, u32[]{:S(2)}, u32[]{:S(2)}) collective-permute-start(bf16[32,7680]{1,0:T(8,128)(2,1)S(1)} %collective-permute-done.refs_4_), channel_id=1, source_target_pairs={{0,96},{32,64},{64,32},{96,0},{1,97},{33,65},{65,33},{97,1},{2,98}... | collective-permute-start | bytes 1474568 | tf_op jit(solution)/shard_map/ppermute | solution.py:40
  27.7 32.7 %collective-permute-start.10 = (bf16[32,7680]{1,0:T(8,128)(2,1)S(1)}, bf16[32,7680]{1,0:T(8,128)(2,1)}, u32[]{:S(2)}, u32[]{:S(2)}) collective-permute-start(bf16[32,7680]{1,0:T(8,128)(2,1)S(1)} %collective-permute-done.8.refs_5_), channel_id=1, source_target_pairs={{0,1},{1,0},{2,3},{3,2},{4,5},{5,4},{6,7},{7,6},{8,9},{9,8},{10,11... | collective-permute-start | bytes 1474568 | tf_op jit(solution)/shard_map/ppermute | solution.py:52
  34.3 41.7 %all-to-all-start = ((bf16[16,16,512]{2,1,0:T(8,128)(2,1)}), bf16[16,16,512]{2,1,0:T(8,128)(2,1)S(1)}, u32[]{:S(2)}, u32[]{:S(2)}) async-start(bf16[16,16,512]{2,1,0:T(8,128)(2,1)} %bitcast.4), calls=%async_computation | async-start | bytes 524288 | tf_op jit(solution)/shard_map/all_to_all | solution.py:633
  57.3 3.3 %collective-permute-start.13 = (bf16[32,7680]{1,0:T(8,128)(2,1)}, bf16[32,7680]{1,0:T(8,128)(2,1)S(1)}, u32[]{:S(2)}, u32[]{:S(2)}) collective-permute-start(bf16[32,7680]{1,0:T(8,128)(2,1)} %collective-permute-done.2.refs_9_), channel_id=1, source_target_pairs={{0,1},{1,0},{2,3},{3,2},{4,5},{5,4},{6,7},{7,6},{8,9},{9,8},{10,11... | collective-permute-start | bytes 1474568 | tf_op jit(solution)/shard_map/ppermute | solution.py:52
  57.5 14.5 %collective-permute-start.3 = (bf16[32,7680]{1,0:T(8,128)(2,1)}, bf16[32,7680]{1,0:T(8,128)(2,1)}, u32[]{:S(2)}, u32[]{:S(2)}) collective-permute-start(bf16[32,7680]{1,0:T(8,128)(2,1)} %collective-permute-done.2.refs_9_), channel_id=1, source_target_pairs={{0,32},{32,0},{64,96},{96,64},{1,33},{33,1},{65,97},{97,65},{2,34}... | collective-permute-start | bytes 1474568 | tf_op jit(solution)/shard_map/ppermute | solution.py:40
  59.9 100.1 %collective-permute-start.23 = (bf16[7168,128]{1,0:T(8,128)(2,1)}, bf16[7168,128]{1,0:T(8,128)(2,1)}, u32[]{:S(2)}, u32[]{:S(2)}) collective-permute-start(bf16[7168,128]{1,0:T(8,128)(2,1)} %gate_a.1), channel_id=1, source_target_pairs={{0,1},{1,0},{2,3},{3,2},{4,5},{5,4},{6,7},{7,6},{8,9},{9,8},{10,11... | collective-permute-start | bytes 5505032 | tf_op jit(solution)/shard_map/ppermute | solution.py:52
  60.0 102.2 %collective-permute-start.24 = (bf16[7168,128]{1,0:T(8,128)(2,1)}, bf16[7168,128]{1,0:T(8,128)(2,1)}, u32[]{:S(2)}, u32[]{:S(2)}) collective-permute-start(bf16[7168,128]{1,0:T(8,128)(2,1)} %up_a.1), channel_id=1, source_target_pairs={{0,1},{1,0},{2,3},{3,2},{4,5},{5,4},{6,7},{7,6},{8,9},{9,8},{10,11... | collective-permute-start | bytes 5505032 | tf_op jit(solution)/shard_map/ppermute | solution.py:52
  60.4 101.8 %collective-permute-start.25 = (bf16[128,7168]{1,0:T(8,128)(2,1)}, bf16[128,7168]{1,0:T(8,128)(2,1)}, u32[]{:S(2)}, u32[]{:S(2)}) collective-permute-start(bf16[128,7168]{1,0:T(8,128)(2,1)} %down_a.1), channel_id=1, source_target_pairs={{0,1},{1,0},{2,3},{3,2},{4,5},{5,4},{6,7},{7,6},{8,9},{9,8},{10,11... | collective-permute-start | bytes 5505032 | tf_op jit(solution)/shard_map/ppermute | solution.py:52
  60.6 0.8 copy-start
  61.4 18.8 %collective-permute-start.4 = (bf16[32,7680]{1,0:T(8,128)(2,1)}, bf16[32,7680]{1,0:T(8,128)(2,1)}, u32[]{:S(2)}, u32[]{:S(2)}) collective-permute-start(bf16[32,7680]{1,0:T(8,128)(2,1)} %collective-permute-done.1.refs_0_), channel_id=1, source_target_pairs={{0,1},{1,0},{2,3},{3,2},{4,5},{5,4},{6,7},{7,6},{8,9},{9,8},{10,11... | collective-permute-start | bytes 1474568 | tf_op jit(solution)/shard_map/ppermute | solution.py:52
  72.0 8.2 %collective-permute-start.5 = (bf16[32,7680]{1,0:T(8,128)(2,1)}, bf16[32,7680]{1,0:T(8,128)(2,1)}, u32[]{:S(2)}, u32[]{:S(2)}) collective-permute-start(bf16[32,7680]{1,0:T(8,128)(2,1)} %collective-permute-done.3.refs_1_), channel_id=1, source_target_pairs={{0,1},{1,0},{2,3},{3,2},{4,5},{5,4},{6,7},{7,6},{8,9},{9,8},{10,11... | collective-permute-start | bytes 1474568 | tf_op jit(solution)/shard_map/ppermute | solution.py:52
  76.0 1.0 copy-start.1
  80.1 30.7 %copy-start.4 = (bf16[7168]{0:T(1024)(128)(2,1)S(1)}, bf16[7168]{0:T(1024)(128)(2,1)}, u32[]{:S(2)}) copy-start(bf16[7168]{0:T(1024)(128)(2,1)} %param.21) | copy-start | bytes 43012
  80.1 30.7 %copy-start.3 = (bf16[2,2,7168]{2,1,0:T(2,128)(2,1)S(1)}, bf16[2,2,7168]{2,1,0:T(2,128)(2,1)}, u32[]{:S(2)}) copy-start(bf16[2,2,7168]{2,1,0:T(2,128)(2,1)} %param.18) | copy-start | bytes 172036
  82.5 36.7 %copy-start.5 = (s32[2,2,8]{2,1,0:T(2,128)S(1)}, s32[2,2,8]{2,1,0:T(2,128)}, u32[]{:S(2)}) copy-start(s32[2,2,8]{2,1,0:T(2,128)} %param.23) | copy-start | bytes 388
  82.5 36.7 %copy-start.6 = (s32[2,2,8]{2,1,0:T(2,128)S(1)}, s32[2,2,8]{2,1,0:T(2,128)}, u32[]{:S(2)}) copy-start(s32[2,2,8]{2,1,0:T(2,128)} %param.24) | copy-start | bytes 388
  82.5 36.7 %copy-start.2 = (bf16[7168,16]{0,1:T(8,128)(2,1)S(1)}, bf16[7168,16]{0,1:T(8,128)(2,1)}, u32[]{:S(2)}) copy-start(bf16[7168,16]{0,1:T(8,128)(2,1)} %param.22) | copy-start | bytes 688132
  82.5 8.2 %collective-permute-start.16 = (bf16[32,1792]{1,0:T(8,128)(2,1)S(1)}, bf16[32,1792]{1,0:T(8,128)(2,1)S(1)}, u32[]{:S(2)}, u32[]{:S(2)}) collective-permute-start(bf16[32,1792]{1,0:T(8,128)(2,1)S(1)} %get-tuple-element.52), channel_id=1, source_target_pairs={{0,4},{2,6},{4,8},{6,10},{8,12},{10,14},{12,16},{14,18},{16,20},{1... | collective-permute-start | bytes 344072 | tf_op jit(solution)/shard_map/ppermute | solution.py:44
  84.9 5.9 %collective-permute-start.17 = (bf16[32,1792]{1,0:T(8,128)(2,1)S(1)}, bf16[32,1792]{1,0:T(8,128)(2,1)S(1)}, u32[]{:S(2)}, u32[]{:S(2)}) collective-permute-start(bf16[32,1792]{1,0:T(8,128)(2,1)S(1)} %get-tuple-element.53), channel_id=1, source_target_pairs={{0,28},{2,30},{4,0},{6,2},{8,4},{10,6},{12,8},{14,10},{16,12},{18,... | collective-permute-start | bytes 344072 | tf_op jit(solution)/shard_map/ppermute | solution.py:44
  90.8 6.7 %collective-permute-start.14 = (bf16[32,3584]{1,0:T(8,128)(2,1)S(1)}, bf16[32,3584]{1,0:T(8,128)(2,1)S(1)}, u32[]{:S(2)}, u32[]{:S(2)}) collective-permute-start(bf16[32,3584]{1,0:T(8,128)(2,1)S(1)} %get-tuple-element.50), channel_id=1, source_target_pairs={{0,2},{2,4},{4,6},{6,8},{8,10},{10,12},{12,14},{14,16},{16,18},{18... | collective-permute-start | bytes 688136 | tf_op jit(solution)/shard_map/ppermute | solution.py:44
  90.8 6.7 %collective-permute-start.15 = (bf16[32,3584]{1,0:T(8,128)(2,1)S(1)}, bf16[32,3584]{1,0:T(8,128)(2,1)S(1)}, u32[]{:S(2)}, u32[]{:S(2)}) collective-permute-start(bf16[32,3584]{1,0:T(8,128)(2,1)S(1)} %get-tuple-element.51), channel_id=1, source_target_pairs={{0,30},{2,0},{4,2},{6,4},{8,6},{10,8},{12,10},{14,12},{16,14},{18,... | collective-permute-start | bytes 688136 | tf_op jit(solution)/shard_map/ppermute | solution.py:44
  97.6 10.4 %collective-permute-start.18 = (bf16[8,3584]{1,0:T(8,128)(2,1)S(1)}, bf16[8,3584]{1,0:T(8,128)(2,1)S(1)}, u32[]{:S(2)}, u32[]{:S(2)}) collective-permute-start(bf16[8,3584]{1,0:T(8,128)(2,1)S(1)} %get-tuple-element.55), channel_id=1, source_target_pairs={{0,8},{8,0},{16,24},{24,16},{1,9},{9,1},{17,25},{25,17},{2,10},{10... | collective-permute-start | bytes 172040 | tf_op jit(solution)/shard_map/ppermute | solution.py:48
  103.4 15.7 %collective-permute-start.19 = (bf16[8,3584]{1,0:T(8,128)(2,1)S(1)}, bf16[8,3584]{1,0:T(8,128)(2,1)S(1)}, u32[]{:S(2)}, u32[]{:S(2)}) collective-permute-start(bf16[8,3584]{1,0:T(8,128)(2,1)S(1)} %get-tuple-element.56), channel_id=1, source_target_pairs={{0,16},{8,24},{16,0},{24,8},{1,17},{9,25},{17,1},{25,9},{2,18},{10... | collective-permute-start | bytes 172040 | tf_op jit(solution)/shard_map/ppermute | solution.py:48
  108.0 11.2 %collective-permute-start.20 = (bf16[8,3584]{1,0:T(8,128)(2,1)S(1)}, bf16[8,3584]{1,0:T(8,128)(2,1)S(1)}, u32[]{:S(2)}, u32[]{:S(2)}) collective-permute-start(bf16[8,3584]{1,0:T(8,128)(2,1)S(1)} %get-tuple-element.57), channel_id=1, source_target_pairs={{0,24},{8,16},{16,8},{24,0},{1,25},{9,17},{17,9},{25,1},{2,26},{10... | collective-permute-start | bytes 172040 | tf_op jit(solution)/shard_map/ppermute | solution.py:48
  155.6 11.7 %collective-permute-start.21 = (bf16[32,7296]{1,0:T(8,128)(2,1)S(1)}, bf16[32,7296]{1,0:T(8,128)(2,1)S(1)}, u32[]{:S(2)}, u32[]{:S(2)}) collective-permute-start(bf16[32,7296]{1,0:T(8,128)(2,1)S(1)} %get-tuple-element.62), channel_id=1, source_target_pairs={{0,32},{32,0},{64,96},{96,64},{1,33},{33,1},{65,97},{97,65},{2,34}... | collective-permute-start | bytes 1400840 | tf_op jit(solution)/shard_map/ppermute | solution.py:40
  160.0 14.8 %collective-permute-start.22 = (bf16[32,7296]{1,0:T(8,128)(2,1)S(1)}, bf16[32,7296]{1,0:T(8,128)(2,1)S(1)}, u32[]{:S(2)}, u32[]{:S(2)}) collective-permute-start(bf16[32,7296]{1,0:T(8,128)(2,1)S(1)} %get-tuple-element.63), channel_id=1, source_target_pairs={{0,96},{32,64},{64,32},{96,0},{1,97},{33,65},{65,33},{97,1},{2,98}... | collective-permute-start | bytes 1400840 | tf_op jit(solution)/shard_map/ppermute | solution.py:40
  160.0 17.8 %collective-permute-start.28 = (bf16[32,7296]{1,0:T(8,128)(2,1)S(1)}, bf16[32,7296]{1,0:T(8,128)(2,1)S(1)}, u32[]{:S(2)}, u32[]{:S(2)}) collective-permute-start(bf16[32,7296]{1,0:T(8,128)(2,1)S(1)} %get-tuple-element.69), channel_id=1, source_target_pairs={{0,64},{32,96},{64,0},{96,32},{1,65},{33,97},{65,1},{97,33},{2,66}... | collective-permute-start | bytes 1400840 | tf_op jit(solution)/shard_map/ppermute | solution.py:40
  177.3 8.5 %collective-permute-start.30 = (bf16[16,7168]{1,0:T(8,128)(2,1)S(1)}, bf16[16,7168]{1,0:T(8,128)(2,1)S(1)}, u32[]{:S(2)}, u32[]{:S(2)}) collective-permute-start(bf16[16,7168]{1,0:T(8,128)(2,1)S(1)} %get-tuple-element.73), channel_id=1, source_target_pairs={{0,32},{32,0},{64,96},{96,64},{1,33},{33,1},{65,97},{97,65},{2,34}... | collective-permute-start | bytes 688136 | tf_op jit(solution)/shard_map/ppermute | solution.py:40
  177.5 11.4 %collective-permute-start.31 = (bf16[16,7168]{1,0:T(8,128)(2,1)S(1)}, bf16[16,7168]{1,0:T(8,128)(2,1)S(1)}, u32[]{:S(2)}, u32[]{:S(2)}) collective-permute-start(bf16[16,7168]{1,0:T(8,128)(2,1)S(1)} %get-tuple-element.74), channel_id=1, source_target_pairs={{0,96},{32,64},{64,32},{96,0},{1,97},{33,65},{65,33},{97,1},{2,98}... | collective-permute-start | bytes 688136 | tf_op jit(solution)/shard_map/ppermute | solution.py:40
  180.5 9.5 %collective-permute-start.32 = (bf16[16,7168]{1,0:T(8,128)(2,1)S(1)}, bf16[16,7168]{1,0:T(8,128)(2,1)S(1)}, u32[]{:S(2)}, u32[]{:S(2)}) collective-permute-start(bf16[16,7168]{1,0:T(8,128)(2,1)S(1)} %get-tuple-element.75), channel_id=1, source_target_pairs={{0,64},{32,96},{64,0},{96,32},{1,65},{33,97},{65,1},{97,33},{2,66}... | collective-permute-start | bytes 688136 | tf_op jit(solution)/shard_map/ppermute | solution.py:40
  184.3 10.6 %collective-permute-start.35 = (bf16[8,7168]{1,0:T(8,128)(2,1)S(1)}, bf16[8,7168]{1,0:T(8,128)(2,1)S(1)}, u32[]{:S(2)}, u32[]{:S(2)}) collective-permute-start(bf16[8,7168]{1,0:T(8,128)(2,1)S(1)} %get-tuple-element.80), channel_id=1, source_target_pairs={{0,32},{32,0},{64,96},{96,64},{1,33},{33,1},{65,97},{97,65},{2,34}... | collective-permute-start | bytes 344072 | tf_op jit(solution)/shard_map/ppermute | solution.py:40
  184.6 10.4 %collective-permute-start.36 = (bf16[8,7168]{1,0:T(8,128)(2,1)S(1)}, bf16[8,7168]{1,0:T(8,128)(2,1)S(1)}, u32[]{:S(2)}, u32[]{:S(2)}) collective-permute-start(bf16[8,7168]{1,0:T(8,128)(2,1)S(1)} %get-tuple-element.81), channel_id=1, source_target_pairs={{0,96},{32,64},{64,32},{96,0},{1,97},{33,65},{65,33},{97,1},{2,98}... | collective-permute-start | bytes 344072 | tf_op jit(solution)/shard_map/ppermute | solution.py:40
  185.9 15.2 %collective-permute-start.26 = (bf16[8,7168]{1,0:T(8,128)(2,1)S(1)}, bf16[8,7168]{1,0:T(8,128)(2,1)S(1)}, u32[]{:S(2)}, u32[]{:S(2)}) collective-permute-start(bf16[8,7168]{1,0:T(8,128)(2,1)S(1)} %get-tuple-element.67), channel_id=1, source_target_pairs={{0,32},{32,0},{64,96},{96,64},{1,33},{33,1},{65,97},{97,65},{2,34}... | collective-permute-start | bytes 344072 | tf_op jit(solution)/shard_map/ppermute | solution.py:40
  188.8 13.7 %collective-permute-start.27 = (bf16[8,7168]{1,0:T(8,128)(2,1)S(1)}, bf16[8,7168]{1,0:T(8,128)(2,1)S(1)}, u32[]{:S(2)}, u32[]{:S(2)}) collective-permute-start(bf16[8,7168]{1,0:T(8,128)(2,1)S(1)} %get-tuple-element.68), channel_id=1, source_target_pairs={{0,96},{32,64},{64,32},{96,0},{1,97},{33,65},{65,33},{97,1},{2,98}... | collective-permute-start | bytes 344072 | tf_op jit(solution)/shard_map/ppermute | solution.py:40
  189.9 7.4 %collective-permute-start.37 = (bf16[8,7168]{1,0:T(8,128)(2,1)S(1)}, bf16[8,7168]{1,0:T(8,128)(2,1)S(1)}, u32[]{:S(2)}, u32[]{:S(2)}) collective-permute-start(bf16[8,7168]{1,0:T(8,128)(2,1)S(1)} %get-tuple-element.82), channel_id=1, source_target_pairs={{0,64},{32,96},{64,0},{96,32},{1,65},{33,97},{65,1},{97,33},{2,66}... | collective-permute-start | bytes 344072 | tf_op jit(solution)/shard_map/ppermute | solution.py:40
  194.9 19.1 %collective-permute-start.33 = (bf16[32,3584]{1,0:T(8,128)(2,1)S(1)}, bf16[32,3584]{1,0:T(8,128)(2,1)S(1)}, u32[]{:S(2)}, u32[]{:S(2)}) collective-permute-start(bf16[32,3584]{1,0:T(8,128)(2,1)S(1)} %get-tuple-element.76), channel_id=1, source_target_pairs={{0,2},{2,4},{4,6},{6,8},{8,10},{10,12},{12,14},{14,16},{16,18},{18... | collective-permute-start | bytes 688136 | tf_op jit(solution)/shard_map/ppermute | solution.py:44
  195.0 18.9 %collective-permute-start.34 = (bf16[32,3584]{1,0:T(8,128)(2,1)S(1)}, bf16[32,3584]{1,0:T(8,128)(2,1)S(1)}, u32[]{:S(2)}, u32[]{:S(2)}) collective-permute-start(bf16[32,3584]{1,0:T(8,128)(2,1)S(1)} %get-tuple-element.77), channel_id=1, source_target_pairs={{0,30},{2,0},{4,2},{6,4},{8,6},{10,8},{12,10},{14,12},{16,14},{18,... | collective-permute-start | bytes 688136 | tf_op jit(solution)/shard_map/ppermute | solution.py:44
  197.3 8.0 %collective-permute-start.29 = (bf16[8,7168]{1,0:T(8,128)(2,1)S(1)}, bf16[8,7168]{1,0:T(8,128)(2,1)S(1)}, u32[]{:S(2)}, u32[]{:S(2)}) collective-permute-start(bf16[8,7168]{1,0:T(8,128)(2,1)S(1)} %get-tuple-element.70), channel_id=1, source_target_pairs={{0,64},{32,96},{64,0},{96,32},{1,65},{33,97},{65,1},{97,33},{2,66}... | collective-permute-start | bytes 344072 | tf_op jit(solution)/shard_map/ppermute | solution.py:40
  201.1 12.9 %collective-permute-start.38 = (bf16[32,1792]{1,0:T(8,128)(2,1)S(1)}, bf16[32,1792]{1,0:T(8,128)(2,1)S(1)}, u32[]{:S(2)}, u32[]{:S(2)}) collective-permute-start(bf16[32,1792]{1,0:T(8,128)(2,1)S(1)} %get-tuple-element.83), channel_id=1, source_target_pairs={{0,4},{2,6},{4,8},{6,10},{8,12},{10,14},{12,16},{14,18},{16,20},{1... | collective-permute-start | bytes 344072 | tf_op jit(solution)/shard_map/ppermute | solution.py:44
  202.5 11.4 %collective-permute-start.39 = (bf16[32,1792]{1,0:T(8,128)(2,1)S(1)}, bf16[32,1792]{1,0:T(8,128)(2,1)S(1)}, u32[]{:S(2)}, u32[]{:S(2)}) collective-permute-start(bf16[32,1792]{1,0:T(8,128)(2,1)S(1)} %get-tuple-element.84), channel_id=1, source_target_pairs={{0,28},{2,30},{4,0},{6,2},{8,4},{10,6},{12,8},{14,10},{16,12},{18,... | collective-permute-start | bytes 344072 | tf_op jit(solution)/shard_map/ppermute | solution.py:44
  214.2 11.4 %collective-permute-start.40 = (bf16[8,3584]{1,0:T(8,128)(2,1)S(1)}, bf16[8,3584]{1,0:T(8,128)(2,1)S(1)}, u32[]{:S(2)}, u32[]{:S(2)}) collective-permute-start(bf16[8,3584]{1,0:T(8,128)(2,1)S(1)} %get-tuple-element.86), channel_id=1, source_target_pairs={{0,8},{8,0},{16,24},{24,16},{1,9},{9,1},{17,25},{25,17},{2,10},{10... | collective-permute-start | bytes 172040 | tf_op jit(solution)/shard_map/ppermute | solution.py:48
  214.3 13.0 %collective-permute-start.41 = (bf16[8,3584]{1,0:T(8,128)(2,1)S(1)}, bf16[8,3584]{1,0:T(8,128)(2,1)S(1)}, u32[]{:S(2)}, u32[]{:S(2)}) collective-permute-start(bf16[8,3584]{1,0:T(8,128)(2,1)S(1)} %get-tuple-element.87), channel_id=1, source_target_pairs={{0,16},{8,24},{16,0},{24,8},{1,17},{9,25},{17,1},{25,9},{2,18},{10... | collective-permute-start | bytes 172040 | tf_op jit(solution)/shard_map/ppermute | solution.py:48
  220.7 9.3 %collective-permute-start.42 = (bf16[8,3584]{1,0:T(8,128)(2,1)S(1)}, bf16[8,3584]{1,0:T(8,128)(2,1)S(1)}, u32[]{:S(2)}, u32[]{:S(2)}) collective-permute-start(bf16[8,3584]{1,0:T(8,128)(2,1)S(1)} %get-tuple-element.88), channel_id=1, source_target_pairs={{0,24},{8,16},{16,8},{24,0},{1,25},{9,17},{17,9},{25,1},{2,26},{10... | collective-permute-start | bytes 172040 | tf_op jit(solution)/shard_map/ppermute | solution.py:48
